TPU v7x, 16 devices: a whole 2x2x2 slice. The times are simulated.
16 devices in a mesh: dp: 2 (over z), tp: 8 (over y, x, core).
Axes of the slice: x: 2, y: 2, z: 2, core: 2. Of those that a mesh axis runs over, the one named last changes fastest.
Arguments:
- y_one: float32 [16, 256, 1280], P('dp'), parts along dimension 0
- y_two: float32 [16, 256, 1280], P('dp'), parts along dimension 0
- dy_one: float32 [16, 256, 1280], P('dp'), parts along dimension 0
- dy_two: float32 [16, 256, 1280], P('dp'), parts along dimension 0
- saved_one: float32 [1, 16, 256, 1280], P(None, 'dp'), parts along dimension 1
- saved_two: float32 [1, 16, 256, 1280], P(None, 'dp'), parts along dimension 1
- w_qkv: bfloat16 [3, 1280, 3, 16, 80], P(None, None, None, 'tp')
- w_o: bfloat16 [3, 16, 80, 1280], P(None, 'tp')
- w_in: bfloat16 [3, 1280, 5120], P(None, None, 'tp')
- w_out: bfloat16 [3, 5120, 1280], P(None, 'tp')
Outputs:
- output 1: float32 [16, 256, 1280], P('dp'), parts along dimension 0
- output 2: float32 [16, 256, 1280], P('dp'), parts along dimension 0
- output 3: float32 [16, 256, 1280], P('dp'), parts along dimension 0
- output 4: float32 [16, 256, 1280], P('dp'), parts along dimension 0
- output 5: float32 [6, 1280, 3, 16, 80], P('dp', None, None, 'tp'), parts along dimension 0
- output 6: float32 [6, 16, 80, 1280], P('dp', 'tp'), parts along dimension 0
- output 7: float32 [6, 1280, 5120], P('dp', None, 'tp'), parts along dimension 0
- output 8: float32 [6, 5120, 1280], P('dp', 'tp'), parts along dimension 0
There are 2 independent parts. A program takes and returns all parts, laid end to end along the dimension named above; an argument that names none is the same for every part.
All inputs are finite; a program needn't handle non-finite values.
Results may differ from a plain program's by a relative error of at most 0.0121767.
Values are sent between devices in bfloat16 or wider.
A program may use at most 1 GiB of HBM per device.

v0:
```python
import jax
import jax.numpy as jnp
from jax import lax
from jax.experimental import pallas as pl
from jax.experimental.pallas import tpu as pltpu
from jax.sharding import PartitionSpec as P

EPS = 1e-6
BF = jnp.bfloat16
F32 = jnp.float32
GELU_C = 0.7978845608028654
GELU_A = 0.044715


def rms_norm(state):
    return state * lax.rsqrt(jnp.mean(state * state, axis=-1, keepdims=True) + EPS)


def rms_vjp(state, cot):
    rinv = lax.rsqrt(jnp.mean(state * state, axis=-1, keepdims=True) + EPS)
    normed = state * rinv
    return rinv * (cot - normed * jnp.mean(cot * normed, axis=-1, keepdims=True))


def dot(left, right, dims=((1,), (0,))):
    return lax.dot_general(left, right, (dims, ((), ())), preferred_element_type=F32)


def dot_nt(left, right):
    return dot(left, right, ((1,), (1,)))


def dot_tn(left, right):
    return dot(left, right, ((0,), (0,)))


def gelu_val(hid):
    return hid * (0.5 * (1.0 + jnp.tanh(GELU_C * (hid + GELU_A * (hid * hid * hid)))))


def gelu_grad(hid):
    sq = hid * hid
    th = jnp.tanh(GELU_C * (hid + GELU_A * (sq * hid)))
    return 0.5 * (1.0 + th) + hid * (0.5 * (1.0 - th * th)) * (GELU_C * (1.0 + 3.0 * GELU_A * sq))


MIB = 1024 * 1024


def seq_call(body, rank, ins, outs, parts, flops, after=()):
    n_in, n_out = len(ins), len(outs)
    seqs = 8

    def run(parity, previous, after):
        steps = seqs if parity is None else seqs // 2

        def seq(g, rk):
            return g if parity is None else (2 * g + parity) ^ rk[0]

        def spec(kind, shape, layer=0):
            if kind == "row":
                return pl.BlockSpec((None,) + tuple(shape[1:]), lambda g, rk: (seq(g, rk), 0, 0))
            if kind == "col":
                return pl.BlockSpec((shape[0], shape[1] // seqs), lambda g, rk: (0, seq(g, rk)))
            if kind == "layer":
                return pl.BlockSpec((None,) + tuple(shape[1:]), lambda g, rk: (layer, 0, 0))
            return pl.BlockSpec(tuple(shape), lambda g, rk: (0,) * len(shape))

        hidden = list(previous) + list(after)
        in_specs = [spec(kind, arr.shape, *layer) for kind, arr, *layer in ins] + [pl.BlockSpec(memory_space=pl.ANY)] * len(hidden)
        out_specs = [spec(kind, shape) for kind, shape, _ in outs]
        out_shape = [jax.ShapeDtypeStruct(shape, dtype) for _, shape, dtype in outs]
        for rows, width, dtype in parts:
            for _ in range(2):
                out_specs.append(pl.BlockSpec((None, rows, width // 2), lambda g, rk: (g, 0, 0)))
                out_shape.append(jax.ShapeDtypeStruct((steps, rows, width // 2), dtype))

        out_specs.append(pl.BlockSpec((8, 128), lambda g, rk: (0, 0)))
        out_shape.append(jax.ShapeDtypeStruct((8, 128), F32))

        def kernel(rank_ref, *refs):
            refs[-1][...] = jnp.zeros((8, 128), F32)
            in_refs = refs[:n_in]
            out_refs = refs[n_in + len(hidden):n_in + len(hidden) + n_out]
            part_refs = refs[n_in + len(hidden) + n_out:]
            for index, value in enumerate(body(in_refs, out_refs)):
                left, right = part_refs[2 * index:2 * index + 2]
                half = value.shape[-1] // 2
                left[...] = value[:, :half].astype(left.dtype)
                right[...] = value[:, half:].astype(right.dtype)

        share = 1 if parity is None else 2
        nbytes = sum(o.size * o.dtype.itemsize for o in out_shape) // share
        return pl.pallas_call(
        kernel,
        grid_spec=pltpu.PrefetchScalarGridSpec(
            num_scalar_prefetch=1, grid=(steps,), in_specs=in_specs, out_specs=out_specs
        ),
        out_shape=out_shape,
        input_output_aliases={1 + n_in + index: index for index in range(len(previous))},
        compiler_params=pltpu.CompilerParams(dimension_semantics=("arbitrary",), vmem_limit_bytes=60 * MIB),
        cost_estimate=pl.CostEstimate(flops=flops // share, bytes_accessed=nbytes, transcendentals=0),
        )(rank, *[arr for _, arr, *_ in ins], *hidden)

    if not parts:
        return list(run(None, (), after))
    sent = list(run(1, (), after))
    kept = list(run(0, sent[:n_out], [sent[-1]]))
    return kept[:n_out] + [sent[n_out], sent[n_out + 1], kept[n_out], kept[n_out + 1], kept[-1]]


def mlp_fwd(rank, x, w_in, layer):
    seqs, rows, width = x.shape
    inner = w_in.shape[2]

    def body(in_refs, out_refs):
        x_ref, win_ref = in_refs
        a_ref, h_ref, act_ref = out_refs
        a = rms_norm(x_ref[...]).astype(BF)
        a_ref[...] = a
        hid = dot(a, win_ref[...])
        h_ref[...] = hid
        act_ref[...] = gelu_val(hid).astype(BF)
        return ()

    mid = (seqs, rows, inner)
    outs = [("row", x.shape, BF), ("row", mid, F32), ("row", mid, BF)]
    return seq_call(body, rank, [("row", x), ("layer", w_in, layer)], outs, [], 2 * seqs * rows * width * inner)


def mlp_back(rank, d, w_out, hid, w_in, layer, after=()):
    seqs, rows, width = d.shape
    inner = w_out.shape[1]

    def body(in_refs, out_refs):
        d_ref, wout_ref, h_ref, win_ref = in_refs
        dbf_ref, dh_ref = out_refs
        d_bf = d_ref[...].astype(BF)
        dbf_ref[...] = d_bf
        dh = (dot_nt(d_bf, wout_ref[...]) * gelu_grad(h_ref[...])).astype(BF)
        dh_ref[...] = dh
        yield dot_nt(dh, win_ref[...])

    ins = [("row", d), ("layer", w_out, layer), ("row", hid), ("layer", w_in, layer)]
    outs = [("row", d.shape, BF), ("row", hid.shape, BF)]
    return seq_call(body, rank, ins, outs, [(rows, width, BF)], 4 * seqs * rows * width * inner, after)


def mlp_out(rank, act, w_out, layer, after=()):
    rows, width = act.shape[1], w_out.shape[2]

    def body(in_refs, out_refs):
        yield dot(in_refs[0][...], in_refs[1][...])

    return seq_call(body, rank, [("row", act), ("layer", w_out, layer)], [], [(rows, width, F32)], 2 * act.size * width, after)


def mlp_pair_fwd(rank, x, w_in, hi, lo, after=()):
    seqs, rows, width = x.shape
    inner = w_in.shape[2]

    def body(in_refs, out_refs):
        x_ref, whi_ref, wlo_ref = in_refs
        a_ref, hhi_ref, acthi_ref, hlo_ref, actlo_ref = out_refs
        a = rms_norm(x_ref[...]).astype(BF)
        a_ref[...] = a
        for w_ref, h_ref, act_ref in ((wlo_ref, hlo_ref, actlo_ref), (whi_ref, hhi_ref, acthi_ref)):
            hid = dot(a, w_ref[...])
            h_ref[...] = hid
            act_ref[...] = gelu_val(hid).astype(BF)
        return ()

    mid = (seqs, rows, inner)
    outs = [("row", x.shape, BF), ("row", mid, F32), ("row", mid, BF), ("row", mid, F32), ("row", mid, BF)]
    ins = [("row", x), ("layer", w_in, hi), ("layer", w_in, lo)]
    return seq_call(body, rank, ins, outs, [], 4 * seqs * rows * width * inner, after)


def mlp_dhid(rank, d, w_out, layer, hid, after=()):
    seqs, rows, width = d.shape
    inner = w_out.shape[1]

    def body(in_refs, out_refs):
        d_ref, w_ref, h_ref = in_refs
        out_refs[0][...] = (dot_nt(d_ref[...], w_ref[...]) * gelu_grad(h_ref[...])).astype(BF)
        return ()

    ins = [("row", d), ("layer", w_out, layer), ("row", hid)]
    return seq_call(body, rank, ins, [("row", hid.shape, BF)], [], 2 * seqs * rows * width * inner, after)


def mlp_pair_back(rank, d, w_out, hid, dh_hi, w_in, hi, lo, after=()):
    seqs, rows, width = d.shape
    inner = w_out.shape[1]

    def body(in_refs, out_refs):
        d_ref, w_ref, h_ref, dhhi_ref, whi_ref, wlo_ref = in_refs
        dh = (dot_nt(d_ref[...], w_ref[...]) * gelu_grad(h_ref[...])).astype(BF)
        out_refs[0][...] = dh
        yield dot_nt(dhhi_ref[...], whi_ref[...]) + dot_nt(dh, wlo_ref[...])

    ins = [("row", d), ("layer", w_out, lo), ("row", hid), ("row", dh_hi), ("layer", w_in, hi), ("layer", w_in, lo)]
    return seq_call(body, rank, ins, [("row", hid.shape, BF)], [(rows, width, BF)], 6 * seqs * rows * width * inner, after)


def attn(rank, head_dim, w_qkv, w_o, layer, x=None, minus=None, norm=False, qkv=None, d=None, after=()):
    seqs, rows, width = (x if x is not None else d).shape
    cols, inner = w_qkv.shape[1], w_o.shape[1]
    heads = inner // head_dim
    scale = head_dim ** -0.5
    forward, backward = x is not None, d is not None
    ins, outs = [("layer", w_qkv, layer)], []
    if forward:
        ins.append(("row", x))
        if minus is not None:
            ins.append(("row", minus))
            outs.append(("row", x.shape, F32))
        if norm:
            outs.append(("row", x.shape, BF))
        outs.append(("col", (inner, seqs * rows), BF))
        if not backward:
            outs.append(("col", (cols, seqs * rows), BF))
    else:
        ins.append(("col", qkv))
    if backward:
        ins += [("layer", w_o, layer), ("row", d)]
        outs.append(("col", (cols, seqs * rows), BF))

    def body(in_refs, out_refs):
        in_refs, out_refs = list(in_refs), list(out_refs)
        wqkv_ref = in_refs.pop(0)
        if forward:
            value = in_refs.pop(0)[...]
            if minus is not None:
                value = value - in_refs.pop(0)[...]
                out_refs.pop(0)[...] = value
            if norm:
                value = rms_norm(value).astype(BF)
                out_refs.pop(0)[...] = value
            o_ref = out_refs.pop(0)
            qkv_t = dot_nt(wqkv_ref[...], value).astype(BF)
            if not backward:
                out_refs.pop(0)[...] = qkv_t
        else:
            qkv_t = in_refs.pop(0)[...]
        if backward:
            wo_ref, d_ref = in_refs
            dqkv_ref = out_refs.pop(0)
            dheads = dot_nt(wo_ref[...], d_ref[...]).astype(BF)
        pieces = [[], [], []]
        for n in range(heads):
            lo = n * head_dim
            q_t, k_t, v_t = (qkv_t[part * inner + lo:part * inner + lo + head_dim] for part in range(3))
            scores = dot_tn(k_t, q_t) * scale
            expd = jnp.exp(scores - jnp.max(scores, axis=0, keepdims=True))
            probs = expd / jnp.sum(expd, axis=0, keepdims=True)
            probs_bf = probs.astype(BF)
            if forward:
                o_ref[pl.ds(lo, head_dim), :] = dot(v_t, probs_bf).astype(BF)
            if backward:
                dhead = dheads[lo:lo + head_dim]
                d_v = dot_nt(dhead, probs_bf)
                d_probs = dot_tn(v_t, dhead)
                d_scores = (probs * (d_probs - jnp.sum(d_probs * probs, axis=0, keepdims=True)) * scale).astype(BF)
                for part, piece in enumerate((dot(k_t, d_scores), dot_nt(q_t, d_scores), d_v)):
                    pieces[part].append(piece.astype(BF))
        if backward:
            dqkv = jnp.concatenate(pieces[0] + pieces[1] + pieces[2], axis=0)
            dqkv_ref[...] = dqkv
            yield dot_tn(dqkv, wqkv_ref[...])

    flops = 2 * seqs * rows * (width * (cols * (forward + backward) + inner * backward) + rows * inner * (2 * forward + 5 * backward))
    return seq_call(body, rank, ins, outs, [(rows, width, BF)] if backward else [], flops, after)


def attn_value(rank, base, o_all, wo_all, after=()):
    def body(in_refs, out_refs):
        base_ref, o_ref, w_ref = in_refs
        out_refs[0][...] = base_ref[...] - dot_tn(o_ref[...], w_ref[...])
        return ()

    ins = [("row", base), ("col", o_all), ("all", wo_all)]
    return seq_call(body, rank, ins, [("row", base.shape, F32)], [], 2 * base.size * wo_all.shape[0], after)


def emit(rank, array, after=()):
    def body(in_refs, out_refs):
        out_refs[0][...] = in_refs[0][...]
        return ()

    return seq_call(body, rank, [("row", array)], [("row", array.shape, array.dtype)], [], 16 * array.size, after)


def weight_grads(stacks, layers, layer, jobs, after=()):
    steps = 5
    in_specs, out_specs, out_shape, args, flops, vmem = [], [], [], [], 0, 0
    for left, right, split in jobs:
        tokens, n_cols = right.shape
        if split == "rows":
            n_rows = left.shape[1]
            in_specs.append(pl.BlockSpec((tokens, n_rows // steps), lambda g: (0, g)))
            in_specs.append(pl.BlockSpec((tokens, n_cols), lambda g: (0, 0)))
            out_specs.append(pl.BlockSpec((None, n_rows // steps, n_cols), lambda g: (layer, g, 0)))
        else:
            n_rows = left.shape[0]
            in_specs.append(pl.BlockSpec((n_rows, tokens), lambda g: (0, 0)))
            in_specs.append(pl.BlockSpec((tokens, n_cols // steps), lambda g: (0, g)))
            out_specs.append(pl.BlockSpec((None, n_rows, n_cols // steps), lambda g: (layer, 0, g)))
        out_shape.append(jax.ShapeDtypeStruct((layers, n_rows, n_cols), F32))
        args += [left, right]
        flops += 2 * tokens * n_rows * n_cols
        vmem += 4 * (left.size + right.size) + 2 * n_rows * n_cols
    n_jobs = len(jobs)
    aliases = {}
    if stacks[0] is not None:
        aliases = {len(args) + index: index for index in range(n_jobs)}
        args += stacks
    args += list(after)
    in_specs += [pl.BlockSpec(memory_space=pl.ANY)] * (len(args) - 2 * n_jobs)
    out_specs.append(pl.BlockSpec((8, 128), lambda g: (0, 0)))
    out_shape.append(jax.ShapeDtypeStruct((8, 128), F32))

    def kernel(*refs):
        outs = refs[len(args):]
        for index, (_, _, split) in enumerate(jobs):
            left_ref, right_ref = refs[2 * index:2 * index + 2]
            outs[index][...] = (dot_tn if split == "rows" else dot)(left_ref[...], right_ref[...])
        outs[-1][...] = jnp.zeros((8, 128), F32)

    call = pl.pallas_call(
        kernel,
        grid=(steps,),
        in_specs=in_specs,
        out_specs=out_specs,
        out_shape=out_shape,
        input_output_aliases=aliases,
        compiler_params=pltpu.CompilerParams(dimension_semantics=("arbitrary",), vmem_limit_bytes=60 * MIB),
        cost_estimate=pl.CostEstimate(flops=flops, bytes_accessed=vmem, transcendentals=0),
    )
    *stacks, token = call(*args)
    return stacks, token


def permute(array, bit):
    return lax.ppermute(array, "tp", [(idx, idx ^ bit) for idx in range(8)])


def tie(value, tokens):
    return lax.optimization_barrier((value, *tokens))[0] if tokens else value


def sum_cores(parts):
    halves = []
    for send, keep, order in ((parts[0], parts[2], (2, 4)), (parts[1], parts[3], (4, 2))):
        grid = (2, 2) + keep.shape[1:]
        halves.append((keep.reshape(grid), permute(send, 1).reshape(grid), order))
    return halves


def sum_first(halves, begin=()):
    moving, sent = [], []
    for keep, recv, order in halves:
        recv = tie(recv, begin)
        pick = (lambda arr, pos: arr[:, pos]) if order[0] == 2 else (lambda arr, pos: arr[pos])
        away = pick(keep, 1) + pick(recv, 1)
        sent.append(away)
        moving.append((pick(keep, 0) + pick(recv, 0), permute(away, order[0]), order))
    return moving, sent


def received(halves):
    return [recv for _, recv, _ in halves]


def sum_second(moving, fill=()):
    value, sent, final = [], [], []
    for here, recv, order in moving:
        recv = tie(recv, fill)
        sent.append(here[1] + recv[1])
        value.append(here[0] + recv[0])
        final.append(permute(sent[-1], order[1]))
    return value, sent, final


def sum_end(value, final, fill=()):
    halves = [here.astype(F32) + tie(recv, fill).astype(F32) for here, recv in zip(value, final)]
    return jnp.concatenate(halves, axis=-1)[None]


def gather(shard):
    return lax.all_gather(shard, "tp", axis=0, tiled=True)


def solution(mesh):
    act_spec = P("dp", None, None)
    saved_spec = P(None, "dp", None, None)
    weight_specs = (P(None, None, None, "tp", None), P(None, "tp", None, None), P(None, None, "tp"), P(None, "tp", None))
    grad_specs = (P("dp", None, None, "tp", None), P("dp", "tp", None, None), P("dp", None, "tp"), P("dp", "tp", None))

    def per_device(y_one, y_two, dy_one, dy_two, saved_one, saved_two, w_qkv, w_o, w_in, w_out):
        index = lax.axis_index("tp")
        rank = index.astype(jnp.int32).reshape((1,))
        n_layers, width, _, n_heads, head_dim = w_qkv.shape
        tokens = y_one.shape[0] * y_one.shape[1]
        qkv_w = w_qkv.transpose(0, 2, 3, 4, 1).reshape(n_layers, 3 * n_heads * head_dim, width)
        o_w = w_o.reshape(n_layers, n_heads * head_dim, width)

        def shard(full):
            return lax.dynamic_slice_in_dim(full, index, 1, axis=0)

        def flat(full):
            return full.reshape(tokens, full.shape[-1])

        stacks = {"attn": [None] * 2, "in": [None], "out": [None]}

        def attn_grads(layer, a, o_t, dqkv_t, d_bf, after=()):
            jobs = [(dqkv_t, flat(a), "cols"), (o_t, flat(d_bf), "cols")]
            stacks["attn"], token = weight_grads(stacks["attn"], n_layers, layer, jobs, after)
            return token

        def mlp_grads(layer, a, act, dh, d_bf, after=()):
            stacks["in"], first = weight_grads(stacks["in"], n_layers, layer, [(flat(a), flat(dh), "rows")], after)
            stacks["out"], second = weight_grads(stacks["out"], n_layers, layer, [(flat(act), flat(d_bf), "rows")], [first])
            return first, second

        top, hi, lo = 2, 1, 0
        s_one, s_two = saved_one[0], saved_two[0]
        wo_all = gather(o_w[lo])
        top_a, h_top, top_act, tok = mlp_fwd(rank, y_one, w_in, top)
        *parts, tok = mlp_out(rank, top_act, w_out, top, [tok])
        sum_out, sent = sum_first(sum_cores(parts))
        d_two_bf, top_dh, *parts, tok = mlp_back(rank, dy_two, w_out, h_top, w_in, top, [tok, *sent])
        sum_g = sum_cores(parts)
        s_a, h_hi, act_hi, h_lo, act_lo, tok = mlp_pair_fwd(rank, s_one, w_in, hi, lo, [tok, *received(sum_g)])
        value, sent, final = sum_second(sum_out, [tok])
        sum_g, sent_g = sum_first(sum_g, sent)
        tok_in, tok = mlp_grads(top, top_a, top_act, top_dh, d_two_bf, [tok, *sent, *sent_g])
        x_two_top = shard(y_two) - sum_end(value, final, [tok_in])
        f_top = gather(rms_norm(x_two_top).astype(BF))
        value, sent, final = sum_second(sum_g, [tok])
        *parts, tok = mlp_out(rank, act_lo, w_out, lo, [tok, *sent])
        back = sum_end(value, final, [tok])
        d_one = shard(dy_one) + rms_vjp(shard(y_one), back)
        d_one_bf = gather(d_one.astype(BF))
        sum_out, sent = sum_first(sum_cores(parts), [back])
        f_hi, o_hi, qkv_hi, tok = attn(rank, head_dim, qkv_w, o_w, hi, x=s_two, norm=True, after=[tok, wo_all, *sent])
        value, sent, final = sum_second(sum_out, [tok])
        o_top, qkv_top, tok = attn(rank, head_dim, qkv_w, o_w, top, x=f_top, after=[tok, *sent])
        g_sum = sum_end(value, final, [tok])
        g_full = gather(g_sum)
        x_two = shard(s_two) - g_sum
        dqkv_top, *parts, tok = attn(rank, head_dim, qkv_w, o_w, top, qkv=qkv_top, d=d_one_bf, after=[tok, g_sum])
        sum_top, sent = sum_first(sum_cores(parts))
        dqkv_hi, *parts, tok = attn(rank, head_dim, qkv_w, o_w, hi, qkv=qkv_hi, d=d_one_bf, after=[tok, *sent])
        sum_hi = sum_cores(parts)
        value, sent, final = sum_second(sum_top, [tok, *received(sum_hi)])
        sum_hi, sent_hi = sum_first(sum_hi, sent)
        tok = attn_grads(top, f_top, o_top, dqkv_top, d_one_bf, [tok, *sent, *sent_hi])
        d_two = shard(dy_two) + rms_vjp(x_two_top, sum_end(value, final, [tok]))
        d_two_hi_bf = gather(d_two.astype(BF))
        value, sent, final = sum_second(sum_hi, [tok])
        tok = attn_grads(hi, f_hi, o_hi, dqkv_hi, d_one_bf, [tok, *sent])
        d_two = d_two + rms_vjp(shard(s_two), sum_end(value, final, [tok]))
        d_two_lo_bf = gather(d_two.astype(BF))
        x_two_full, f_lo, o_lo, qkv_lo, tok = attn(rank, head_dim, qkv_w, o_w, lo, x=s_two, minus=g_full, norm=True, after=[tok])
        o_all = gather(o_lo)
        dh_hi, tok = mlp_dhid(rank, d_two_hi_bf, w_out, hi, h_hi, [tok])
        _, tok = mlp_grads(hi, s_a, act_hi, dh_hi, d_two_hi_bf, [tok])
        dh_lo, *parts, tok = mlp_pair_back(rank, d_two_lo_bf, w_out, h_lo, dh_hi, w_in, hi, lo, [tok])
        sum_g, sent = sum_first(sum_cores(parts))
        tok_in, tok = mlp_grads(lo, s_a, act_lo, dh_lo, d_two_lo_bf, [tok, *sent])
        value, sent, final = sum_second(sum_g, [tok_in])
        d_one = d_one + rms_vjp(shard(s_one), sum_end(value, final))
        d_one_bf = gather(tie(d_one.astype(BF), [o_all]))
        x_one_full, tok = attn_value(rank, s_one, o_all, wo_all, [tok])
        dqkv_lo, *parts, tok = attn(rank, head_dim, qkv_w, o_w, lo, qkv=qkv_lo, d=d_one_bf, after=[tok])
        sum_lo, sent = sum_first(sum_cores(parts))
        tok = attn_grads(lo, f_lo, o_lo, dqkv_lo, d_one_bf, [tok, *sent])
        value, sent, final = sum_second(sum_lo, [tok])
        d_two = d_two + rms_vjp(x_two, sum_end(value, final))
        d_one_full, _ = emit(rank, gather(d_one), [tok])
        grad_qkv = stacks["attn"][0].reshape(n_layers, 3, n_heads, head_dim, width).transpose(0, 4, 1, 2, 3)
        grad_o = stacks["attn"][1].reshape(w_o.shape)
        return (x_one_full, x_two_full, d_one_full, gather(d_two), grad_qkv, grad_o, stacks["in"][0], stacks["out"][0])

    return jax.shard_map(
        per_device,
        mesh=mesh,
        in_specs=(act_spec,) * 4 + (saved_spec,) * 2 + weight_specs,
        out_specs=(act_spec,) * 4 + grad_specs,
        check_vma=False,
    )
```

profile of v0, /device:TPU:0, one launch (start us, length us, event | category | flops | bytes accessed | tf_op | source)
XLA Modules:
  0.0 702.1 jit_solution(6321327602684919248)
XLA Ops:
  7.2 13.6 %shard_map.161 = (bf16[8,256,1280]{2,1,0:T(8,128)(2,1)}, f32[8,256,640]{2,1,0:T(8,128)}, bf16[8,256,640]{2,1,0:T(8,128)(2,1)}, f32[8,128]{1,0:T(8,128)}) custom-call(s32[1]{0:T(128)} %bitcast.rank_ref, f32[8,256,1280]{2,1,0:T(8,128)} %refs_0_.3, bf16[3,1280,640]{2,1,0:T(8,128)(2,1)} %refs_5_.3), custom_call_target="tpu_custom_call" | custom-call | flops 3355443200 | bytes 13111296 | tf_op jit(solution)/shard_map/pallas_call | solution.py:94
  20.9 5.7 shard_map.162
  29.2 5.8 shard_map.163
  36.4 4.2 slice_add_fusion.3
  40.6 3.1 slice_add_fusion.2
  43.8 9.7 %shard_map.164 = (bf16[8,256,1280]{2,1,0:T(8,128)(2,1)}, bf16[8,256,640]{2,1,0:T(8,128)(2,1)}, bf16[4,256,640]{2,1,0:T(8,128)(2,1)}, bf16[4,256,640]{2,1,0:T(8,128)(2,1)}, f32[8,128]{1,0:T(8,128)}) custom-call(s32[1]{0:T(128)} %bitcast.rank_ref, f32[8,256,1280]{2,1,0:T(8,128)} %refs_0_.5, bf16[3,640,1280]{2,1,0:T(8,128)(2,1)} %refs_1_.21, ...), custom_call_target="tpu_custom_call" | custom-call | flops 3355443200 | bytes 5244928 | tf_op jit(solution)/shard_map/pallas_call | solution.py:94
  54.0 2.5 collective-permute-start.4
  58.0 9.6 %shard_map.165 = (bf16[8,256,1280]{2,1,0:T(8,128)(2,1)}, bf16[8,256,640]{2,1,0:T(8,128)(2,1)}, bf16[4,256,640]{2,1,0:T(8,128)(2,1)}, bf16[4,256,640]{2,1,0:T(8,128)(2,1)}, f32[8,128]{1,0:T(8,128)}) custom-call(s32[1]{0:T(128)} %bitcast.rank_ref, f32[8,256,1280]{2,1,0:T(8,128)} %refs_0_.5, ...), custom_call_target="tpu_custom_call", output_to_operand_aliasing={{0}: (5, {}), {1}: (6, {})} | custom-call | flops 3355443200 | bytes 5244928 | tf_op jit(solution)/shard_map/pallas_call | solution.py:94
  67.7 16.5 %shard_map.166 = (bf16[8,256,1280]{2,1,0:T(8,128)(2,1)}, f32[8,256,640]{2,1,0:T(8,128)}, bf16[8,256,640]{2,1,0:T(8,128)(2,1)}, f32[8,256,640]{2,1,0:T(8,128)}, b...) custom-call(s32[1]{0:T(128)} %bitcast.rank_ref, f32[8,256,1280]{2,1,0:T(8,128)} %bitcast.366, ...), custom_call_target="tpu_custom_call" | custom-call | flops 6710886400 | bytes 20975616 | tf_op jit(solution)/shard_map/pallas_call | solution.py:94
  84.1 3.3 collective-permute-done.4
  87.4 2.6 fusion.23
  94.5 2.6 bitcast_add_fusion.4
  97.0 8.9 %shard_map.167 = (f32[3,1280,640]{2,1,0:T(8,128)}, f32[8,128]{1,0:T(8,128)}) custom-call(bf16[2048,1280]{1,0:T(8,128)(2,1)} %bitcast.373, bf16[2048,640]{1,0:T(8,128)(2,1)} %bitcast.358, f32[8,128]{1,0:T(8,128)} %get-tuple-element.160.refs_2_, f32[256,640]{1,0:T(8,128)} %get-tuple-element.318.refs_3_, f32[256,640]{1,0:T(8,128)} %get-tuple-element.317.refs_4_, ...), custom_call_target="tpu_custom_call" | custom-call | flops 3355443200 | bytes 17367040 | tf_op jit(solution)/shard_map/pallas_call | solution.py:340
  117.2 9.2 %shard_map.168 = (f32[3,640,1280]{2,1,0:T(8,128)}, f32[8,128]{1,0:T(8,128)}) custom-call(bf16[2048,640]{1,0:T(8,128)(2,1)} %bitcast.349, bf16[2048,1280]{1,0:T(8,128)(2,1)} %bitcast.355, f32[8,128]{1,0:T(8,128)} %get-tuple-element.167.refs_2_), custom_call_target="tpu_custom_call" | custom-call | flops 3355443200 | bytes 17367040 | tf_op jit(solution)/shard_map/pallas_call | solution.py:340
  126.5 9.9 %collective-permute-done.7 = bf16[2,256,640]{2,1,0:T(8,128)(2,1)S(1)} collective-permute-done((bf16[2,256,640]{2,1,0:T(8,128)(2,1)}, bf16[2,256,640]{2,1,0:T(8,128)(2,1)S(1)}, u32[]{:S(2)}, u32[]{:S(2)}) %collective-permute-start.7) | collective-permute-done | bytes 655392 | tf_op jit(solution)/shard_map/ppermute | solution.py:345
  141.0 5.8 shard_map.169
  146.8 5.8 shard_map.170
  157.5 3.4 fusion.66
  161.5 4.6 collective-permute-done.8
  166.1 3.7 collective-permute-done.12
  169.9 3.4 slice_add_fusion.1
  178.3 15.1 %shard_map.171 = (bf16[8,256,1280]{2,1,0:T(8,128)(2,1)}, bf16[160,2048]{1,0:T(8,128)(2,1)}, bf16[480,2048]{1,0:T(8,128)(2,1)}, f32[8,128]{1,0:T(8,128)}) custom-call(s32[1]{0:T(128)} %bitcast.rank_ref, bf16[3,480,1280]{2,1,0:T(8,128)(2,1)} %bitcast.321, f32[8,256,1280]{2,1,0:T(8,128)} %bitcast.332, f32[8,128]{1,0:T(8,128)} %get-tuple-element.174.refs_2_, ...), custom_call_target="tpu_custom_call" | custom-call | flops 2852126720 | bytes 7868416 | tf_op jit(solution)/shard_map/pallas_call | solution.py:94
  193.4 27.4 %collective-permute-done.11 = f32[2,256,640]{2,1,0:T(8,128)} collective-permute-done((f32[2,256,640]{2,1,0:T(8,128)S(1)}, f32[2,256,640]{2,1,0:T(8,128)}, u32[]{:S(2)}, u32[]{:S(2)}) %collective-permute-start.11) | collective-permute-done | bytes 1310752 | tf_op jit(solution)/shard_map/ppermute | solution.py:345
  227.9 13.0 %shard_map.172 = (bf16[160,2048]{1,0:T(8,128)(2,1)}, bf16[480,2048]{1,0:T(8,128)(2,1)}, f32[8,128]{1,0:T(8,128)}) custom-call(s32[1]{0:T(128)} %bitcast.rank_ref, bf16[3,480,1280]{2,1,0:T(8,128)(2,1)} %bitcast.322, bf16[8,256,1280]{2,1,0:T(8,128)(2,1)} %all-gather.14.cloned.1.call-done.refs_1_, f32[8,128]{1,0:T(8,128)} %get-tuple-element.181.refs_2_, ...), custom_call_target="tpu_custom_call" | custom-call | flops 2852126720 | bytes 2625536 | tf_op jit(solution)/shard_map/pallas_call | solution.py:94
  248.2 11.1 %shard_map.173 = (bf16[480,2048]{1,0:T(8,128)(2,1)}, bf16[4,256,640]{2,1,0:T(8,128)(2,1)}, bf16[4,256,640]{2,1,0:T(8,128)(2,1)}, f32[8,128]{1,0:T(8,128)}) custom-call(s32[1]{0:T(128)} %bitcast.rank_ref, bf16[3,480,1280]{2,1,0:T(8,128)(2,1)} %bitcast.323, bf16[480,2048]{1,0:T(8,128)(2,1)} %get-tuple-element.190.refs_1_, bf16[3,160,1280]{2,1,0:T(8,128)(2,1)} %bitcast.334, ...), custom_call_target="tpu_custom_call" | custom-call | flops 2097152000 | bytes 2295808 | tf_op jit(solution)/shard_map/pallas_call | solution.py:94
  259.9 11.1 %shard_map.174 = (bf16[480,2048]{1,0:T(8,128)(2,1)}, bf16[4,256,640]{2,1,0:T(8,128)(2,1)}, bf16[4,256,640]{2,1,0:T(8,128)(2,1)}, f32[8,128]{1,0:T(8,128)}) custom-call(s32[1]{0:T(128)} %bitcast.rank_ref, bf16[3,480,1280]{2,1,0:T(8,128)(2,1)} %bitcast.324, bf16[480,2048]{1,0:T(8,128)(2,1)} %get-tuple-element.190.refs_1_, ...), custom_call_target="tpu_custom_call", output_to_operand_aliasing={{0}: (5, {})} | custom-call | flops 2097152000 | bytes 2295808 | tf_op jit(solution)/shard_map/pallas_call | solution.py:94
  271.0 3.0 slice_add_fusion.17
  273.9 3.0 slice_add_fusion.16
  276.9 11.2 %shard_map.175 = (bf16[480,2048]{1,0:T(8,128)(2,1)}, bf16[4,256,640]{2,1,0:T(8,128)(2,1)}, bf16[4,256,640]{2,1,0:T(8,128)(2,1)}, f32[8,128]{1,0:T(8,128)}) custom-call(s32[1]{0:T(128)} %bitcast.rank_ref, bf16[3,480,1280]{2,1,0:T(8,128)(2,1)} %bitcast.325, bf16[480,2048]{1,0:T(8,128)(2,1)} %get-tuple-element.189.refs_1_, bf16[3,160,1280]{2,1,0:T(8,128)(2,1)} %bitcast.336, ...), custom_call_target="tpu_custom_call" | custom-call | flops 2097152000 | bytes 2295808 | tf_op jit(solution)/shard_map/pallas_call | solution.py:94
  291.0 11.3 %shard_map.176 = (bf16[480,2048]{1,0:T(8,128)(2,1)}, bf16[4,256,640]{2,1,0:T(8,128)(2,1)}, bf16[4,256,640]{2,1,0:T(8,128)(2,1)}, f32[8,128]{1,0:T(8,128)}) custom-call(s32[1]{0:T(128)} %bitcast.rank_ref, bf16[3,480,1280]{2,1,0:T(8,128)(2,1)} %bitcast.326, bf16[480,2048]{1,0:T(8,128)(2,1)} %get-tuple-element.189.refs_1_, ...), custom_call_target="tpu_custom_call", output_to_operand_aliasing={{0}: (5, {})} | custom-call | flops 2097152000 | bytes 2295808 | tf_op jit(solution)/shard_map/pallas_call | solution.py:94
  302.3 16.8 %collective-permute-done.23 = bf16[2,256,640]{2,1,0:T(8,128)(2,1)} collective-permute-done((bf16[2,256,640]{2,1,0:T(8,128)(2,1)}, bf16[2,256,640]{2,1,0:T(8,128)(2,1)}, u32[]{:S(2)}, u32[]{:S(2)}) %collective-permute-start.23) | collective-permute-done | bytes 655392 | tf_op jit(solution)/shard_map/ppermute | solution.py:345
  324.2 2.7 bitcast_add_fusion.2
  326.9 2.6 slice_add_fusion.14
  329.5 9.6 %shard_map.177 = (f32[3,480,1280]{2,1,0:T(8,128)}, f32[3,160,1280]{2,1,0:T(8,128)}, f32[8,128]{1,0:T(8,128)}) custom-call(bf16[480,2048]{1,0:T(8,128)(2,1)} %get-tuple-element.203.refs_0_, bf16[2048,1280]{1,0:T(8,128)(2,1)} %bitcast.356, bf16[160,2048]{1,0:T(8,128)(2,1)} %get-tuple-element.204.refs_2_, bf16[2048,1280]{1,0:T(8,128)(2,1)} %bitcast.330, ...), custom_call_target="tpu_custom_call" | custom-call | flops 3355443200 | bytes 27852800 | tf_op jit(solution)/shard_map/pallas_call | solution.py:340
  341.9 3.0 fusion.64
  348.5 19.4 %collective-permute-done.25 = bf16[2,256,640]{2,1,0:T(8,128)(2,1)S(1)} collective-permute-done((bf16[2,256,640]{2,1,0:T(8,128)(2,1)S(1)}, bf16[2,256,640]{2,1,0:T(8,128)(2,1)S(1)}, u32[]{:S(2)}, u32[]{:S(2)}) %collective-permute-start.25) | collective-permute-done | bytes 655392 | tf_op jit(solution)/shard_map/ppermute | solution.py:345
  371.5 9.6 %shard_map.178 = (f32[3,480,1280]{2,1,0:T(8,128)}, f32[3,160,1280]{2,1,0:T(8,128)}, f32[8,128]{1,0:T(8,128)}) custom-call(bf16[480,2048]{1,0:T(8,128)(2,1)} %get-tuple-element.200.refs_0_, bf16[2048,1280]{1,0:T(8,128)(2,1)} %bitcast.357, bf16[160,2048]{1,0:T(8,128)(2,1)} %get-tuple-element.202.refs_2_, ...), custom_call_target="tpu_custom_call", output_to_operand_aliasing={{0}: (4, {}), {1}: (5, {})} | custom-call | flops 3355443200 | bytes 27852800 | tf_op jit(solution)/shard_map/pallas_call | solution.py:340
  388.9 2.5 fusion.65
  391.5 18.2 %shard_map.179 = (f32[8,256,1280]{2,1,0:T(8,128)}, bf16[8,256,1280]{2,1,0:T(8,128)(2,1)}, bf16[160,2048]{1,0:T(8,128)(2,1)}, bf16[480,2048]{1,0:T(8,128)(2,1)}, f32[8,128]{1,0:T(8,128)}) custom-call(s32[1]{0:T(128)} %bitcast.rank_ref, bf16[3,480,1280]{2,1,0:T(8,128)(2,1)} %bitcast.327, f32[8,256,1280]{2,1,0:T(8,128)} %bitcast.333, ...), custom_call_target="tpu_custom_call" | custom-call | flops 2852126720 | bytes 18354176 | tf_op jit(solution)/shard_map/pallas_call | solution.py:94
  410.0 11.4 %shard_map.180 = (bf16[8,256,640]{2,1,0:T(8,128)(2,1)}, f32[8,128]{1,0:T(8,128)}) custom-call(s32[1]{0:T(128)} %bitcast.rank_ref, bf16[8,256,1280]{2,1,0:T(8,128)(2,1)} %all-gather.22.cloned.1.call-done.refs_0_, bf16[3,640,1280]{2,1,0:T(8,128)(2,1)} %refs_1_.21, f32[8,256,640]{2,1,0:T(8,128)} %get-tuple-element.228.refs_2_, f32[8,128]{1,0:T(8,128)} %get-tuple-element.229.refs_3_), custom_call_target="tpu_custom_call" | custom-call | flops 3355443200 | bytes 2625536 | tf_op jit(solution)/shard_map/pallas_call | solution.py:94
  421.4 9.0 %shard_map.181 = (f32[3,1280,640]{2,1,0:T(8,128)}, f32[8,128]{1,0:T(8,128)}) custom-call(bf16[2048,1280]{1,0:T(8,128)(2,1)} %bitcast.346, bf16[2048,640]{1,0:T(8,128)(2,1)} %bitcast.343, f32[3,1280,640]{2,1,0:T(8,128)} %get-tuple-element.231.refs_2_, f32[8,128]{1,0:T(8,128)} %get-tuple-element.232.refs_3_), custom_call_target="tpu_custom_call", output_to_operand_aliasing={{0}: (2, {})} | custom-call | flops 3355443200 | bytes 17367040 | tf_op jit(solution)/shard_map/pallas_call | solution.py:340
  430.4 8.9 %shard_map.182 = (f32[3,640,1280]{2,1,0:T(8,128)}, f32[8,128]{1,0:T(8,128)}) custom-call(bf16[2048,640]{1,0:T(8,128)(2,1)} %bitcast.359, bf16[2048,1280]{1,0:T(8,128)(2,1)} %bitcast.345, f32[3,640,1280]{2,1,0:T(8,128)} %get-tuple-element.226.refs_2_, f32[8,128]{1,0:T(8,128)} %get-tuple-element.233.refs_3_), custom_call_target="tpu_custom_call", output_to_operand_aliasing={{0}: (2, {})} | custom-call | flops 3355443200 | bytes 17367040 | tf_op jit(solution)/shard_map/pallas_call | solution.py:340
  439.2 12.9 %shard_map.183 = (bf16[8,256,640]{2,1,0:T(8,128)(2,1)}, bf16[4,256,640]{2,1,0:T(8,128)(2,1)}, bf16[4,256,640]{2,1,0:T(8,128)(2,1)}, f32[8,128]{1,0:T(8,128)}) custom-call(s32[1]{0:T(128)} %bitcast.rank_ref, bf16[8,256,1280]{2,1,0:T(8,128)(2,1)} %all-gather.20.cloned.1.call-done.refs_0_, bf16[3,640,1280]{2,1,0:T(8,128)(2,1)} %refs_1_.21, ...), custom_call_target="tpu_custom_call" | custom-call | flops 5033164800 | bytes 2623488 | tf_op jit(solution)/shard_map/pallas_call | solution.py:94
  452.6 13.4 %shard_map.184 = (bf16[8,256,640]{2,1,0:T(8,128)(2,1)}, bf16[4,256,640]{2,1,0:T(8,128)(2,1)}, bf16[4,256,640]{2,1,0:T(8,128)(2,1)}, f32[8,128]{1,0:T(8,128)}) custom-call(s32[1]{0:T(128)} %bitcast.rank_ref, bf16[8,256,1280]{2,1,0:T(8,128)(2,1)} %all-gather.20.cloned.1.call-done.refs_0_, ...), custom_call_target="tpu_custom_call", output_to_operand_aliasing={{0}: (7, {})} | custom-call | flops 5033164800 | bytes 2623488 | tf_op jit(solution)/shard_map/pallas_call | solution.py:94
  466.0 2.9 slice_add_fusion.11
  470.8 2.5 slice_add_fusion.10
  475.4 9.0 %shard_map.185 = (f32[3,1280,640]{2,1,0:T(8,128)}, f32[8,128]{1,0:T(8,128)}) custom-call(bf16[2048,1280]{1,0:T(8,128)(2,1)} %bitcast.347, bf16[2048,640]{1,0:T(8,128)(2,1)} %bitcast.350, f32[3,1280,640]{2,1,0:T(8,128)} %get-tuple-element.240.refs_2_, f32[8,128]{1,0:T(8,128)} %get-tuple-element.241.refs_3_, ...), custom_call_target="tpu_custom_call", output_to_operand_aliasing={{0}: (2, {})} | custom-call | flops 3355443200 | bytes 17367040 | tf_op jit(solution)/shard_map/pallas_call | solution.py:340
  488.1 2.9 collective-permute-done.34
  492.2 4.7 collective-permute-done.33
  502.5 2.9 fusion.63
  506.5 8.8 %shard_map.186 = (f32[3,640,1280]{2,1,0:T(8,128)}, f32[8,128]{1,0:T(8,128)}) custom-call(bf16[2048,640]{1,0:T(8,128)(2,1)} %bitcast.344, bf16[2048,1280]{1,0:T(8,128)(2,1)} %bitcast.341, f32[3,640,1280]{2,1,0:T(8,128)} %get-tuple-element.234.refs_2_, f32[8,128]{1,0:T(8,128)} %get-tuple-element.246.refs_3_), custom_call_target="tpu_custom_call", output_to_operand_aliasing={{0}: (2, {})} | custom-call | flops 3355443200 | bytes 17367040 | tf_op jit(solution)/shard_map/pallas_call | solution.py:340
  515.3 16.0 %shard_map.187 = (f32[8,256,1280]{2,1,0:T(8,128)}, f32[8,128]{1,0:T(8,128)}) custom-call(s32[1]{0:T(128)} %bitcast.rank_ref, f32[8,256,1280]{2,1,0:T(8,128)} %bitcast.367, bf16[1280,2048]{1,0:T(8,128)(2,1)} %all-gather.18.cloned.1.call-done.refs_1_, bf16[1280,1280]{1,0:T(8,128)(2,1)} %all-gather.12.cloned.1.call-done.refs_3_.refs_2_, ...), custom_call_target="tpu_custom_call" | custom-call | flops 6710886400 | bytes 10489856 | tf_op jit(solution)/shard_map/pallas_call | solution.py:94
  531.4 10.8 %all-gather.26.cloned.1.call-done.refs_3_ = bf16[8,256,1280]{2,1,0:T(8,128)(2,1)} async-done(((bf16[1,256,1280]{2,1,0:T(8,128)(2,1)}), bf16[8,256,1280]{2,1,0:T(8,128)(2,1)}) %all-gather.26.cloned.1.call-update) | async-done | bytes 5242896 | tf_op jit(solution)/shard_map/all_gather | solution.py:391
  542.2 11.1 %shard_map.188 = (bf16[480,2048]{1,0:T(8,128)(2,1)}, bf16[4,256,640]{2,1,0:T(8,128)(2,1)}, bf16[4,256,640]{2,1,0:T(8,128)(2,1)}, f32[8,128]{1,0:T(8,128)}) custom-call(s32[1]{0:T(128)} %bitcast.rank_ref, bf16[3,480,1280]{2,1,0:T(8,128)(2,1)} %bitcast.328, bf16[480,2048]{1,0:T(8,128)(2,1)} %get-tuple-element.252.refs_1_, bf16[3,160,1280]{2,1,0:T(8,128)(2,1)} %bitcast.338, ...), custom_call_target="tpu_custom_call" | custom-call | flops 2097152000 | bytes 2295808 | tf_op jit(solution)/shard_map/pallas_call | solution.py:94
  553.7 11.1 %shard_map.189 = (bf16[480,2048]{1,0:T(8,128)(2,1)}, bf16[4,256,640]{2,1,0:T(8,128)(2,1)}, bf16[4,256,640]{2,1,0:T(8,128)(2,1)}, f32[8,128]{1,0:T(8,128)}) custom-call(s32[1]{0:T(128)} %bitcast.rank_ref, bf16[3,480,1280]{2,1,0:T(8,128)(2,1)} %bitcast.329, bf16[480,2048]{1,0:T(8,128)(2,1)} %get-tuple-element.252.refs_1_, ...), custom_call_target="tpu_custom_call", output_to_operand_aliasing={{0}: (5, {})} | custom-call | flops 2097152000 | bytes 2295808 | tf_op jit(solution)/shard_map/pallas_call | solution.py:94
  564.8 2.8 slice_add_fusion.7
  569.1 2.5 slice_add_fusion.6
  572.2 9.8 %shard_map.190 = (f32[3,480,1280]{2,1,0:T(8,128)}, f32[3,160,1280]{2,1,0:T(8,128)}, f32[8,128]{1,0:T(8,128)}) custom-call(bf16[480,2048]{1,0:T(8,128)(2,1)} %get-tuple-element.257.refs_0_, bf16[2048,1280]{1,0:T(8,128)(2,1)} %bitcast.354, bf16[160,2048]{1,0:T(8,128)(2,1)} %get-tuple-element.220.refs_2_, ...), custom_call_target="tpu_custom_call", output_to_operand_aliasing={{0}: (4, {}), {1}: (5, {})} | custom-call | flops 3355443200 | bytes 27852800 | tf_op jit(solution)/shard_map/pallas_call | solution.py:340
  582.0 14.6 %collective-permute-done.38 = bf16[2,256,640]{2,1,0:T(8,128)(2,1)} collective-permute-done((bf16[2,256,640]{2,1,0:T(8,128)(2,1)S(1)}, bf16[2,256,640]{2,1,0:T(8,128)(2,1)}, u32[]{:S(2)}, u32[]{:S(2)}) %collective-permute-start.38) | collective-permute-done | bytes 655392 | tf_op jit(solution)/shard_map/ppermute | solution.py:345
  598.8 4.8 collective-permute-done.40
  605.3 11.9 %collective-permute-done.39 = bf16[256,640]{1,0:T(8,128)(2,1)S(1)} collective-permute-done((bf16[256,640]{1,0:T(8,128)(2,1)S(1)}, bf16[256,640]{1,0:T(8,128)(2,1)S(1)}, u32[]{:S(2)}, u32[]{:S(2)}) %collective-permute-start.39) | collective-permute-done | bytes 327712 | tf_op jit(solution)/shard_map/ppermute | solution.py:345
  624.5 10.4 %shard_map.191 = (f32[8,256,1280]{2,1,0:T(8,128)}, f32[8,128]{1,0:T(8,128)}) custom-call(s32[1]{0:T(128)} %bitcast.rank_ref, f32[8,256,1280]{2,1,0:T(8,128)} %all-gather.24.cloned.1.call-done.refs_0_, f32[8,128]{1,0:T(8,128)} %get-tuple-element.266.refs_1_), custom_call_target="tpu_custom_call" | custom-call | flops 41943040 | bytes 10489856 | tf_op jit(solution)/shard_map/pallas_call | solution.py:94
  634.8 51.3 %all-gather.28.cloned.1.call-done = f32[8,256,1280]{2,1,0:T(8,128)} async-done(((f32[1,256,1280]{2,1,0:T(8,128)}), f32[8,256,1280]{2,1,0:T(8,128)}) %all-gather.28.cloned.1.call-update) | async-done | bytes 10485776 | tf_op jit(solution)/shard_map/all_gather | solution.py:391
  686.2 8.8 %copy.47 = f32[8,256,1280]{2,1,0:T(8,128)} copy(f32[8,256,1280]{2,1,0:T(8,128)} %all-gather.28.cloned.1.call-done) | data formatting | bytes 20971520
  (226 shorter events, 107.6 us)
Async XLA Ops:
  7.2 171.1 %all-gather.12.cloned.1.call-start = ((), (), s32[]{:S(2)}) async-start(), calls=%async_computation | async-start | bytes 3686400 | tf_op jit(solution)/shard_map/all_gather | solution.py:391
  26.6 8.3 %collective-permute-start = (f32[4,256,640]{2,1,0:T(8,128)}, f32[4,256,640]{2,1,0:T(8,128)S(1)}, u32[]{:S(2)}, u32[]{:S(2)}) collective-permute-start(f32[4,256,640]{2,1,0:T(8,128)} %get-tuple-element.147), channel_id=1, source_target_pairs={{0,1},{1,0},{2,3},{3,2},{4,5},{5,4},{6,7},{7,6},{8,9},{9,8},{10,11... | collective-permute-start | bytes 7864328 | tf_op jit(solution)/shard_map/ppermute | solution.py:345
  27.3 13.3 %collective-permute-start.1 = (f32[4,256,640]{2,1,0:T(8,128)}, f32[4,256,640]{2,1,0:T(8,128)}, u32[]{:S(2)}, u32[]{:S(2)}) collective-permute-start(f32[4,256,640]{2,1,0:T(8,128)} %get-tuple-element.149), channel_id=1, source_target_pairs={{0,1},{1,0},{2,3},{3,2},{4,5},{5,4},{6,7},{7,6},{8,9},{9,8},{10,11... | collective-permute-start | bytes 7864328 | tf_op jit(solution)/shard_map/ppermute | solution.py:345
  29.1 198.7 %all-gather.14.cloned.1.call-start = ((), (), s32[]{:S(2)}) async-start(), calls=%async_computation.1 | async-start | bytes 5898240 | tf_op jit(solution)/shard_map/all_gather | solution.py:391
  53.5 14.2 %collective-permute-start.2 = (bf16[4,256,640]{2,1,0:T(8,128)(2,1)}, bf16[4,256,640]{2,1,0:T(8,128)(2,1)}, u32[]{:S(2)}, u32[]{:S(2)}) collective-permute-start(bf16[4,256,640]{2,1,0:T(8,128)(2,1)} %get-tuple-element.154), channel_id=1, source_target_pairs={{0,1},{1,0},{2,3},{3,2},{4,5},{5,4},{6,7},{7,6},{8,9},{9,8},{10,11... | collective-permute-start | bytes 3932168 | tf_op jit(solution)/shard_map/ppermute | solution.py:345
  53.8 13.9 %collective-permute-start.3 = (bf16[4,256,640]{2,1,0:T(8,128)(2,1)}, bf16[4,256,640]{2,1,0:T(8,128)(2,1)}, u32[]{:S(2)}, u32[]{:S(2)}) collective-permute-start(bf16[4,256,640]{2,1,0:T(8,128)(2,1)} %get-tuple-element.155), channel_id=1, source_target_pairs={{0,1},{1,0},{2,3},{3,2},{4,5},{5,4},{6,7},{7,6},{8,9},{9,8},{10,11... | collective-permute-start | bytes 3932168 | tf_op jit(solution)/shard_map/ppermute | solution.py:345
  54.0 33.4 %collective-permute-start.4 = (f32[2,256,640]{2,1,0:T(8,128)}, f32[2,256,640]{2,1,0:T(8,128)}, u32[]{:S(2)}, u32[]{:S(2)}) collective-permute-start(f32[2,256,640]{2,1,0:T(8,128)} %get-tuple-element.294.refs_5_), channel_id=1, source_target_pairs={{0,2},{1,3},{2,0},{3,1},{4,6},{5,7},{6,4},{7,5},{8,10},{9,11},{10,... | collective-permute-start | bytes 3932168 | tf_op jit(solution)/shard_map/ppermute | solution.py:345
  56.5 30.9 %collective-permute-start.5 = (f32[2,256,640]{2,1,0:T(8,128)}, f32[2,256,640]{2,1,0:T(8,128)}, u32[]{:S(2)}, u32[]{:S(2)}) collective-permute-start(f32[2,256,640]{2,1,0:T(8,128)} %get-tuple-element.292.refs_6_), channel_id=1, source_target_pairs={{0,4},{1,5},{2,6},{3,7},{4,0},{5,1},{6,2},{7,3},{8,12},{9,13},{10,... | collective-permute-start | bytes 3932168 | tf_op jit(solution)/shard_map/ppermute | solution.py:345
  90.0 16.9 %collective-permute-start.14 = (f32[256,640]{1,0:T(8,128)}, f32[256,640]{1,0:T(8,128)}, u32[]{:S(2)}, u32[]{:S(2)}) collective-permute-start(f32[256,640]{1,0:T(8,128)} %get-tuple-element.318.refs_3_), channel_id=1, source_target_pairs={{0,4},{1,5},{2,6},{3,7},{4,0},{5,1},{6,2},{7,3},{8,12},{9,13},{10,... | collective-permute-start | bytes 1966088 | tf_op jit(solution)/shard_map/ppermute | solution.py:345
  91.5 16.5 %collective-permute-start.15 = (f32[256,640]{1,0:T(8,128)}, f32[256,640]{1,0:T(8,128)}, u32[]{:S(2)}, u32[]{:S(2)}) collective-permute-start(f32[256,640]{1,0:T(8,128)} %get-tuple-element.317.refs_4_), channel_id=1, source_target_pairs={{0,2},{1,3},{2,0},{3,1},{4,6},{5,7},{6,4},{7,5},{8,10},{9,11},{10,... | collective-permute-start | bytes 1966088 | tf_op jit(solution)/shard_map/ppermute | solution.py:345
  113.4 134.8 %all-gather.16.cloned.1.call-start = ((), (), s32[]{:S(2)}) async-start(), calls=%async_computation.2 | async-start | bytes 5898240 | tf_op jit(solution)/shard_map/all_gather | solution.py:391
  113.7 22.6 %collective-permute-start.7 = (bf16[2,256,640]{2,1,0:T(8,128)(2,1)}, bf16[2,256,640]{2,1,0:T(8,128)(2,1)S(1)}, u32[]{:S(2)}, u32[]{:S(2)}) collective-permute-start(bf16[2,256,640]{2,1,0:T(8,128)(2,1)} %get-tuple-element.312.refs_6_), channel_id=1, source_target_pairs={{0,4},{1,5},{2,6},{3,7},{4,0},{5,1},{6,2},{7,3},{8,12},{9,13},{10,... | collective-permute-start | bytes 1966088 | tf_op jit(solution)/shard_map/ppermute | solution.py:345
  114.4 22.5 %collective-permute-start.6 = (bf16[2,256,640]{2,1,0:T(8,128)(2,1)}, bf16[2,256,640]{2,1,0:T(8,128)(2,1)}, u32[]{:S(2)}, u32[]{:S(2)}) collective-permute-start(bf16[2,256,640]{2,1,0:T(8,128)(2,1)} %get-tuple-element.314.refs_5_), channel_id=1, source_target_pairs={{0,2},{1,3},{2,0},{3,1},{4,6},{5,7},{6,4},{7,5},{8,10},{9,11},{10,... | collective-permute-start | bytes 1966088 | tf_op jit(solution)/shard_map/ppermute | solution.py:345
  117.2 22.0 %copy-start.13 = (bf16[2,256,640]{2,1,0:T(8,128)(2,1)S(1)}, bf16[2,256,640]{2,1,0:T(8,128)(2,1)}, u32[]{:S(2)}) copy-start(bf16[2,256,640]{2,1,0:T(8,128)(2,1)} %get-tuple-element.311) | copy-start | bytes 1966084
  137.9 14.6 %collective-permute-start.9 = (bf16[256,640]{1,0:T(8,128)(2,1)S(1)}, bf16[256,640]{1,0:T(8,128)(2,1)}, u32[]{:S(2)}, u32[]{:S(2)}) collective-permute-start(bf16[256,640]{1,0:T(8,128)(2,1)S(1)} %fusion.61.refs_3_), channel_id=1, source_target_pairs={{0,4},{1,5},{2,6},{3,7},{4,0},{5,1},{6,2},{7,3},{8,12},{9,13},{10,... | collective-permute-start | bytes 983048 | tf_op jit(solution)/shard_map/ppermute | solution.py:345
  140.3 14.3 %collective-permute-start.10 = (bf16[256,640]{1,0:T(8,128)(2,1)S(1)}, bf16[256,640]{1,0:T(8,128)(2,1)S(1)}, u32[]{:S(2)}, u32[]{:S(2)}) collective-permute-start(bf16[256,640]{1,0:T(8,128)(2,1)S(1)} %fusion.59.refs_4_), channel_id=1, source_target_pairs={{0,2},{1,3},{2,0},{3,1},{4,6},{5,7},{6,4},{7,5},{8,10},{9,11},{10,... | collective-permute-start | bytes 983048 | tf_op jit(solution)/shard_map/ppermute | solution.py:345
  160.9 230.5 %all-gather.30.cloned.1.call-start = ((), (), s32[]{:S(2)}) async-start(), calls=%async_computation.9 | async-start | bytes 11796480 | tf_op jit(solution)/shard_map/all_gather | solution.py:391
  161.0 5.2 collective-permute-start.8
  161.0 8.9 %collective-permute-start.12 = (f32[4,256,640]{2,1,0:T(8,128)}, f32[4,256,640]{2,1,0:T(8,128)S(1)}, u32[]{:S(2)}, u32[]{:S(2)}) collective-permute-start(f32[4,256,640]{2,1,0:T(8,128)} %get-tuple-element.179), channel_id=1, source_target_pairs={{0,1},{1,0},{2,3},{3,2},{4,5},{5,4},{6,7},{7,6},{8,9},{9,8},{10,11... | collective-permute-start | bytes 7864328 | tf_op jit(solution)/shard_map/ppermute | solution.py:345
  173.3 47.5 %collective-permute-start.11 = (f32[2,256,640]{2,1,0:T(8,128)S(1)}, f32[2,256,640]{2,1,0:T(8,128)}, u32[]{:S(2)}, u32[]{:S(2)}) collective-permute-start(f32[2,256,640]{2,1,0:T(8,128)S(1)} %get-tuple-element.288.refs_4_), channel_id=1, source_target_pairs={{0,2},{1,3},{2,0},{3,1},{4,6},{5,7},{6,4},{7,5},{8,10},{9,11},{10,... | collective-permute-start | bytes 3932168 | tf_op jit(solution)/shard_map/ppermute | solution.py:345
  176.8 44.9 %collective-permute-start.16 = (f32[2,256,640]{2,1,0:T(8,128)}, f32[2,256,640]{2,1,0:T(8,128)}, u32[]{:S(2)}, u32[]{:S(2)}) collective-permute-start(f32[2,256,640]{2,1,0:T(8,128)} %get-tuple-element.289.refs_5_), channel_id=1, source_target_pairs={{0,4},{1,5},{2,6},{3,7},{4,0},{5,1},{6,2},{7,3},{8,12},{9,13},{10,... | collective-permute-start | bytes 3932168 | tf_op jit(solution)/shard_map/ppermute | solution.py:345
  193.4 32.0 %copy-start.4 = (f32[2,256,640]{2,1,0:T(8,128)S(1)}, f32[2,256,640]{2,1,0:T(8,128)}, u32[]{:S(2)}) copy-start(f32[2,256,640]{2,1,0:T(8,128)} %get-tuple-element.290) | copy-start | bytes 3932164
  223.9 16.9 %collective-permute-start.13 = (f32[256,640]{1,0:T(8,128)}, f32[256,640]{1,0:T(8,128)S(1)}, u32[]{:S(2)}, u32[]{:S(2)}) collective-permute-start(f32[256,640]{1,0:T(8,128)} %fusion.18.refs_3_), channel_id=1, source_target_pairs={{0,4},{1,5},{2,6},{3,7},{4,0},{5,1},{6,2},{7,3},{8,12},{9,13},{10,... | collective-permute-start | bytes 1966088 | tf_op jit(solution)/shard_map/ppermute | solution.py:345
  227.4 15.7 %copy-start.3 = (f32[2,1,256,640]{3,2,1,0:T(8,128)S(1)}, f32[2,1,256,640]{3,2,1,0:T(8,128)}, u32[]{:S(2)}) copy-start(f32[2,1,256,640]{3,2,1,0:T(8,128)} %get-tuple-element.287) | copy-start | bytes 3932164
  227.4 15.7 %collective-permute-start.17 = (f32[256,640]{1,0:T(8,128)}, f32[256,640]{1,0:T(8,128)}, u32[]{:S(2)}, u32[]{:S(2)}) collective-permute-start(f32[256,640]{1,0:T(8,128)} %fusion.11.refs_4_), channel_id=1, source_target_pairs={{0,2},{1,3},{2,0},{3,1},{4,6},{5,7},{6,4},{7,5},{8,10},{9,11},{10,... | collective-permute-start | bytes 1966088 | tf_op jit(solution)/shard_map/ppermute | solution.py:345
  247.6 162.4 %all-gather.22.cloned.1.call-start = ((), (), s32[]{:S(2)}) async-start(), calls=%async_computation.5 | async-start | bytes 5898240 | tf_op jit(solution)/shard_map/all_gather | solution.py:391
  259.3 11.6 %collective-permute-start.18 = (bf16[4,256,640]{2,1,0:T(8,128)(2,1)}, bf16[4,256,640]{2,1,0:T(8,128)(2,1)}, u32[]{:S(2)}, u32[]{:S(2)}) collective-permute-start(bf16[4,256,640]{2,1,0:T(8,128)(2,1)} %get-tuple-element.195), channel_id=1, source_target_pairs={{0,1},{1,0},{2,3},{3,2},{4,5},{5,4},{6,7},{7,6},{8,9},{9,8},{10,11... | collective-permute-start | bytes 3932168 | tf_op jit(solution)/shard_map/ppermute | solution.py:345
  259.3 14.6 %collective-permute-start.19 = (bf16[4,256,640]{2,1,0:T(8,128)(2,1)}, bf16[4,256,640]{2,1,0:T(8,128)(2,1)}, u32[]{:S(2)}, u32[]{:S(2)}) collective-permute-start(bf16[4,256,640]{2,1,0:T(8,128)(2,1)} %get-tuple-element.197), channel_id=1, source_target_pairs={{0,1},{1,0},{2,3},{3,2},{4,5},{5,4},{6,7},{7,6},{8,9},{9,8},{10,11... | collective-permute-start | bytes 3932168 | tf_op jit(solution)/shard_map/ppermute | solution.py:345
  276.9 12.6 %copy-start.7 = (bf16[2,256,640]{2,1,0:T(8,128)(2,1)S(1)}, bf16[2,256,640]{2,1,0:T(8,128)(2,1)}, u32[]{:S(2)}) copy-start(bf16[2,256,640]{2,1,0:T(8,128)(2,1)} %get-tuple-element.310.refs_5_) | copy-start | bytes 1966084
  288.1 31.0 %collective-permute-start.21 = (bf16[4,256,640]{2,1,0:T(8,128)(2,1)}, bf16[4,256,640]{2,1,0:T(8,128)(2,1)}, u32[]{:S(2)}, u32[]{:S(2)}) collective-permute-start(bf16[4,256,640]{2,1,0:T(8,128)(2,1)} %get-tuple-element.206), channel_id=1, source_target_pairs={{0,1},{1,0},{2,3},{3,2},{4,5},{5,4},{6,7},{7,6},{8,9},{9,8},{10,11... | collective-permute-start | bytes 3932168 | tf_op jit(solution)/shard_map/ppermute | solution.py:345
  288.1 31.0 %collective-permute-start.22 = (bf16[4,256,640]{2,1,0:T(8,128)(2,1)}, bf16[4,256,640]{2,1,0:T(8,128)(2,1)}, u32[]{:S(2)}, u32[]{:S(2)}) collective-permute-start(bf16[4,256,640]{2,1,0:T(8,128)(2,1)} %get-tuple-element.207), channel_id=1, source_target_pairs={{0,1},{1,0},{2,3},{3,2},{4,5},{5,4},{6,7},{7,6},{8,9},{9,8},{10,11... | collective-permute-start | bytes 3932168 | tf_op jit(solution)/shard_map/ppermute | solution.py:345
  288.6 30.5 %collective-permute-start.23 = (bf16[2,256,640]{2,1,0:T(8,128)(2,1)}, bf16[2,256,640]{2,1,0:T(8,128)(2,1)}, u32[]{:S(2)}, u32[]{:S(2)}) collective-permute-start(bf16[2,256,640]{2,1,0:T(8,128)(2,1)} %get-tuple-element.308.refs_6_), channel_id=1, source_target_pairs={{0,4},{1,5},{2,6},{3,7},{4,0},{5,1},{6,2},{7,3},{8,12},{9,13},{10,... | collective-permute-start | bytes 1966088 | tf_op jit(solution)/shard_map/ppermute | solution.py:345
  289.5 29.6 %collective-permute-start.20 = (bf16[2,256,640]{2,1,0:T(8,128)(2,1)S(1)}, bf16[2,256,640]{2,1,0:T(8,128)(2,1)}, u32[]{:S(2)}, u32[]{:S(2)}) collective-permute-start(bf16[2,256,640]{2,1,0:T(8,128)(2,1)S(1)} %copy-done.7), channel_id=1, source_target_pairs={{0,2},{1,3},{2,0},{3,1},{4,6},{5,7},{6,4},{7,5},{8,10},{9,11},{10,... | collective-permute-start | bytes 1966088 | tf_op jit(solution)/shard_map/ppermute | solution.py:345
  302.3 21.9 %copy-start.23 = (bf16[4,256,640]{2,1,0:T(8,128)(2,1)S(1)}, bf16[4,256,640]{2,1,0:T(8,128)(2,1)}, u32[]{:S(2)}) copy-start(bf16[4,256,640]{2,1,0:T(8,128)(2,1)} %get-tuple-element.212) | copy-start | bytes 3932164
  320.2 6.7 copy-start.27
  322.2 16.8 %collective-permute-start.26 = (bf16[256,640]{1,0:T(8,128)(2,1)}, bf16[256,640]{1,0:T(8,128)(2,1)}, u32[]{:S(2)}, u32[]{:S(2)}) collective-permute-start(bf16[256,640]{1,0:T(8,128)(2,1)} %fusion.55.refs_5_), channel_id=1, source_target_pairs={{0,4},{1,5},{2,6},{3,7},{4,0},{5,1},{6,2},{7,3},{8,12},{9,13},{10,... | collective-permute-start | bytes 983048 | tf_op jit(solution)/shard_map/ppermute | solution.py:345
  323.7 15.4 %collective-permute-start.27 = (bf16[256,640]{1,0:T(8,128)(2,1)S(1)}, bf16[256,640]{1,0:T(8,128)(2,1)}, u32[]{:S(2)}, u32[]{:S(2)}) collective-permute-start(bf16[256,640]{1,0:T(8,128)(2,1)S(1)} %fusion.53.refs_6_), channel_id=1, source_target_pairs={{0,2},{1,3},{2,0},{3,1},{4,6},{5,7},{6,4},{7,5},{8,10},{9,11},{10,... | collective-permute-start | bytes 983048 | tf_op jit(solution)/shard_map/ppermute | solution.py:345
  329.5 9.6 %copy-start.15 = (bf16[2,1,256,640]{3,2,1,0:T(8,128)(2,1)S(1)}, bf16[2,1,256,640]{3,2,1,0:T(8,128)(2,1)}, u32[]{:S(2)}) copy-start(bf16[2,1,256,640]{3,2,1,0:T(8,128)(2,1)} %get-tuple-element.309) | copy-start | bytes 1966084
  344.9 24.5 %copy-start.14 = (bf16[2,1,256,640]{3,2,1,0:T(8,128)(2,1)S(1)}, bf16[2,1,256,640]{3,2,1,0:T(8,128)(2,1)}, u32[]{:S(2)}) copy-start(bf16[2,1,256,640]{3,2,1,0:T(8,128)(2,1)} %get-tuple-element.305) | copy-start | bytes 1966084
  344.9 25.1 %copy-start.12 = (bf16[2,256,640]{2,1,0:T(8,128)(2,1)S(1)}, bf16[2,256,640]{2,1,0:T(8,128)(2,1)}, u32[]{:S(2)}) copy-start(bf16[2,256,640]{2,1,0:T(8,128)(2,1)} %get-tuple-element.303) | copy-start | bytes 1966084
  344.9 94.3 %all-gather.20.cloned.1.call-start = ((), (), s32[]{:S(2)}) async-start(), calls=%async_computation.4 | async-start | bytes 5898240 | tf_op jit(solution)/shard_map/all_gather | solution.py:391
  345.0 23.0 %collective-permute-start.25 = (bf16[2,256,640]{2,1,0:T(8,128)(2,1)S(1)}, bf16[2,256,640]{2,1,0:T(8,128)(2,1)S(1)}, u32[]{:S(2)}, u32[]{:S(2)}) collective-permute-start(bf16[2,256,640]{2,1,0:T(8,128)(2,1)S(1)} %copy-done.6), channel_id=1, source_target_pairs={{0,4},{1,5},{2,6},{3,7},{4,0},{5,1},{6,2},{7,3},{8,12},{9,13},{10,... | collective-permute-start | bytes 1966088 | tf_op jit(solution)/shard_map/ppermute | solution.py:345
  346.6 22.7 %collective-permute-start.24 = (bf16[2,256,640]{2,1,0:T(8,128)(2,1)}, bf16[2,256,640]{2,1,0:T(8,128)(2,1)S(1)}, u32[]{:S(2)}, u32[]{:S(2)}) collective-permute-start(bf16[2,256,640]{2,1,0:T(8,128)(2,1)} %get-tuple-element.306.refs_7_), channel_id=1, source_target_pairs={{0,2},{1,3},{2,0},{3,1},{4,6},{5,7},{6,4},{7,5},{8,10},{9,11},{10,... | collective-permute-start | bytes 1966088 | tf_op jit(solution)/shard_map/ppermute | solution.py:345
  369.4 14.1 %collective-permute-start.28 = (bf16[256,640]{1,0:T(8,128)(2,1)S(1)}, bf16[256,640]{1,0:T(8,128)(2,1)S(1)}, u32[]{:S(2)}, u32[]{:S(2)}) collective-permute-start(bf16[256,640]{1,0:T(8,128)(2,1)S(1)} %fusion.52.refs_7_), channel_id=1, source_target_pairs={{0,4},{1,5},{2,6},{3,7},{4,0},{5,1},{6,2},{7,3},{8,12},{9,13},{10,... | collective-permute-start | bytes 983048 | tf_op jit(solution)/shard_map/ppermute | solution.py:345
  370.3 14.5 %collective-permute-start.29 = (bf16[256,640]{1,0:T(8,128)(2,1)S(1)}, bf16[256,640]{1,0:T(8,128)(2,1)}, u32[]{:S(2)}, u32[]{:S(2)}) collective-permute-start(bf16[256,640]{1,0:T(8,128)(2,1)S(1)} %fusion.50.refs_8_), channel_id=1, source_target_pairs={{0,2},{1,3},{2,0},{3,1},{4,6},{5,7},{6,4},{7,5},{8,10},{9,11},{10,... | collective-permute-start | bytes 983048 | tf_op jit(solution)/shard_map/ppermute | solution.py:345
  391.4 114.1 %all-gather.18.cloned.1.call-start = ((), (), s32[]{:S(2)}) async-start(), calls=%async_computation.3 | async-start | bytes 5898240 | tf_op jit(solution)/shard_map/all_gather | solution.py:391
  409.7 132.4 %all-gather.26.cloned.1.call-start = ((), (), s32[]{:S(2)}) async-start(), calls=%async_computation.7 | async-start | bytes 5898240 | tf_op jit(solution)/shard_map/all_gather | solution.py:391
  452.1 13.9 %collective-permute-start.30 = (bf16[4,256,640]{2,1,0:T(8,128)(2,1)}, bf16[4,256,640]{2,1,0:T(8,128)(2,1)}, u32[]{:S(2)}, u32[]{:S(2)}) collective-permute-start(bf16[4,256,640]{2,1,0:T(8,128)(2,1)} %get-tuple-element.243), channel_id=1, source_target_pairs={{0,1},{1,0},{2,3},{3,2},{4,5},{5,4},{6,7},{7,6},{8,9},{9,8},{10,11... | collective-permute-start | bytes 3932168 | tf_op jit(solution)/shard_map/ppermute | solution.py:345
  452.1 18.7 %collective-permute-start.31 = (bf16[4,256,640]{2,1,0:T(8,128)(2,1)}, bf16[4,256,640]{2,1,0:T(8,128)(2,1)}, u32[]{:S(2)}, u32[]{:S(2)}) collective-permute-start(bf16[4,256,640]{2,1,0:T(8,128)(2,1)} %get-tuple-element.245), channel_id=1, source_target_pairs={{0,1},{1,0},{2,3},{3,2},{4,5},{5,4},{6,7},{7,6},{8,9},{9,8},{10,11... | collective-permute-start | bytes 3932168 | tf_op jit(solution)/shard_map/ppermute | solution.py:345
  468.9 17.1 %collective-permute-start.32 = (bf16[2,256,640]{2,1,0:T(8,128)(2,1)}, bf16[2,256,640]{2,1,0:T(8,128)(2,1)}, u32[]{:S(2)}, u32[]{:S(2)}) collective-permute-start(bf16[2,256,640]{2,1,0:T(8,128)(2,1)} %get-tuple-element.300.refs_4_), channel_id=1, source_target_pairs={{0,2},{1,3},{2,0},{3,1},{4,6},{5,7},{6,4},{7,5},{8,10},{9,11},{10,... | collective-permute-start | bytes 1966088 | tf_op jit(solution)/shard_map/ppermute | solution.py:345
  473.4 17.6 %collective-permute-start.34 = (bf16[2,256,640]{2,1,0:T(8,128)(2,1)}, bf16[2,256,640]{2,1,0:T(8,128)(2,1)}, u32[]{:S(2)}, u32[]{:S(2)}) collective-permute-start(bf16[2,256,640]{2,1,0:T(8,128)(2,1)} %get-tuple-element.302.refs_5_), channel_id=1, source_target_pairs={{0,4},{1,5},{2,6},{3,7},{4,0},{5,1},{6,2},{7,3},{8,12},{9,13},{10,... | collective-permute-start | bytes 1966088 | tf_op jit(solution)/shard_map/ppermute | solution.py:345
  487.0 9.9 %collective-permute-start.33 = (bf16[256,640]{1,0:T(8,128)(2,1)S(1)}, bf16[256,640]{1,0:T(8,128)(2,1)S(1)}, u32[]{:S(2)}, u32[]{:S(2)}) collective-permute-start(bf16[256,640]{1,0:T(8,128)(2,1)S(1)} %fusion.41), channel_id=1, source_target_pairs={{0,4},{1,5},{2,6},{3,7},{4,0},{5,1},{6,2},{7,3},{8,12},{9,13},{10,... | collective-permute-start | bytes 983048 | tf_op jit(solution)/shard_map/ppermute | solution.py:345
  491.0 8.7 %copy-start.19 = (bf16[2,256,640]{2,1,0:T(8,128)(2,1)S(1)}, bf16[2,256,640]{2,1,0:T(8,128)(2,1)}, u32[]{:S(2)}) copy-start(bf16[2,256,640]{2,1,0:T(8,128)(2,1)} %get-tuple-element.301) | copy-start | bytes 1966084
  492.1 7.5 %collective-permute-start.35 = (bf16[256,640]{1,0:T(8,128)(2,1)S(1)}, bf16[256,640]{1,0:T(8,128)(2,1)S(1)}, u32[]{:S(2)}, u32[]{:S(2)}) collective-permute-start(bf16[256,640]{1,0:T(8,128)(2,1)S(1)} %fusion.38), channel_id=1, source_target_pairs={{0,2},{1,3},{2,0},{3,1},{4,6},{5,7},{6,4},{7,5},{8,10},{9,11},{10,... | collective-permute-start | bytes 983048 | tf_op jit(solution)/shard_map/ppermute | solution.py:345
  505.5 119.0 %all-gather.24.cloned.1.call-start = ((), (), s32[]{:S(2)}) async-start(), calls=%async_computation.6 | async-start | bytes 11796480 | tf_op jit(solution)/shard_map/all_gather | solution.py:391
  506.2 179.9 %all-gather.28.cloned.1.call-start = ((), (), s32[]{:S(2)}) async-start(), calls=%async_computation.8 | async-start | bytes 11796480 | tf_op jit(solution)/shard_map/all_gather | solution.py:391
  553.2 11.6 %collective-permute-start.36 = (bf16[4,256,640]{2,1,0:T(8,128)(2,1)}, bf16[4,256,640]{2,1,0:T(8,128)(2,1)}, u32[]{:S(2)}, u32[]{:S(2)}) collective-permute-start(bf16[4,256,640]{2,1,0:T(8,128)(2,1)} %get-tuple-element.263), channel_id=1, source_target_pairs={{0,1},{1,0},{2,3},{3,2},{4,5},{5,4},{6,7},{7,6},{8,9},{9,8},{10,11... | collective-permute-start | bytes 3932168 | tf_op jit(solution)/shard_map/ppermute | solution.py:345
  553.5 15.6 %collective-permute-start.37 = (bf16[4,256,640]{2,1,0:T(8,128)(2,1)}, bf16[4,256,640]{2,1,0:T(8,128)(2,1)}, u32[]{:S(2)}, u32[]{:S(2)}) collective-permute-start(bf16[4,256,640]{2,1,0:T(8,128)(2,1)} %get-tuple-element.265), channel_id=1, source_target_pairs={{0,1},{1,0},{2,3},{3,2},{4,5},{5,4},{6,7},{7,6},{8,9},{9,8},{10,11... | collective-permute-start | bytes 3932168 | tf_op jit(solution)/shard_map/ppermute | solution.py:345
  567.6 29.0 %collective-permute-start.38 = (bf16[2,256,640]{2,1,0:T(8,128)(2,1)S(1)}, bf16[2,256,640]{2,1,0:T(8,128)(2,1)}, u32[]{:S(2)}, u32[]{:S(2)}) collective-permute-start(bf16[2,256,640]{2,1,0:T(8,128)(2,1)S(1)} %get-tuple-element.296.refs_7_), channel_id=1, source_target_pairs={{0,2},{1,3},{2,0},{3,1},{4,6},{5,7},{6,4},{7,5},{8,10},{9,11},{10,... | collective-permute-start | bytes 1966088 | tf_op jit(solution)/shard_map/ppermute | solution.py:345
  571.6 32.0 %collective-permute-start.40 = (bf16[2,256,640]{2,1,0:T(8,128)(2,1)}, bf16[2,256,640]{2,1,0:T(8,128)(2,1)}, u32[]{:S(2)}, u32[]{:S(2)}) collective-permute-start(bf16[2,256,640]{2,1,0:T(8,128)(2,1)} %get-tuple-element.298.refs_8_), channel_id=1, source_target_pairs={{0,4},{1,5},{2,6},{3,7},{4,0},{5,1},{6,2},{7,3},{8,12},{9,13},{10,... | collective-permute-start | bytes 1966088 | tf_op jit(solution)/shard_map/ppermute | solution.py:345
  582.0 35.2 %copy-start.17 = (bf16[2,1,256,640]{3,2,1,0:T(8,128)(2,1)S(1)}, bf16[2,1,256,640]{3,2,1,0:T(8,128)(2,1)}, u32[]{:S(2)}) copy-start(bf16[2,1,256,640]{3,2,1,0:T(8,128)(2,1)} %get-tuple-element.295) | copy-start | bytes 1966084
  597.7 19.5 %collective-permute-start.39 = (bf16[256,640]{1,0:T(8,128)(2,1)S(1)}, bf16[256,640]{1,0:T(8,128)(2,1)S(1)}, u32[]{:S(2)}, u32[]{:S(2)}) collective-permute-start(bf16[256,640]{1,0:T(8,128)(2,1)S(1)} %fusion.35), channel_id=1, source_target_pairs={{0,4},{1,5},{2,6},{3,7},{4,0},{5,1},{6,2},{7,3},{8,12},{9,13},{10,... | collective-permute-start | bytes 983048 | tf_op jit(solution)/shard_map/ppermute | solution.py:345
  603.6 16.0 %copy-start.18 = (bf16[2,256,640]{2,1,0:T(8,128)(2,1)S(1)}, bf16[2,256,640]{2,1,0:T(8,128)(2,1)}, u32[]{:S(2)}) copy-start(bf16[2,256,640]{2,1,0:T(8,128)(2,1)} %get-tuple-element.297) | copy-start | bytes 1966084
  604.8 14.8 %collective-permute-start.41 = (bf16[256,640]{1,0:T(8,128)(2,1)S(1)}, bf16[256,640]{1,0:T(8,128)(2,1)S(1)}, u32[]{:S(2)}, u32[]{:S(2)}) collective-permute-start(bf16[256,640]{1,0:T(8,128)(2,1)S(1)} %fusion.32), channel_id=1, source_target_pairs={{0,2},{1,3},{2,0},{3,1},{4,6},{5,7},{6,4},{7,5},{8,10},{9,11},{10,... | collective-permute-start | bytes 983048 | tf_op jit(solution)/shard_map/ppermute | solution.py:345
  (26 other events, 72.9 us)
Sparse Core Ops, SparseCore 0:
  29.3 33.0 all-gather.11
  113.5 47.5 all-gather.13
  162.9 54.5 all-gather.15
  247.7 72.7 all-gather.29
  345.0 48.0 all-gather.21
  394.8 37.3 all-gather.19
  434.1 37.2 all-gather.17
  505.6 36.4 all-gather.25
  544.0 80.4 all-gather.23
  626.7 59.3 all-gather.27
where the time goes:
time: 713 us; the launch traced here: 702 us
  Pallas kernels  332 us (47%)
  waiting for transfers between devices  206 us (29%)
  other arithmetic  99.4 us (14%)
  starting transfers between devices  36.2 us (5%)
  between operations  14.9 us (2%)
  local copies, waits for them, and re-layouts  13.3 us (2%)
    pallas_call x22, Pallas kernels, run(): pl.pallas_call(kernel, grid_spec=pltpu.PrefetchScalarGridSpec(num_scalar_...  250 us
    ppermute x42, waiting for transfers between devices, permute(): return lax.ppermute(array, 'tp', [(idx, idx ^ bit) for idx in range(8)])  141 us
    pallas_call x9, Pallas kernels, weight_grads(): *stacks, token = call(*args)  82.7 us
    all_gather x10, waiting for transfers between devices, gather(): return lax.all_gather(shard, 'tp', axis=0, tiled=True)  64.2 us
    add x13, other arithmetic, sum_first(): pick(keep, 0) + pick(recv, 0)  37.6 us
    ppermute x42, starting transfers between devices, permute(): return lax.ppermute(array, 'tp', [(idx, idx ^ bit) for idx in range(8)])  34.6 us
    add x13, other arithmetic, sum_second(): sent.append(here[1] + recv[1])  16.5 us
  transfers between devices with their start and end apart: 52, of which 27 were waited for; matrix products, arithmetic and copies ran while one was open for 14% of the time, Pallas kernels for 45%

commit v1 on v0

--- a/solution.py
+++ b/solution.py
@@ -34,14 +34,11 @@
     return dot(left, right, ((0,), (0,)))
 
 
-def gelu_val(hid):
-    return hid * (0.5 * (1.0 + jnp.tanh(GELU_C * (hid + GELU_A * (hid * hid * hid)))))
-
-
-def gelu_grad(hid):
+def gelu_both(hid):
     sq = hid * hid
     th = jnp.tanh(GELU_C * (hid + GELU_A * (sq * hid)))
-    return 0.5 * (1.0 + th) + hid * (0.5 * (1.0 - th * th)) * (GELU_C * (1.0 + 3.0 * GELU_A * sq))
+    cdf = 0.5 * (1.0 + th)
+    return hid * cdf, cdf + hid * (0.5 * (1.0 - th * th)) * (GELU_C * (1.0 + 3.0 * GELU_A * sq))
 
 
 MIB = 1024 * 1024
@@ -115,12 +112,12 @@
 
     def body(in_refs, out_refs):
         x_ref, win_ref = in_refs
-        a_ref, h_ref, act_ref = out_refs
+        a_ref, slope_ref, act_ref = out_refs
         a = rms_norm(x_ref[...]).astype(BF)
         a_ref[...] = a
         hid = dot(a, win_ref[...])
-        h_ref[...] = hid
-        act_ref[...] = gelu_val(hid).astype(BF)
+        act, slope_ref[...] = gelu_both(hid)
+        act_ref[...] = act.astype(BF)
         return ()
 
     mid = (seqs, rows, inner)
@@ -128,21 +125,21 @@
     return seq_call(body, rank, [("row", x), ("layer", w_in, layer)], outs, [], 2 * seqs * rows * width * inner)
 
 
-def mlp_back(rank, d, w_out, hid, w_in, layer, after=()):
+def mlp_back(rank, d, w_out, slope, w_in, layer, after=()):
     seqs, rows, width = d.shape
     inner = w_out.shape[1]
 
     def body(in_refs, out_refs):
-        d_ref, wout_ref, h_ref, win_ref = in_refs
+        d_ref, wout_ref, slope_ref, win_ref = in_refs
         dbf_ref, dh_ref = out_refs
         d_bf = d_ref[...].astype(BF)
         dbf_ref[...] = d_bf
-        dh = (dot_nt(d_bf, wout_ref[...]) * gelu_grad(h_ref[...])).astype(BF)
+        dh = (dot_nt(d_bf, wout_ref[...]) * slope_ref[...]).astype(BF)
         dh_ref[...] = dh
         yield dot_nt(dh, win_ref[...])
 
-    ins = [("row", d), ("layer", w_out, layer), ("row", hid), ("layer", w_in, layer)]
-    outs = [("row", d.shape, BF), ("row", hid.shape, BF)]
+    ins = [("row", d), ("layer", w_out, layer), ("row", slope), ("layer", w_in, layer)]
+    outs = [("row", d.shape, BF), ("row", slope.shape, BF)]
     return seq_call(body, rank, ins, outs, [(rows, width, BF)], 4 * seqs * rows * width * inner, after)
 
 
@@ -161,13 +158,13 @@
 
     def body(in_refs, out_refs):
         x_ref, whi_ref, wlo_ref = in_refs
-        a_ref, hhi_ref, acthi_ref, hlo_ref, actlo_ref = out_refs
+        a_ref, shi_ref, acthi_ref, slo_ref, actlo_ref = out_refs
         a = rms_norm(x_ref[...]).astype(BF)
         a_ref[...] = a
-        for w_ref, h_ref, act_ref in ((wlo_ref, hlo_ref, actlo_ref), (whi_ref, hhi_ref, acthi_ref)):
+        for w_ref, slope_ref, act_ref in ((wlo_ref, slo_ref, actlo_ref), (whi_ref, shi_ref, acthi_ref)):
             hid = dot(a, w_ref[...])
-            h_ref[...] = hid
-            act_ref[...] = gelu_val(hid).astype(BF)
+            act, slope_ref[...] = gelu_both(hid)
+            act_ref[...] = act.astype(BF)
         return ()
 
     mid = (seqs, rows, inner)
@@ -176,31 +173,31 @@
     return seq_call(body, rank, ins, outs, [], 4 * seqs * rows * width * inner, after)
 
 
-def mlp_dhid(rank, d, w_out, layer, hid, after=()):
+def mlp_dhid(rank, d, w_out, layer, slope, after=()):
     seqs, rows, width = d.shape
     inner = w_out.shape[1]
 
     def body(in_refs, out_refs):
-        d_ref, w_ref, h_ref = in_refs
-        out_refs[0][...] = (dot_nt(d_ref[...], w_ref[...]) * gelu_grad(h_ref[...])).astype(BF)
+        d_ref, w_ref, slope_ref = in_refs
+        out_refs[0][...] = (dot_nt(d_ref[...], w_ref[...]) * slope_ref[...]).astype(BF)
         return ()
 
-    ins = [("row", d), ("layer", w_out, layer), ("row", hid)]
-    return seq_call(body, rank, ins, [("row", hid.shape, BF)], [], 2 * seqs * rows * width * inner, after)
-
-
-def mlp_pair_back(rank, d, w_out, hid, dh_hi, w_in, hi, lo, after=()):
+    ins = [("row", d), ("layer", w_out, layer), ("row", slope)]
+    return seq_call(body, rank, ins, [("row", slope.shape, BF)], [], 2 * seqs * rows * width * inner, after)
+
+
+def mlp_pair_back(rank, d, w_out, slope, dh_hi, w_in, hi, lo, after=()):
     seqs, rows, width = d.shape
     inner = w_out.shape[1]
 
     def body(in_refs, out_refs):
-        d_ref, w_ref, h_ref, dhhi_ref, whi_ref, wlo_ref = in_refs
-        dh = (dot_nt(d_ref[...], w_ref[...]) * gelu_grad(h_ref[...])).astype(BF)
+        d_ref, w_ref, slope_ref, dshi_ref, whi_ref, wlo_ref = in_refs
+        dh = (dot_nt(d_ref[...], w_ref[...]) * slope_ref[...]).astype(BF)
         out_refs[0][...] = dh
-        yield dot_nt(dhhi_ref[...], whi_ref[...]) + dot_nt(dh, wlo_ref[...])
-
-    ins = [("row", d), ("layer", w_out, lo), ("row", hid), ("row", dh_hi), ("layer", w_in, hi), ("layer", w_in, lo)]
-    return seq_call(body, rank, ins, [("row", hid.shape, BF)], [(rows, width, BF)], 6 * seqs * rows * width * inner, after)
+        yield dot_nt(dshi_ref[...], whi_ref[...]) + dot_nt(dh, wlo_ref[...])
+
+    ins = [("row", d), ("layer", w_out, lo), ("row", slope), ("row", dh_hi), ("layer", w_in, hi), ("layer", w_in, lo)]
+    return seq_call(body, rank, ins, [("row", slope.shape, BF)], [(rows, width, BF)], 6 * seqs * rows * width * inner, after)
 
 
 def attn(rank, head_dim, w_qkv, w_o, layer, x=None, minus=None, norm=False, qkv=None, d=None, after=()):
@@ -418,25 +415,27 @@
             stacks["attn"], token = weight_grads(stacks["attn"], n_layers, layer, jobs, after)
             return token
 
-        def mlp_grads(layer, a, act, dh, d_bf, after=()):
-            stacks["in"], first = weight_grads(stacks["in"], n_layers, layer, [(flat(a), flat(dh), "rows")], after)
-            stacks["out"], second = weight_grads(stacks["out"], n_layers, layer, [(flat(act), flat(d_bf), "rows")], [first])
-            return first, second
+        def mlp_grad(which, layer, left, right, after):
+            stacks[which], token = weight_grads(
+                stacks[which], n_layers, layer, [(flat(left), flat(right), "rows")], after
+            )
+            return token
 
         top, hi, lo = 2, 1, 0
         s_one, s_two = saved_one[0], saved_two[0]
         wo_all = gather(o_w[lo])
-        top_a, h_top, top_act, tok = mlp_fwd(rank, y_one, w_in, top)
+        top_a, s_top, top_act, tok = mlp_fwd(rank, y_one, w_in, top)
         *parts, tok = mlp_out(rank, top_act, w_out, top, [tok])
         sum_out, sent = sum_first(sum_cores(parts))
-        d_two_bf, top_dh, *parts, tok = mlp_back(rank, dy_two, w_out, h_top, w_in, top, [tok, *sent])
+        d_two_bf, top_dh, *parts, tok = mlp_back(rank, dy_two, w_out, s_top, w_in, top, [tok, *sent])
         sum_g = sum_cores(parts)
-        s_a, h_hi, act_hi, h_lo, act_lo, tok = mlp_pair_fwd(rank, s_one, w_in, hi, lo, [tok, *received(sum_g)])
-        value, sent, final = sum_second(sum_out, [tok])
+        tok_in = mlp_grad("in", top, top_a, top_dh, [tok, *received(sum_g)])
+        value, sent, final = sum_second(sum_out, [tok_in])
         sum_g, sent_g = sum_first(sum_g, sent)
-        tok_in, tok = mlp_grads(top, top_a, top_act, top_dh, d_two_bf, [tok, *sent, *sent_g])
-        x_two_top = shard(y_two) - sum_end(value, final, [tok_in])
+        tok = mlp_grad("out", top, top_act, d_two_bf, [tok_in, *sent, *sent_g])
+        x_two_top = shard(y_two) - sum_end(value, final, [tok])
         f_top = gather(rms_norm(x_two_top).astype(BF))
+        s_a, sl_hi, act_hi, sl_lo, act_lo, tok = mlp_pair_fwd(rank, s_one, w_in, hi, lo, [tok])
         value, sent, final = sum_second(sum_g, [tok])
         *parts, tok = mlp_out(rank, act_lo, w_out, lo, [tok, *sent])
         back = sum_end(value, final, [tok])
@@ -444,12 +443,12 @@
         d_one_bf = gather(d_one.astype(BF))
         sum_out, sent = sum_first(sum_cores(parts), [back])
         f_hi, o_hi, qkv_hi, tok = attn(rank, head_dim, qkv_w, o_w, hi, x=s_two, norm=True, after=[tok, wo_all, *sent])
+        o_top, qkv_top, tok = attn(rank, head_dim, qkv_w, o_w, top, x=f_top, after=[tok])
         value, sent, final = sum_second(sum_out, [tok])
-        o_top, qkv_top, tok = attn(rank, head_dim, qkv_w, o_w, top, x=f_top, after=[tok, *sent])
+        dqkv_top, *parts, tok = attn(rank, head_dim, qkv_w, o_w, top, qkv=qkv_top, d=d_one_bf, after=[tok, *sent])
         g_sum = sum_end(value, final, [tok])
         g_full = gather(g_sum)
         x_two = shard(s_two) - g_sum
-        dqkv_top, *parts, tok = attn(rank, head_dim, qkv_w, o_w, top, qkv=qkv_top, d=d_one_bf, after=[tok, g_sum])
         sum_top, sent = sum_first(sum_cores(parts))
         dqkv_hi, *parts, tok = attn(rank, head_dim, qkv_w, o_w, hi, qkv=qkv_hi, d=d_one_bf, after=[tok, *sent])
         sum_hi = sum_cores(parts)
@@ -464,11 +463,13 @@
         d_two_lo_bf = gather(d_two.astype(BF))
         x_two_full, f_lo, o_lo, qkv_lo, tok = attn(rank, head_dim, qkv_w, o_w, lo, x=s_two, minus=g_full, norm=True, after=[tok])
         o_all = gather(o_lo)
-        dh_hi, tok = mlp_dhid(rank, d_two_hi_bf, w_out, hi, h_hi, [tok])
-        _, tok = mlp_grads(hi, s_a, act_hi, dh_hi, d_two_hi_bf, [tok])
-        dh_lo, *parts, tok = mlp_pair_back(rank, d_two_lo_bf, w_out, h_lo, dh_hi, w_in, hi, lo, [tok])
+        dh_hi, tok = mlp_dhid(rank, d_two_hi_bf, w_out, hi, sl_hi, [tok])
+        tok = mlp_grad("in", hi, s_a, dh_hi, [tok])
+        tok = mlp_grad("out", hi, act_hi, d_two_hi_bf, [tok])
+        dh_lo, *parts, tok = mlp_pair_back(rank, d_two_lo_bf, w_out, sl_lo, dh_hi, w_in, hi, lo, [tok])
         sum_g, sent = sum_first(sum_cores(parts))
-        tok_in, tok = mlp_grads(lo, s_a, act_lo, dh_lo, d_two_lo_bf, [tok, *sent])
+        tok_in = mlp_grad("in", lo, s_a, dh_lo, [tok, *sent])
+        tok = mlp_grad("out", lo, act_lo, d_two_lo_bf, [tok_in])
         value, sent, final = sum_second(sum_g, [tok_in])
         d_one = d_one + rms_vjp(shard(s_one), sum_end(value, final))
         d_one_bf = gather(tie(d_one.astype(BF), [o_all]))

time: 713 us -> 691 us (0.969)
  waiting for transfers between devices: 206 us -> 184 us
    ppermute x42, waiting for transfers between devices: 141 us -> 120 us  [permute(): return lax.ppermute(array, 'tp', [(idx, idx ^ bit) for idx in range(8)])]
  transfers between devices with their start and end apart: 52 -> 52, of which waited for: 27 -> 27; matrix products, arithmetic and copies ran while one was open for 14% -> 14% of each run, Pallas kernels for 45% -> 46%
where the time goes in v1:
time: 691 us; the launch traced here: 681 us
  Pallas kernels  333 us (48%)
  waiting for transfers between devices  184 us (27%)
  other arithmetic  96.3 us (14%)
  starting transfers between devices  39.6 us (6%)
  between operations  14.9 us (2%)
  local copies, waits for them, and re-layouts  13.2 us (2%)
    pallas_call x22, Pallas kernels, run(): pl.pallas_call(kernel, grid_spec=pltpu.PrefetchScalarGridSpec(num_scalar_...  250 us
    ppermute x42, waiting for transfers between devices, permute(): return lax.ppermute(array, 'tp', [(idx, idx ^ bit) for idx in range(8)])  120 us
    pallas_call x9, Pallas kernels, weight_grads(): *stacks, token = call(*args)  83.5 us
    all_gather x10, waiting for transfers between devices, gather(): return lax.all_gather(shard, 'tp', axis=0, tiled=True)  63.5 us
    ppermute x42, starting transfers between devices, permute(): return lax.ppermute(array, 'tp', [(idx, idx ^ bit) for idx in range(8)])  38 us
    add x13, other arithmetic, sum_first(): pick(keep, 0) + pick(recv, 0)  35.6 us
    add x13, other arithmetic, sum_second(): sent.append(here[1] + recv[1])  15.6 us
  transfers between devices with their start and end apart: 52, of which 27 were waited for; matrix products, arithmetic and copies ran while one was open for 14% of the time, Pallas kernels for 46%

profile of v1, /device:TPU:0, one launch (start us, length us, event | category | flops | bytes accessed | tf_op | source)
XLA Modules:
  0.0 681.2 jit_solution(8285920001985048906)
XLA Ops:
  7.2 13.6 %shard_map.161 = (bf16[8,256,1280]{2,1,0:T(8,128)(2,1)}, f32[8,256,640]{2,1,0:T(8,128)}, bf16[8,256,640]{2,1,0:T(8,128)(2,1)}, f32[8,128]{1,0:T(8,128)}) custom-call(s32[1]{0:T(128)} %bitcast.rank_ref, f32[8,256,1280]{2,1,0:T(8,128)} %refs_0_.3, bf16[3,1280,640]{2,1,0:T(8,128)(2,1)} %refs_5_.3), custom_call_target="tpu_custom_call" | custom-call | flops 3355443200 | bytes 13111296 | tf_op jit(solution)/shard_map/pallas_call | solution.py:91
  20.8 5.7 shard_map.162
  29.2 5.8 shard_map.163
  36.4 4.2 slice_add_fusion.3
  40.6 3.1 slice_add_fusion.2
  43.8 9.7 %shard_map.164 = (bf16[8,256,1280]{2,1,0:T(8,128)(2,1)}, bf16[8,256,640]{2,1,0:T(8,128)(2,1)}, bf16[4,256,640]{2,1,0:T(8,128)(2,1)}, bf16[4,256,640]{2,1,0:T(8,128)(2,1)}, f32[8,128]{1,0:T(8,128)}) custom-call(s32[1]{0:T(128)} %bitcast.rank_ref, f32[8,256,1280]{2,1,0:T(8,128)} %refs_0_.5, bf16[3,640,1280]{2,1,0:T(8,128)(2,1)} %refs_1_.21, ...), custom_call_target="tpu_custom_call" | custom-call | flops 3355443200 | bytes 5244928 | tf_op jit(solution)/shard_map/pallas_call | solution.py:91
  58.0 9.4 %shard_map.165 = (bf16[8,256,1280]{2,1,0:T(8,128)(2,1)}, bf16[8,256,640]{2,1,0:T(8,128)(2,1)}, bf16[4,256,640]{2,1,0:T(8,128)(2,1)}, bf16[4,256,640]{2,1,0:T(8,128)(2,1)}, f32[8,128]{1,0:T(8,128)}) custom-call(s32[1]{0:T(128)} %bitcast.rank_ref, f32[8,256,1280]{2,1,0:T(8,128)} %refs_0_.5, ...), custom_call_target="tpu_custom_call", output_to_operand_aliasing={{0}: (5, {}), {1}: (6, {})} | custom-call | flops 3355443200 | bytes 5244928 | tf_op jit(solution)/shard_map/pallas_call | solution.py:91
  67.4 9.0 %shard_map.166 = (f32[3,1280,640]{2,1,0:T(8,128)}, f32[8,128]{1,0:T(8,128)}) custom-call(bf16[2048,1280]{1,0:T(8,128)(2,1)} %bitcast.372, bf16[2048,640]{1,0:T(8,128)(2,1)} %bitcast.356, f32[8,128]{1,0:T(8,128)} %get-tuple-element.156.refs_2_, bf16[2,2,256,640]{3,2,1,0:T(8,128)(2,1)} %bitcast.12.refs_3_, bf16[2,2,256,640]{3,2,1,0:T(8,128)(2,1)} %bitcast.13.refs_4_), custom_call_target="tpu_custom_call" | custom-call | flops 3355443200 | bytes 17367040 | tf_op jit(solution)/shard_map/pallas_call | solution.py:337
  76.4 11.0 %collective-permute-done.4 = f32[2,256,640]{2,1,0:T(8,128)} collective-permute-done((f32[2,256,640]{2,1,0:T(8,128)}, f32[2,256,640]{2,1,0:T(8,128)}, u32[]{:S(2)}, u32[]{:S(2)}) %collective-permute-start.4) | collective-permute-done | bytes 1310752 | tf_op jit(solution)/shard_map/ppermute | solution.py:342
  87.4 2.6 fusion.23
  94.4 2.5 bitcast_add_fusion.4
  97.0 8.8 %shard_map.167 = (f32[3,640,1280]{2,1,0:T(8,128)}, f32[8,128]{1,0:T(8,128)}) custom-call(bf16[2048,640]{1,0:T(8,128)(2,1)} %bitcast.347, bf16[2048,1280]{1,0:T(8,128)(2,1)} %bitcast.353, f32[8,128]{1,0:T(8,128)} %get-tuple-element.159.refs_2_, f32[256,640]{1,0:T(8,128)} %get-tuple-element.316.refs_3_, f32[256,640]{1,0:T(8,128)} %get-tuple-element.315.refs_4_, ...), custom_call_target="tpu_custom_call" | custom-call | flops 3355443200 | bytes 17367040 | tf_op jit(solution)/shard_map/pallas_call | solution.py:337
  117.3 18.1 %shard_map.168 = (bf16[8,256,1280]{2,1,0:T(8,128)(2,1)}, f32[8,256,640]{2,1,0:T(8,128)}, bf16[8,256,640]{2,1,0:T(8,128)(2,1)}, f32[8,256,640]{2,1,0:T(8,128)}, b...) custom-call(s32[1]{0:T(128)} %bitcast.rank_ref, f32[8,256,1280]{2,1,0:T(8,128)} %bitcast.364, ...), custom_call_target="tpu_custom_call" | custom-call | flops 6710886400 | bytes 20975616 | tf_op jit(solution)/shard_map/pallas_call | solution.py:91
  141.0 5.8 shard_map.169
  146.8 5.8 shard_map.170
  157.6 3.3 fusion.65
  161.5 4.6 collective-permute-done.8
  166.2 3.7 collective-permute-done.14
  169.9 3.3 slice_add_fusion.1
  178.3 15.1 %shard_map.171 = (bf16[8,256,1280]{2,1,0:T(8,128)(2,1)}, bf16[160,2048]{1,0:T(8,128)(2,1)}, bf16[480,2048]{1,0:T(8,128)(2,1)}, f32[8,128]{1,0:T(8,128)}) custom-call(s32[1]{0:T(128)} %bitcast.rank_ref, bf16[3,480,1280]{2,1,0:T(8,128)(2,1)} %bitcast.319, f32[8,256,1280]{2,1,0:T(8,128)} %bitcast.330, f32[8,128]{1,0:T(8,128)} %get-tuple-element.174.refs_2_, ...), custom_call_target="tpu_custom_call" | custom-call | flops 2852126720 | bytes 7868416 | tf_op jit(solution)/shard_map/pallas_call | solution.py:91
  193.4 13.0 %shard_map.172 = (bf16[160,2048]{1,0:T(8,128)(2,1)}, bf16[480,2048]{1,0:T(8,128)(2,1)}, f32[8,128]{1,0:T(8,128)}) custom-call(s32[1]{0:T(128)} %bitcast.rank_ref, bf16[3,480,1280]{2,1,0:T(8,128)(2,1)} %bitcast.320, bf16[8,256,1280]{2,1,0:T(8,128)(2,1)} %all-gather.12.cloned.1.call-done.refs_1_, f32[8,128]{1,0:T(8,128)} %get-tuple-element.183.refs_2_), custom_call_target="tpu_custom_call" | custom-call | flops 2852126720 | bytes 2625536 | tf_op jit(solution)/shard_map/pallas_call | solution.py:91
  206.4 14.5 %collective-permute-done.11 = f32[2,256,640]{2,1,0:T(8,128)} collective-permute-done((f32[2,256,640]{2,1,0:T(8,128)S(1)}, f32[2,256,640]{2,1,0:T(8,128)}, u32[]{:S(2)}, u32[]{:S(2)}) %collective-permute-start.11) | collective-permute-done | bytes 1310752 | tf_op jit(solution)/shard_map/ppermute | solution.py:342
  227.0 11.1 %shard_map.173 = (bf16[480,2048]{1,0:T(8,128)(2,1)}, bf16[4,256,640]{2,1,0:T(8,128)(2,1)}, bf16[4,256,640]{2,1,0:T(8,128)(2,1)}, f32[8,128]{1,0:T(8,128)}) custom-call(s32[1]{0:T(128)} %bitcast.rank_ref, bf16[3,480,1280]{2,1,0:T(8,128)(2,1)} %bitcast.321, bf16[480,2048]{1,0:T(8,128)(2,1)} %get-tuple-element.186.refs_1_, bf16[3,160,1280]{2,1,0:T(8,128)(2,1)} %bitcast.332, ...), custom_call_target="tpu_custom_call" | custom-call | flops 2097152000 | bytes 2295808 | tf_op jit(solution)/shard_map/pallas_call | solution.py:91
  238.2 11.3 %shard_map.174 = (bf16[480,2048]{1,0:T(8,128)(2,1)}, bf16[4,256,640]{2,1,0:T(8,128)(2,1)}, bf16[4,256,640]{2,1,0:T(8,128)(2,1)}, f32[8,128]{1,0:T(8,128)}) custom-call(s32[1]{0:T(128)} %bitcast.rank_ref, bf16[3,480,1280]{2,1,0:T(8,128)(2,1)} %bitcast.322, bf16[480,2048]{1,0:T(8,128)(2,1)} %get-tuple-element.186.refs_1_, ...), custom_call_target="tpu_custom_call", output_to_operand_aliasing={{0}: (5, {})} | custom-call | flops 2097152000 | bytes 2295808 | tf_op jit(solution)/shard_map/pallas_call | solution.py:91
  254.8 2.7 collective-permute-done.18
  257.6 2.8 slice_add_fusion.17
  261.6 11.2 %shard_map.175 = (bf16[480,2048]{1,0:T(8,128)(2,1)}, bf16[4,256,640]{2,1,0:T(8,128)(2,1)}, bf16[4,256,640]{2,1,0:T(8,128)(2,1)}, f32[8,128]{1,0:T(8,128)}) custom-call(s32[1]{0:T(128)} %bitcast.rank_ref, bf16[3,480,1280]{2,1,0:T(8,128)(2,1)} %bitcast.323, bf16[480,2048]{1,0:T(8,128)(2,1)} %get-tuple-element.193.refs_1_, bf16[3,160,1280]{2,1,0:T(8,128)(2,1)} %bitcast.334, ...), custom_call_target="tpu_custom_call" | custom-call | flops 2097152000 | bytes 2295808 | tf_op jit(solution)/shard_map/pallas_call | solution.py:91
  275.5 11.1 %shard_map.176 = (bf16[480,2048]{1,0:T(8,128)(2,1)}, bf16[4,256,640]{2,1,0:T(8,128)(2,1)}, bf16[4,256,640]{2,1,0:T(8,128)(2,1)}, f32[8,128]{1,0:T(8,128)}) custom-call(s32[1]{0:T(128)} %bitcast.rank_ref, bf16[3,480,1280]{2,1,0:T(8,128)(2,1)} %bitcast.324, bf16[480,2048]{1,0:T(8,128)(2,1)} %get-tuple-element.193.refs_1_, ...), custom_call_target="tpu_custom_call", output_to_operand_aliasing={{0}: (5, {})} | custom-call | flops 2097152000 | bytes 2295808 | tf_op jit(solution)/shard_map/pallas_call | solution.py:91
  286.6 11.7 %collective-permute-done.23 = bf16[2,256,640]{2,1,0:T(8,128)(2,1)} collective-permute-done((bf16[2,256,640]{2,1,0:T(8,128)(2,1)}, bf16[2,256,640]{2,1,0:T(8,128)(2,1)}, u32[]{:S(2)}, u32[]{:S(2)}) %collective-permute-start.23) | collective-permute-done | bytes 655392 | tf_op jit(solution)/shard_map/ppermute | solution.py:342
  304.9 2.7 bitcast_add_fusion.2
  307.6 2.5 slice_add_fusion.14
  310.1 9.6 %shard_map.177 = (f32[3,480,1280]{2,1,0:T(8,128)}, f32[3,160,1280]{2,1,0:T(8,128)}, f32[8,128]{1,0:T(8,128)}) custom-call(bf16[480,2048]{1,0:T(8,128)(2,1)} %get-tuple-element.203.refs_0_, bf16[2048,1280]{1,0:T(8,128)(2,1)} %bitcast.354, bf16[160,2048]{1,0:T(8,128)(2,1)} %get-tuple-element.204.refs_2_, bf16[2048,1280]{1,0:T(8,128)(2,1)} %bitcast.328, ...), custom_call_target="tpu_custom_call" | custom-call | flops 3355443200 | bytes 27852800 | tf_op jit(solution)/shard_map/pallas_call | solution.py:337
  322.6 3.1 fusion.63
  330.1 15.1 %collective-permute-done.25 = bf16[2,256,640]{2,1,0:T(8,128)(2,1)S(1)} collective-permute-done((bf16[2,256,640]{2,1,0:T(8,128)(2,1)S(1)}, bf16[2,256,640]{2,1,0:T(8,128)(2,1)S(1)}, u32[]{:S(2)}, u32[]{:S(2)}) %collective-permute-start.25) | collective-permute-done | bytes 655392 | tf_op jit(solution)/shard_map/ppermute | solution.py:342
  345.2 4.8 collective-permute-done.24
  353.2 10.4 %shard_map.178 = (f32[3,480,1280]{2,1,0:T(8,128)}, f32[3,160,1280]{2,1,0:T(8,128)}, f32[8,128]{1,0:T(8,128)}) custom-call(bf16[480,2048]{1,0:T(8,128)(2,1)} %get-tuple-element.200.refs_0_, bf16[2048,1280]{1,0:T(8,128)(2,1)} %bitcast.355, bf16[160,2048]{1,0:T(8,128)(2,1)} %get-tuple-element.202.refs_2_, ...), custom_call_target="tpu_custom_call", output_to_operand_aliasing={{0}: (4, {}), {1}: (5, {})} | custom-call | flops 3355443200 | bytes 27852800 | tf_op jit(solution)/shard_map/pallas_call | solution.py:337
  368.7 2.5 fusion.64
  371.4 18.2 %shard_map.179 = (f32[8,256,1280]{2,1,0:T(8,128)}, bf16[8,256,1280]{2,1,0:T(8,128)(2,1)}, bf16[160,2048]{1,0:T(8,128)(2,1)}, bf16[480,2048]{1,0:T(8,128)(2,1)}, f32[8,128]{1,0:T(8,128)}) custom-call(s32[1]{0:T(128)} %bitcast.rank_ref, bf16[3,480,1280]{2,1,0:T(8,128)(2,1)} %bitcast.325, f32[8,256,1280]{2,1,0:T(8,128)} %bitcast.331, ...), custom_call_target="tpu_custom_call" | custom-call | flops 2852126720 | bytes 18354176 | tf_op jit(solution)/shard_map/pallas_call | solution.py:91
  389.9 11.1 %shard_map.180 = (bf16[8,256,640]{2,1,0:T(8,128)(2,1)}, f32[8,128]{1,0:T(8,128)}) custom-call(s32[1]{0:T(128)} %bitcast.rank_ref, bf16[8,256,1280]{2,1,0:T(8,128)(2,1)} %all-gather.22.cloned.1.call-done.refs_0_, bf16[3,640,1280]{2,1,0:T(8,128)(2,1)} %refs_1_.21, f32[8,256,640]{2,1,0:T(8,128)} %get-tuple-element.228.refs_2_, f32[8,128]{1,0:T(8,128)} %get-tuple-element.229.refs_3_), custom_call_target="tpu_custom_call" | custom-call | flops 3355443200 | bytes 2625536 | tf_op jit(solution)/shard_map/pallas_call | solution.py:91
  401.0 9.0 %shard_map.181 = (f32[3,1280,640]{2,1,0:T(8,128)}, f32[8,128]{1,0:T(8,128)}) custom-call(bf16[2048,1280]{1,0:T(8,128)(2,1)} %bitcast.344, bf16[2048,640]{1,0:T(8,128)(2,1)} %bitcast.341, f32[3,1280,640]{2,1,0:T(8,128)} %get-tuple-element.231.refs_2_, f32[8,128]{1,0:T(8,128)} %get-tuple-element.232.refs_3_), custom_call_target="tpu_custom_call", output_to_operand_aliasing={{0}: (2, {})} | custom-call | flops 3355443200 | bytes 17367040 | tf_op jit(solution)/shard_map/pallas_call | solution.py:337
  410.0 8.8 %shard_map.182 = (f32[3,640,1280]{2,1,0:T(8,128)}, f32[8,128]{1,0:T(8,128)}) custom-call(bf16[2048,640]{1,0:T(8,128)(2,1)} %bitcast.357, bf16[2048,1280]{1,0:T(8,128)(2,1)} %bitcast.343, f32[3,640,1280]{2,1,0:T(8,128)} %get-tuple-element.226.refs_2_, f32[8,128]{1,0:T(8,128)} %get-tuple-element.233.refs_3_), custom_call_target="tpu_custom_call", output_to_operand_aliasing={{0}: (2, {})} | custom-call | flops 3355443200 | bytes 17367040 | tf_op jit(solution)/shard_map/pallas_call | solution.py:337
  418.8 12.7 %shard_map.183 = (bf16[8,256,640]{2,1,0:T(8,128)(2,1)}, bf16[4,256,640]{2,1,0:T(8,128)(2,1)}, bf16[4,256,640]{2,1,0:T(8,128)(2,1)}, f32[8,128]{1,0:T(8,128)}) custom-call(s32[1]{0:T(128)} %bitcast.rank_ref, bf16[8,256,1280]{2,1,0:T(8,128)(2,1)} %all-gather.20.cloned.1.call-done.refs_0_, bf16[3,640,1280]{2,1,0:T(8,128)(2,1)} %refs_1_.21, ...), custom_call_target="tpu_custom_call" | custom-call | flops 5033164800 | bytes 2623488 | tf_op jit(solution)/shard_map/pallas_call | solution.py:91
  432.0 12.2 %shard_map.184 = (bf16[8,256,640]{2,1,0:T(8,128)(2,1)}, bf16[4,256,640]{2,1,0:T(8,128)(2,1)}, bf16[4,256,640]{2,1,0:T(8,128)(2,1)}, f32[8,128]{1,0:T(8,128)}) custom-call(s32[1]{0:T(128)} %bitcast.rank_ref, bf16[8,256,1280]{2,1,0:T(8,128)(2,1)} %all-gather.20.cloned.1.call-done.refs_0_, ...), custom_call_target="tpu_custom_call", output_to_operand_aliasing={{0}: (7, {})} | custom-call | flops 5033164800 | bytes 2623488 | tf_op jit(solution)/shard_map/pallas_call | solution.py:91
  444.2 2.9 slice_add_fusion.11
  447.1 3.3 collective-permute-start.32
  450.4 2.6 slice_add_fusion.10
  455.1 9.0 %shard_map.185 = (f32[3,1280,640]{2,1,0:T(8,128)}, f32[8,128]{1,0:T(8,128)}) custom-call(bf16[2048,1280]{1,0:T(8,128)(2,1)} %bitcast.345, bf16[2048,640]{1,0:T(8,128)(2,1)} %bitcast.348, f32[3,1280,640]{2,1,0:T(8,128)} %get-tuple-element.240.refs_2_, f32[8,128]{1,0:T(8,128)} %get-tuple-element.241.refs_3_, ...), custom_call_target="tpu_custom_call", output_to_operand_aliasing={{0}: (2, {})} | custom-call | flops 3355443200 | bytes 17367040 | tf_op jit(solution)/shard_map/pallas_call | solution.py:337
  467.6 2.8 collective-permute-done.34
  471.7 4.7 collective-permute-done.33
  482.0 2.9 fusion.62
  485.9 9.0 %shard_map.186 = (f32[3,640,1280]{2,1,0:T(8,128)}, f32[8,128]{1,0:T(8,128)}) custom-call(bf16[2048,640]{1,0:T(8,128)(2,1)} %bitcast.342, bf16[2048,1280]{1,0:T(8,128)(2,1)} %bitcast.339, f32[3,640,1280]{2,1,0:T(8,128)} %get-tuple-element.234.refs_2_, f32[8,128]{1,0:T(8,128)} %get-tuple-element.246.refs_3_), custom_call_target="tpu_custom_call", output_to_operand_aliasing={{0}: (2, {})} | custom-call | flops 3355443200 | bytes 17367040 | tf_op jit(solution)/shard_map/pallas_call | solution.py:337
  494.9 16.2 %shard_map.187 = (f32[8,256,1280]{2,1,0:T(8,128)}, f32[8,128]{1,0:T(8,128)}) custom-call(s32[1]{0:T(128)} %bitcast.rank_ref, f32[8,256,1280]{2,1,0:T(8,128)} %bitcast.365, bf16[1280,2048]{1,0:T(8,128)(2,1)} %all-gather.18.cloned.1.call-done.refs_1_, bf16[1280,1280]{1,0:T(8,128)(2,1)} %all-gather.14.cloned.1.call-done.refs_3_.refs_2_, ...), custom_call_target="tpu_custom_call" | custom-call | flops 6710886400 | bytes 10489856 | tf_op jit(solution)/shard_map/pallas_call | solution.py:91
  511.1 9.6 %all-gather.26.cloned.1.call-done.refs_3_ = bf16[8,256,1280]{2,1,0:T(8,128)(2,1)} async-done(((bf16[1,256,1280]{2,1,0:T(8,128)(2,1)}), bf16[8,256,1280]{2,1,0:T(8,128)(2,1)}) %all-gather.26.cloned.1.call-update) | async-done | bytes 5242896 | tf_op jit(solution)/shard_map/all_gather | solution.py:388
  520.7 11.1 %shard_map.188 = (bf16[480,2048]{1,0:T(8,128)(2,1)}, bf16[4,256,640]{2,1,0:T(8,128)(2,1)}, bf16[4,256,640]{2,1,0:T(8,128)(2,1)}, f32[8,128]{1,0:T(8,128)}) custom-call(s32[1]{0:T(128)} %bitcast.rank_ref, bf16[3,480,1280]{2,1,0:T(8,128)(2,1)} %bitcast.326, bf16[480,2048]{1,0:T(8,128)(2,1)} %get-tuple-element.252.refs_1_, bf16[3,160,1280]{2,1,0:T(8,128)(2,1)} %bitcast.336, ...), custom_call_target="tpu_custom_call" | custom-call | flops 2097152000 | bytes 2295808 | tf_op jit(solution)/shard_map/pallas_call | solution.py:91
  532.3 11.1 %shard_map.189 = (bf16[480,2048]{1,0:T(8,128)(2,1)}, bf16[4,256,640]{2,1,0:T(8,128)(2,1)}, bf16[4,256,640]{2,1,0:T(8,128)(2,1)}, f32[8,128]{1,0:T(8,128)}) custom-call(s32[1]{0:T(128)} %bitcast.rank_ref, bf16[3,480,1280]{2,1,0:T(8,128)(2,1)} %bitcast.327, bf16[480,2048]{1,0:T(8,128)(2,1)} %get-tuple-element.252.refs_1_, ...), custom_call_target="tpu_custom_call", output_to_operand_aliasing={{0}: (5, {})} | custom-call | flops 2097152000 | bytes 2295808 | tf_op jit(solution)/shard_map/pallas_call | solution.py:91
  543.4 2.8 slice_add_fusion.7
  547.7 2.5 slice_add_fusion.6
  550.8 10.0 %shard_map.190 = (f32[3,480,1280]{2,1,0:T(8,128)}, f32[3,160,1280]{2,1,0:T(8,128)}, f32[8,128]{1,0:T(8,128)}) custom-call(bf16[480,2048]{1,0:T(8,128)(2,1)} %get-tuple-element.257.refs_0_, bf16[2048,1280]{1,0:T(8,128)(2,1)} %bitcast.352, bf16[160,2048]{1,0:T(8,128)(2,1)} %get-tuple-element.220.refs_2_, ...), custom_call_target="tpu_custom_call", output_to_operand_aliasing={{0}: (4, {}), {1}: (5, {})} | custom-call | flops 3355443200 | bytes 27852800 | tf_op jit(solution)/shard_map/pallas_call | solution.py:337
  560.8 13.8 %collective-permute-done.38 = bf16[2,256,640]{2,1,0:T(8,128)(2,1)} collective-permute-done((bf16[2,256,640]{2,1,0:T(8,128)(2,1)S(1)}, bf16[2,256,640]{2,1,0:T(8,128)(2,1)}, u32[]{:S(2)}, u32[]{:S(2)}) %collective-permute-start.38) | collective-permute-done | bytes 655392 | tf_op jit(solution)/shard_map/ppermute | solution.py:342
  576.8 5.3 collective-permute-done.40
  583.8 11.9 %collective-permute-done.39 = bf16[256,640]{1,0:T(8,128)(2,1)S(1)} collective-permute-done((bf16[256,640]{1,0:T(8,128)(2,1)S(1)}, bf16[256,640]{1,0:T(8,128)(2,1)S(1)}, u32[]{:S(2)}, u32[]{:S(2)}) %collective-permute-start.39) | collective-permute-done | bytes 327712 | tf_op jit(solution)/shard_map/ppermute | solution.py:342
  603.6 10.4 %shard_map.191 = (f32[8,256,1280]{2,1,0:T(8,128)}, f32[8,128]{1,0:T(8,128)}) custom-call(s32[1]{0:T(128)} %bitcast.rank_ref, f32[8,256,1280]{2,1,0:T(8,128)} %all-gather.24.cloned.1.call-done.refs_0_, f32[8,128]{1,0:T(8,128)} %get-tuple-element.266.refs_1_), custom_call_target="tpu_custom_call" | custom-call | flops 41943040 | bytes 10489856 | tf_op jit(solution)/shard_map/pallas_call | solution.py:91
  614.0 51.3 %all-gather.28.cloned.1.call-done = f32[8,256,1280]{2,1,0:T(8,128)} async-done(((f32[1,256,1280]{2,1,0:T(8,128)}), f32[8,256,1280]{2,1,0:T(8,128)}) %all-gather.28.cloned.1.call-update) | async-done | bytes 10485776 | tf_op jit(solution)/shard_map/all_gather | solution.py:388
  665.3 8.8 %copy.47 = f32[8,256,1280]{2,1,0:T(8,128)} copy(f32[8,256,1280]{2,1,0:T(8,128)} %all-gather.28.cloned.1.call-done) | data formatting | bytes 20971520
  (226 shorter events, 106.9 us)
Async XLA Ops:
  7.2 171.1 %all-gather.14.cloned.1.call-start = ((), (), s32[]{:S(2)}) async-start(), calls=%async_computation.1 | async-start | bytes 3686400 | tf_op jit(solution)/shard_map/all_gather | solution.py:388
  26.6 8.3 %collective-permute-start = (f32[4,256,640]{2,1,0:T(8,128)}, f32[4,256,640]{2,1,0:T(8,128)S(1)}, u32[]{:S(2)}, u32[]{:S(2)}) collective-permute-start(f32[4,256,640]{2,1,0:T(8,128)} %get-tuple-element.147), channel_id=1, source_target_pairs={{0,1},{1,0},{2,3},{3,2},{4,5},{5,4},{6,7},{7,6},{8,9},{9,8},{10,11... | collective-permute-start | bytes 7864328 | tf_op jit(solution)/shard_map/ppermute | solution.py:342
  27.3 13.3 %collective-permute-start.1 = (f32[4,256,640]{2,1,0:T(8,128)}, f32[4,256,640]{2,1,0:T(8,128)}, u32[]{:S(2)}, u32[]{:S(2)}) collective-permute-start(f32[4,256,640]{2,1,0:T(8,128)} %get-tuple-element.149), channel_id=1, source_target_pairs={{0,1},{1,0},{2,3},{3,2},{4,5},{5,4},{6,7},{7,6},{8,9},{9,8},{10,11... | collective-permute-start | bytes 7864328 | tf_op jit(solution)/shard_map/ppermute | solution.py:342
  29.1 164.2 %all-gather.12.cloned.1.call-start = ((), (), s32[]{:S(2)}) async-start(), calls=%async_computation | async-start | bytes 5898240 | tf_op jit(solution)/shard_map/all_gather | solution.py:388
  53.5 13.9 %collective-permute-start.2 = (bf16[4,256,640]{2,1,0:T(8,128)(2,1)}, bf16[4,256,640]{2,1,0:T(8,128)(2,1)}, u32[]{:S(2)}, u32[]{:S(2)}) collective-permute-start(bf16[4,256,640]{2,1,0:T(8,128)(2,1)} %get-tuple-element.157), channel_id=1, source_target_pairs={{0,1},{1,0},{2,3},{3,2},{4,5},{5,4},{6,7},{7,6},{8,9},{9,8},{10,11... | collective-permute-start | bytes 3932168 | tf_op jit(solution)/shard_map/ppermute | solution.py:342
  53.8 13.6 %collective-permute-start.3 = (bf16[4,256,640]{2,1,0:T(8,128)(2,1)}, bf16[4,256,640]{2,1,0:T(8,128)(2,1)}, u32[]{:S(2)}, u32[]{:S(2)}) collective-permute-start(bf16[4,256,640]{2,1,0:T(8,128)(2,1)} %get-tuple-element.158), channel_id=1, source_target_pairs={{0,1},{1,0},{2,3},{3,2},{4,5},{5,4},{6,7},{7,6},{8,9},{9,8},{10,11... | collective-permute-start | bytes 3932168 | tf_op jit(solution)/shard_map/ppermute | solution.py:342
  54.0 33.4 %collective-permute-start.4 = (f32[2,256,640]{2,1,0:T(8,128)}, f32[2,256,640]{2,1,0:T(8,128)}, u32[]{:S(2)}, u32[]{:S(2)}) collective-permute-start(f32[2,256,640]{2,1,0:T(8,128)} %get-tuple-element.294.refs_5_), channel_id=1, source_target_pairs={{0,2},{1,3},{2,0},{3,1},{4,6},{5,7},{6,4},{7,5},{8,10},{9,11},{10,... | collective-permute-start | bytes 3932168 | tf_op jit(solution)/shard_map/ppermute | solution.py:342
  56.5 30.9 %collective-permute-start.5 = (f32[2,256,640]{2,1,0:T(8,128)}, f32[2,256,640]{2,1,0:T(8,128)}, u32[]{:S(2)}, u32[]{:S(2)}) collective-permute-start(f32[2,256,640]{2,1,0:T(8,128)} %get-tuple-element.292.refs_6_), channel_id=1, source_target_pairs={{0,4},{1,5},{2,6},{3,7},{4,0},{5,1},{6,2},{7,3},{8,12},{9,13},{10,... | collective-permute-start | bytes 3932168 | tf_op jit(solution)/shard_map/ppermute | solution.py:342
  90.0 16.9 %collective-permute-start.12 = (f32[256,640]{1,0:T(8,128)}, f32[256,640]{1,0:T(8,128)}, u32[]{:S(2)}, u32[]{:S(2)}) collective-permute-start(f32[256,640]{1,0:T(8,128)} %get-tuple-element.316.refs_3_), channel_id=1, source_target_pairs={{0,4},{1,5},{2,6},{3,7},{4,0},{5,1},{6,2},{7,3},{8,12},{9,13},{10,... | collective-permute-start | bytes 1966088 | tf_op jit(solution)/shard_map/ppermute | solution.py:342
  91.5 16.5 %collective-permute-start.13 = (f32[256,640]{1,0:T(8,128)}, f32[256,640]{1,0:T(8,128)}, u32[]{:S(2)}, u32[]{:S(2)}) collective-permute-start(f32[256,640]{1,0:T(8,128)} %get-tuple-element.315.refs_4_), channel_id=1, source_target_pairs={{0,2},{1,3},{2,0},{3,1},{4,6},{5,7},{6,4},{7,5},{8,10},{9,11},{10,... | collective-permute-start | bytes 1966088 | tf_op jit(solution)/shard_map/ppermute | solution.py:342
  113.4 113.6 %all-gather.16.cloned.1.call-start = ((), (), s32[]{:S(2)}) async-start(), calls=%async_computation.2 | async-start | bytes 5898240 | tf_op jit(solution)/shard_map/all_gather | solution.py:388
  113.8 22.6 %collective-permute-start.7 = (bf16[2,256,640]{2,1,0:T(8,128)(2,1)}, bf16[2,256,640]{2,1,0:T(8,128)(2,1)S(1)}, u32[]{:S(2)}, u32[]{:S(2)}) collective-permute-start(bf16[2,256,640]{2,1,0:T(8,128)(2,1)} %get-tuple-element.312.refs_6_), channel_id=1, source_target_pairs={{0,4},{1,5},{2,6},{3,7},{4,0},{5,1},{6,2},{7,3},{8,12},{9,13},{10,... | collective-permute-start | bytes 1966088 | tf_op jit(solution)/shard_map/ppermute | solution.py:342
  114.4 22.5 %collective-permute-start.6 = (bf16[2,256,640]{2,1,0:T(8,128)(2,1)}, bf16[2,256,640]{2,1,0:T(8,128)(2,1)}, u32[]{:S(2)}, u32[]{:S(2)}) collective-permute-start(bf16[2,256,640]{2,1,0:T(8,128)(2,1)} %get-tuple-element.314.refs_5_), channel_id=1, source_target_pairs={{0,2},{1,3},{2,0},{3,1},{4,6},{5,7},{6,4},{7,5},{8,10},{9,11},{10,... | collective-permute-start | bytes 1966088 | tf_op jit(solution)/shard_map/ppermute | solution.py:342
  117.3 22.0 %copy-start.14 = (bf16[2,256,640]{2,1,0:T(8,128)(2,1)S(1)}, bf16[2,256,640]{2,1,0:T(8,128)(2,1)}, u32[]{:S(2)}) copy-start(bf16[2,256,640]{2,1,0:T(8,128)(2,1)} %get-tuple-element.311) | copy-start | bytes 1966084
  138.0 14.6 %collective-permute-start.9 = (bf16[256,640]{1,0:T(8,128)(2,1)S(1)}, bf16[256,640]{1,0:T(8,128)(2,1)}, u32[]{:S(2)}, u32[]{:S(2)}) collective-permute-start(bf16[256,640]{1,0:T(8,128)(2,1)S(1)} %fusion.61.refs_3_), channel_id=1, source_target_pairs={{0,4},{1,5},{2,6},{3,7},{4,0},{5,1},{6,2},{7,3},{8,12},{9,13},{10,... | collective-permute-start | bytes 983048 | tf_op jit(solution)/shard_map/ppermute | solution.py:342
  140.3 14.3 %collective-permute-start.10 = (bf16[256,640]{1,0:T(8,128)(2,1)S(1)}, bf16[256,640]{1,0:T(8,128)(2,1)S(1)}, u32[]{:S(2)}, u32[]{:S(2)}) collective-permute-start(bf16[256,640]{1,0:T(8,128)(2,1)S(1)} %fusion.59.refs_4_), channel_id=1, source_target_pairs={{0,2},{1,3},{2,0},{3,1},{4,6},{5,7},{6,4},{7,5},{8,10},{9,11},{10,... | collective-permute-start | bytes 983048 | tf_op jit(solution)/shard_map/ppermute | solution.py:342
  160.9 210.4 %all-gather.30.cloned.1.call-start = ((), (), s32[]{:S(2)}) async-start(), calls=%async_computation.9 | async-start | bytes 11796480 | tf_op jit(solution)/shard_map/all_gather | solution.py:388
  161.0 5.2 collective-permute-start.8
  161.0 8.9 %collective-permute-start.14 = (f32[4,256,640]{2,1,0:T(8,128)}, f32[4,256,640]{2,1,0:T(8,128)S(1)}, u32[]{:S(2)}, u32[]{:S(2)}) collective-permute-start(f32[4,256,640]{2,1,0:T(8,128)} %get-tuple-element.181), channel_id=1, source_target_pairs={{0,1},{1,0},{2,3},{3,2},{4,5},{5,4},{6,7},{7,6},{8,9},{9,8},{10,11... | collective-permute-start | bytes 7864328 | tf_op jit(solution)/shard_map/ppermute | solution.py:342
  173.3 47.6 %collective-permute-start.11 = (f32[2,256,640]{2,1,0:T(8,128)S(1)}, f32[2,256,640]{2,1,0:T(8,128)}, u32[]{:S(2)}, u32[]{:S(2)}) collective-permute-start(f32[2,256,640]{2,1,0:T(8,128)S(1)} %get-tuple-element.288.refs_4_), channel_id=1, source_target_pairs={{0,2},{1,3},{2,0},{3,1},{4,6},{5,7},{6,4},{7,5},{8,10},{9,11},{10,... | collective-permute-start | bytes 3932168 | tf_op jit(solution)/shard_map/ppermute | solution.py:342
  176.7 44.9 %collective-permute-start.16 = (f32[2,256,640]{2,1,0:T(8,128)}, f32[2,256,640]{2,1,0:T(8,128)}, u32[]{:S(2)}, u32[]{:S(2)}) collective-permute-start(f32[2,256,640]{2,1,0:T(8,128)} %get-tuple-element.289.refs_5_), channel_id=1, source_target_pairs={{0,4},{1,5},{2,6},{3,7},{4,0},{5,1},{6,2},{7,3},{8,12},{9,13},{10,... | collective-permute-start | bytes 3932168 | tf_op jit(solution)/shard_map/ppermute | solution.py:342
  206.4 18.2 %copy-start.4 = (f32[2,256,640]{2,1,0:T(8,128)S(1)}, f32[2,256,640]{2,1,0:T(8,128)}, u32[]{:S(2)}) copy-start(f32[2,256,640]{2,1,0:T(8,128)} %get-tuple-element.290) | copy-start | bytes 3932164
  223.0 26.4 %collective-permute-start.15 = (f32[256,640]{1,0:T(8,128)S(1)}, f32[256,640]{1,0:T(8,128)}, u32[]{:S(2)}, u32[]{:S(2)}) collective-permute-start(f32[256,640]{1,0:T(8,128)S(1)} %fusion.13.refs_5_), channel_id=1, source_target_pairs={{0,4},{1,5},{2,6},{3,7},{4,0},{5,1},{6,2},{7,3},{8,12},{9,13},{10,... | collective-permute-start | bytes 1966088 | tf_op jit(solution)/shard_map/ppermute | solution.py:342
  226.6 24.4 %collective-permute-start.17 = (f32[256,640]{1,0:T(8,128)}, f32[256,640]{1,0:T(8,128)}, u32[]{:S(2)}, u32[]{:S(2)}) collective-permute-start(f32[256,640]{1,0:T(8,128)} %fusion.11.refs_6_), channel_id=1, source_target_pairs={{0,2},{1,3},{2,0},{3,1},{4,6},{5,7},{6,4},{7,5},{8,10},{9,11},{10,... | collective-permute-start | bytes 1966088 | tf_op jit(solution)/shard_map/ppermute | solution.py:342
  238.2 11.3 %copy-start.3 = (f32[2,1,256,640]{3,2,1,0:T(8,128)S(1)}, f32[2,1,256,640]{3,2,1,0:T(8,128)}, u32[]{:S(2)}) copy-start(f32[2,1,256,640]{3,2,1,0:T(8,128)} %get-tuple-element.287) | copy-start | bytes 3932164
  253.7 136.1 %all-gather.22.cloned.1.call-start = ((), (), s32[]{:S(2)}) async-start(), calls=%async_computation.5 | async-start | bytes 5898240 | tf_op jit(solution)/shard_map/all_gather | solution.py:388
  254.3 3.3 collective-permute-start.18
  254.3 6.0 collective-permute-start.19
  261.6 13.0 %copy-start.8 = (bf16[2,256,640]{2,1,0:T(8,128)(2,1)S(1)}, bf16[2,256,640]{2,1,0:T(8,128)(2,1)}, u32[]{:S(2)}) copy-start(bf16[2,256,640]{2,1,0:T(8,128)(2,1)} %get-tuple-element.310.refs_5_) | copy-start | bytes 1966084
  272.8 25.6 %collective-permute-start.21 = (bf16[4,256,640]{2,1,0:T(8,128)(2,1)}, bf16[4,256,640]{2,1,0:T(8,128)(2,1)}, u32[]{:S(2)}, u32[]{:S(2)}) collective-permute-start(bf16[4,256,640]{2,1,0:T(8,128)(2,1)} %get-tuple-element.206), channel_id=1, source_target_pairs={{0,1},{1,0},{2,3},{3,2},{4,5},{5,4},{6,7},{7,6},{8,9},{9,8},{10,11... | collective-permute-start | bytes 3932168 | tf_op jit(solution)/shard_map/ppermute | solution.py:342
  272.9 25.4 %collective-permute-start.22 = (bf16[4,256,640]{2,1,0:T(8,128)(2,1)}, bf16[4,256,640]{2,1,0:T(8,128)(2,1)}, u32[]{:S(2)}, u32[]{:S(2)}) collective-permute-start(bf16[4,256,640]{2,1,0:T(8,128)(2,1)} %get-tuple-element.207), channel_id=1, source_target_pairs={{0,1},{1,0},{2,3},{3,2},{4,5},{5,4},{6,7},{7,6},{8,9},{9,8},{10,11... | collective-permute-start | bytes 3932168 | tf_op jit(solution)/shard_map/ppermute | solution.py:342
  273.3 25.1 %collective-permute-start.23 = (bf16[2,256,640]{2,1,0:T(8,128)(2,1)}, bf16[2,256,640]{2,1,0:T(8,128)(2,1)}, u32[]{:S(2)}, u32[]{:S(2)}) collective-permute-start(bf16[2,256,640]{2,1,0:T(8,128)(2,1)} %get-tuple-element.308.refs_6_), channel_id=1, source_target_pairs={{0,4},{1,5},{2,6},{3,7},{4,0},{5,1},{6,2},{7,3},{8,12},{9,13},{10,... | collective-permute-start | bytes 1966088 | tf_op jit(solution)/shard_map/ppermute | solution.py:342
  274.5 24.6 %collective-permute-start.20 = (bf16[2,256,640]{2,1,0:T(8,128)(2,1)S(1)}, bf16[2,256,640]{2,1,0:T(8,128)(2,1)}, u32[]{:S(2)}, u32[]{:S(2)}) collective-permute-start(bf16[2,256,640]{2,1,0:T(8,128)(2,1)S(1)} %copy-done.8), channel_id=1, source_target_pairs={{0,2},{1,3},{2,0},{3,1},{4,6},{5,7},{6,4},{7,5},{8,10},{9,11},{10,... | collective-permute-start | bytes 1966088 | tf_op jit(solution)/shard_map/ppermute | solution.py:342
  286.6 18.2 %copy-start.25 = (bf16[4,256,640]{2,1,0:T(8,128)(2,1)S(1)}, bf16[4,256,640]{2,1,0:T(8,128)(2,1)}, u32[]{:S(2)}) copy-start(bf16[4,256,640]{2,1,0:T(8,128)(2,1)} %get-tuple-element.212) | copy-start | bytes 3932164
  300.2 7.3 %copy-start.28 = (bf16[256,640]{1,0:T(8,128)(2,1)}, bf16[256,640]{1,0:T(8,128)(2,1)S(1)}, u32[]{:S(2)}) copy-start(bf16[256,640]{1,0:T(8,128)(2,1)S(1)} %fusion.53.refs_6_) | copy-start | bytes 983044
  302.2 17.5 %collective-permute-start.26 = (bf16[256,640]{1,0:T(8,128)(2,1)}, bf16[256,640]{1,0:T(8,128)(2,1)}, u32[]{:S(2)}, u32[]{:S(2)}) collective-permute-start(bf16[256,640]{1,0:T(8,128)(2,1)} %fusion.55.refs_5_), channel_id=1, source_target_pairs={{0,4},{1,5},{2,6},{3,7},{4,0},{5,1},{6,2},{7,3},{8,12},{9,13},{10,... | collective-permute-start | bytes 983048 | tf_op jit(solution)/shard_map/ppermute | solution.py:342
  302.7 17.0 %collective-permute-start.27 = (bf16[256,640]{1,0:T(8,128)(2,1)S(1)}, bf16[256,640]{1,0:T(8,128)(2,1)}, u32[]{:S(2)}, u32[]{:S(2)}) collective-permute-start(bf16[256,640]{1,0:T(8,128)(2,1)S(1)} %fusion.53.refs_6_), channel_id=1, source_target_pairs={{0,2},{1,3},{2,0},{3,1},{4,6},{5,7},{6,4},{7,5},{8,10},{9,11},{10,... | collective-permute-start | bytes 983048 | tf_op jit(solution)/shard_map/ppermute | solution.py:342
  310.1 9.6 %copy-start.16 = (bf16[2,1,256,640]{3,2,1,0:T(8,128)(2,1)S(1)}, bf16[2,1,256,640]{3,2,1,0:T(8,128)(2,1)}, u32[]{:S(2)}) copy-start(bf16[2,1,256,640]{3,2,1,0:T(8,128)(2,1)} %get-tuple-element.309) | copy-start | bytes 1966084
  325.7 24.2 %copy-start.15 = (bf16[2,1,256,640]{3,2,1,0:T(8,128)(2,1)S(1)}, bf16[2,1,256,640]{3,2,1,0:T(8,128)(2,1)}, u32[]{:S(2)}) copy-start(bf16[2,1,256,640]{3,2,1,0:T(8,128)(2,1)} %get-tuple-element.305) | copy-start | bytes 1966084
  325.7 24.3 %copy-start.13 = (bf16[2,256,640]{2,1,0:T(8,128)(2,1)S(1)}, bf16[2,256,640]{2,1,0:T(8,128)(2,1)}, u32[]{:S(2)}) copy-start(bf16[2,256,640]{2,1,0:T(8,128)(2,1)} %get-tuple-element.303) | copy-start | bytes 1966084
  325.7 93.0 %all-gather.20.cloned.1.call-start = ((), (), s32[]{:S(2)}) async-start(), calls=%async_computation.4 | async-start | bytes 5898240 | tf_op jit(solution)/shard_map/all_gather | solution.py:388
  325.8 19.4 %collective-permute-start.25 = (bf16[2,256,640]{2,1,0:T(8,128)(2,1)S(1)}, bf16[2,256,640]{2,1,0:T(8,128)(2,1)S(1)}, u32[]{:S(2)}, u32[]{:S(2)}) collective-permute-start(bf16[2,256,640]{2,1,0:T(8,128)(2,1)S(1)} %copy-done.7), channel_id=1, source_target_pairs={{0,4},{1,5},{2,6},{3,7},{4,0},{5,1},{6,2},{7,3},{8,12},{9,13},{10,... | collective-permute-start | bytes 1966088 | tf_op jit(solution)/shard_map/ppermute | solution.py:342
  327.1 22.9 %collective-permute-start.24 = (bf16[2,256,640]{2,1,0:T(8,128)(2,1)}, bf16[2,256,640]{2,1,0:T(8,128)(2,1)S(1)}, u32[]{:S(2)}, u32[]{:S(2)}) collective-permute-start(bf16[2,256,640]{2,1,0:T(8,128)(2,1)} %get-tuple-element.306.refs_7_), channel_id=1, source_target_pairs={{0,2},{1,3},{2,0},{3,1},{4,6},{5,7},{6,4},{7,5},{8,10},{9,11},{10,... | collective-permute-start | bytes 1966088 | tf_op jit(solution)/shard_map/ppermute | solution.py:342
  350.0 13.6 %collective-permute-start.28 = (bf16[256,640]{1,0:T(8,128)(2,1)S(1)}, bf16[256,640]{1,0:T(8,128)(2,1)S(1)}, u32[]{:S(2)}, u32[]{:S(2)}) collective-permute-start(bf16[256,640]{1,0:T(8,128)(2,1)S(1)} %fusion.52.refs_7_), channel_id=1, source_target_pairs={{0,4},{1,5},{2,6},{3,7},{4,0},{5,1},{6,2},{7,3},{8,12},{9,13},{10,... | collective-permute-start | bytes 983048 | tf_op jit(solution)/shard_map/ppermute | solution.py:342
  350.8 13.9 %collective-permute-start.29 = (bf16[256,640]{1,0:T(8,128)(2,1)S(1)}, bf16[256,640]{1,0:T(8,128)(2,1)}, u32[]{:S(2)}, u32[]{:S(2)}) collective-permute-start(bf16[256,640]{1,0:T(8,128)(2,1)S(1)} %fusion.50.refs_8_), channel_id=1, source_target_pairs={{0,2},{1,3},{2,0},{3,1},{4,6},{5,7},{6,4},{7,5},{8,10},{9,11},{10,... | collective-permute-start | bytes 983048 | tf_op jit(solution)/shard_map/ppermute | solution.py:342
  371.3 113.6 %all-gather.18.cloned.1.call-start = ((), (), s32[]{:S(2)}) async-start(), calls=%async_computation.3 | async-start | bytes 5898240 | tf_op jit(solution)/shard_map/all_gather | solution.py:388
  389.6 131.1 %all-gather.26.cloned.1.call-start = ((), (), s32[]{:S(2)}) async-start(), calls=%async_computation.7 | async-start | bytes 5898240 | tf_op jit(solution)/shard_map/all_gather | solution.py:388
  431.5 12.7 %collective-permute-start.30 = (bf16[4,256,640]{2,1,0:T(8,128)(2,1)}, bf16[4,256,640]{2,1,0:T(8,128)(2,1)}, u32[]{:S(2)}, u32[]{:S(2)}) collective-permute-start(bf16[4,256,640]{2,1,0:T(8,128)(2,1)} %get-tuple-element.243), channel_id=1, source_target_pairs={{0,1},{1,0},{2,3},{3,2},{4,5},{5,4},{6,7},{7,6},{8,9},{9,8},{10,11... | collective-permute-start | bytes 3932168 | tf_op jit(solution)/shard_map/ppermute | solution.py:342
  431.5 18.9 %collective-permute-start.31 = (bf16[4,256,640]{2,1,0:T(8,128)(2,1)}, bf16[4,256,640]{2,1,0:T(8,128)(2,1)}, u32[]{:S(2)}, u32[]{:S(2)}) collective-permute-start(bf16[4,256,640]{2,1,0:T(8,128)(2,1)} %get-tuple-element.245), channel_id=1, source_target_pairs={{0,1},{1,0},{2,3},{3,2},{4,5},{5,4},{6,7},{7,6},{8,9},{9,8},{10,11... | collective-permute-start | bytes 3932168 | tf_op jit(solution)/shard_map/ppermute | solution.py:342
  447.1 18.4 %collective-permute-start.32 = (bf16[2,256,640]{2,1,0:T(8,128)(2,1)}, bf16[2,256,640]{2,1,0:T(8,128)(2,1)}, u32[]{:S(2)}, u32[]{:S(2)}) collective-permute-start(bf16[2,256,640]{2,1,0:T(8,128)(2,1)} %get-tuple-element.300.refs_4_), channel_id=1, source_target_pairs={{0,2},{1,3},{2,0},{3,1},{4,6},{5,7},{6,4},{7,5},{8,10},{9,11},{10,... | collective-permute-start | bytes 1966088 | tf_op jit(solution)/shard_map/ppermute | solution.py:342
  452.9 17.5 %collective-permute-start.34 = (bf16[2,256,640]{2,1,0:T(8,128)(2,1)}, bf16[2,256,640]{2,1,0:T(8,128)(2,1)}, u32[]{:S(2)}, u32[]{:S(2)}) collective-permute-start(bf16[2,256,640]{2,1,0:T(8,128)(2,1)} %get-tuple-element.302.refs_5_), channel_id=1, source_target_pairs={{0,4},{1,5},{2,6},{3,7},{4,0},{5,1},{6,2},{7,3},{8,12},{9,13},{10,... | collective-permute-start | bytes 1966088 | tf_op jit(solution)/shard_map/ppermute | solution.py:342
  466.5 9.9 %collective-permute-start.33 = (bf16[256,640]{1,0:T(8,128)(2,1)S(1)}, bf16[256,640]{1,0:T(8,128)(2,1)S(1)}, u32[]{:S(2)}, u32[]{:S(2)}) collective-permute-start(bf16[256,640]{1,0:T(8,128)(2,1)S(1)} %fusion.41), channel_id=1, source_target_pairs={{0,4},{1,5},{2,6},{3,7},{4,0},{5,1},{6,2},{7,3},{8,12},{9,13},{10,... | collective-permute-start | bytes 983048 | tf_op jit(solution)/shard_map/ppermute | solution.py:342
  470.4 8.7 %copy-start.20 = (bf16[2,256,640]{2,1,0:T(8,128)(2,1)S(1)}, bf16[2,256,640]{2,1,0:T(8,128)(2,1)}, u32[]{:S(2)}) copy-start(bf16[2,256,640]{2,1,0:T(8,128)(2,1)} %get-tuple-element.301) | copy-start | bytes 1966084
  471.6 7.5 %collective-permute-start.35 = (bf16[256,640]{1,0:T(8,128)(2,1)S(1)}, bf16[256,640]{1,0:T(8,128)(2,1)S(1)}, u32[]{:S(2)}, u32[]{:S(2)}) collective-permute-start(bf16[256,640]{1,0:T(8,128)(2,1)S(1)} %fusion.38), channel_id=1, source_target_pairs={{0,2},{1,3},{2,0},{3,1},{4,6},{5,7},{6,4},{7,5},{8,10},{9,11},{10,... | collective-permute-start | bytes 983048 | tf_op jit(solution)/shard_map/ppermute | solution.py:342
  484.9 118.7 %all-gather.24.cloned.1.call-start = ((), (), s32[]{:S(2)}) async-start(), calls=%async_computation.6 | async-start | bytes 11796480 | tf_op jit(solution)/shard_map/all_gather | solution.py:388
  485.7 179.6 %all-gather.28.cloned.1.call-start = ((), (), s32[]{:S(2)}) async-start(), calls=%async_computation.8 | async-start | bytes 11796480 | tf_op jit(solution)/shard_map/all_gather | solution.py:388
  531.8 11.6 %collective-permute-start.36 = (bf16[4,256,640]{2,1,0:T(8,128)(2,1)}, bf16[4,256,640]{2,1,0:T(8,128)(2,1)}, u32[]{:S(2)}, u32[]{:S(2)}) collective-permute-start(bf16[4,256,640]{2,1,0:T(8,128)(2,1)} %get-tuple-element.263), channel_id=1, source_target_pairs={{0,1},{1,0},{2,3},{3,2},{4,5},{5,4},{6,7},{7,6},{8,9},{9,8},{10,11... | collective-permute-start | bytes 3932168 | tf_op jit(solution)/shard_map/ppermute | solution.py:342
  532.1 15.6 %collective-permute-start.37 = (bf16[4,256,640]{2,1,0:T(8,128)(2,1)}, bf16[4,256,640]{2,1,0:T(8,128)(2,1)}, u32[]{:S(2)}, u32[]{:S(2)}) collective-permute-start(bf16[4,256,640]{2,1,0:T(8,128)(2,1)} %get-tuple-element.265), channel_id=1, source_target_pairs={{0,1},{1,0},{2,3},{3,2},{4,5},{5,4},{6,7},{7,6},{8,9},{9,8},{10,11... | collective-permute-start | bytes 3932168 | tf_op jit(solution)/shard_map/ppermute | solution.py:342
  546.2 28.5 %collective-permute-start.38 = (bf16[2,256,640]{2,1,0:T(8,128)(2,1)S(1)}, bf16[2,256,640]{2,1,0:T(8,128)(2,1)}, u32[]{:S(2)}, u32[]{:S(2)}) collective-permute-start(bf16[2,256,640]{2,1,0:T(8,128)(2,1)S(1)} %get-tuple-element.296.refs_7_), channel_id=1, source_target_pairs={{0,2},{1,3},{2,0},{3,1},{4,6},{5,7},{6,4},{7,5},{8,10},{9,11},{10,... | collective-permute-start | bytes 1966088 | tf_op jit(solution)/shard_map/ppermute | solution.py:342
  550.2 32.0 %collective-permute-start.40 = (bf16[2,256,640]{2,1,0:T(8,128)(2,1)}, bf16[2,256,640]{2,1,0:T(8,128)(2,1)}, u32[]{:S(2)}, u32[]{:S(2)}) collective-permute-start(bf16[2,256,640]{2,1,0:T(8,128)(2,1)} %get-tuple-element.298.refs_8_), channel_id=1, source_target_pairs={{0,4},{1,5},{2,6},{3,7},{4,0},{5,1},{6,2},{7,3},{8,12},{9,13},{10,... | collective-permute-start | bytes 1966088 | tf_op jit(solution)/shard_map/ppermute | solution.py:342
  560.8 34.9 %copy-start.18 = (bf16[2,1,256,640]{3,2,1,0:T(8,128)(2,1)S(1)}, bf16[2,1,256,640]{3,2,1,0:T(8,128)(2,1)}, u32[]{:S(2)}) copy-start(bf16[2,1,256,640]{3,2,1,0:T(8,128)(2,1)} %get-tuple-element.295) | copy-start | bytes 1966084
  575.8 19.9 %collective-permute-start.39 = (bf16[256,640]{1,0:T(8,128)(2,1)S(1)}, bf16[256,640]{1,0:T(8,128)(2,1)S(1)}, u32[]{:S(2)}, u32[]{:S(2)}) collective-permute-start(bf16[256,640]{1,0:T(8,128)(2,1)S(1)} %fusion.35), channel_id=1, source_target_pairs={{0,4},{1,5},{2,6},{3,7},{4,0},{5,1},{6,2},{7,3},{8,12},{9,13},{10,... | collective-permute-start | bytes 983048 | tf_op jit(solution)/shard_map/ppermute | solution.py:342
  582.2 16.0 %copy-start.19 = (bf16[2,256,640]{2,1,0:T(8,128)(2,1)S(1)}, bf16[2,256,640]{2,1,0:T(8,128)(2,1)}, u32[]{:S(2)}) copy-start(bf16[2,256,640]{2,1,0:T(8,128)(2,1)} %get-tuple-element.297) | copy-start | bytes 1966084
  583.4 14.9 %collective-permute-start.41 = (bf16[256,640]{1,0:T(8,128)(2,1)S(1)}, bf16[256,640]{1,0:T(8,128)(2,1)S(1)}, u32[]{:S(2)}, u32[]{:S(2)}) collective-permute-start(bf16[256,640]{1,0:T(8,128)(2,1)S(1)} %fusion.32), channel_id=1, source_target_pairs={{0,2},{1,3},{2,0},{3,1},{4,6},{5,7},{6,4},{7,5},{8,10},{9,11},{10,... | collective-permute-start | bytes 983048 | tf_op jit(solution)/shard_map/ppermute | solution.py:342
  (26 other events, 78.5 us)
Sparse Core Ops, SparseCore 0:
  29.2 33.0 all-gather.13
  113.5 47.5 all-gather.11
  163.0 54.5 all-gather.15
  253.8 74.5 all-gather.29
  330.1 43.6 all-gather.21
  375.5 38.0 all-gather.19
  415.4 37.2 all-gather.17
  485.0 35.6 all-gather.25
  523.1 80.4 all-gather.23
  605.8 59.3 all-gather.27

commit v2 on v1

--- a/solution.py
+++ b/solution.py
@@ -280,12 +280,43 @@
     return seq_call(body, rank, ins, [("row", base.shape, F32)], [], 2 * base.size * wo_all.shape[0], after)
 
 
-def emit(rank, array, after=()):
-    def body(in_refs, out_refs):
-        out_refs[0][...] = in_refs[0][...]
-        return ()
-
-    return seq_call(body, rank, [("row", array)], [("row", array.shape, array.dtype)], [], 16 * array.size, after)
+def assemble(rank, pieces, after=()):
+    rows, width = pieces[0].shape
+    half = width // 2
+
+    def kernel(rank_ref, *refs):
+        out_ref, token_ref = refs[-2:]
+        token_ref[...] = jnp.zeros((8, 128), F32)
+        step = pl.program_id(0)
+        for place in range(6):
+
+            @pl.when(step == place)
+            def _(place=place):
+                out_ref[...] = refs[place][...]
+
+        for place in range(2):
+
+            @pl.when(step == 6 + place)
+            def _(place=place):
+                out_ref[:, :half] = refs[6 + 2 * place][...]
+                out_ref[:, half:] = refs[7 + 2 * place][...]
+
+    return pl.pallas_call(
+        kernel,
+        grid_spec=pltpu.PrefetchScalarGridSpec(
+            num_scalar_prefetch=1,
+            grid=(8,),
+            in_specs=[pl.BlockSpec(piece.shape, lambda g, rk: (0, 0)) for piece in pieces]
+            + [pl.BlockSpec(memory_space=pl.ANY)] * len(after),
+            out_specs=[
+                pl.BlockSpec((None, rows, width), lambda g, rk: (g ^ rk[0], 0, 0)),
+                pl.BlockSpec((8, 128), lambda g, rk: (0, 0)),
+            ],
+        ),
+        out_shape=[jax.ShapeDtypeStruct((8, rows, width), F32), jax.ShapeDtypeStruct((8, 128), F32)],
+        compiler_params=pltpu.CompilerParams(dimension_semantics=("arbitrary",), vmem_limit_bytes=60 * MIB),
+        cost_estimate=pl.CostEstimate(flops=2 * 10**9, bytes_accessed=64 * rows * width, transcendentals=0),
+    )(rank, *pieces, *after)
 
 
 def weight_grads(stacks, layers, layer, jobs, after=()):
@@ -388,6 +419,24 @@
     return lax.all_gather(shard, "tp", axis=0, tiled=True)
 
 
+def spread_first(shard):
+    return [permute(shard, bit) for bit in (1, 2, 4)]
+
+
+def spread_second(near, fill):
+    _, near_x, near_y = near
+    near_x, near_y = tie(near_x, fill), tie(near_y, fill)
+    half = near_x.shape[-1] // 2
+    halves = (permute(near_y[:, :half], 2), permute(near_x[:, half:], 4))
+    return halves, (permute(near_x, 1), permute(near_y, 1))
+
+
+def spread_last(shard, near, halves, cross, fill):
+    left, right = (tie(half, fill) for half in halves)
+    cross_halves = [permute(half, 1) for half in (left, right)]
+    return [shard, near[0], near[1], cross[0], near[2], cross[1], left, right, *cross_halves]
+
+
 def solution(mesh):
     act_spec = P("dp", None, None)
     saved_spec = P(None, "dp", None, None)
@@ -441,45 +490,53 @@
         back = sum_end(value, final, [tok])
         d_one = shard(dy_one) + rms_vjp(shard(y_one), back)
         d_one_bf = gather(d_one.astype(BF))
-        sum_out, sent = sum_first(sum_cores(parts), [back])
-        f_hi, o_hi, qkv_hi, tok = attn(rank, head_dim, qkv_w, o_w, hi, x=s_two, norm=True, after=[tok, wo_all, *sent])
+        sum_out, sent_low = sum_first(sum_cores(parts), [d_one_bf])
+        f_hi, o_hi, qkv_hi, tok = attn(rank, head_dim, qkv_w, o_w, hi, x=s_two, norm=True, after=[tok, wo_all])
         o_top, qkv_top, tok = attn(rank, head_dim, qkv_w, o_w, top, x=f_top, after=[tok])
-        value, sent, final = sum_second(sum_out, [tok])
-        dqkv_top, *parts, tok = attn(rank, head_dim, qkv_w, o_w, top, qkv=qkv_top, d=d_one_bf, after=[tok, *sent])
-        g_sum = sum_end(value, final, [tok])
-        g_full = gather(g_sum)
-        x_two = shard(s_two) - g_sum
+        dqkv_top, *parts, tok = attn(rank, head_dim, qkv_w, o_w, top, qkv=qkv_top, d=d_one_bf, after=[tok, *sent_low])
         sum_top, sent = sum_first(sum_cores(parts))
         dqkv_hi, *parts, tok = attn(rank, head_dim, qkv_w, o_w, hi, qkv=qkv_hi, d=d_one_bf, after=[tok, *sent])
         sum_hi = sum_cores(parts)
         value, sent, final = sum_second(sum_top, [tok, *received(sum_hi)])
         sum_hi, sent_hi = sum_first(sum_hi, sent)
-        tok = attn_grads(top, f_top, o_top, dqkv_top, d_one_bf, [tok, *sent, *sent_hi])
+        value_low, sent_low, final_low = sum_second(sum_out, [tok, *sent_hi])
+        tok = attn_grads(top, f_top, o_top, dqkv_top, d_one_bf, [tok, *sent, *sent_hi, *sent_low])
         d_two = shard(dy_two) + rms_vjp(x_two_top, sum_end(value, final, [tok]))
-        d_two_hi_bf = gather(d_two.astype(BF))
+        rounded, d_two = lax.optimization_barrier((d_two.astype(BF), d_two))
+        d_two_hi_bf = gather(rounded)
         value, sent, final = sum_second(sum_hi, [tok])
         tok = attn_grads(hi, f_hi, o_hi, dqkv_hi, d_one_bf, [tok, *sent])
         d_two = d_two + rms_vjp(shard(s_two), sum_end(value, final, [tok]))
         d_two_lo_bf = gather(d_two.astype(BF))
-        x_two_full, f_lo, o_lo, qkv_lo, tok = attn(rank, head_dim, qkv_w, o_w, lo, x=s_two, minus=g_full, norm=True, after=[tok])
-        o_all = gather(o_lo)
-        dh_hi, tok = mlp_dhid(rank, d_two_hi_bf, w_out, hi, sl_hi, [tok])
+        x_two = shard(s_two) - sum_end(value_low, final_low, [tok])
+        x_two_shard = tie(x_two, [d_two])[0]
+        near = spread_first(x_two_shard)
+        dh_hi, tok = mlp_dhid(rank, d_two_hi_bf, w_out, hi, sl_hi, [tok, x_two_shard])
         tok = mlp_grad("in", hi, s_a, dh_hi, [tok])
         tok = mlp_grad("out", hi, act_hi, d_two_hi_bf, [tok])
-        dh_lo, *parts, tok = mlp_pair_back(rank, d_two_lo_bf, w_out, sl_lo, dh_hi, w_in, hi, lo, [tok])
+        far, cross = spread_second(near, [tok])
+        dh_lo, *parts, tok = mlp_pair_back(rank, d_two_lo_bf, w_out, sl_lo, dh_hi, w_in, hi, lo, [tok, near[1], near[2]])
+        pieces = spread_last(x_two_shard, near, far, cross, [tok])
         sum_g, sent = sum_first(sum_cores(parts))
         tok_in = mlp_grad("in", lo, s_a, dh_lo, [tok, *sent])
         tok = mlp_grad("out", lo, act_lo, d_two_lo_bf, [tok_in])
         value, sent, final = sum_second(sum_g, [tok_in])
         d_one = d_one + rms_vjp(shard(s_one), sum_end(value, final))
-        d_one_bf = gather(tie(d_one.astype(BF), [o_all]))
-        x_one_full, tok = attn_value(rank, s_one, o_all, wo_all, [tok])
+        d_one_bf = gather(d_one.astype(BF))
+        x_two_full, tok = assemble(rank, pieces, [tok])
+        f_lo, o_lo, qkv_lo, tok = attn(rank, head_dim, qkv_w, o_w, lo, x=x_two_full, norm=True, after=[tok])
+        o_all = gather(o_lo)
+        d_one_shard = tie(d_one, [d_one_bf])[0]
+        near = spread_first(d_one_shard)
         dqkv_lo, *parts, tok = attn(rank, head_dim, qkv_w, o_w, lo, qkv=qkv_lo, d=d_one_bf, after=[tok])
         sum_lo, sent = sum_first(sum_cores(parts))
         tok = attn_grads(lo, f_lo, o_lo, dqkv_lo, d_one_bf, [tok, *sent])
         value, sent, final = sum_second(sum_lo, [tok])
+        far, cross = spread_second(near, [tok, *sent])
+        x_one_full, tok_x = attn_value(rank, s_one, o_all, wo_all, [tok, *sent])
         d_two = d_two + rms_vjp(x_two, sum_end(value, final))
-        d_one_full, _ = emit(rank, gather(d_one), [tok])
+        pieces = spread_last(d_one_shard, near, far, cross, [tok_x])
+        d_one_full, _ = assemble(rank, pieces, [tok_x])
         grad_qkv = stacks["attn"][0].reshape(n_layers, 3, n_heads, head_dim, width).transpose(0, 4, 1, 2, 3)
         grad_o = stacks["attn"][1].reshape(w_o.shape)
         return (x_one_full, x_two_full, d_one_full, gather(d_two), grad_qkv, grad_o, stacks["in"][0], stacks["out"][0])

time: 691 us -> 734 us (1.062)
  waiting for transfers between devices: 184 us -> 216 us
  local copies, waits for them, and re-layouts: 13.2 us -> 23.3 us
  other arithmetic: 96.3 us -> 88.1 us
    ppermute x42 -> x60, waiting for transfers between devices: 120 us -> 194 us  [permute(): return lax.ppermute(array, 'tp', [(idx, idx ^ bit) for idx in range(8)])]
    all_gather x10 -> x8, waiting for transfers between devices: 63.5 us -> 21.7 us  [gather(): return lax.all_gather(shard, 'tp', axis=0, tiled=True)]
    pallas_call x0 -> x2, Pallas kernels: none -> 18.5 us  [assemble(): pl.pallas_call(kernel, grid_spec=pltpu.PrefetchScalarGridSpec(num_scalar_...]
    pallas_call x22 -> x21, Pallas kernels: 250 us -> 235 us  [run(): pl.pallas_call(kernel, grid_spec=pltpu.PrefetchScalarGridSpec(num_scalar_...]
    ppermute x42 -> x60, starting transfers between devices: 38 us -> 44.2 us  [permute(): return lax.ppermute(array, 'tp', [(idx, idx ^ bit) for idx in range(8)])]
    unnamed x77 -> x113, local copies, waits for them, and re-layouts: 11.4 us -> 17.2 us
  transfers between devices with their start and end apart: 52 -> 68, of which waited for: 27 -> 30; matrix products, arithmetic and copies ran while one was open for 14% -> 11% of each run, Pallas kernels for 46% -> 39%
where the time goes in v2:
time: 734 us; the launch traced here: 723 us
  Pallas kernels  336 us (46%)
  waiting for transfers between devices  216 us (29%)
  other arithmetic  88.1 us (12%)
  starting transfers between devices  45.4 us (6%)
  local copies, waits for them, and re-layouts  23.3 us (3%)
  between operations  15 us (2%)
    pallas_call x21, Pallas kernels, run(): pl.pallas_call(kernel, grid_spec=pltpu.PrefetchScalarGridSpec(num_scalar_...  235 us
    ppermute x60, waiting for transfers between devices, permute(): return lax.ppermute(array, 'tp', [(idx, idx ^ bit) for idx in range(8)])  194 us
    pallas_call x9, Pallas kernels, weight_grads(): *stacks, token = call(*args)  82.6 us
    ppermute x60, starting transfers between devices, permute(): return lax.ppermute(array, 'tp', [(idx, idx ^ bit) for idx in range(8)])  44.2 us
    add x13, other arithmetic, sum_first(): pick(keep, 0) + pick(recv, 0)  30.4 us
    all_gather x8, waiting for transfers between devices, gather(): return lax.all_gather(shard, 'tp', axis=0, tiled=True)  21.7 us
    pallas_call x2, Pallas kernels, assemble(): pl.pallas_call(kernel, grid_spec=pltpu.PrefetchScalarGridSpec(num_scalar_...  18.5 us
    unnamed x113, local copies, waits for them, and re-layouts  17.2 us
  transfers between devices with their start and end apart: 68, of which 30 were waited for; matrix products, arithmetic and copies ran while one was open for 11% of the time, Pallas kernels for 39%

profile of v2, /device:TPU:0, one launch (start us, length us, event | category | flops | bytes accessed | tf_op | source)
XLA Modules:
  0.0 723.5 jit_solution(10289113044148212484)
XLA Ops:
  7.2 13.6 %shard_map.161 = (bf16[8,256,1280]{2,1,0:T(8,128)(2,1)}, f32[8,256,640]{2,1,0:T(8,128)}, bf16[8,256,640]{2,1,0:T(8,128)(2,1)}, f32[8,128]{1,0:T(8,128)}) custom-call(s32[1]{0:T(128)} %bitcast.rank_ref, f32[8,256,1280]{2,1,0:T(8,128)} %refs_0_.3, bf16[3,1280,640]{2,1,0:T(8,128)(2,1)} %refs_5_.3), custom_call_target="tpu_custom_call" | custom-call | flops 3355443200 | bytes 13111296 | tf_op jit(solution)/shard_map/pallas_call | solution.py:91
  20.8 5.7 shard_map.162
  29.2 5.8 shard_map.163
  36.4 4.2 slice_add_fusion.3
  40.6 3.1 slice_add_fusion.2
  43.8 9.7 %shard_map.164 = (bf16[8,256,1280]{2,1,0:T(8,128)(2,1)}, bf16[8,256,640]{2,1,0:T(8,128)(2,1)}, bf16[4,256,640]{2,1,0:T(8,128)(2,1)}, bf16[4,256,640]{2,1,0:T(8,128)(2,1)}, f32[8,128]{1,0:T(8,128)}) custom-call(s32[1]{0:T(128)} %bitcast.rank_ref, f32[8,256,1280]{2,1,0:T(8,128)} %refs_0_.5, bf16[3,640,1280]{2,1,0:T(8,128)(2,1)} %refs_1_.21, ...), custom_call_target="tpu_custom_call" | custom-call | flops 3355443200 | bytes 5244928 | tf_op jit(solution)/shard_map/pallas_call | solution.py:91
  54.0 2.5 collective-permute-start.5
  58.0 9.4 %shard_map.165 = (bf16[8,256,1280]{2,1,0:T(8,128)(2,1)}, bf16[8,256,640]{2,1,0:T(8,128)(2,1)}, bf16[4,256,640]{2,1,0:T(8,128)(2,1)}, bf16[4,256,640]{2,1,0:T(8,128)(2,1)}, f32[8,128]{1,0:T(8,128)}) custom-call(s32[1]{0:T(128)} %bitcast.rank_ref, f32[8,256,1280]{2,1,0:T(8,128)} %refs_0_.5, ...), custom_call_target="tpu_custom_call", output_to_operand_aliasing={{0}: (5, {}), {1}: (6, {})} | custom-call | flops 3355443200 | bytes 5244928 | tf_op jit(solution)/shard_map/pallas_call | solution.py:91
  67.4 9.0 %shard_map.166 = (f32[3,1280,640]{2,1,0:T(8,128)}, f32[8,128]{1,0:T(8,128)}) custom-call(bf16[2048,1280]{1,0:T(8,128)(2,1)} %bitcast.385, bf16[2048,640]{1,0:T(8,128)(2,1)} %bitcast.370, f32[8,128]{1,0:T(8,128)} %get-tuple-element.168.refs_2_, bf16[2,2,256,640]{3,2,1,0:T(8,128)(2,1)} %bitcast.12.refs_3_, bf16[2,2,256,640]{3,2,1,0:T(8,128)(2,1)} %bitcast.13.refs_4_), custom_call_target="tpu_custom_call" | custom-call | flops 3355443200 | bytes 17367040 | tf_op jit(solution)/shard_map/pallas_call | solution.py:368
  76.3 11.1 %collective-permute-done.5 = f32[2,256,640]{2,1,0:T(8,128)} collective-permute-done((f32[2,256,640]{2,1,0:T(8,128)}, f32[2,256,640]{2,1,0:T(8,128)}, u32[]{:S(2)}, u32[]{:S(2)}) %collective-permute-start.5) | collective-permute-done | bytes 1310752 | tf_op jit(solution)/shard_map/ppermute | solution.py:373
  87.4 2.6 fusion.25
  96.9 8.8 %shard_map.167 = (f32[3,640,1280]{2,1,0:T(8,128)}, f32[8,128]{1,0:T(8,128)}) custom-call(bf16[2048,640]{1,0:T(8,128)(2,1)} %bitcast.359, bf16[2048,1280]{1,0:T(8,128)(2,1)} %bitcast.363, f32[8,128]{1,0:T(8,128)} %get-tuple-element.171.refs_2_, f32[256,640]{1,0:T(8,128)} %get-tuple-element.341.refs_3_, f32[256,640]{1,0:T(8,128)} %get-tuple-element.340.refs_4_, ...), custom_call_target="tpu_custom_call" | custom-call | flops 3355443200 | bytes 17367040 | tf_op jit(solution)/shard_map/pallas_call | solution.py:368
  117.4 18.1 %shard_map.168 = (bf16[8,256,1280]{2,1,0:T(8,128)(2,1)}, f32[8,256,640]{2,1,0:T(8,128)}, bf16[8,256,640]{2,1,0:T(8,128)(2,1)}, f32[8,256,640]{2,1,0:T(8,128)}, b...) custom-call(s32[1]{0:T(128)} %bitcast.rank_ref, f32[8,256,1280]{2,1,0:T(8,128)} %bitcast.376, ...), custom_call_target="tpu_custom_call" | custom-call | flops 6710886400 | bytes 20975616 | tf_op jit(solution)/shard_map/pallas_call | solution.py:91
  141.2 5.8 shard_map.169
  147.0 5.9 shard_map.170
  157.9 3.4 fusion.68
  162.0 14.9 %shard_map.171 = (bf16[8,256,1280]{2,1,0:T(8,128)(2,1)}, bf16[160,2048]{1,0:T(8,128)(2,1)}, bf16[480,2048]{1,0:T(8,128)(2,1)}, f32[8,128]{1,0:T(8,128)}) custom-call(s32[1]{0:T(128)} %bitcast.rank_ref, bf16[3,480,1280]{2,1,0:T(8,128)(2,1)} %bitcast.328, f32[8,256,1280]{2,1,0:T(8,128)} %bitcast.358, f32[8,128]{1,0:T(8,128)} %get-tuple-element.186.refs_2_, ...), custom_call_target="tpu_custom_call" | custom-call | flops 2852126720 | bytes 7868416 | tf_op jit(solution)/shard_map/pallas_call | solution.py:91
  176.9 13.0 %shard_map.172 = (bf16[160,2048]{1,0:T(8,128)(2,1)}, bf16[480,2048]{1,0:T(8,128)(2,1)}, f32[8,128]{1,0:T(8,128)}) custom-call(s32[1]{0:T(128)} %bitcast.rank_ref, bf16[3,480,1280]{2,1,0:T(8,128)(2,1)} %bitcast.329, bf16[8,256,1280]{2,1,0:T(8,128)(2,1)} %all-gather.13.cloned.1.call-done.refs_1_, f32[8,128]{1,0:T(8,128)} %get-tuple-element.193.refs_2_), custom_call_target="tpu_custom_call" | custom-call | flops 2852126720 | bytes 2625536 | tf_op jit(solution)/shard_map/pallas_call | solution.py:91
  189.9 10.9 %all-gather.9.cloned.1.call-done.refs_3_ = bf16[8,256,1280]{2,1,0:T(8,128)(2,1)} async-done(((bf16[1,256,1280]{2,1,0:T(8,128)(2,1)}), bf16[8,256,1280]{2,1,0:T(8,128)(2,1)}) %all-gather.9.cloned.1.call-update) | async-done | bytes 5242896 | tf_op jit(solution)/shard_map/all_gather | solution.py:419
  200.8 4.4 slice_add_fusion.1
  205.2 3.6 bitcast_add_fusion.1
  208.8 11.2 %shard_map.173 = (bf16[480,2048]{1,0:T(8,128)(2,1)}, bf16[4,256,640]{2,1,0:T(8,128)(2,1)}, bf16[4,256,640]{2,1,0:T(8,128)(2,1)}, f32[8,128]{1,0:T(8,128)}) custom-call(s32[1]{0:T(128)} %bitcast.rank_ref, bf16[3,480,1280]{2,1,0:T(8,128)(2,1)} %bitcast.330, bf16[480,2048]{1,0:T(8,128)(2,1)} %get-tuple-element.194.refs_1_, bf16[3,160,1280]{2,1,0:T(8,128)(2,1)} %bitcast.339, ...), custom_call_target="tpu_custom_call" | custom-call | flops 2097152000 | bytes 2295808 | tf_op jit(solution)/shard_map/pallas_call | solution.py:91
  220.5 11.1 %shard_map.174 = (bf16[480,2048]{1,0:T(8,128)(2,1)}, bf16[4,256,640]{2,1,0:T(8,128)(2,1)}, bf16[4,256,640]{2,1,0:T(8,128)(2,1)}, f32[8,128]{1,0:T(8,128)}) custom-call(s32[1]{0:T(128)} %bitcast.rank_ref, bf16[3,480,1280]{2,1,0:T(8,128)(2,1)} %bitcast.331, bf16[480,2048]{1,0:T(8,128)(2,1)} %get-tuple-element.194.refs_1_, ...), custom_call_target="tpu_custom_call", output_to_operand_aliasing={{0}: (5, {})} | custom-call | flops 2097152000 | bytes 2295808 | tf_op jit(solution)/shard_map/pallas_call | solution.py:91
  231.7 3.0 slice_add_fusion.18
  235.9 11.3 %shard_map.175 = (bf16[480,2048]{1,0:T(8,128)(2,1)}, bf16[4,256,640]{2,1,0:T(8,128)(2,1)}, bf16[4,256,640]{2,1,0:T(8,128)(2,1)}, f32[8,128]{1,0:T(8,128)}) custom-call(s32[1]{0:T(128)} %bitcast.rank_ref, bf16[3,480,1280]{2,1,0:T(8,128)(2,1)} %bitcast.332, bf16[480,2048]{1,0:T(8,128)(2,1)} %get-tuple-element.190.refs_1_, bf16[3,160,1280]{2,1,0:T(8,128)(2,1)} %bitcast.341, ...), custom_call_target="tpu_custom_call" | custom-call | flops 2097152000 | bytes 2295808 | tf_op jit(solution)/shard_map/pallas_call | solution.py:91
  250.9 14.1 %collective-permute-done.20 = bf16[2,256,640]{2,1,0:T(8,128)(2,1)} collective-permute-done((bf16[2,256,640]{2,1,0:T(8,128)(2,1)}, bf16[2,256,640]{2,1,0:T(8,128)(2,1)}, u32[]{:S(2)}, u32[]{:S(2)}) %collective-permute-start.20) | collective-permute-done | bytes 655392 | tf_op jit(solution)/shard_map/ppermute | solution.py:373
  266.2 11.1 %shard_map.176 = (bf16[480,2048]{1,0:T(8,128)(2,1)}, bf16[4,256,640]{2,1,0:T(8,128)(2,1)}, bf16[4,256,640]{2,1,0:T(8,128)(2,1)}, f32[8,128]{1,0:T(8,128)}) custom-call(s32[1]{0:T(128)} %bitcast.rank_ref, bf16[3,480,1280]{2,1,0:T(8,128)(2,1)} %bitcast.333, bf16[480,2048]{1,0:T(8,128)(2,1)} %get-tuple-element.190.refs_1_, ...), custom_call_target="tpu_custom_call", output_to_operand_aliasing={{0}: (5, {})} | custom-call | flops 2097152000 | bytes 2295808 | tf_op jit(solution)/shard_map/pallas_call | solution.py:91
  281.8 2.6 slice_add_fusion.15
  284.5 2.6 bitcast_add_fusion.2
  287.2 7.5 %collective-permute-done.11 = f32[2,256,640]{2,1,0:T(8,128)} collective-permute-done((f32[2,256,640]{2,1,0:T(8,128)S(1)}, f32[2,256,640]{2,1,0:T(8,128)}, u32[]{:S(2)}, u32[]{:S(2)}) %collective-permute-start.11) | collective-permute-done | bytes 1310752 | tf_op jit(solution)/shard_map/ppermute | solution.py:373
  300.9 9.6 %shard_map.177 = (f32[3,480,1280]{2,1,0:T(8,128)}, f32[3,160,1280]{2,1,0:T(8,128)}, f32[8,128]{1,0:T(8,128)}) custom-call(bf16[480,2048]{1,0:T(8,128)(2,1)} %get-tuple-element.221.refs_0_, bf16[2048,1280]{1,0:T(8,128)(2,1)} %bitcast.364, bf16[160,2048]{1,0:T(8,128)(2,1)} %get-tuple-element.222.refs_2_, bf16[2048,1280]{1,0:T(8,128)(2,1)} %bitcast.337, ...), custom_call_target="tpu_custom_call" | custom-call | flops 3355443200 | bytes 27852800 | tf_op jit(solution)/shard_map/pallas_call | solution.py:368
  313.2 2.6 fusion.66
  321.7 19.3 %collective-permute-done.24 = bf16[2,256,640]{2,1,0:T(8,128)(2,1)S(1)} collective-permute-done((bf16[2,256,640]{2,1,0:T(8,128)(2,1)}, bf16[2,256,640]{2,1,0:T(8,128)(2,1)S(1)}, u32[]{:S(2)}, u32[]{:S(2)}) %collective-permute-start.24) | collective-permute-done | bytes 655392 | tf_op jit(solution)/shard_map/ppermute | solution.py:373
  344.1 9.6 %shard_map.178 = (f32[3,480,1280]{2,1,0:T(8,128)}, f32[3,160,1280]{2,1,0:T(8,128)}, f32[8,128]{1,0:T(8,128)}) custom-call(bf16[480,2048]{1,0:T(8,128)(2,1)} %get-tuple-element.218.refs_0_, bf16[2048,1280]{1,0:T(8,128)(2,1)} %bitcast.369, bf16[160,2048]{1,0:T(8,128)(2,1)} %get-tuple-element.220.refs_2_, ...), custom_call_target="tpu_custom_call", output_to_operand_aliasing={{0}: (4, {}), {1}: (5, {})} | custom-call | flops 3355443200 | bytes 27852800 | tf_op jit(solution)/shard_map/pallas_call | solution.py:368
  353.7 13.9 %collective-permute-done.25 = f32[256,640]{1,0:T(8,128)} collective-permute-done((f32[256,640]{1,0:T(8,128)}, f32[256,640]{1,0:T(8,128)}, u32[]{:S(2)}, u32[]{:S(2)}) %collective-permute-start.25) | collective-permute-done | bytes 655392 | tf_op jit(solution)/shard_map/ppermute | solution.py:373
  370.8 2.5 collective-permute-done.29
  377.3 3.1 fusion.65
  382.5 10.8 %shard_map.179 = (bf16[8,256,640]{2,1,0:T(8,128)(2,1)}, f32[8,128]{1,0:T(8,128)}) custom-call(s32[1]{0:T(128)} %bitcast.rank_ref, bf16[8,256,1280]{2,1,0:T(8,128)(2,1)} %all-gather.15.cloned.1.call-done.refs_0_, bf16[3,640,1280]{2,1,0:T(8,128)(2,1)} %refs_1_.21, f32[8,256,640]{2,1,0:T(8,128)} %get-tuple-element.242.refs_2_, ...), custom_call_target="tpu_custom_call" | custom-call | flops 3355443200 | bytes 2625536 | tf_op jit(solution)/shard_map/pallas_call | solution.py:91
  393.2 8.9 %shard_map.180 = (f32[3,1280,640]{2,1,0:T(8,128)}, f32[8,128]{1,0:T(8,128)}) custom-call(bf16[2048,1280]{1,0:T(8,128)(2,1)} %bitcast.356, bf16[2048,640]{1,0:T(8,128)(2,1)} %bitcast.353, f32[3,1280,640]{2,1,0:T(8,128)} %get-tuple-element.244.refs_2_, f32[8,128]{1,0:T(8,128)} %get-tuple-element.245.refs_3_), custom_call_target="tpu_custom_call", output_to_operand_aliasing={{0}: (2, {})} | custom-call | flops 3355443200 | bytes 17367040 | tf_op jit(solution)/shard_map/pallas_call | solution.py:368
  402.2 8.9 %shard_map.181 = (f32[3,640,1280]{2,1,0:T(8,128)}, f32[8,128]{1,0:T(8,128)}) custom-call(bf16[2048,640]{1,0:T(8,128)(2,1)} %bitcast.371, bf16[2048,1280]{1,0:T(8,128)(2,1)} %bitcast.355, f32[3,640,1280]{2,1,0:T(8,128)} %get-tuple-element.240.refs_2_, f32[8,128]{1,0:T(8,128)} %get-tuple-element.246.refs_3_), custom_call_target="tpu_custom_call", output_to_operand_aliasing={{0}: (2, {})} | custom-call | flops 3355443200 | bytes 17367040 | tf_op jit(solution)/shard_map/pallas_call | solution.py:368
  411.0 3.9 collective-permute-done.31.refs_7_.refs_2_
  416.1 10.8 %all-gather.17.cloned.1.call-done.refs_0_ = bf16[8,256,1280]{2,1,0:T(8,128)(2,1)} async-done(((bf16[1,256,1280]{2,1,0:T(8,128)(2,1)}), bf16[8,256,1280]{2,1,0:T(8,128)(2,1)}) %all-gather.17.cloned.1.call-update) | async-done | bytes 5242896 | tf_op jit(solution)/shard_map/all_gather | solution.py:419
  426.8 12.2 %shard_map.182 = (bf16[8,256,640]{2,1,0:T(8,128)(2,1)}, bf16[4,256,640]{2,1,0:T(8,128)(2,1)}, bf16[4,256,640]{2,1,0:T(8,128)(2,1)}, f32[8,128]{1,0:T(8,128)}) custom-call(s32[1]{0:T(128)} %bitcast.rank_ref, bf16[8,256,1280]{2,1,0:T(8,128)(2,1)} %all-gather.17.cloned.1.call-done.refs_0_, bf16[3,640,1280]{2,1,0:T(8,128)(2,1)} %refs_1_.21, ...), custom_call_target="tpu_custom_call" | custom-call | flops 5033164800 | bytes 2623488 | tf_op jit(solution)/shard_map/pallas_call | solution.py:91
  439.5 12.2 %shard_map.183 = (bf16[8,256,640]{2,1,0:T(8,128)(2,1)}, bf16[4,256,640]{2,1,0:T(8,128)(2,1)}, bf16[4,256,640]{2,1,0:T(8,128)(2,1)}, f32[8,128]{1,0:T(8,128)}) custom-call(s32[1]{0:T(128)} %bitcast.rank_ref, bf16[8,256,1280]{2,1,0:T(8,128)(2,1)} %all-gather.17.cloned.1.call-done.refs_0_, ...), custom_call_target="tpu_custom_call", output_to_operand_aliasing={{0}: (7, {})} | custom-call | flops 5033164800 | bytes 2623488 | tf_op jit(solution)/shard_map/pallas_call | solution.py:91
  459.0 9.0 %shard_map.184 = (f32[3,1280,640]{2,1,0:T(8,128)}, f32[8,128]{1,0:T(8,128)}) custom-call(bf16[2048,1280]{1,0:T(8,128)(2,1)} %bitcast.357, bf16[2048,640]{1,0:T(8,128)(2,1)} %bitcast.360, f32[3,1280,640]{2,1,0:T(8,128)} %get-tuple-element.258.refs_2_, f32[8,128]{1,0:T(8,128)} %get-tuple-element.253.refs_3_, ...), custom_call_target="tpu_custom_call", output_to_operand_aliasing={{0}: (2, {})} | custom-call | flops 3355443200 | bytes 17367040 | tf_op jit(solution)/shard_map/pallas_call | solution.py:368
  468.0 3.8 collective-permute-done.43
  475.4 6.4 collective-permute-done.44
  485.2 2.9 fusion.64
  492.5 19.2 %collective-permute-done.35.refs_6_ = f32[256,640]{1,0:T(8,128)S(1)} collective-permute-done((f32[256,640]{1,0:T(8,128)S(1)}, f32[256,640]{1,0:T(8,128)S(1)}, u32[]{:S(2)}, u32[]{:S(2)}) %collective-permute-start.35) | collective-permute-done | bytes 655392 | tf_op jit(solution)/shard_map/ppermute | solution.py:373
  513.6 9.2 %shard_map.185 = (f32[3,640,1280]{2,1,0:T(8,128)}, f32[8,128]{1,0:T(8,128)}) custom-call(bf16[2048,640]{1,0:T(8,128)(2,1)} %bitcast.354, bf16[2048,1280]{1,0:T(8,128)(2,1)} %bitcast.346, f32[3,640,1280]{2,1,0:T(8,128)} %get-tuple-element.256.refs_2_, f32[8,128]{1,0:T(8,128)} %get-tuple-element.263.refs_3_), custom_call_target="tpu_custom_call", output_to_operand_aliasing={{0}: (2, {})} | custom-call | flops 3355443200 | bytes 17367040 | tf_op jit(solution)/shard_map/pallas_call | solution.py:368
  522.9 9.2 %shard_map.186 = (f32[8,256,1280]{2,1,0:T(8,128)}, f32[8,128]{1,0:T(8,128)}) custom-call(s32[1]{0:T(128)} %bitcast.rank_ref, f32[256,1280]{1,0:T(8,128)} %bitcast.350, f32[256,1280]{1,0:T(8,128)} %collective-permute-done.30.refs_1_, f32[256,1280]{1,0:T(8,128)} %copy-done.3, f32[256,1280]{1,0:T(8,128)} %collective-permute-done.32.refs_3_, ...), custom_call_target="tpu_custom_call" | custom-call | flops 2000000000 | bytes 20971520 | tf_op jit(solution)/shard_map/pallas_call | solution.py:304
  532.1 14.9 %shard_map.187 = (bf16[8,256,1280]{2,1,0:T(8,128)(2,1)}, bf16[160,2048]{1,0:T(8,128)(2,1)}, bf16[480,2048]{1,0:T(8,128)(2,1)}, f32[8,128]{1,0:T(8,128)}) custom-call(s32[1]{0:T(128)} %bitcast.rank_ref, bf16[3,480,1280]{2,1,0:T(8,128)(2,1)} %bitcast.334, f32[8,256,1280]{2,1,0:T(8,128)} %get-tuple-element.351.refs_1_, f32[8,128]{1,0:T(8,128)} %get-tuple-element.266.refs_2_), custom_call_target="tpu_custom_call" | custom-call | flops 2852126720 | bytes 7868416 | tf_op jit(solution)/shard_map/pallas_call | solution.py:91
  547.1 11.1 %shard_map.188 = (bf16[480,2048]{1,0:T(8,128)(2,1)}, bf16[4,256,640]{2,1,0:T(8,128)(2,1)}, bf16[4,256,640]{2,1,0:T(8,128)(2,1)}, f32[8,128]{1,0:T(8,128)}) custom-call(s32[1]{0:T(128)} %bitcast.rank_ref, bf16[3,480,1280]{2,1,0:T(8,128)(2,1)} %bitcast.335, bf16[480,2048]{1,0:T(8,128)(2,1)} %get-tuple-element.268.refs_1_, bf16[3,160,1280]{2,1,0:T(8,128)(2,1)} %bitcast.343, ...), custom_call_target="tpu_custom_call" | custom-call | flops 2097152000 | bytes 2295808 | tf_op jit(solution)/shard_map/pallas_call | solution.py:91
  558.8 11.1 %shard_map.189 = (bf16[480,2048]{1,0:T(8,128)(2,1)}, bf16[4,256,640]{2,1,0:T(8,128)(2,1)}, bf16[4,256,640]{2,1,0:T(8,128)(2,1)}, f32[8,128]{1,0:T(8,128)}) custom-call(s32[1]{0:T(128)} %bitcast.rank_ref, bf16[3,480,1280]{2,1,0:T(8,128)(2,1)} %bitcast.336, bf16[480,2048]{1,0:T(8,128)(2,1)} %get-tuple-element.268.refs_1_, ...), custom_call_target="tpu_custom_call", output_to_operand_aliasing={{0}: (5, {})} | custom-call | flops 2097152000 | bytes 2295808 | tf_op jit(solution)/shard_map/pallas_call | solution.py:91
  574.9 9.7 %shard_map.190 = (f32[3,480,1280]{2,1,0:T(8,128)}, f32[3,160,1280]{2,1,0:T(8,128)}, f32[8,128]{1,0:T(8,128)}) custom-call(bf16[480,2048]{1,0:T(8,128)(2,1)} %get-tuple-element.274.refs_0_, bf16[2048,1280]{1,0:T(8,128)(2,1)} %bitcast.362, bf16[160,2048]{1,0:T(8,128)(2,1)} %get-tuple-element.267.refs_2_, ...), custom_call_target="tpu_custom_call", output_to_operand_aliasing={{0}: (4, {}), {1}: (5, {})} | custom-call | flops 3355443200 | bytes 27852800 | tf_op jit(solution)/shard_map/pallas_call | solution.py:368
  584.6 11.8 %collective-permute-done.47 = bf16[2,256,640]{2,1,0:T(8,128)(2,1)} collective-permute-done((bf16[2,256,640]{2,1,0:T(8,128)(2,1)S(1)}, bf16[2,256,640]{2,1,0:T(8,128)(2,1)}, u32[]{:S(2)}, u32[]{:S(2)}) %collective-permute-start.47) | collective-permute-done | bytes 655392 | tf_op jit(solution)/shard_map/ppermute | solution.py:373
  599.6 6.5 collective-permute-done.59
  615.3 43.5 %collective-permute-done.52.refs_4_ = f32[256,1280]{1,0:T(8,128)S(1)} collective-permute-done((f32[256,1280]{1,0:T(8,128)S(1)}, f32[256,1280]{1,0:T(8,128)S(1)}, u32[]{:S(2)}, u32[]{:S(2)}) %collective-permute-start.52) | collective-permute-done | bytes 1310752 | tf_op jit(solution)/shard_map/ppermute | solution.py:373
  659.8 2.8 collective-permute-done.50.refs_2_
  665.1 15.8 %shard_map.191 = (f32[8,256,1280]{2,1,0:T(8,128)}, f32[8,128]{1,0:T(8,128)}) custom-call(s32[1]{0:T(128)} %bitcast.rank_ref, f32[8,256,1280]{2,1,0:T(8,128)} %bitcast.377, bf16[1280,2048]{1,0:T(8,128)(2,1)} %all-gather.19.cloned.1.call-done.refs_1_, bf16[1280,1280]{1,0:T(8,128)(2,1)} %all-gather.11.cloned.1.call-done.refs_3_.refs_2_, ...), custom_call_target="tpu_custom_call" | custom-call | flops 6710886400 | bytes 10489856 | tf_op jit(solution)/shard_map/pallas_call | solution.py:91
  680.9 9.2 %collective-permute-done.54.refs_6_ = f32[256,640]{1,0:T(8,128)S(1)} collective-permute-done((f32[256,640]{1,0:T(8,128)}, f32[256,640]{1,0:T(8,128)S(1)}, u32[]{:S(2)}, u32[]{:S(2)}) %collective-permute-start.54) | collective-permute-done | bytes 655392 | tf_op jit(solution)/shard_map/ppermute | solution.py:373
  690.1 4.1 collective-permute-done.55.refs_7_
  698.3 9.3 %shard_map.192 = (f32[8,256,1280]{2,1,0:T(8,128)}, f32[8,128]{1,0:T(8,128)}) custom-call(s32[1]{0:T(128)} %bitcast.rank_ref, f32[256,1280]{1,0:T(8,128)} %bitcast.365, f32[256,1280]{1,0:T(8,128)} %collective-permute-done.49.refs_1_, f32[256,1280]{1,0:T(8,128)} %collective-permute-done.50.refs_2_, f32[256,1280]{1,0:T(8,128)} %collective-permute-done.51.refs_3_, ...), custom_call_target="tpu_custom_call" | custom-call | flops 2000000000 | bytes 20971520 | tf_op jit(solution)/shard_map/pallas_call | solution.py:304
  707.6 8.8 %copy.47 = f32[8,256,1280]{2,1,0:T(8,128)} copy(f32[8,256,1280]{2,1,0:T(8,128)} %all-gather.23.cloned.1.call-done) | data formatting | bytes 20971520
  (296 shorter events, 122.2 us)
Async XLA Ops:
  7.2 154.8 %all-gather.11.cloned.1.call-start = ((), (), s32[]{:S(2)}) async-start(), calls=%async_computation.1 | async-start | bytes 3686400 | tf_op jit(solution)/shard_map/all_gather | solution.py:419
  27.3 13.3 %collective-permute-start.1 = (f32[4,256,640]{2,1,0:T(8,128)}, f32[4,256,640]{2,1,0:T(8,128)}, u32[]{:S(2)}, u32[]{:S(2)}) collective-permute-start(f32[4,256,640]{2,1,0:T(8,128)} %get-tuple-element.161), channel_id=1, source_target_pairs={{0,1},{1,0},{2,3},{3,2},{4,5},{5,4},{6,7},{7,6},{8,9},{9,8},{10,11... | collective-permute-start | bytes 7864328 | tf_op jit(solution)/shard_map/ppermute | solution.py:373
  29.1 147.8 %all-gather.13.cloned.1.call-start = ((), (), s32[]{:S(2)}) async-start(), calls=%async_computation.2 | async-start | bytes 5898240 | tf_op jit(solution)/shard_map/all_gather | solution.py:419
  53.5 13.9 %collective-permute-start.2 = (bf16[4,256,640]{2,1,0:T(8,128)(2,1)}, bf16[4,256,640]{2,1,0:T(8,128)(2,1)}, u32[]{:S(2)}, u32[]{:S(2)}) collective-permute-start(bf16[4,256,640]{2,1,0:T(8,128)(2,1)} %get-tuple-element.169), channel_id=1, source_target_pairs={{0,1},{1,0},{2,3},{3,2},{4,5},{5,4},{6,7},{7,6},{8,9},{9,8},{10,11... | collective-permute-start | bytes 3932168 | tf_op jit(solution)/shard_map/ppermute | solution.py:373
  53.8 13.6 %collective-permute-start.3 = (bf16[4,256,640]{2,1,0:T(8,128)(2,1)}, bf16[4,256,640]{2,1,0:T(8,128)(2,1)}, u32[]{:S(2)}, u32[]{:S(2)}) collective-permute-start(bf16[4,256,640]{2,1,0:T(8,128)(2,1)} %get-tuple-element.170), channel_id=1, source_target_pairs={{0,1},{1,0},{2,3},{3,2},{4,5},{5,4},{6,7},{7,6},{8,9},{9,8},{10,11... | collective-permute-start | bytes 3932168 | tf_op jit(solution)/shard_map/ppermute | solution.py:373
  54.0 33.4 %collective-permute-start.5 = (f32[2,256,640]{2,1,0:T(8,128)}, f32[2,256,640]{2,1,0:T(8,128)}, u32[]{:S(2)}, u32[]{:S(2)}) collective-permute-start(f32[2,256,640]{2,1,0:T(8,128)} %get-tuple-element.317.refs_6_), channel_id=1, source_target_pairs={{0,4},{1,5},{2,6},{3,7},{4,0},{5,1},{6,2},{7,3},{8,12},{9,13},{10,... | collective-permute-start | bytes 3932168 | tf_op jit(solution)/shard_map/ppermute | solution.py:373
  56.5 30.9 %collective-permute-start.4 = (f32[2,256,640]{2,1,0:T(8,128)}, f32[2,256,640]{2,1,0:T(8,128)}, u32[]{:S(2)}, u32[]{:S(2)}) collective-permute-start(f32[2,256,640]{2,1,0:T(8,128)} %get-tuple-element.319.refs_5_), channel_id=1, source_target_pairs={{0,2},{1,3},{2,0},{3,1},{4,6},{5,7},{6,4},{7,5},{8,10},{9,11},{10,... | collective-permute-start | bytes 3932168 | tf_op jit(solution)/shard_map/ppermute | solution.py:373
  90.0 16.9 %collective-permute-start.13 = (f32[256,640]{1,0:T(8,128)}, f32[256,640]{1,0:T(8,128)}, u32[]{:S(2)}, u32[]{:S(2)}) collective-permute-start(f32[256,640]{1,0:T(8,128)} %get-tuple-element.340.refs_4_), channel_id=1, source_target_pairs={{0,2},{1,3},{2,0},{3,1},{4,6},{5,7},{6,4},{7,5},{8,10},{9,11},{10,... | collective-permute-start | bytes 1966088 | tf_op jit(solution)/shard_map/ppermute | solution.py:373
  91.4 16.5 %collective-permute-start.12 = (f32[256,640]{1,0:T(8,128)}, f32[256,640]{1,0:T(8,128)}, u32[]{:S(2)}, u32[]{:S(2)}) collective-permute-start(f32[256,640]{1,0:T(8,128)} %get-tuple-element.341.refs_3_), channel_id=1, source_target_pairs={{0,4},{1,5},{2,6},{3,7},{4,0},{5,1},{6,2},{7,3},{8,12},{9,13},{10,... | collective-permute-start | bytes 1966088 | tf_op jit(solution)/shard_map/ppermute | solution.py:373
  113.4 87.4 %all-gather.9.cloned.1.call-start = ((), (), s32[]{:S(2)}) async-start(), calls=%async_computation | async-start | bytes 5898240 | tf_op jit(solution)/shard_map/all_gather | solution.py:419
  113.9 22.6 %collective-permute-start.6 = (bf16[2,256,640]{2,1,0:T(8,128)(2,1)}, bf16[2,256,640]{2,1,0:T(8,128)(2,1)S(1)}, u32[]{:S(2)}, u32[]{:S(2)}) collective-permute-start(bf16[2,256,640]{2,1,0:T(8,128)(2,1)} %get-tuple-element.339.refs_5_), channel_id=1, source_target_pairs={{0,2},{1,3},{2,0},{3,1},{4,6},{5,7},{6,4},{7,5},{8,10},{9,11},{10,... | collective-permute-start | bytes 1966088 | tf_op jit(solution)/shard_map/ppermute | solution.py:373
  114.6 22.5 %collective-permute-start.7 = (bf16[2,256,640]{2,1,0:T(8,128)(2,1)}, bf16[2,256,640]{2,1,0:T(8,128)(2,1)}, u32[]{:S(2)}, u32[]{:S(2)}) collective-permute-start(bf16[2,256,640]{2,1,0:T(8,128)(2,1)} %get-tuple-element.337.refs_6_), channel_id=1, source_target_pairs={{0,4},{1,5},{2,6},{3,7},{4,0},{5,1},{6,2},{7,3},{8,12},{9,13},{10,... | collective-permute-start | bytes 1966088 | tf_op jit(solution)/shard_map/ppermute | solution.py:373
  138.1 14.8 %collective-permute-start.10 = (bf16[256,640]{1,0:T(8,128)(2,1)S(1)}, bf16[256,640]{1,0:T(8,128)(2,1)}, u32[]{:S(2)}, u32[]{:S(2)}) collective-permute-start(bf16[256,640]{1,0:T(8,128)(2,1)S(1)} %fusion.61.refs_4_), channel_id=1, source_target_pairs={{0,2},{1,3},{2,0},{3,1},{4,6},{5,7},{6,4},{7,5},{8,10},{9,11},{10,... | collective-permute-start | bytes 983048 | tf_op jit(solution)/shard_map/ppermute | solution.py:373
  140.4 14.5 %collective-permute-start.9 = (bf16[256,640]{1,0:T(8,128)(2,1)S(1)}, bf16[256,640]{1,0:T(8,128)(2,1)S(1)}, u32[]{:S(2)}, u32[]{:S(2)}) collective-permute-start(bf16[256,640]{1,0:T(8,128)(2,1)S(1)} %fusion.63.refs_3_), channel_id=1, source_target_pairs={{0,4},{1,5},{2,6},{3,7},{4,0},{5,1},{6,2},{7,3},{8,12},{9,13},{10,... | collective-permute-start | bytes 983048 | tf_op jit(solution)/shard_map/ppermute | solution.py:373
  161.4 221.1 %all-gather.15.cloned.1.call-start = ((), (), s32[]{:S(2)}) async-start(), calls=%async_computation.3 | async-start | bytes 5898240 | tf_op jit(solution)/shard_map/all_gather | solution.py:419
  161.4 28.5 %collective-permute-start.8 = (f32[4,256,640]{2,1,0:T(8,128)}, f32[4,256,640]{2,1,0:T(8,128)}, u32[]{:S(2)}, u32[]{:S(2)}) collective-permute-start(f32[4,256,640]{2,1,0:T(8,128)} %get-tuple-element.185), channel_id=1, source_target_pairs={{0,1},{1,0},{2,3},{3,2},{4,5},{5,4},{6,7},{7,6},{8,9},{9,8},{10,11... | collective-permute-start | bytes 7864328 | tf_op jit(solution)/shard_map/ppermute | solution.py:373
  161.5 39.3 %collective-permute-start.14 = (f32[4,256,640]{2,1,0:T(8,128)}, f32[4,256,640]{2,1,0:T(8,128)}, u32[]{:S(2)}, u32[]{:S(2)}) collective-permute-start(f32[4,256,640]{2,1,0:T(8,128)} %get-tuple-element.197), channel_id=1, source_target_pairs={{0,1},{1,0},{2,3},{3,2},{4,5},{5,4},{6,7},{7,6},{8,9},{9,8},{10,11... | collective-permute-start | bytes 7864328 | tf_op jit(solution)/shard_map/ppermute | solution.py:373
  220.0 11.6 %collective-permute-start.15 = (bf16[4,256,640]{2,1,0:T(8,128)(2,1)}, bf16[4,256,640]{2,1,0:T(8,128)(2,1)}, u32[]{:S(2)}, u32[]{:S(2)}) collective-permute-start(bf16[4,256,640]{2,1,0:T(8,128)(2,1)} %get-tuple-element.203), channel_id=1, source_target_pairs={{0,1},{1,0},{2,3},{3,2},{4,5},{5,4},{6,7},{7,6},{8,9},{9,8},{10,11... | collective-permute-start | bytes 3932168 | tf_op jit(solution)/shard_map/ppermute | solution.py:373
  220.2 14.4 %collective-permute-start.16 = (bf16[4,256,640]{2,1,0:T(8,128)(2,1)}, bf16[4,256,640]{2,1,0:T(8,128)(2,1)S(1)}, u32[]{:S(2)}, u32[]{:S(2)}) collective-permute-start(bf16[4,256,640]{2,1,0:T(8,128)(2,1)} %get-tuple-element.205), channel_id=1, source_target_pairs={{0,1},{1,0},{2,3},{3,2},{4,5},{5,4},{6,7},{7,6},{8,9},{9,8},{10,11... | collective-permute-start | bytes 3932168 | tf_op jit(solution)/shard_map/ppermute | solution.py:373
  247.2 30.1 %collective-permute-start.17 = (bf16[4,256,640]{2,1,0:T(8,128)(2,1)}, bf16[4,256,640]{2,1,0:T(8,128)(2,1)}, u32[]{:S(2)}, u32[]{:S(2)}) collective-permute-start(bf16[4,256,640]{2,1,0:T(8,128)(2,1)} %get-tuple-element.210), channel_id=1, source_target_pairs={{0,1},{1,0},{2,3},{3,2},{4,5},{5,4},{6,7},{7,6},{8,9},{9,8},{10,11... | collective-permute-start | bytes 3932168 | tf_op jit(solution)/shard_map/ppermute | solution.py:373
  247.5 29.8 %collective-permute-start.19 = (bf16[4,256,640]{2,1,0:T(8,128)(2,1)}, bf16[4,256,640]{2,1,0:T(8,128)(2,1)}, u32[]{:S(2)}, u32[]{:S(2)}) collective-permute-start(bf16[4,256,640]{2,1,0:T(8,128)(2,1)} %get-tuple-element.211), channel_id=1, source_target_pairs={{0,1},{1,0},{2,3},{3,2},{4,5},{5,4},{6,7},{7,6},{8,9},{9,8},{10,11... | collective-permute-start | bytes 3932168 | tf_op jit(solution)/shard_map/ppermute | solution.py:373
  247.7 17.2 %collective-permute-start.20 = (bf16[2,256,640]{2,1,0:T(8,128)(2,1)}, bf16[2,256,640]{2,1,0:T(8,128)(2,1)}, u32[]{:S(2)}, u32[]{:S(2)}) collective-permute-start(bf16[2,256,640]{2,1,0:T(8,128)(2,1)} %get-tuple-element.333.refs_6_), channel_id=1, source_target_pairs={{0,4},{1,5},{2,6},{3,7},{4,0},{5,1},{6,2},{7,3},{8,12},{9,13},{10,... | collective-permute-start | bytes 1966088 | tf_op jit(solution)/shard_map/ppermute | solution.py:373
  248.8 30.3 %collective-permute-start.18 = (bf16[2,256,640]{2,1,0:T(8,128)(2,1)S(1)}, bf16[2,256,640]{2,1,0:T(8,128)(2,1)}, u32[]{:S(2)}, u32[]{:S(2)}) collective-permute-start(bf16[2,256,640]{2,1,0:T(8,128)(2,1)S(1)} %copy-done.15), channel_id=1, source_target_pairs={{0,2},{1,3},{2,0},{3,1},{4,6},{5,7},{6,4},{7,5},{8,10},{9,11},{10,... | collective-permute-start | bytes 1966088 | tf_op jit(solution)/shard_map/ppermute | solution.py:373
  249.6 45.0 %collective-permute-start.11 = (f32[2,256,640]{2,1,0:T(8,128)S(1)}, f32[2,256,640]{2,1,0:T(8,128)}, u32[]{:S(2)}, u32[]{:S(2)}) collective-permute-start(f32[2,256,640]{2,1,0:T(8,128)S(1)} %copy-done.8), channel_id=1, source_target_pairs={{0,2},{1,3},{2,0},{3,1},{4,6},{5,7},{6,4},{7,5},{8,10},{9,11},{10,... | collective-permute-start | bytes 3932168 | tf_op jit(solution)/shard_map/ppermute | solution.py:373
  264.9 32.0 %collective-permute-start.22 = (f32[2,256,640]{2,1,0:T(8,128)}, f32[2,256,640]{2,1,0:T(8,128)}, u32[]{:S(2)}, u32[]{:S(2)}) collective-permute-start(f32[2,256,640]{2,1,0:T(8,128)} %get-tuple-element.314.refs_6_), channel_id=1, source_target_pairs={{0,4},{1,5},{2,6},{3,7},{4,0},{5,1},{6,2},{7,3},{8,12},{9,13},{10,... | collective-permute-start | bytes 3932168 | tf_op jit(solution)/shard_map/ppermute | solution.py:373
  278.5 32.0 %collective-permute-start.27 = (bf16[256,640]{1,0:T(8,128)(2,1)S(1)}, bf16[256,640]{1,0:T(8,128)(2,1)}, u32[]{:S(2)}, u32[]{:S(2)}) collective-permute-start(bf16[256,640]{1,0:T(8,128)(2,1)S(1)} %fusion.55.refs_6_), channel_id=1, source_target_pairs={{0,2},{1,3},{2,0},{3,1},{4,6},{5,7},{6,4},{7,5},{8,10},{9,11},{10,... | collective-permute-start | bytes 983048 | tf_op jit(solution)/shard_map/ppermute | solution.py:373
  280.3 31.5 %collective-permute-start.26 = (bf16[256,640]{1,0:T(8,128)(2,1)S(1)}, bf16[256,640]{1,0:T(8,128)(2,1)S(1)}, u32[]{:S(2)}, u32[]{:S(2)}) collective-permute-start(bf16[256,640]{1,0:T(8,128)(2,1)S(1)} %fusion.57.refs_5_), channel_id=1, source_target_pairs={{0,4},{1,5},{2,6},{3,7},{4,0},{5,1},{6,2},{7,3},{8,12},{9,13},{10,... | collective-permute-start | bytes 983048 | tf_op jit(solution)/shard_map/ppermute | solution.py:373
  315.8 111.0 %all-gather.17.cloned.1.call-start = ((), (), s32[]{:S(2)}) async-start(), calls=%async_computation.4 | async-start | bytes 5898240 | tf_op jit(solution)/shard_map/all_gather | solution.py:419
  316.0 24.9 %collective-permute-start.24 = (bf16[2,256,640]{2,1,0:T(8,128)(2,1)}, bf16[2,256,640]{2,1,0:T(8,128)(2,1)S(1)}, u32[]{:S(2)}, u32[]{:S(2)}) collective-permute-start(bf16[2,256,640]{2,1,0:T(8,128)(2,1)} %get-tuple-element.329.refs_8_), channel_id=1, source_target_pairs={{0,4},{1,5},{2,6},{3,7},{4,0},{5,1},{6,2},{7,3},{8,12},{9,13},{10,... | collective-permute-start | bytes 1966088 | tf_op jit(solution)/shard_map/ppermute | solution.py:373
  317.3 25.8 %collective-permute-start.23 = (bf16[2,256,640]{2,1,0:T(8,128)(2,1)}, bf16[2,256,640]{2,1,0:T(8,128)(2,1)S(1)}, u32[]{:S(2)}, u32[]{:S(2)}) collective-permute-start(bf16[2,256,640]{2,1,0:T(8,128)(2,1)} %get-tuple-element.331.refs_7_), channel_id=1, source_target_pairs={{0,2},{1,3},{2,0},{3,1},{4,6},{5,7},{6,4},{7,5},{8,10},{9,11},{10,... | collective-permute-start | bytes 1966088 | tf_op jit(solution)/shard_map/ppermute | solution.py:373
  319.5 48.1 %collective-permute-start.25 = (f32[256,640]{1,0:T(8,128)}, f32[256,640]{1,0:T(8,128)}, u32[]{:S(2)}, u32[]{:S(2)}) collective-permute-start(f32[256,640]{1,0:T(8,128)} %fusion.10.refs_10_), channel_id=1, source_target_pairs={{0,2},{1,3},{2,0},{3,1},{4,6},{5,7},{6,4},{7,5},{8,10},{9,11},{10,... | collective-permute-start | bytes 1966088 | tf_op jit(solution)/shard_map/ppermute | solution.py:373
  320.9 48.2 %collective-permute-start.21 = (f32[256,640]{1,0:T(8,128)S(1)}, f32[256,640]{1,0:T(8,128)}, u32[]{:S(2)}, u32[]{:S(2)}) collective-permute-start(f32[256,640]{1,0:T(8,128)S(1)} %copy-done.14), channel_id=1, source_target_pairs={{0,4},{1,5},{2,6},{3,7},{4,0},{5,1},{6,2},{7,3},{8,12},{9,13},{10,... | collective-permute-start | bytes 1966088 | tf_op jit(solution)/shard_map/ppermute | solution.py:373
  341.7 31.6 %collective-permute-start.29 = (bf16[256,640]{1,0:T(8,128)(2,1)}, bf16[256,640]{1,0:T(8,128)(2,1)}, u32[]{:S(2)}, u32[]{:S(2)}) collective-permute-start(bf16[256,640]{1,0:T(8,128)(2,1)} %fusion.52.refs_8_), channel_id=1, source_target_pairs={{0,2},{1,3},{2,0},{3,1},{4,6},{5,7},{6,4},{7,5},{8,10},{9,11},{10,... | collective-permute-start | bytes 983048 | tf_op jit(solution)/shard_map/ppermute | solution.py:373
  343.2 30.2 %collective-permute-start.28 = (bf16[256,640]{1,0:T(8,128)(2,1)S(1)}, bf16[256,640]{1,0:T(8,128)(2,1)}, u32[]{:S(2)}, u32[]{:S(2)}) collective-permute-start(bf16[256,640]{1,0:T(8,128)(2,1)S(1)} %fusion.54.refs_7_), channel_id=1, source_target_pairs={{0,4},{1,5},{2,6},{3,7},{4,0},{5,1},{6,2},{7,3},{8,12},{9,13},{10,... | collective-permute-start | bytes 983048 | tf_op jit(solution)/shard_map/ppermute | solution.py:373
  380.4 166.7 %all-gather.21.cloned.1.call-start = ((), (), s32[]{:S(2)}) async-start(), calls=%async_computation.6 | async-start | bytes 5898240 | tf_op jit(solution)/shard_map/all_gather | solution.py:419
  380.5 34.5 %collective-permute-start.31 = (f32[256,1280]{1,0:T(8,128)S(1)}, f32[256,1280]{1,0:T(8,128)S(1)}, u32[]{:S(2)}, u32[]{:S(2)}) collective-permute-start(f32[256,1280]{1,0:T(8,128)S(1)} %bitcast.347), channel_id=1, source_target_pairs={{0,2},{1,3},{2,0},{3,1},{4,6},{5,7},{6,4},{7,5},{8,10},{9,11},{10,... | collective-permute-start | bytes 3932168 | tf_op jit(solution)/shard_map/ppermute | solution.py:373
  380.9 35.2 %collective-permute-start.33 = (f32[256,1280]{1,0:T(8,128)S(1)}, f32[256,1280]{1,0:T(8,128)}, u32[]{:S(2)}, u32[]{:S(2)}) collective-permute-start(f32[256,1280]{1,0:T(8,128)S(1)} %bitcast.348), channel_id=1, source_target_pairs={{0,4},{1,5},{2,6},{3,7},{4,0},{5,1},{6,2},{7,3},{8,12},{9,13},{10,... | collective-permute-start | bytes 3932168 | tf_op jit(solution)/shard_map/ppermute | solution.py:373
  439.0 12.7 %collective-permute-start.40 = (bf16[4,256,640]{2,1,0:T(8,128)(2,1)}, bf16[4,256,640]{2,1,0:T(8,128)(2,1)S(1)}, u32[]{:S(2)}, u32[]{:S(2)}) collective-permute-start(bf16[4,256,640]{2,1,0:T(8,128)(2,1)} %get-tuple-element.262), channel_id=1, source_target_pairs={{0,1},{1,0},{2,3},{3,2},{4,5},{5,4},{6,7},{7,6},{8,9},{9,8},{10,11... | collective-permute-start | bytes 3932168 | tf_op jit(solution)/shard_map/ppermute | solution.py:373
  439.3 16.8 %collective-permute-start.39 = (bf16[4,256,640]{2,1,0:T(8,128)(2,1)}, bf16[4,256,640]{2,1,0:T(8,128)(2,1)S(1)}, u32[]{:S(2)}, u32[]{:S(2)}) collective-permute-start(bf16[4,256,640]{2,1,0:T(8,128)(2,1)} %get-tuple-element.260), channel_id=1, source_target_pairs={{0,1},{1,0},{2,3},{3,2},{4,5},{5,4},{6,7},{7,6},{8,9},{9,8},{10,11... | collective-permute-start | bytes 3932168 | tf_op jit(solution)/shard_map/ppermute | solution.py:373
  454.7 17.0 %collective-permute-start.43 = (bf16[2,256,640]{2,1,0:T(8,128)(2,1)S(1)}, bf16[2,256,640]{2,1,0:T(8,128)(2,1)}, u32[]{:S(2)}, u32[]{:S(2)}) collective-permute-start(bf16[2,256,640]{2,1,0:T(8,128)(2,1)S(1)} %get-tuple-element.327.refs_5_), channel_id=1, source_target_pairs={{0,4},{1,5},{2,6},{3,7},{4,0},{5,1},{6,2},{7,3},{8,12},{9,13},{10,... | collective-permute-start | bytes 1966088 | tf_op jit(solution)/shard_map/ppermute | solution.py:373
  456.3 18.2 %collective-permute-start.41 = (bf16[2,256,640]{2,1,0:T(8,128)(2,1)S(1)}, bf16[2,256,640]{2,1,0:T(8,128)(2,1)S(1)}, u32[]{:S(2)}, u32[]{:S(2)}) collective-permute-start(bf16[2,256,640]{2,1,0:T(8,128)(2,1)S(1)} %get-tuple-element.325.refs_4_), channel_id=1, source_target_pairs={{0,2},{1,3},{2,0},{3,1},{4,6},{5,7},{6,4},{7,5},{8,10},{9,11},{10,... | collective-permute-start | bytes 1966088 | tf_op jit(solution)/shard_map/ppermute | solution.py:373
  472.7 9.0 %collective-permute-start.44 = (bf16[256,640]{1,0:T(8,128)(2,1)S(1)}, bf16[256,640]{1,0:T(8,128)(2,1)S(1)}, u32[]{:S(2)}, u32[]{:S(2)}) collective-permute-start(bf16[256,640]{1,0:T(8,128)(2,1)S(1)} %fusion.40), channel_id=1, source_target_pairs={{0,2},{1,3},{2,0},{3,1},{4,6},{5,7},{6,4},{7,5},{8,10},{9,11},{10,... | collective-permute-start | bytes 983048 | tf_op jit(solution)/shard_map/ppermute | solution.py:373
  488.1 177.0 %all-gather.19.cloned.1.call-start = ((), (), s32[]{:S(2)}) async-start(), calls=%async_computation.5 | async-start | bytes 5898240 | tf_op jit(solution)/shard_map/all_gather | solution.py:419
  489.7 22.0 %collective-permute-start.35 = (f32[256,640]{1,0:T(8,128)S(1)}, f32[256,640]{1,0:T(8,128)S(1)}, u32[]{:S(2)}, u32[]{:S(2)}) collective-permute-start(f32[256,640]{1,0:T(8,128)S(1)} %slice.507), channel_id=1, source_target_pairs={{0,2},{1,3},{2,0},{3,1},{4,6},{5,7},{6,4},{7,5},{8,10},{9,11},{10,... | collective-permute-start | bytes 1966088 | tf_op jit(solution)/shard_map/ppermute | solution.py:373
  491.1 22.1 %collective-permute-start.36 = (f32[256,640]{1,0:T(8,128)S(1)}, f32[256,640]{1,0:T(8,128)}, u32[]{:S(2)}, u32[]{:S(2)}) collective-permute-start(f32[256,640]{1,0:T(8,128)S(1)} %slice.508), channel_id=1, source_target_pairs={{0,4},{1,5},{2,6},{3,7},{4,0},{5,1},{6,2},{7,3},{8,12},{9,13},{10,... | collective-permute-start | bytes 1966088 | tf_op jit(solution)/shard_map/ppermute | solution.py:373
  491.9 30.9 %collective-permute-start.30 = (f32[256,1280]{1,0:T(8,128)S(1)}, f32[256,1280]{1,0:T(8,128)}, u32[]{:S(2)}, u32[]{:S(2)}) collective-permute-start(f32[256,1280]{1,0:T(8,128)S(1)} %bitcast.351), channel_id=1, source_target_pairs={{0,1},{1,0},{2,3},{3,2},{4,5},{5,4},{6,7},{7,6},{8,9},{9,8},{10,11... | collective-permute-start | bytes 3932168 | tf_op jit(solution)/shard_map/ppermute | solution.py:373
  491.9 31.0 %collective-permute-start.32 = (f32[256,1280]{1,0:T(8,128)S(1)}, f32[256,1280]{1,0:T(8,128)}, u32[]{:S(2)}, u32[]{:S(2)}) collective-permute-start(f32[256,1280]{1,0:T(8,128)S(1)} %copy-done.4), channel_id=1, source_target_pairs={{0,1},{1,0},{2,3},{3,2},{4,5},{5,4},{6,7},{7,6},{8,9},{9,8},{10,11... | collective-permute-start | bytes 3932168 | tf_op jit(solution)/shard_map/ppermute | solution.py:373
  492.5 30.5 %collective-permute-start.34 = (f32[256,1280]{1,0:T(8,128)}, f32[256,1280]{1,0:T(8,128)}, u32[]{:S(2)}, u32[]{:S(2)}) collective-permute-start(f32[256,1280]{1,0:T(8,128)} %collective-permute-done.33.refs_8_.refs_4_), channel_id=1, source_target_pairs={{0,1},{1,0},{2,3},{3,2},{4,5},{5,4},{6,7},{7,6},{8,9},{9,8},{10,11... | collective-permute-start | bytes 3932168 | tf_op jit(solution)/shard_map/ppermute | solution.py:373
  513.1 9.8 %collective-permute-start.37 = (f32[256,640]{1,0:T(8,128)S(1)}, f32[256,640]{1,0:T(8,128)}, u32[]{:S(2)}, u32[]{:S(2)}) collective-permute-start(f32[256,640]{1,0:T(8,128)S(1)} %collective-permute-done.35.refs_6_), channel_id=1, source_target_pairs={{0,1},{1,0},{2,3},{3,2},{4,5},{5,4},{6,7},{7,6},{8,9},{9,8},{10,11... | collective-permute-start | bytes 1966088 | tf_op jit(solution)/shard_map/ppermute | solution.py:373
  513.1 9.8 %collective-permute-start.38 = (f32[256,640]{1,0:T(8,128)}, f32[256,640]{1,0:T(8,128)}, u32[]{:S(2)}, u32[]{:S(2)}) collective-permute-start(f32[256,640]{1,0:T(8,128)} %collective-permute-done.36.refs_7_), channel_id=1, source_target_pairs={{0,1},{1,0},{2,3},{3,2},{4,5},{5,4},{6,7},{7,6},{8,9},{9,8},{10,11... | collective-permute-start | bytes 1966088 | tf_op jit(solution)/shard_map/ppermute | solution.py:373
  547.1 160.5 %all-gather.23.cloned.1.call-start = ((), (), s32[]{:S(2)}) async-start(), calls=%async_computation.7 | async-start | bytes 11796480 | tf_op jit(solution)/shard_map/all_gather | solution.py:419
  558.3 11.6 %collective-permute-start.45 = (bf16[4,256,640]{2,1,0:T(8,128)(2,1)}, bf16[4,256,640]{2,1,0:T(8,128)(2,1)S(1)}, u32[]{:S(2)}, u32[]{:S(2)}) collective-permute-start(bf16[4,256,640]{2,1,0:T(8,128)(2,1)} %get-tuple-element.280), channel_id=1, source_target_pairs={{0,1},{1,0},{2,3},{3,2},{4,5},{5,4},{6,7},{7,6},{8,9},{9,8},{10,11... | collective-permute-start | bytes 3932168 | tf_op jit(solution)/shard_map/ppermute | solution.py:373
  558.6 15.0 %collective-permute-start.46 = (bf16[4,256,640]{2,1,0:T(8,128)(2,1)}, bf16[4,256,640]{2,1,0:T(8,128)(2,1)S(1)}, u32[]{:S(2)}, u32[]{:S(2)}) collective-permute-start(bf16[4,256,640]{2,1,0:T(8,128)(2,1)} %get-tuple-element.282), channel_id=1, source_target_pairs={{0,1},{1,0},{2,3},{3,2},{4,5},{5,4},{6,7},{7,6},{8,9},{9,8},{10,11... | collective-permute-start | bytes 3932168 | tf_op jit(solution)/shard_map/ppermute | solution.py:373
  572.9 23.5 %collective-permute-start.47 = (bf16[2,256,640]{2,1,0:T(8,128)(2,1)S(1)}, bf16[2,256,640]{2,1,0:T(8,128)(2,1)}, u32[]{:S(2)}, u32[]{:S(2)}) collective-permute-start(bf16[2,256,640]{2,1,0:T(8,128)(2,1)S(1)} %get-tuple-element.323.refs_7_), channel_id=1, source_target_pairs={{0,2},{1,3},{2,0},{3,1},{4,6},{5,7},{6,4},{7,5},{8,10},{9,11},{10,... | collective-permute-start | bytes 1966088 | tf_op jit(solution)/shard_map/ppermute | solution.py:373
  573.8 22.6 %collective-permute-start.48 = (bf16[2,256,640]{2,1,0:T(8,128)(2,1)S(1)}, bf16[2,256,640]{2,1,0:T(8,128)(2,1)S(1)}, u32[]{:S(2)}, u32[]{:S(2)}) collective-permute-start(bf16[2,256,640]{2,1,0:T(8,128)(2,1)S(1)} %get-tuple-element.321.refs_8_), channel_id=1, source_target_pairs={{0,4},{1,5},{2,6},{3,7},{4,0},{5,1},{6,2},{7,3},{8,12},{9,13},{10,... | collective-permute-start | bytes 1966088 | tf_op jit(solution)/shard_map/ppermute | solution.py:373
  596.4 9.6 %collective-permute-start.59 = (bf16[256,640]{1,0:T(8,128)(2,1)S(1)}, bf16[256,640]{1,0:T(8,128)(2,1)S(1)}, u32[]{:S(2)}, u32[]{:S(2)}) collective-permute-start(bf16[256,640]{1,0:T(8,128)(2,1)S(1)} %fusion.37.refs_5_), channel_id=1, source_target_pairs={{0,2},{1,3},{2,0},{3,1},{4,6},{5,7},{6,4},{7,5},{8,10},{9,11},{10,... | collective-permute-start | bytes 983048 | tf_op jit(solution)/shard_map/ppermute | solution.py:373
  598.8 9.2 %collective-permute-start.58 = (bf16[256,640]{1,0:T(8,128)(2,1)S(1)}, bf16[256,640]{1,0:T(8,128)(2,1)S(1)}, u32[]{:S(2)}, u32[]{:S(2)}) collective-permute-start(bf16[256,640]{1,0:T(8,128)(2,1)S(1)} %fusion.39.refs_4_), channel_id=1, source_target_pairs={{0,4},{1,5},{2,6},{3,7},{4,0},{5,1},{6,2},{7,3},{8,12},{9,13},{10,... | collective-permute-start | bytes 983048 | tf_op jit(solution)/shard_map/ppermute | solution.py:373
  613.2 45.6 %collective-permute-start.52 = (f32[256,1280]{1,0:T(8,128)S(1)}, f32[256,1280]{1,0:T(8,128)S(1)}, u32[]{:S(2)}, u32[]{:S(2)}) collective-permute-start(f32[256,1280]{1,0:T(8,128)S(1)} %bitcast.366), channel_id=1, source_target_pairs={{0,4},{1,5},{2,6},{3,7},{4,0},{5,1},{6,2},{7,3},{8,12},{9,13},{10,... | collective-permute-start | bytes 3932168 | tf_op jit(solution)/shard_map/ppermute | solution.py:373
  613.9 48.7 %collective-permute-start.50 = (f32[256,1280]{1,0:T(8,128)S(1)}, f32[256,1280]{1,0:T(8,128)}, u32[]{:S(2)}, u32[]{:S(2)}) collective-permute-start(f32[256,1280]{1,0:T(8,128)S(1)} %bitcast.367), channel_id=1, source_target_pairs={{0,2},{1,3},{2,0},{3,1},{4,6},{5,7},{6,4},{7,5},{8,10},{9,11},{10,... | collective-permute-start | bytes 3932168 | tf_op jit(solution)/shard_map/ppermute | solution.py:373
  659.8 30.3 %collective-permute-start.54 = (f32[256,640]{1,0:T(8,128)}, f32[256,640]{1,0:T(8,128)S(1)}, u32[]{:S(2)}, u32[]{:S(2)}) collective-permute-start(f32[256,640]{1,0:T(8,128)} %slice.540), channel_id=1, source_target_pairs={{0,2},{1,3},{2,0},{3,1},{4,6},{5,7},{6,4},{7,5},{8,10},{9,11},{10,... | collective-permute-start | bytes 1966088 | tf_op jit(solution)/shard_map/ppermute | solution.py:373
  664.6 29.6 %collective-permute-start.55 = (f32[256,640]{1,0:T(8,128)}, f32[256,640]{1,0:T(8,128)}, u32[]{:S(2)}, u32[]{:S(2)}) collective-permute-start(f32[256,640]{1,0:T(8,128)} %slice.541), channel_id=1, source_target_pairs={{0,4},{1,5},{2,6},{3,7},{4,0},{5,1},{6,2},{7,3},{8,12},{9,13},{10,... | collective-permute-start | bytes 1966088 | tf_op jit(solution)/shard_map/ppermute | solution.py:373
  664.6 30.1 %collective-permute-start.49 = (f32[256,1280]{1,0:T(8,128)S(1)}, f32[256,1280]{1,0:T(8,128)}, u32[]{:S(2)}, u32[]{:S(2)}) collective-permute-start(f32[256,1280]{1,0:T(8,128)S(1)} %bitcast.368), channel_id=1, source_target_pairs={{0,1},{1,0},{2,3},{3,2},{4,5},{5,4},{6,7},{7,6},{8,9},{9,8},{10,11... | collective-permute-start | bytes 3932168 | tf_op jit(solution)/shard_map/ppermute | solution.py:373
  664.6 33.7 %collective-permute-start.51 = (f32[256,1280]{1,0:T(8,128)}, f32[256,1280]{1,0:T(8,128)}, u32[]{:S(2)}, u32[]{:S(2)}) collective-permute-start(f32[256,1280]{1,0:T(8,128)} %collective-permute-done.50.refs_2_), channel_id=1, source_target_pairs={{0,1},{1,0},{2,3},{3,2},{4,5},{5,4},{6,7},{7,6},{8,9},{9,8},{10,11... | collective-permute-start | bytes 3932168 | tf_op jit(solution)/shard_map/ppermute | solution.py:373
  665.1 33.2 %collective-permute-start.53 = (f32[256,1280]{1,0:T(8,128)S(1)}, f32[256,1280]{1,0:T(8,128)}, u32[]{:S(2)}, u32[]{:S(2)}) collective-permute-start(f32[256,1280]{1,0:T(8,128)S(1)} %collective-permute-done.52.refs_4_), channel_id=1, source_target_pairs={{0,1},{1,0},{2,3},{3,2},{4,5},{5,4},{6,7},{7,6},{8,9},{9,8},{10,11... | collective-permute-start | bytes 3932168 | tf_op jit(solution)/shard_map/ppermute | solution.py:373
  (60 other events, 359.5 us)
Sparse Core Ops, SparseCore 0:
  29.2 33.1 all-gather.10
  113.5 48.1 all-gather.12
  163.6 37.1 all-gather.8
  315.9 56.5 all-gather.14
  380.5 46.2 all-gather.16
  488.3 43.6 all-gather.20
  547.2 42.9 all-gather.18
  612.0 88.8 all-gather.22

commit v3 on v2

--- a/solution.py
+++ b/solution.py
@@ -396,10 +396,6 @@
     return moving, sent
 
 
-def received(halves):
-    return [recv for _, recv, _ in halves]
-
-
 def sum_second(moving, fill=()):
     value, sent, final = [], [], []
     for here, recv, order in moving:
@@ -474,69 +470,69 @@
         s_one, s_two = saved_one[0], saved_two[0]
         wo_all = gather(o_w[lo])
         top_a, s_top, top_act, tok = mlp_fwd(rank, y_one, w_in, top)
-        *parts, tok = mlp_out(rank, top_act, w_out, top, [tok])
-        sum_out, sent = sum_first(sum_cores(parts))
-        d_two_bf, top_dh, *parts, tok = mlp_back(rank, dy_two, w_out, s_top, w_in, top, [tok, *sent])
-        sum_g = sum_cores(parts)
-        tok_in = mlp_grad("in", top, top_a, top_dh, [tok, *received(sum_g)])
-        value, sent, final = sum_second(sum_out, [tok_in])
-        sum_g, sent_g = sum_first(sum_g, sent)
-        tok = mlp_grad("out", top, top_act, d_two_bf, [tok_in, *sent, *sent_g])
+        d_two_bf, top_dh, *parts, tok = mlp_back(rank, dy_two, w_out, s_top, w_in, top, [tok])
+        sum_g, sent = sum_first(sum_cores(parts))
+        *parts, tok = mlp_out(rank, top_act, w_out, top, [tok, *sent])
+        sum_out = sum_cores(parts)
+        value, sent, final = sum_second(sum_g, [tok])
+        sum_out, sent_out = sum_first(sum_out, sent)
+        tok = mlp_grad("in", top, top_a, top_dh, [tok, *sent, *sent_out])
+        d_one = shard(dy_one) + rms_vjp(shard(y_one), sum_end(value, final, [tok]))
+        rounded, d_one = lax.optimization_barrier((d_one.astype(BF), d_one))
+        d_one_bf = gather(rounded)
+        s_a, sl_hi, act_hi, sl_lo, act_lo, tok = mlp_pair_fwd(rank, s_one, w_in, hi, lo, [tok, rounded])
+        value, sent, final = sum_second(sum_out, [tok])
+        *parts, tok = mlp_out(rank, act_lo, w_out, lo, [tok, *sent])
         x_two_top = shard(y_two) - sum_end(value, final, [tok])
         f_top = gather(rms_norm(x_two_top).astype(BF))
-        s_a, sl_hi, act_hi, sl_lo, act_lo, tok = mlp_pair_fwd(rank, s_one, w_in, hi, lo, [tok])
-        value, sent, final = sum_second(sum_g, [tok])
-        *parts, tok = mlp_out(rank, act_lo, w_out, lo, [tok, *sent])
-        back = sum_end(value, final, [tok])
-        d_one = shard(dy_one) + rms_vjp(shard(y_one), back)
-        d_one_bf = gather(d_one.astype(BF))
-        sum_out, sent_low = sum_first(sum_cores(parts), [d_one_bf])
-        f_hi, o_hi, qkv_hi, tok = attn(rank, head_dim, qkv_w, o_w, hi, x=s_two, norm=True, after=[tok, wo_all])
-        o_top, qkv_top, tok = attn(rank, head_dim, qkv_w, o_w, top, x=f_top, after=[tok])
-        dqkv_top, *parts, tok = attn(rank, head_dim, qkv_w, o_w, top, qkv=qkv_top, d=d_one_bf, after=[tok, *sent_low])
+        sum_out, sent = sum_first(sum_cores(parts), [x_two_top])
+        f_hi, o_hi, dqkv_hi, *parts, tok = attn(
+            rank, head_dim, qkv_w, o_w, hi, x=s_two, norm=True, d=d_one_bf, after=[tok, wo_all, *sent]
+        )
+        sum_hi, sent = sum_first(sum_cores(parts))
+        value_low, sent_low, final_low = sum_second(sum_out, [tok])
+        tok = mlp_grad("out", top, top_act, d_two_bf, [tok, *sent, *sent_low])
+        value_hi, sent, final_hi = sum_second(sum_hi, [tok])
+        o_top, dqkv_top, *parts, tok = attn(rank, head_dim, qkv_w, o_w, top, x=f_top, d=d_one_bf, after=[tok, *sent])
+        x_two = shard(s_two) - sum_end(value_low, final_low, [tok])
         sum_top, sent = sum_first(sum_cores(parts))
-        dqkv_hi, *parts, tok = attn(rank, head_dim, qkv_w, o_w, hi, qkv=qkv_hi, d=d_one_bf, after=[tok, *sent])
-        sum_hi = sum_cores(parts)
-        value, sent, final = sum_second(sum_top, [tok, *received(sum_hi)])
-        sum_hi, sent_hi = sum_first(sum_hi, sent)
-        value_low, sent_low, final_low = sum_second(sum_out, [tok, *sent_hi])
-        tok = attn_grads(top, f_top, o_top, dqkv_top, d_one_bf, [tok, *sent, *sent_hi, *sent_low])
+        tok = attn_grads(hi, f_hi, o_hi, dqkv_hi, d_one_bf, [tok, *sent])
+        value, sent, final = sum_second(sum_top, [tok])
+        x_two_shard = tie(x_two, sent)[0]
+        near = spread_first(x_two_shard)
+        tok = attn_grads(top, f_top, o_top, dqkv_top, d_one_bf, [tok, *sent, x_two_shard])
         d_two = shard(dy_two) + rms_vjp(x_two_top, sum_end(value, final, [tok]))
         rounded, d_two = lax.optimization_barrier((d_two.astype(BF), d_two))
         d_two_hi_bf = gather(rounded)
-        value, sent, final = sum_second(sum_hi, [tok])
-        tok = attn_grads(hi, f_hi, o_hi, dqkv_hi, d_one_bf, [tok, *sent])
-        d_two = d_two + rms_vjp(shard(s_two), sum_end(value, final, [tok]))
-        d_two_lo_bf = gather(d_two.astype(BF))
-        x_two = shard(s_two) - sum_end(value_low, final_low, [tok])
-        x_two_shard = tie(x_two, [d_two])[0]
-        near = spread_first(x_two_shard)
-        dh_hi, tok = mlp_dhid(rank, d_two_hi_bf, w_out, hi, sl_hi, [tok, x_two_shard])
-        tok = mlp_grad("in", hi, s_a, dh_hi, [tok])
-        tok = mlp_grad("out", hi, act_hi, d_two_hi_bf, [tok])
-        far, cross = spread_second(near, [tok])
-        dh_lo, *parts, tok = mlp_pair_back(rank, d_two_lo_bf, w_out, sl_lo, dh_hi, w_in, hi, lo, [tok, near[1], near[2]])
+        d_two = d_two + rms_vjp(shard(s_two), sum_end(value_hi, final_hi, [tok]))
+        rounded, d_two = lax.optimization_barrier((d_two.astype(BF), d_two))
+        d_two_lo_bf = gather(rounded)
+        far, cross = spread_second(near, [rounded])
+        dh_hi, tok = mlp_dhid(rank, d_two_hi_bf, w_out, hi, sl_hi, [tok, near[1], near[2]])
         pieces = spread_last(x_two_shard, near, far, cross, [tok])
-        sum_g, sent = sum_first(sum_cores(parts))
-        tok_in = mlp_grad("in", lo, s_a, dh_lo, [tok, *sent])
-        tok = mlp_grad("out", lo, act_lo, d_two_lo_bf, [tok_in])
-        value, sent, final = sum_second(sum_g, [tok_in])
-        d_one = d_one + rms_vjp(shard(s_one), sum_end(value, final))
-        d_one_bf = gather(d_one.astype(BF))
         x_two_full, tok = assemble(rank, pieces, [tok])
         f_lo, o_lo, qkv_lo, tok = attn(rank, head_dim, qkv_w, o_w, lo, x=x_two_full, norm=True, after=[tok])
         o_all = gather(o_lo)
+        dh_lo, *parts, tok = mlp_pair_back(rank, d_two_lo_bf, w_out, sl_lo, dh_hi, w_in, hi, lo, [tok])
+        sum_g, sent = sum_first(sum_cores(parts))
+        tok = mlp_grad("in", lo, s_a, dh_lo, [tok, *sent])
+        value, sent, final = sum_second(sum_g, [tok])
+        d_one = d_one + rms_vjp(shard(s_one), sum_end(value, final))
+        d_one_bf = gather(d_one.astype(BF))
+        tok = mlp_grad("out", lo, act_lo, d_two_lo_bf, [tok, *sent])
+        tok = mlp_grad("in", hi, s_a, dh_hi, [tok])
+        tok = mlp_grad("out", hi, act_hi, d_two_hi_bf, [tok])
         d_one_shard = tie(d_one, [d_one_bf])[0]
         near = spread_first(d_one_shard)
         dqkv_lo, *parts, tok = attn(rank, head_dim, qkv_w, o_w, lo, qkv=qkv_lo, d=d_one_bf, after=[tok])
         sum_lo, sent = sum_first(sum_cores(parts))
         tok = attn_grads(lo, f_lo, o_lo, dqkv_lo, d_one_bf, [tok, *sent])
         value, sent, final = sum_second(sum_lo, [tok])
+        d_two = d_two + rms_vjp(x_two, sum_end(value, final))
         far, cross = spread_second(near, [tok, *sent])
-        x_one_full, tok_x = attn_value(rank, s_one, o_all, wo_all, [tok, *sent])
-        d_two = d_two + rms_vjp(x_two, sum_end(value, final))
-        pieces = spread_last(d_one_shard, near, far, cross, [tok_x])
-        d_one_full, _ = assemble(rank, pieces, [tok_x])
+        x_one_full, tok = attn_value(rank, s_one, o_all, wo_all, [tok, *sent, d_two])
+        pieces = spread_last(d_one_shard, near, far, cross, [tok])
+        d_one_full, _ = assemble(rank, pieces, [tok])
         grad_qkv = stacks["attn"][0].reshape(n_layers, 3, n_heads, head_dim, width).transpose(0, 4, 1, 2, 3)
         grad_o = stacks["attn"][1].reshape(w_o.shape)
         return (x_one_full, x_two_full, d_one_full, gather(d_two), grad_qkv, grad_o, stacks["in"][0], stacks["out"][0])

time: 734 us -> 734 us (level)
  Pallas kernels: 336 us -> 321 us
  waiting for transfers between devices: 216 us -> 229 us
    ppermute x60, waiting for transfers between devices: 194 us -> 219 us  [permute(): return lax.ppermute(array, 'tp', [(idx, idx ^ bit) for idx in range(8)])]
    pallas_call x21 -> x19, Pallas kernels: 235 us -> 220 us  [run(): pl.pallas_call(kernel, grid_spec=pltpu.PrefetchScalarGridSpec(num_scalar_...]
    all_gather x8, waiting for transfers between devices: 21.7 us -> 8.89 us  [gather(): return lax.all_gather(shard, 'tp', axis=0, tiled=True)]
    add x13 -> x11, other arithmetic: 30.4 us -> 28.2 us  [sum_first(): pick(keep, 0) + pick(recv, 0)]
    unnamed x113 -> x89, local copies, waits for them, and re-layouts: 17.2 us -> 15.4 us
  transfers between devices with their start and end apart: 68 -> 68, of which waited for: 30 -> 28; matrix products, arithmetic and copies ran while one was open for 11% -> 13% of each run, Pallas kernels for 39% -> 38%
where the time goes in v3:
time: 734 us; the launch traced here: 721 us
  Pallas kernels  321 us (44%)
  waiting for transfers between devices  229 us (31%)
  other arithmetic  94 us (13%)
  starting transfers between devices  39.3 us (5%)
  local copies, waits for them, and re-layouts  23.1 us (3%)
  between operations  14.9 us (2%)
    pallas_call x19, Pallas kernels, run(): pl.pallas_call(kernel, grid_spec=pltpu.PrefetchScalarGridSpec(num_scalar_...  220 us
    ppermute x60, waiting for transfers between devices, permute(): return lax.ppermute(array, 'tp', [(idx, idx ^ bit) for idx in range(8)])  219 us
    pallas_call x9, Pallas kernels, weight_grads(): *stacks, token = call(*args)  82.5 us
    ppermute x60, starting transfers between devices, permute(): return lax.ppermute(array, 'tp', [(idx, idx ^ bit) for idx in range(8)])  38.9 us
    add x11, other arithmetic, sum_first(): pick(keep, 0) + pick(recv, 0)  28.2 us
    add x13, other arithmetic, sum_second(): sent.append(here[1] + recv[1])  18.6 us
    pallas_call x2, Pallas kernels, assemble(): pl.pallas_call(kernel, grid_spec=pltpu.PrefetchScalarGridSpec(num_scalar_...  18.3 us
    unnamed x89, local copies, waits for them, and re-layouts  15.4 us
  transfers between devices with their start and end apart: 68, of which 28 were waited for; matrix products, arithmetic and copies ran while one was open for 13% of the time, Pallas kernels for 38%

profile of v3, /device:TPU:0, one launch (start us, length us, event | category | flops | bytes accessed | tf_op | source)
XLA Modules:
  0.0 721.3 jit_solution(15701962176185333528)
XLA Ops:
  7.2 13.6 %shard_map.161 = (bf16[8,256,1280]{2,1,0:T(8,128)(2,1)}, f32[8,256,640]{2,1,0:T(8,128)}, bf16[8,256,640]{2,1,0:T(8,128)(2,1)}, f32[8,128]{1,0:T(8,128)}) custom-call(s32[1]{0:T(128)} %bitcast.rank_ref, f32[8,256,1280]{2,1,0:T(8,128)} %refs_0_.3, bf16[3,1280,640]{2,1,0:T(8,128)(2,1)} %refs_5_.3), custom_call_target="tpu_custom_call" | custom-call | flops 3355443200 | bytes 13111296 | tf_op jit(solution)/shard_map/pallas_call | solution.py:91
  20.8 9.4 %shard_map.162 = (bf16[8,256,1280]{2,1,0:T(8,128)(2,1)}, bf16[8,256,640]{2,1,0:T(8,128)(2,1)}, bf16[4,256,640]{2,1,0:T(8,128)(2,1)}, bf16[4,256,640]{2,1,0:T(8,128)(2,1)}, f32[8,128]{1,0:T(8,128)}) custom-call(s32[1]{0:T(128)} %bitcast.rank_ref, f32[8,256,1280]{2,1,0:T(8,128)} %refs_0_.5, bf16[3,640,1280]{2,1,0:T(8,128)(2,1)} %refs_1_.21, ...), custom_call_target="tpu_custom_call" | custom-call | flops 3355443200 | bytes 5244928 | tf_op jit(solution)/shard_map/pallas_call | solution.py:91
  32.8 9.4 %shard_map.163 = (bf16[8,256,1280]{2,1,0:T(8,128)(2,1)}, bf16[8,256,640]{2,1,0:T(8,128)(2,1)}, bf16[4,256,640]{2,1,0:T(8,128)(2,1)}, bf16[4,256,640]{2,1,0:T(8,128)(2,1)}, f32[8,128]{1,0:T(8,128)}) custom-call(s32[1]{0:T(128)} %bitcast.rank_ref, f32[8,256,1280]{2,1,0:T(8,128)} %refs_0_.5, ...), custom_call_target="tpu_custom_call", output_to_operand_aliasing={{0}: (5, {}), {1}: (6, {})} | custom-call | flops 3355443200 | bytes 5244928 | tf_op jit(solution)/shard_map/pallas_call | solution.py:91
  42.3 2.4 slice_add_fusion.25
  45.7 6.0 shard_map.164
  52.2 2.9 collective-permute-start.2
  58.2 5.8 shard_map.165
  63.9 13.0 %collective-permute-done.2 = bf16[2,256,640]{2,1,0:T(8,128)(2,1)S(1)} collective-permute-done((bf16[2,256,640]{2,1,0:T(8,128)(2,1)S(1)}, bf16[2,256,640]{2,1,0:T(8,128)(2,1)S(1)}, u32[]{:S(2)}, u32[]{:S(2)}) %collective-permute-start.2) | collective-permute-done | bytes 655392 | tf_op jit(solution)/shard_map/ppermute | solution.py:373
  81.1 4.0 bitcast_add_fusion.2
  85.1 3.1 slice_add_fusion.2
  88.2 8.9 %shard_map.166 = (f32[3,1280,640]{2,1,0:T(8,128)}, f32[8,128]{1,0:T(8,128)}) custom-call(bf16[2048,1280]{1,0:T(8,128)(2,1)} %bitcast.380, bf16[2048,640]{1,0:T(8,128)(2,1)} %bitcast.364, f32[8,128]{1,0:T(8,128)} %get-tuple-element.168.refs_2_, bf16[256,640]{1,0:T(8,128)(2,1)} %get-tuple-element.342.refs_3_, bf16[256,640]{1,0:T(8,128)(2,1)} %get-tuple-element.341.refs_4_, ...), custom_call_target="tpu_custom_call" | custom-call | flops 3355443200 | bytes 17367040 | tf_op jit(solution)/shard_map/pallas_call | solution.py:368
  101.2 3.4 fusion.68
  106.7 17.7 %shard_map.167 = (bf16[8,256,1280]{2,1,0:T(8,128)(2,1)}, f32[8,256,640]{2,1,0:T(8,128)}, bf16[8,256,640]{2,1,0:T(8,128)(2,1)}, f32[8,256,640]{2,1,0:T(8,128)}, b...) custom-call(s32[1]{0:T(128)} %bitcast.rank_ref, f32[8,256,1280]{2,1,0:T(8,128)} %bitcast.371, ...), custom_call_target="tpu_custom_call" | custom-call | flops 6710886400 | bytes 20975616 | tf_op jit(solution)/shard_map/pallas_call | solution.py:91
  124.4 28.1 %collective-permute-done.9 = f32[2,256,640]{2,1,0:T(8,128)} collective-permute-done((f32[2,256,640]{2,1,0:T(8,128)}, f32[2,256,640]{2,1,0:T(8,128)}, u32[]{:S(2)}, u32[]{:S(2)}) %collective-permute-start.9) | collective-permute-done | bytes 1310752 | tf_op jit(solution)/shard_map/ppermute | solution.py:373
  160.2 5.7 shard_map.168
  166.0 5.8 shard_map.169
  177.7 4.6 collective-permute-done.10
  182.3 3.7 collective-permute-done.14
  186.1 3.8 slice_add_fusion.1
  191.9 15.5 %shard_map.170 = (bf16[8,256,1280]{2,1,0:T(8,128)(2,1)}, bf16[160,2048]{1,0:T(8,128)(2,1)}, bf16[480,2048]{1,0:T(8,128)(2,1)}, bf16[4,256,640]{2,1,0:T(8,128)(2,...) custom-call(s32[1]{0:T(128)} %bitcast.rank_ref, bf16[3,480,1280]{2,1,0:T(8,128)(2,1)} %bitcast.325, ...), custom_call_target="tpu_custom_call" | custom-call | flops 3523215360 | bytes 5244928 | tf_op jit(solution)/shard_map/pallas_call | solution.py:91
  209.4 15.0 %shard_map.171 = (bf16[8,256,1280]{2,1,0:T(8,128)(2,1)}, bf16[160,2048]{1,0:T(8,128)(2,1)}, bf16[480,2048]{1,0:T(8,128)(2,1)}, bf16[4,256,640]{2,1,0:T(8,128)(2,...) custom-call(s32[1]{0:T(128)} %bitcast.rank_ref, ...), custom_call_target="tpu_custom_call", output_to_operand_aliasing={{0}: (5, {}), {1}: (6, {}), {2}: (7, {})} | custom-call | flops 3523215360 | bytes 5244928 | tf_op jit(solution)/shard_map/pallas_call | solution.py:91
  224.4 10.6 %collective-permute-done.13 = f32[2,256,640]{2,1,0:T(8,128)} collective-permute-done((f32[2,256,640]{2,1,0:T(8,128)}, f32[2,256,640]{2,1,0:T(8,128)}, u32[]{:S(2)}, u32[]{:S(2)}) %collective-permute-start.13) | collective-permute-done | bytes 1310752 | tf_op jit(solution)/shard_map/ppermute | solution.py:373
  235.0 2.8 slice_add_fusion.17
  238.7 2.6 slice_add_fusion.18
  246.2 8.8 %shard_map.172 = (f32[3,640,1280]{2,1,0:T(8,128)}, f32[8,128]{1,0:T(8,128)}) custom-call(bf16[2048,640]{1,0:T(8,128)(2,1)} %bitcast.356, bf16[2048,1280]{1,0:T(8,128)(2,1)} %bitcast.359, f32[8,128]{1,0:T(8,128)} %get-tuple-element.199.refs_2_, bf16[2,256,640]{2,1,0:T(8,128)(2,1)} %get-tuple-element.336.refs_3_, ...), custom_call_target="tpu_custom_call" | custom-call | flops 3355443200 | bytes 17367040 | tf_op jit(solution)/shard_map/pallas_call | solution.py:368
  255.0 2.2 collective-permute-done.19
  260.8 14.1 %shard_map.173 = (bf16[160,2048]{1,0:T(8,128)(2,1)}, bf16[480,2048]{1,0:T(8,128)(2,1)}, bf16[4,256,640]{2,1,0:T(8,128)(2,1)}, bf16[4,256,640]{2,1,0:T(8,128)(2,1)}, f32[8,128]{1,0:T(8,128)}) custom-call(s32[1]{0:T(128)} %bitcast.rank_ref, bf16[3,480,1280]{2,1,0:T(8,128)(2,1)} %bitcast.327, bf16[8,256,1280]{2,1,0:T(8,128)(2,1)} %all-gather.13.cloned.1.call-done.refs_1_, ...), custom_call_target="tpu_custom_call" | custom-call | flops 3523215360 | bytes 2623488 | tf_op jit(solution)/shard_map/pallas_call | solution.py:91
  276.8 14.2 %shard_map.174 = (bf16[160,2048]{1,0:T(8,128)(2,1)}, bf16[480,2048]{1,0:T(8,128)(2,1)}, bf16[4,256,640]{2,1,0:T(8,128)(2,1)}, bf16[4,256,640]{2,1,0:T(8,128)(2,1)}, f32[8,128]{1,0:T(8,128)}) custom-call(s32[1]{0:T(128)} %bitcast.rank_ref, bf16[3,480,1280]{2,1,0:T(8,128)(2,1)} %bitcast.328, ...), custom_call_target="tpu_custom_call", output_to_operand_aliasing={{0}: (5, {}), {1}: (6, {})} | custom-call | flops 3523215360 | bytes 2623488 | tf_op jit(solution)/shard_map/pallas_call | solution.py:91
  294.6 2.4 slice_add_fusion.12
  298.0 2.4 fusion.7
  302.6 2.6 multiply_reduce_fusion.1
  305.2 9.5 %shard_map.175 = (f32[3,480,1280]{2,1,0:T(8,128)}, f32[3,160,1280]{2,1,0:T(8,128)}, f32[8,128]{1,0:T(8,128)}) custom-call(bf16[480,2048]{1,0:T(8,128)(2,1)} %get-tuple-element.218.refs_0_, bf16[2048,1280]{1,0:T(8,128)(2,1)} %bitcast.354, bf16[160,2048]{1,0:T(8,128)(2,1)} %get-tuple-element.220.refs_2_, bf16[2048,1280]{1,0:T(8,128)(2,1)} %bitcast.323, ...), custom_call_target="tpu_custom_call" | custom-call | flops 3355443200 | bytes 27852800 | tf_op jit(solution)/shard_map/pallas_call | solution.py:368
  320.6 9.7 %shard_map.176 = (f32[3,480,1280]{2,1,0:T(8,128)}, f32[3,160,1280]{2,1,0:T(8,128)}, f32[8,128]{1,0:T(8,128)}) custom-call(bf16[480,2048]{1,0:T(8,128)(2,1)} %get-tuple-element.227.refs_0_, bf16[2048,1280]{1,0:T(8,128)(2,1)} %bitcast.341, bf16[160,2048]{1,0:T(8,128)(2,1)} %get-tuple-element.228.refs_2_, ...), custom_call_target="tpu_custom_call", output_to_operand_aliasing={{0}: (4, {}), {1}: (5, {})} | custom-call | flops 3355443200 | bytes 27852800 | tf_op jit(solution)/shard_map/pallas_call | solution.py:368
  333.0 2.5 fusion.66
  337.9 5.0 collective-permute-done.30
  347.9 3.1 fusion.65
  353.4 40.2 %collective-permute-done.27.refs_4_.refs_2_ = f32[256,1280]{1,0:T(8,128)S(1)} collective-permute-done((f32[256,1280]{1,0:T(8,128)S(1)}, f32[256,1280]{1,0:T(8,128)S(1)}, u32[]{:S(2)}, u32[]{:S(2)}) %collective-permute-start.27) | collective-permute-done | bytes 1310752 | tf_op jit(solution)/shard_map/ppermute | solution.py:373
  399.1 10.7 %shard_map.177 = (bf16[8,256,640]{2,1,0:T(8,128)(2,1)}, f32[8,128]{1,0:T(8,128)}) custom-call(s32[1]{0:T(128)} %bitcast.rank_ref, bf16[8,256,1280]{2,1,0:T(8,128)(2,1)} %all-gather.15.cloned.1.call-done.refs_0_, bf16[3,640,1280]{2,1,0:T(8,128)(2,1)} %refs_1_.21, f32[8,256,640]{2,1,0:T(8,128)} %get-tuple-element.241.refs_2_, ...), custom_call_target="tpu_custom_call" | custom-call | flops 3355443200 | bytes 2625536 | tf_op jit(solution)/shard_map/pallas_call | solution.py:91
  409.8 5.8 collective-permute-done.36.refs_7_
  415.6 6.2 collective-permute-done.35.refs_6_
  424.5 9.2 %shard_map.178 = (f32[8,256,1280]{2,1,0:T(8,128)}, f32[8,128]{1,0:T(8,128)}) custom-call(s32[1]{0:T(128)} %bitcast.rank_ref, f32[256,1280]{1,0:T(8,128)} %bitcast.344, f32[256,1280]{1,0:T(8,128)} %collective-permute-done.26.refs_1_, f32[256,1280]{1,0:T(8,128)} %copy-done.2, f32[256,1280]{1,0:T(8,128)} %collective-permute-done.32.refs_3_, ...), custom_call_target="tpu_custom_call" | custom-call | flops 2000000000 | bytes 20971520 | tf_op jit(solution)/shard_map/pallas_call | solution.py:304
  433.7 14.9 %shard_map.179 = (bf16[8,256,1280]{2,1,0:T(8,128)(2,1)}, bf16[160,2048]{1,0:T(8,128)(2,1)}, bf16[480,2048]{1,0:T(8,128)(2,1)}, f32[8,128]{1,0:T(8,128)}) custom-call(s32[1]{0:T(128)} %bitcast.rank_ref, bf16[3,480,1280]{2,1,0:T(8,128)(2,1)} %bitcast.329, f32[8,256,1280]{2,1,0:T(8,128)} %get-tuple-element.352.refs_1_, f32[8,128]{1,0:T(8,128)} %get-tuple-element.246.refs_2_), custom_call_target="tpu_custom_call" | custom-call | flops 2852126720 | bytes 7868416 | tf_op jit(solution)/shard_map/pallas_call | solution.py:91
  448.7 12.2 %shard_map.180 = (bf16[8,256,640]{2,1,0:T(8,128)(2,1)}, bf16[4,256,640]{2,1,0:T(8,128)(2,1)}, bf16[4,256,640]{2,1,0:T(8,128)(2,1)}, f32[8,128]{1,0:T(8,128)}) custom-call(s32[1]{0:T(128)} %bitcast.rank_ref, bf16[8,256,1280]{2,1,0:T(8,128)(2,1)} %all-gather.19.cloned.1.call-done.refs_0_, bf16[3,640,1280]{2,1,0:T(8,128)(2,1)} %refs_1_.21, ...), custom_call_target="tpu_custom_call" | custom-call | flops 5033164800 | bytes 2623488 | tf_op jit(solution)/shard_map/pallas_call | solution.py:91
  461.3 12.1 %shard_map.181 = (bf16[8,256,640]{2,1,0:T(8,128)(2,1)}, bf16[4,256,640]{2,1,0:T(8,128)(2,1)}, bf16[4,256,640]{2,1,0:T(8,128)(2,1)}, f32[8,128]{1,0:T(8,128)}) custom-call(s32[1]{0:T(128)} %bitcast.rank_ref, bf16[8,256,1280]{2,1,0:T(8,128)(2,1)} %all-gather.19.cloned.1.call-done.refs_0_, ...), custom_call_target="tpu_custom_call", output_to_operand_aliasing={{0}: (7, {})} | custom-call | flops 5033164800 | bytes 2623488 | tf_op jit(solution)/shard_map/pallas_call | solution.py:91
  479.0 8.9 %shard_map.182 = (f32[3,1280,640]{2,1,0:T(8,128)}, f32[8,128]{1,0:T(8,128)}) custom-call(bf16[2048,1280]{1,0:T(8,128)(2,1)} %bitcast.351, bf16[2048,640]{1,0:T(8,128)(2,1)} %bitcast.355, f32[3,1280,640]{2,1,0:T(8,128)} %get-tuple-element.259.refs_2_, f32[8,128]{1,0:T(8,128)} %get-tuple-element.260.refs_3_, ...), custom_call_target="tpu_custom_call", output_to_operand_aliasing={{0}: (2, {})} | custom-call | flops 3355443200 | bytes 17367040 | tf_op jit(solution)/shard_map/pallas_call | solution.py:368
  488.0 5.4 collective-permute-done.40
  495.3 7.9 %collective-permute-done.42 = bf16[256,640]{1,0:T(8,128)(2,1)S(1)} collective-permute-done((bf16[256,640]{1,0:T(8,128)(2,1)S(1)}, bf16[256,640]{1,0:T(8,128)(2,1)S(1)}, u32[]{:S(2)}, u32[]{:S(2)}) %collective-permute-start.42) | collective-permute-done | bytes 327712 | tf_op jit(solution)/shard_map/ppermute | solution.py:373
  506.3 2.5 fusion.64
  509.6 9.0 %shard_map.183 = (f32[3,640,1280]{2,1,0:T(8,128)}, f32[8,128]{1,0:T(8,128)}) custom-call(bf16[2048,640]{1,0:T(8,128)(2,1)} %bitcast.350, bf16[2048,1280]{1,0:T(8,128)(2,1)} %bitcast.342, f32[3,640,1280]{2,1,0:T(8,128)} %get-tuple-element.267.refs_2_, f32[8,128]{1,0:T(8,128)} %get-tuple-element.263.refs_3_, ...), custom_call_target="tpu_custom_call", output_to_operand_aliasing={{0}: (2, {})} | custom-call | flops 3355443200 | bytes 17367040 | tf_op jit(solution)/shard_map/pallas_call | solution.py:368
  518.7 8.9 %shard_map.184 = (f32[3,1280,640]{2,1,0:T(8,128)}, f32[8,128]{1,0:T(8,128)}) custom-call(bf16[2048,1280]{1,0:T(8,128)(2,1)} %bitcast.352, bf16[2048,640]{1,0:T(8,128)(2,1)} %bitcast.349, f32[3,1280,640]{2,1,0:T(8,128)} %get-tuple-element.269.refs_2_, f32[8,128]{1,0:T(8,128)} %get-tuple-element.270.refs_3_), custom_call_target="tpu_custom_call", output_to_operand_aliasing={{0}: (2, {})} | custom-call | flops 3355443200 | bytes 17367040 | tf_op jit(solution)/shard_map/pallas_call | solution.py:368
  527.6 9.1 %shard_map.185 = (f32[3,640,1280]{2,1,0:T(8,128)}, f32[8,128]{1,0:T(8,128)}) custom-call(bf16[2048,640]{1,0:T(8,128)(2,1)} %bitcast.365, bf16[2048,1280]{1,0:T(8,128)(2,1)} %bitcast.353, f32[3,640,1280]{2,1,0:T(8,128)} %get-tuple-element.268.refs_2_, f32[8,128]{1,0:T(8,128)} %get-tuple-element.271.refs_3_), custom_call_target="tpu_custom_call", output_to_operand_aliasing={{0}: (2, {})} | custom-call | flops 3355443200 | bytes 17367040 | tf_op jit(solution)/shard_map/pallas_call | solution.py:368
  536.7 8.9 %all-gather.21.cloned.1.call-done.refs_3_ = bf16[8,256,1280]{2,1,0:T(8,128)(2,1)} async-done(((bf16[1,256,1280]{2,1,0:T(8,128)(2,1)}), bf16[8,256,1280]{2,1,0:T(8,128)(2,1)}) %all-gather.21.cloned.1.call-update) | async-done | bytes 5242896 | tf_op jit(solution)/shard_map/all_gather | solution.py:415
  545.5 11.1 %shard_map.186 = (bf16[480,2048]{1,0:T(8,128)(2,1)}, bf16[4,256,640]{2,1,0:T(8,128)(2,1)}, bf16[4,256,640]{2,1,0:T(8,128)(2,1)}, f32[8,128]{1,0:T(8,128)}) custom-call(s32[1]{0:T(128)} %bitcast.rank_ref, bf16[3,480,1280]{2,1,0:T(8,128)(2,1)} %bitcast.330, bf16[480,2048]{1,0:T(8,128)(2,1)} %get-tuple-element.248.refs_1_, bf16[3,160,1280]{2,1,0:T(8,128)(2,1)} %bitcast.338, ...), custom_call_target="tpu_custom_call" | custom-call | flops 2097152000 | bytes 2295808 | tf_op jit(solution)/shard_map/pallas_call | solution.py:91
  557.1 11.1 %shard_map.187 = (bf16[480,2048]{1,0:T(8,128)(2,1)}, bf16[4,256,640]{2,1,0:T(8,128)(2,1)}, bf16[4,256,640]{2,1,0:T(8,128)(2,1)}, f32[8,128]{1,0:T(8,128)}) custom-call(s32[1]{0:T(128)} %bitcast.rank_ref, bf16[3,480,1280]{2,1,0:T(8,128)(2,1)} %bitcast.331, bf16[480,2048]{1,0:T(8,128)(2,1)} %get-tuple-element.248.refs_1_, ...), custom_call_target="tpu_custom_call", output_to_operand_aliasing={{0}: (5, {})} | custom-call | flops 2097152000 | bytes 2295808 | tf_op jit(solution)/shard_map/pallas_call | solution.py:91
  572.7 2.3 slice_add_fusion.5
  575.8 9.5 %shard_map.188 = (f32[3,480,1280]{2,1,0:T(8,128)}, f32[3,160,1280]{2,1,0:T(8,128)}, f32[8,128]{1,0:T(8,128)}) custom-call(bf16[480,2048]{1,0:T(8,128)(2,1)} %get-tuple-element.275.refs_0_, bf16[2048,1280]{1,0:T(8,128)(2,1)} %bitcast.358, bf16[160,2048]{1,0:T(8,128)(2,1)} %get-tuple-element.247.refs_2_, ...), custom_call_target="tpu_custom_call", output_to_operand_aliasing={{0}: (4, {}), {1}: (5, {})} | custom-call | flops 3355443200 | bytes 27852800 | tf_op jit(solution)/shard_map/pallas_call | solution.py:368
  585.3 11.7 %collective-permute-done.48 = bf16[2,256,640]{2,1,0:T(8,128)(2,1)} collective-permute-done((bf16[2,256,640]{2,1,0:T(8,128)(2,1)S(1)}, bf16[2,256,640]{2,1,0:T(8,128)(2,1)}, u32[]{:S(2)}, u32[]{:S(2)}) %collective-permute-start.48) | collective-permute-done | bytes 655392 | tf_op jit(solution)/shard_map/ppermute | solution.py:373
  601.3 6.4 collective-permute-done.49
  615.9 41.3 %collective-permute-done.52.refs_2_ = f32[256,1280]{1,0:T(8,128)S(1)} collective-permute-done((f32[256,1280]{1,0:T(8,128)S(1)}, f32[256,1280]{1,0:T(8,128)S(1)}, u32[]{:S(2)}, u32[]{:S(2)}) %collective-permute-start.52) | collective-permute-done | bytes 1310752 | tf_op jit(solution)/shard_map/ppermute | solution.py:373
  662.9 15.7 %shard_map.189 = (f32[8,256,1280]{2,1,0:T(8,128)}, f32[8,128]{1,0:T(8,128)}) custom-call(s32[1]{0:T(128)} %bitcast.rank_ref, f32[8,256,1280]{2,1,0:T(8,128)} %bitcast.372, bf16[1280,2048]{1,0:T(8,128)(2,1)} %all-gather.17.cloned.1.call-done.refs_1_, bf16[1280,1280]{1,0:T(8,128)(2,1)} %all-gather.11.cloned.1.call-done.refs_5_.refs_2_, ...), custom_call_target="tpu_custom_call" | custom-call | flops 6710886400 | bytes 10489856 | tf_op jit(solution)/shard_map/pallas_call | solution.py:91
  678.6 10.4 %collective-permute-done.57.refs_7_ = f32[256,640]{1,0:T(8,128)S(1)} collective-permute-done((f32[256,640]{1,0:T(8,128)}, f32[256,640]{1,0:T(8,128)S(1)}, u32[]{:S(2)}, u32[]{:S(2)}) %collective-permute-start.57) | collective-permute-done | bytes 655392 | tf_op jit(solution)/shard_map/ppermute | solution.py:373
  689.0 3.8 collective-permute-done.56.refs_6_
  696.3 9.1 %shard_map.190 = (f32[8,256,1280]{2,1,0:T(8,128)}, f32[8,128]{1,0:T(8,128)}) custom-call(s32[1]{0:T(128)} %bitcast.rank_ref, f32[256,1280]{1,0:T(8,128)} %bitcast.363, f32[256,1280]{1,0:T(8,128)} %collective-permute-done.51.refs_1_, f32[256,1280]{1,0:T(8,128)} %copy-done.11, f32[256,1280]{1,0:T(8,128)} %collective-permute-done.53.refs_3_, ...), custom_call_target="tpu_custom_call" | custom-call | flops 2000000000 | bytes 20971520 | tf_op jit(solution)/shard_map/pallas_call | solution.py:304
  705.4 8.8 %copy.53 = f32[8,256,1280]{2,1,0:T(8,128)} copy(f32[8,256,1280]{2,1,0:T(8,128)} %all-gather.23.cloned.1.call-done) | data formatting | bytes 20971520
  (270 shorter events, 118.5 us)
Async XLA Ops:
  7.2 184.7 %all-gather.11.cloned.1.call-start = ((), (), s32[]{:S(2)}) async-start(), calls=%async_computation.1 | async-start | bytes 3686400 | tf_op jit(solution)/shard_map/all_gather | solution.py:415
  30.2 12.0 %collective-permute-start = (bf16[4,256,640]{2,1,0:T(8,128)(2,1)}, bf16[4,256,640]{2,1,0:T(8,128)(2,1)S(1)}, u32[]{:S(2)}, u32[]{:S(2)}) collective-permute-start(bf16[4,256,640]{2,1,0:T(8,128)(2,1)} %get-tuple-element.164), channel_id=1, source_target_pairs={{0,1},{1,0},{2,3},{3,2},{4,5},{5,4},{6,7},{7,6},{8,9},{9,8},{10,11... | collective-permute-start | bytes 3932168 | tf_op jit(solution)/shard_map/ppermute | solution.py:373
  30.9 13.7 %collective-permute-start.1 = (bf16[4,256,640]{2,1,0:T(8,128)(2,1)}, bf16[4,256,640]{2,1,0:T(8,128)(2,1)S(1)}, u32[]{:S(2)}, u32[]{:S(2)}) collective-permute-start(bf16[4,256,640]{2,1,0:T(8,128)(2,1)} %get-tuple-element.166), channel_id=1, source_target_pairs={{0,1},{1,0},{2,3},{3,2},{4,5},{5,4},{6,7},{7,6},{8,9},{9,8},{10,11... | collective-permute-start | bytes 3932168 | tf_op jit(solution)/shard_map/ppermute | solution.py:373
  32.8 159.1 %all-gather.9.cloned.1.call-start = ((), (), s32[]{:S(2)}) async-start(), calls=%async_computation | async-start | bytes 5898240 | tf_op jit(solution)/shard_map/all_gather | solution.py:415
  51.6 29.4 %collective-permute-start.5 = (f32[4,256,640]{2,1,0:T(8,128)}, f32[4,256,640]{2,1,0:T(8,128)}, u32[]{:S(2)}, u32[]{:S(2)}) collective-permute-start(f32[4,256,640]{2,1,0:T(8,128)} %get-tuple-element.175), channel_id=1, source_target_pairs={{0,1},{1,0},{2,3},{3,2},{4,5},{5,4},{6,7},{7,6},{8,9},{9,8},{10,11... | collective-permute-start | bytes 7864328 | tf_op jit(solution)/shard_map/ppermute | solution.py:373
  52.1 29.0 %collective-permute-start.4 = (f32[4,256,640]{2,1,0:T(8,128)}, f32[4,256,640]{2,1,0:T(8,128)}, u32[]{:S(2)}, u32[]{:S(2)}) collective-permute-start(f32[4,256,640]{2,1,0:T(8,128)} %get-tuple-element.172), channel_id=1, source_target_pairs={{0,1},{1,0},{2,3},{3,2},{4,5},{5,4},{6,7},{7,6},{8,9},{9,8},{10,11... | collective-permute-start | bytes 7864328 | tf_op jit(solution)/shard_map/ppermute | solution.py:373
  52.2 24.7 %collective-permute-start.2 = (bf16[2,256,640]{2,1,0:T(8,128)(2,1)S(1)}, bf16[2,256,640]{2,1,0:T(8,128)(2,1)S(1)}, u32[]{:S(2)}, u32[]{:S(2)}) collective-permute-start(bf16[2,256,640]{2,1,0:T(8,128)(2,1)S(1)} %copy-done.13), channel_id=1, source_target_pairs={{0,2},{1,3},{2,0},{3,1},{4,6},{5,7},{6,4},{7,5},{8,10},{9,11},{10,... | collective-permute-start | bytes 1966088 | tf_op jit(solution)/shard_map/ppermute | solution.py:373
  55.1 21.9 %collective-permute-start.3 = (bf16[2,256,640]{2,1,0:T(8,128)(2,1)S(1)}, bf16[2,256,640]{2,1,0:T(8,128)(2,1)}, u32[]{:S(2)}, u32[]{:S(2)}) collective-permute-start(bf16[2,256,640]{2,1,0:T(8,128)(2,1)S(1)} %copy-done.14), channel_id=1, source_target_pairs={{0,4},{1,5},{2,6},{3,7},{4,0},{5,1},{6,2},{7,3},{8,12},{9,13},{10,... | collective-permute-start | bytes 1966088 | tf_op jit(solution)/shard_map/ppermute | solution.py:373
  79.0 18.1 %collective-permute-start.6 = (bf16[256,640]{1,0:T(8,128)(2,1)}, bf16[256,640]{1,0:T(8,128)(2,1)S(1)}, u32[]{:S(2)}, u32[]{:S(2)}) collective-permute-start(bf16[256,640]{1,0:T(8,128)(2,1)} %get-tuple-element.342.refs_3_), channel_id=1, source_target_pairs={{0,4},{1,5},{2,6},{3,7},{4,0},{5,1},{6,2},{7,3},{8,12},{9,13},{10,... | collective-permute-start | bytes 983048 | tf_op jit(solution)/shard_map/ppermute | solution.py:373
  80.5 16.6 %collective-permute-start.7 = (bf16[256,640]{1,0:T(8,128)(2,1)}, bf16[256,640]{1,0:T(8,128)(2,1)}, u32[]{:S(2)}, u32[]{:S(2)}) collective-permute-start(bf16[256,640]{1,0:T(8,128)(2,1)} %get-tuple-element.341.refs_4_), channel_id=1, source_target_pairs={{0,2},{1,3},{2,0},{3,1},{4,6},{5,7},{6,4},{7,5},{8,10},{9,11},{10,... | collective-permute-start | bytes 983048 | tf_op jit(solution)/shard_map/ppermute | solution.py:373
  104.6 156.1 %all-gather.13.cloned.1.call-start = ((), (), s32[]{:S(2)}) async-start(), calls=%async_computation.2 | async-start | bytes 5898240 | tf_op jit(solution)/shard_map/all_gather | solution.py:415
  104.7 47.8 %collective-permute-start.9 = (f32[2,256,640]{2,1,0:T(8,128)}, f32[2,256,640]{2,1,0:T(8,128)}, u32[]{:S(2)}, u32[]{:S(2)}) collective-permute-start(f32[2,256,640]{2,1,0:T(8,128)} %get-tuple-element.318.refs_6_), channel_id=1, source_target_pairs={{0,4},{1,5},{2,6},{3,7},{4,0},{5,1},{6,2},{7,3},{8,12},{9,13},{10,... | collective-permute-start | bytes 3932168 | tf_op jit(solution)/shard_map/ppermute | solution.py:373
  106.0 48.6 %collective-permute-start.8 = (f32[2,256,640]{2,1,0:T(8,128)}, f32[2,256,640]{2,1,0:T(8,128)}, u32[]{:S(2)}, u32[]{:S(2)}) collective-permute-start(f32[2,256,640]{2,1,0:T(8,128)} %get-tuple-element.320.refs_5_), channel_id=1, source_target_pairs={{0,2},{1,3},{2,0},{3,1},{4,6},{5,7},{6,4},{7,5},{8,10},{9,11},{10,... | collective-permute-start | bytes 3932168 | tf_op jit(solution)/shard_map/ppermute | solution.py:373
  155.8 15.9 %collective-permute-start.11 = (f32[256,640]{1,0:T(8,128)S(1)}, f32[256,640]{1,0:T(8,128)}, u32[]{:S(2)}, u32[]{:S(2)}) collective-permute-start(f32[256,640]{1,0:T(8,128)S(1)} %fusion.26.refs_3_), channel_id=1, source_target_pairs={{0,4},{1,5},{2,6},{3,7},{4,0},{5,1},{6,2},{7,3},{8,12},{9,13},{10,... | collective-permute-start | bytes 1966088 | tf_op jit(solution)/shard_map/ppermute | solution.py:373
  158.2 13.5 %collective-permute-start.12 = (f32[256,640]{1,0:T(8,128)}, f32[256,640]{1,0:T(8,128)}, u32[]{:S(2)}, u32[]{:S(2)}) collective-permute-start(f32[256,640]{1,0:T(8,128)} %fusion.24.refs_4_), channel_id=1, source_target_pairs={{0,2},{1,3},{2,0},{3,1},{4,6},{5,7},{6,4},{7,5},{8,10},{9,11},{10,... | collective-permute-start | bytes 1966088 | tf_op jit(solution)/shard_map/ppermute | solution.py:373
  177.1 222.0 %all-gather.15.cloned.1.call-start = ((), (), s32[]{:S(2)}) async-start(), calls=%async_computation.3 | async-start | bytes 5898240 | tf_op jit(solution)/shard_map/all_gather | solution.py:415
  177.2 8.9 %collective-permute-start.14 = (f32[4,256,640]{2,1,0:T(8,128)}, f32[4,256,640]{2,1,0:T(8,128)S(1)}, u32[]{:S(2)}, u32[]{:S(2)}) collective-permute-start(f32[4,256,640]{2,1,0:T(8,128)} %get-tuple-element.193), channel_id=1, source_target_pairs={{0,1},{1,0},{2,3},{3,2},{4,5},{5,4},{6,7},{7,6},{8,9},{9,8},{10,11... | collective-permute-start | bytes 7864328 | tf_op jit(solution)/shard_map/ppermute | solution.py:373
  189.8 45.2 %collective-permute-start.13 = (f32[2,256,640]{2,1,0:T(8,128)}, f32[2,256,640]{2,1,0:T(8,128)}, u32[]{:S(2)}, u32[]{:S(2)}) collective-permute-start(f32[2,256,640]{2,1,0:T(8,128)} %get-tuple-element.314.refs_6_), channel_id=1, source_target_pairs={{0,2},{1,3},{2,0},{3,1},{4,6},{5,7},{6,4},{7,5},{8,10},{9,11},{10,... | collective-permute-start | bytes 3932168 | tf_op jit(solution)/shard_map/ppermute | solution.py:373
  207.4 27.6 %collective-permute-start.17 = (bf16[4,256,640]{2,1,0:T(8,128)(2,1)}, bf16[4,256,640]{2,1,0:T(8,128)(2,1)}, u32[]{:S(2)}, u32[]{:S(2)}) collective-permute-start(bf16[4,256,640]{2,1,0:T(8,128)(2,1)} %get-tuple-element.205), channel_id=1, source_target_pairs={{0,1},{1,0},{2,3},{3,2},{4,5},{5,4},{6,7},{7,6},{8,9},{9,8},{10,11... | collective-permute-start | bytes 3932168 | tf_op jit(solution)/shard_map/ppermute | solution.py:373
  207.4 31.3 %collective-permute-start.16 = (bf16[4,256,640]{2,1,0:T(8,128)(2,1)}, bf16[4,256,640]{2,1,0:T(8,128)(2,1)}, u32[]{:S(2)}, u32[]{:S(2)}) collective-permute-start(bf16[4,256,640]{2,1,0:T(8,128)(2,1)} %get-tuple-element.203), channel_id=1, source_target_pairs={{0,1},{1,0},{2,3},{3,2},{4,5},{5,4},{6,7},{7,6},{8,9},{9,8},{10,11... | collective-permute-start | bytes 3932168 | tf_op jit(solution)/shard_map/ppermute | solution.py:373
  207.9 36.3 %collective-permute-start.18 = (f32[2,256,640]{2,1,0:T(8,128)S(1)}, f32[2,256,640]{2,1,0:T(8,128)}, u32[]{:S(2)}, u32[]{:S(2)}) collective-permute-start(f32[2,256,640]{2,1,0:T(8,128)S(1)} %copy-done.3), channel_id=1, source_target_pairs={{0,4},{1,5},{2,6},{3,7},{4,0},{5,1},{6,2},{7,3},{8,12},{9,13},{10,... | collective-permute-start | bytes 3932168 | tf_op jit(solution)/shard_map/ppermute | solution.py:373
  237.8 17.3 %collective-permute-start.20 = (bf16[2,256,640]{2,1,0:T(8,128)(2,1)}, bf16[2,256,640]{2,1,0:T(8,128)(2,1)}, u32[]{:S(2)}, u32[]{:S(2)}) collective-permute-start(bf16[2,256,640]{2,1,0:T(8,128)(2,1)} %get-tuple-element.334.refs_4_), channel_id=1, source_target_pairs={{0,4},{1,5},{2,6},{3,7},{4,0},{5,1},{6,2},{7,3},{8,12},{9,13},{10,... | collective-permute-start | bytes 1966088 | tf_op jit(solution)/shard_map/ppermute | solution.py:373
  241.3 16.0 %collective-permute-start.19 = (bf16[2,256,640]{2,1,0:T(8,128)(2,1)}, bf16[2,256,640]{2,1,0:T(8,128)(2,1)}, u32[]{:S(2)}, u32[]{:S(2)}) collective-permute-start(bf16[2,256,640]{2,1,0:T(8,128)(2,1)} %get-tuple-element.336.refs_3_), channel_id=1, source_target_pairs={{0,2},{1,3},{2,0},{3,1},{4,6},{5,7},{6,4},{7,5},{8,10},{9,11},{10,... | collective-permute-start | bytes 1966088 | tf_op jit(solution)/shard_map/ppermute | solution.py:373
  274.9 19.7 %collective-permute-start.24 = (bf16[4,256,640]{2,1,0:T(8,128)(2,1)}, bf16[4,256,640]{2,1,0:T(8,128)(2,1)}, u32[]{:S(2)}, u32[]{:S(2)}) collective-permute-start(bf16[4,256,640]{2,1,0:T(8,128)(2,1)} %get-tuple-element.222), channel_id=1, source_target_pairs={{0,1},{1,0},{2,3},{3,2},{4,5},{5,4},{6,7},{7,6},{8,9},{9,8},{10,11... | collective-permute-start | bytes 3932168 | tf_op jit(solution)/shard_map/ppermute | solution.py:373
  274.9 23.1 %collective-permute-start.22 = (bf16[4,256,640]{2,1,0:T(8,128)(2,1)}, bf16[4,256,640]{2,1,0:T(8,128)(2,1)}, u32[]{:S(2)}, u32[]{:S(2)}) collective-permute-start(bf16[4,256,640]{2,1,0:T(8,128)(2,1)} %get-tuple-element.217), channel_id=1, source_target_pairs={{0,1},{1,0},{2,3},{3,2},{4,5},{5,4},{6,7},{7,6},{8,9},{9,8},{10,11... | collective-permute-start | bytes 3932168 | tf_op jit(solution)/shard_map/ppermute | solution.py:373
  275.4 17.0 %collective-permute-start.15 = (f32[256,640]{1,0:T(8,128)}, f32[256,640]{1,0:T(8,128)}, u32[]{:S(2)}, u32[]{:S(2)}) collective-permute-start(f32[256,640]{1,0:T(8,128)} %fusion.14.refs_5_), channel_id=1, source_target_pairs={{0,4},{1,5},{2,6},{3,7},{4,0},{5,1},{6,2},{7,3},{8,12},{9,13},{10,... | collective-permute-start | bytes 1966088 | tf_op jit(solution)/shard_map/ppermute | solution.py:373
  276.5 16.7 %collective-permute-start.21 = (f32[256,640]{1,0:T(8,128)}, f32[256,640]{1,0:T(8,128)}, u32[]{:S(2)}, u32[]{:S(2)}) collective-permute-start(f32[256,640]{1,0:T(8,128)} %fusion.11.refs_6_), channel_id=1, source_target_pairs={{0,2},{1,3},{2,0},{3,1},{4,6},{5,7},{6,4},{7,5},{8,10},{9,11},{10,... | collective-permute-start | bytes 1966088 | tf_op jit(solution)/shard_map/ppermute | solution.py:373
  297.0 17.7 %collective-permute-start.25 = (bf16[2,256,640]{2,1,0:T(8,128)(2,1)}, bf16[2,256,640]{2,1,0:T(8,128)(2,1)}, u32[]{:S(2)}, u32[]{:S(2)}) collective-permute-start(bf16[2,256,640]{2,1,0:T(8,128)(2,1)} %get-tuple-element.330.refs_6_), channel_id=1, source_target_pairs={{0,4},{1,5},{2,6},{3,7},{4,0},{5,1},{6,2},{7,3},{8,12},{9,13},{10,... | collective-permute-start | bytes 1966088 | tf_op jit(solution)/shard_map/ppermute | solution.py:373
  300.4 15.6 %collective-permute-start.23 = (bf16[2,256,640]{2,1,0:T(8,128)(2,1)}, bf16[2,256,640]{2,1,0:T(8,128)(2,1)}, u32[]{:S(2)}, u32[]{:S(2)}) collective-permute-start(bf16[2,256,640]{2,1,0:T(8,128)(2,1)} %get-tuple-element.331.refs_5_), channel_id=1, source_target_pairs={{0,2},{1,3},{2,0},{3,1},{4,6},{5,7},{6,4},{7,5},{8,10},{9,11},{10,... | collective-permute-start | bytes 1966088 | tf_op jit(solution)/shard_map/ppermute | solution.py:373
  317.7 12.5 %collective-permute-start.28 = (bf16[256,640]{1,0:T(8,128)(2,1)}, bf16[256,640]{1,0:T(8,128)(2,1)}, u32[]{:S(2)}, u32[]{:S(2)}) collective-permute-start(bf16[256,640]{1,0:T(8,128)(2,1)} %fusion.54.refs_7_), channel_id=1, source_target_pairs={{0,4},{1,5},{2,6},{3,7},{4,0},{5,1},{6,2},{7,3},{8,12},{9,13},{10,... | collective-permute-start | bytes 983048 | tf_op jit(solution)/shard_map/ppermute | solution.py:373
  319.8 11.6 %collective-permute-start.29 = (bf16[256,640]{1,0:T(8,128)(2,1)S(1)}, bf16[256,640]{1,0:T(8,128)(2,1)}, u32[]{:S(2)}, u32[]{:S(2)}) collective-permute-start(bf16[256,640]{1,0:T(8,128)(2,1)S(1)} %fusion.52.refs_8_), channel_id=1, source_target_pairs={{0,2},{1,3},{2,0},{3,1},{4,6},{5,7},{6,4},{7,5},{8,10},{9,11},{10,... | collective-permute-start | bytes 983048 | tf_op jit(solution)/shard_map/ppermute | solution.py:373
  335.5 113.2 %all-gather.19.cloned.1.call-start = ((), (), s32[]{:S(2)}) async-start(), calls=%async_computation.5 | async-start | bytes 5898240 | tf_op jit(solution)/shard_map/all_gather | solution.py:415
  335.5 7.4 %collective-permute-start.30 = (bf16[256,640]{1,0:T(8,128)(2,1)}, bf16[256,640]{1,0:T(8,128)(2,1)S(1)}, u32[]{:S(2)}, u32[]{:S(2)}) collective-permute-start(bf16[256,640]{1,0:T(8,128)(2,1)} %fusion.57.refs_5_), channel_id=1, source_target_pairs={{0,4},{1,5},{2,6},{3,7},{4,0},{5,1},{6,2},{7,3},{8,12},{9,13},{10,... | collective-permute-start | bytes 983048 | tf_op jit(solution)/shard_map/ppermute | solution.py:373
  336.6 7.3 %collective-permute-start.31 = (bf16[256,640]{1,0:T(8,128)(2,1)}, bf16[256,640]{1,0:T(8,128)(2,1)S(1)}, u32[]{:S(2)}, u32[]{:S(2)}) collective-permute-start(bf16[256,640]{1,0:T(8,128)(2,1)} %fusion.55.refs_6_), channel_id=1, source_target_pairs={{0,2},{1,3},{2,0},{3,1},{4,6},{5,7},{6,4},{7,5},{8,10},{9,11},{10,... | collective-permute-start | bytes 983048 | tf_op jit(solution)/shard_map/ppermute | solution.py:373
  351.0 194.5 %all-gather.21.cloned.1.call-start = ((), (), s32[]{:S(2)}) async-start(), calls=%async_computation.6 | async-start | bytes 5898240 | tf_op jit(solution)/shard_map/all_gather | solution.py:415
  351.1 42.5 %collective-permute-start.27 = (f32[256,1280]{1,0:T(8,128)S(1)}, f32[256,1280]{1,0:T(8,128)S(1)}, u32[]{:S(2)}, u32[]{:S(2)}) collective-permute-start(f32[256,1280]{1,0:T(8,128)S(1)} %bitcast.345), channel_id=1, source_target_pairs={{0,2},{1,3},{2,0},{3,1},{4,6},{5,7},{6,4},{7,5},{8,10},{9,11},{10,... | collective-permute-start | bytes 3932168 | tf_op jit(solution)/shard_map/ppermute | solution.py:373
  353.1 42.9 %collective-permute-start.33 = (f32[256,1280]{1,0:T(8,128)S(1)}, f32[256,1280]{1,0:T(8,128)}, u32[]{:S(2)}, u32[]{:S(2)}) collective-permute-start(f32[256,1280]{1,0:T(8,128)S(1)} %bitcast.346), channel_id=1, source_target_pairs={{0,4},{1,5},{2,6},{3,7},{4,0},{5,1},{6,2},{7,3},{8,12},{9,13},{10,... | collective-permute-start | bytes 3932168 | tf_op jit(solution)/shard_map/ppermute | solution.py:373
  353.4 68.4 %collective-permute-start.26 = (f32[256,1280]{1,0:T(8,128)S(1)}, f32[256,1280]{1,0:T(8,128)}, u32[]{:S(2)}, u32[]{:S(2)}) collective-permute-start(f32[256,1280]{1,0:T(8,128)S(1)} %bitcast.347), channel_id=1, source_target_pairs={{0,1},{1,0},{2,3},{3,2},{4,5},{5,4},{6,7},{7,6},{8,9},{9,8},{10,11... | collective-permute-start | bytes 3932168 | tf_op jit(solution)/shard_map/ppermute | solution.py:373
  394.5 21.1 %collective-permute-start.36 = (f32[256,640]{1,0:T(8,128)}, f32[256,640]{1,0:T(8,128)S(1)}, u32[]{:S(2)}, u32[]{:S(2)}) collective-permute-start(f32[256,640]{1,0:T(8,128)} %slice.510), channel_id=1, source_target_pairs={{0,4},{1,5},{2,6},{3,7},{4,0},{5,1},{6,2},{7,3},{8,12},{9,13},{10,... | collective-permute-start | bytes 1966088 | tf_op jit(solution)/shard_map/ppermute | solution.py:373
  398.1 23.8 %collective-permute-start.35 = (f32[256,640]{1,0:T(8,128)}, f32[256,640]{1,0:T(8,128)}, u32[]{:S(2)}, u32[]{:S(2)}) collective-permute-start(f32[256,640]{1,0:T(8,128)} %slice.509), channel_id=1, source_target_pairs={{0,2},{1,3},{2,0},{3,1},{4,6},{5,7},{6,4},{7,5},{8,10},{9,11},{10,... | collective-permute-start | bytes 1966088 | tf_op jit(solution)/shard_map/ppermute | solution.py:373
  398.6 23.3 %collective-permute-start.34 = (f32[256,1280]{1,0:T(8,128)}, f32[256,1280]{1,0:T(8,128)}, u32[]{:S(2)}, u32[]{:S(2)}) collective-permute-start(f32[256,1280]{1,0:T(8,128)} %collective-permute-done.33.refs_5_.refs_4_), channel_id=1, source_target_pairs={{0,1},{1,0},{2,3},{3,2},{4,5},{5,4},{6,7},{7,6},{8,9},{9,8},{10,11... | collective-permute-start | bytes 3932168 | tf_op jit(solution)/shard_map/ppermute | solution.py:373
  398.6 23.3 %collective-permute-start.32 = (f32[256,1280]{1,0:T(8,128)S(1)}, f32[256,1280]{1,0:T(8,128)}, u32[]{:S(2)}, u32[]{:S(2)}) collective-permute-start(f32[256,1280]{1,0:T(8,128)S(1)} %collective-permute-done.27.refs_4_.refs_2_), channel_id=1, source_target_pairs={{0,1},{1,0},{2,3},{3,2},{4,5},{5,4},{6,7},{7,6},{8,9},{9,8},{10,11... | collective-permute-start | bytes 3932168 | tf_op jit(solution)/shard_map/ppermute | solution.py:373
  415.6 6.2 collective-permute-start.38
  460.8 12.6 %collective-permute-start.39 = (bf16[4,256,640]{2,1,0:T(8,128)(2,1)}, bf16[4,256,640]{2,1,0:T(8,128)(2,1)S(1)}, u32[]{:S(2)}, u32[]{:S(2)}) collective-permute-start(bf16[4,256,640]{2,1,0:T(8,128)(2,1)} %get-tuple-element.256), channel_id=1, source_target_pairs={{0,1},{1,0},{2,3},{3,2},{4,5},{5,4},{6,7},{7,6},{8,9},{9,8},{10,11... | collective-permute-start | bytes 3932168 | tf_op jit(solution)/shard_map/ppermute | solution.py:373
  460.9 15.8 %collective-permute-start.41 = (bf16[4,256,640]{2,1,0:T(8,128)(2,1)}, bf16[4,256,640]{2,1,0:T(8,128)(2,1)S(1)}, u32[]{:S(2)}, u32[]{:S(2)}) collective-permute-start(bf16[4,256,640]{2,1,0:T(8,128)(2,1)} %get-tuple-element.262), channel_id=1, source_target_pairs={{0,1},{1,0},{2,3},{3,2},{4,5},{5,4},{6,7},{7,6},{8,9},{9,8},{10,11... | collective-permute-start | bytes 3932168 | tf_op jit(solution)/shard_map/ppermute | solution.py:373
  476.5 16.9 %collective-permute-start.40 = (bf16[2,256,640]{2,1,0:T(8,128)(2,1)S(1)}, bf16[2,256,640]{2,1,0:T(8,128)(2,1)}, u32[]{:S(2)}, u32[]{:S(2)}) collective-permute-start(bf16[2,256,640]{2,1,0:T(8,128)(2,1)S(1)} %get-tuple-element.326.refs_4_), channel_id=1, source_target_pairs={{0,2},{1,3},{2,0},{3,1},{4,6},{5,7},{6,4},{7,5},{8,10},{9,11},{10,... | collective-permute-start | bytes 1966088 | tf_op jit(solution)/shard_map/ppermute | solution.py:373
  477.3 17.1 %collective-permute-start.43 = (bf16[2,256,640]{2,1,0:T(8,128)(2,1)S(1)}, bf16[2,256,640]{2,1,0:T(8,128)(2,1)S(1)}, u32[]{:S(2)}, u32[]{:S(2)}) collective-permute-start(bf16[2,256,640]{2,1,0:T(8,128)(2,1)S(1)} %get-tuple-element.327.refs_5_), channel_id=1, source_target_pairs={{0,4},{1,5},{2,6},{3,7},{4,0},{5,1},{6,2},{7,3},{8,12},{9,13},{10,... | collective-permute-start | bytes 1966088 | tf_op jit(solution)/shard_map/ppermute | solution.py:373
  494.4 8.9 %collective-permute-start.42 = (bf16[256,640]{1,0:T(8,128)(2,1)S(1)}, bf16[256,640]{1,0:T(8,128)(2,1)S(1)}, u32[]{:S(2)}, u32[]{:S(2)}) collective-permute-start(bf16[256,640]{1,0:T(8,128)(2,1)S(1)} %fusion.43.refs_4_), channel_id=1, source_target_pairs={{0,4},{1,5},{2,6},{3,7},{4,0},{5,1},{6,2},{7,3},{8,12},{9,13},{10,... | collective-permute-start | bytes 983048 | tf_op jit(solution)/shard_map/ppermute | solution.py:373
  494.5 9.9 %collective-permute-start.44 = (bf16[256,640]{1,0:T(8,128)(2,1)S(1)}, bf16[256,640]{1,0:T(8,128)(2,1)S(1)}, u32[]{:S(2)}, u32[]{:S(2)}) collective-permute-start(bf16[256,640]{1,0:T(8,128)(2,1)S(1)} %fusion.40.refs_5_), channel_id=1, source_target_pairs={{0,2},{1,3},{2,0},{3,1},{4,6},{5,7},{6,4},{7,5},{8,10},{9,11},{10,... | collective-permute-start | bytes 983048 | tf_op jit(solution)/shard_map/ppermute | solution.py:373
  508.8 154.1 %all-gather.17.cloned.1.call-start = ((), (), s32[]{:S(2)}) async-start(), calls=%async_computation.4 | async-start | bytes 5898240 | tf_op jit(solution)/shard_map/all_gather | solution.py:415
  509.6 195.8 %all-gather.23.cloned.1.call-start = ((), (), s32[]{:S(2)}) async-start(), calls=%async_computation.7 | async-start | bytes 11796480 | tf_op jit(solution)/shard_map/all_gather | solution.py:415
  556.6 11.6 %collective-permute-start.46 = (bf16[4,256,640]{2,1,0:T(8,128)(2,1)}, bf16[4,256,640]{2,1,0:T(8,128)(2,1)S(1)}, u32[]{:S(2)}, u32[]{:S(2)}) collective-permute-start(bf16[4,256,640]{2,1,0:T(8,128)(2,1)} %get-tuple-element.283), channel_id=1, source_target_pairs={{0,1},{1,0},{2,3},{3,2},{4,5},{5,4},{6,7},{7,6},{8,9},{9,8},{10,11... | collective-permute-start | bytes 3932168 | tf_op jit(solution)/shard_map/ppermute | solution.py:373
  556.9 15.8 %collective-permute-start.45 = (bf16[4,256,640]{2,1,0:T(8,128)(2,1)}, bf16[4,256,640]{2,1,0:T(8,128)(2,1)}, u32[]{:S(2)}, u32[]{:S(2)}) collective-permute-start(bf16[4,256,640]{2,1,0:T(8,128)(2,1)} %get-tuple-element.281), channel_id=1, source_target_pairs={{0,1},{1,0},{2,3},{3,2},{4,5},{5,4},{6,7},{7,6},{8,9},{9,8},{10,11... | collective-permute-start | bytes 3932168 | tf_op jit(solution)/shard_map/ppermute | solution.py:373
  571.3 25.7 %collective-permute-start.48 = (bf16[2,256,640]{2,1,0:T(8,128)(2,1)S(1)}, bf16[2,256,640]{2,1,0:T(8,128)(2,1)}, u32[]{:S(2)}, u32[]{:S(2)}) collective-permute-start(bf16[2,256,640]{2,1,0:T(8,128)(2,1)S(1)} %get-tuple-element.322.refs_8_), channel_id=1, source_target_pairs={{0,4},{1,5},{2,6},{3,7},{4,0},{5,1},{6,2},{7,3},{8,12},{9,13},{10,... | collective-permute-start | bytes 1966088 | tf_op jit(solution)/shard_map/ppermute | solution.py:373
  575.0 22.1 %collective-permute-start.47 = (bf16[2,256,640]{2,1,0:T(8,128)(2,1)S(1)}, bf16[2,256,640]{2,1,0:T(8,128)(2,1)}, u32[]{:S(2)}, u32[]{:S(2)}) collective-permute-start(bf16[2,256,640]{2,1,0:T(8,128)(2,1)S(1)} %get-tuple-element.324.refs_7_), channel_id=1, source_target_pairs={{0,2},{1,3},{2,0},{3,1},{4,6},{5,7},{6,4},{7,5},{8,10},{9,11},{10,... | collective-permute-start | bytes 1966088 | tf_op jit(solution)/shard_map/ppermute | solution.py:373
  598.2 9.6 %collective-permute-start.49 = (bf16[256,640]{1,0:T(8,128)(2,1)S(1)}, bf16[256,640]{1,0:T(8,128)(2,1)S(1)}, u32[]{:S(2)}, u32[]{:S(2)}) collective-permute-start(bf16[256,640]{1,0:T(8,128)(2,1)S(1)} %fusion.39.refs_4_), channel_id=1, source_target_pairs={{0,4},{1,5},{2,6},{3,7},{4,0},{5,1},{6,2},{7,3},{8,12},{9,13},{10,... | collective-permute-start | bytes 983048 | tf_op jit(solution)/shard_map/ppermute | solution.py:373
  600.7 9.2 %collective-permute-start.50 = (bf16[256,640]{1,0:T(8,128)(2,1)S(1)}, bf16[256,640]{1,0:T(8,128)(2,1)S(1)}, u32[]{:S(2)}, u32[]{:S(2)}) collective-permute-start(bf16[256,640]{1,0:T(8,128)(2,1)S(1)} %fusion.37.refs_5_), channel_id=1, source_target_pairs={{0,2},{1,3},{2,0},{3,1},{4,6},{5,7},{6,4},{7,5},{8,10},{9,11},{10,... | collective-permute-start | bytes 983048 | tf_op jit(solution)/shard_map/ppermute | solution.py:373
  613.7 43.5 %collective-permute-start.52 = (f32[256,1280]{1,0:T(8,128)S(1)}, f32[256,1280]{1,0:T(8,128)S(1)}, u32[]{:S(2)}, u32[]{:S(2)}) collective-permute-start(f32[256,1280]{1,0:T(8,128)S(1)} %bitcast.360), channel_id=1, source_target_pairs={{0,2},{1,3},{2,0},{3,1},{4,6},{5,7},{6,4},{7,5},{8,10},{9,11},{10,... | collective-permute-start | bytes 3932168 | tf_op jit(solution)/shard_map/ppermute | solution.py:373
  614.4 45.9 %collective-permute-start.54 = (f32[256,1280]{1,0:T(8,128)S(1)}, f32[256,1280]{1,0:T(8,128)}, u32[]{:S(2)}, u32[]{:S(2)}) collective-permute-start(f32[256,1280]{1,0:T(8,128)S(1)} %bitcast.361), channel_id=1, source_target_pairs={{0,4},{1,5},{2,6},{3,7},{4,0},{5,1},{6,2},{7,3},{8,12},{9,13},{10,... | collective-permute-start | bytes 3932168 | tf_op jit(solution)/shard_map/ppermute | solution.py:373
  658.1 30.9 %collective-permute-start.57 = (f32[256,640]{1,0:T(8,128)}, f32[256,640]{1,0:T(8,128)S(1)}, u32[]{:S(2)}, u32[]{:S(2)}) collective-permute-start(f32[256,640]{1,0:T(8,128)} %slice.548), channel_id=1, source_target_pairs={{0,4},{1,5},{2,6},{3,7},{4,0},{5,1},{6,2},{7,3},{8,12},{9,13},{10,... | collective-permute-start | bytes 1966088 | tf_op jit(solution)/shard_map/ppermute | solution.py:373
  662.3 30.5 %collective-permute-start.56 = (f32[256,640]{1,0:T(8,128)}, f32[256,640]{1,0:T(8,128)}, u32[]{:S(2)}, u32[]{:S(2)}) collective-permute-start(f32[256,640]{1,0:T(8,128)} %slice.547), channel_id=1, source_target_pairs={{0,2},{1,3},{2,0},{3,1},{4,6},{5,7},{6,4},{7,5},{8,10},{9,11},{10,... | collective-permute-start | bytes 1966088 | tf_op jit(solution)/shard_map/ppermute | solution.py:373
  662.4 30.4 %collective-permute-start.51 = (f32[256,1280]{1,0:T(8,128)S(1)}, f32[256,1280]{1,0:T(8,128)}, u32[]{:S(2)}, u32[]{:S(2)}) collective-permute-start(f32[256,1280]{1,0:T(8,128)S(1)} %bitcast.362), channel_id=1, source_target_pairs={{0,1},{1,0},{2,3},{3,2},{4,5},{5,4},{6,7},{7,6},{8,9},{9,8},{10,11... | collective-permute-start | bytes 3932168 | tf_op jit(solution)/shard_map/ppermute | solution.py:373
  662.4 33.9 %collective-permute-start.55 = (f32[256,1280]{1,0:T(8,128)}, f32[256,1280]{1,0:T(8,128)}, u32[]{:S(2)}, u32[]{:S(2)}) collective-permute-start(f32[256,1280]{1,0:T(8,128)} %collective-permute-done.54.refs_4_), channel_id=1, source_target_pairs={{0,1},{1,0},{2,3},{3,2},{4,5},{5,4},{6,7},{7,6},{8,9},{9,8},{10,11... | collective-permute-start | bytes 3932168 | tf_op jit(solution)/shard_map/ppermute | solution.py:373
  662.9 33.4 %collective-permute-start.53 = (f32[256,1280]{1,0:T(8,128)S(1)}, f32[256,1280]{1,0:T(8,128)}, u32[]{:S(2)}, u32[]{:S(2)}) collective-permute-start(f32[256,1280]{1,0:T(8,128)S(1)} %collective-permute-done.52.refs_2_), channel_id=1, source_target_pairs={{0,1},{1,0},{2,3},{3,2},{4,5},{5,4},{6,7},{7,6},{8,9},{9,8},{10,11... | collective-permute-start | bytes 3932168 | tf_op jit(solution)/shard_map/ppermute | solution.py:373
  (48 other events, 443.9 us)
Sparse Core Ops, SparseCore 0:
  32.9 38.2 all-gather.10
  104.8 54.6 all-gather.8
  177.2 50.6 all-gather.12
  335.6 52.4 all-gather.14
  389.8 44.8 all-gather.18
  508.9 36.5 all-gather.20
  547.4 45.9 all-gather.16
  613.8 88.0 all-gather.22

commit v4 on v3

--- a/solution.py
+++ b/solution.py
@@ -106,41 +106,27 @@
     return kept[:n_out] + [sent[n_out], sent[n_out + 1], kept[n_out], kept[n_out + 1], kept[-1]]
 
 
-def mlp_fwd(rank, x, w_in, layer):
+def mlp_top(rank, x, w_in, w_out, layer, d):
     seqs, rows, width = x.shape
     inner = w_in.shape[2]
 
     def body(in_refs, out_refs):
-        x_ref, win_ref = in_refs
-        a_ref, slope_ref, act_ref = out_refs
+        x_ref, win_ref, wout_ref, d_ref = in_refs
+        a_ref, act_ref, dh_ref, dbf_ref = out_refs
         a = rms_norm(x_ref[...]).astype(BF)
         a_ref[...] = a
-        hid = dot(a, win_ref[...])
-        act, slope_ref[...] = gelu_both(hid)
-        act_ref[...] = act.astype(BF)
-        return ()
-
-    mid = (seqs, rows, inner)
-    outs = [("row", x.shape, BF), ("row", mid, F32), ("row", mid, BF)]
-    return seq_call(body, rank, [("row", x), ("layer", w_in, layer)], outs, [], 2 * seqs * rows * width * inner)
-
-
-def mlp_back(rank, d, w_out, slope, w_in, layer, after=()):
-    seqs, rows, width = d.shape
-    inner = w_out.shape[1]
-
-    def body(in_refs, out_refs):
-        d_ref, wout_ref, slope_ref, win_ref = in_refs
-        dbf_ref, dh_ref = out_refs
         d_bf = d_ref[...].astype(BF)
         dbf_ref[...] = d_bf
-        dh = (dot_nt(d_bf, wout_ref[...]) * slope_ref[...]).astype(BF)
+        act, slope = gelu_both(dot(a, win_ref[...]))
+        act_ref[...] = act.astype(BF)
+        dh = (dot_nt(d_bf, wout_ref[...]) * slope).astype(BF)
         dh_ref[...] = dh
         yield dot_nt(dh, win_ref[...])
 
-    ins = [("row", d), ("layer", w_out, layer), ("row", slope), ("layer", w_in, layer)]
-    outs = [("row", d.shape, BF), ("row", slope.shape, BF)]
-    return seq_call(body, rank, ins, outs, [(rows, width, BF)], 4 * seqs * rows * width * inner, after)
+    mid = (seqs, rows, inner)
+    outs = [("row", x.shape, BF), ("row", mid, BF), ("row", mid, BF), ("row", d.shape, BF)]
+    ins = [("row", x), ("layer", w_in, layer), ("layer", w_out, layer), ("row", d)]
+    return seq_call(body, rank, ins, outs, [(rows, width, BF)], 6 * seqs * rows * width * inner)
 
 
 def mlp_out(rank, act, w_out, layer, after=()):
@@ -468,9 +454,7 @@
 
         top, hi, lo = 2, 1, 0
         s_one, s_two = saved_one[0], saved_two[0]
-        wo_all = gather(o_w[lo])
-        top_a, s_top, top_act, tok = mlp_fwd(rank, y_one, w_in, top)
-        d_two_bf, top_dh, *parts, tok = mlp_back(rank, dy_two, w_out, s_top, w_in, top, [tok])
+        top_a, top_act, top_dh, d_two_bf, *parts, tok = mlp_top(rank, y_one, w_in, w_out, top, dy_two)
         sum_g, sent = sum_first(sum_cores(parts))
         *parts, tok = mlp_out(rank, top_act, w_out, top, [tok, *sent])
         sum_out = sum_cores(parts)
@@ -487,16 +471,15 @@
         f_top = gather(rms_norm(x_two_top).astype(BF))
         sum_out, sent = sum_first(sum_cores(parts), [x_two_top])
         f_hi, o_hi, dqkv_hi, *parts, tok = attn(
-            rank, head_dim, qkv_w, o_w, hi, x=s_two, norm=True, d=d_one_bf, after=[tok, wo_all, *sent]
+            rank, head_dim, qkv_w, o_w, hi, x=s_two, norm=True, d=d_one_bf, after=[tok, *sent]
         )
         sum_hi, sent = sum_first(sum_cores(parts))
         value_low, sent_low, final_low = sum_second(sum_out, [tok])
-        tok = mlp_grad("out", top, top_act, d_two_bf, [tok, *sent, *sent_low])
-        value_hi, sent, final_hi = sum_second(sum_hi, [tok])
-        o_top, dqkv_top, *parts, tok = attn(rank, head_dim, qkv_w, o_w, top, x=f_top, d=d_one_bf, after=[tok, *sent])
+        o_top, dqkv_top, *parts, tok = attn(rank, head_dim, qkv_w, o_w, top, x=f_top, d=d_one_bf, after=[tok, *sent, *sent_low])
         x_two = shard(s_two) - sum_end(value_low, final_low, [tok])
         sum_top, sent = sum_first(sum_cores(parts))
-        tok = attn_grads(hi, f_hi, o_hi, dqkv_hi, d_one_bf, [tok, *sent])
+        value_hi, sent_hi, final_hi = sum_second(sum_hi, [tok, *sent])
+        tok = attn_grads(hi, f_hi, o_hi, dqkv_hi, d_one_bf, [tok, *sent, *sent_hi])
         value, sent, final = sum_second(sum_top, [tok])
         x_two_shard = tie(x_two, sent)[0]
         near = spread_first(x_two_shard)
@@ -507,7 +490,8 @@
         d_two = d_two + rms_vjp(shard(s_two), sum_end(value_hi, final_hi, [tok]))
         rounded, d_two = lax.optimization_barrier((d_two.astype(BF), d_two))
         d_two_lo_bf = gather(rounded)
-        far, cross = spread_second(near, [rounded])
+        tok = mlp_grad("out", top, top_act, d_two_bf, [tok, rounded])
+        far, cross = spread_second(near, [tok])
         dh_hi, tok = mlp_dhid(rank, d_two_hi_bf, w_out, hi, sl_hi, [tok, near[1], near[2]])
         pieces = spread_last(x_two_shard, near, far, cross, [tok])
         x_two_full, tok = assemble(rank, pieces, [tok])
@@ -518,20 +502,21 @@
         tok = mlp_grad("in", lo, s_a, dh_lo, [tok, *sent])
         value, sent, final = sum_second(sum_g, [tok])
         d_one = d_one + rms_vjp(shard(s_one), sum_end(value, final))
-        d_one_bf = gather(d_one.astype(BF))
-        tok = mlp_grad("out", lo, act_lo, d_two_lo_bf, [tok, *sent])
+        rounded, d_one_shard = lax.optimization_barrier((d_one.astype(BF), d_one[0]))
+        d_one_bf = gather(rounded)
+        near = spread_first(d_one_shard)
+        tok = mlp_grad("out", lo, act_lo, d_two_lo_bf, [tok, rounded])
         tok = mlp_grad("in", hi, s_a, dh_hi, [tok])
         tok = mlp_grad("out", hi, act_hi, d_two_hi_bf, [tok])
-        d_one_shard = tie(d_one, [d_one_bf])[0]
-        near = spread_first(d_one_shard)
-        dqkv_lo, *parts, tok = attn(rank, head_dim, qkv_w, o_w, lo, qkv=qkv_lo, d=d_one_bf, after=[tok])
+        far, cross = spread_second(near, [tok, d_one_bf])
+        wo_all = gather(tie(o_w[lo], [d_one_bf]))
+        dqkv_lo, *parts, tok = attn(rank, head_dim, qkv_w, o_w, lo, qkv=qkv_lo, d=d_one_bf, after=[tok, near[1], near[2]])
+        pieces = spread_last(d_one_shard, near, far, cross, [tok])
         sum_lo, sent = sum_first(sum_cores(parts))
         tok = attn_grads(lo, f_lo, o_lo, dqkv_lo, d_one_bf, [tok, *sent])
         value, sent, final = sum_second(sum_lo, [tok])
         d_two = d_two + rms_vjp(x_two, sum_end(value, final))
-        far, cross = spread_second(near, [tok, *sent])
         x_one_full, tok = attn_value(rank, s_one, o_all, wo_all, [tok, *sent, d_two])
-        pieces = spread_last(d_one_shard, near, far, cross, [tok])
         d_one_full, _ = assemble(rank, pieces, [tok])
         grad_qkv = stacks["attn"][0].reshape(n_layers, 3, n_heads, head_dim, width).transpose(0, 4, 1, 2, 3)
         grad_o = stacks["attn"][1].reshape(w_o.shape)

time: 734 us -> 727 us (level)
  Pallas kernels: 321 us -> 312 us
    all_gather x8, waiting for transfers between devices: 8.89 us -> 63.6 us  [gather(): return lax.all_gather(shard, 'tp', axis=0, tiled=True)]
    ppermute x60, waiting for transfers between devices: 219 us -> 170 us  [permute(): return lax.ppermute(array, 'tp', [(idx, idx ^ bit) for idx in range(8)])]
    pallas_call x19 -> x18, Pallas kernels: 220 us -> 211 us  [run(): pl.pallas_call(kernel, grid_spec=pltpu.PrefetchScalarGridSpec(num_scalar_...]
    unnamed x89 -> x101, local copies, waits for them, and re-layouts: 15.4 us -> 16.9 us
  transfers between devices with their start and end apart: 68 -> 68, of which waited for: 28 -> 25; matrix products, arithmetic and copies ran while one was open for 13% -> 11% of each run, Pallas kernels for 38% -> 40%
where the time goes in v4:
time: 727 us; the launch traced here: 715 us
  Pallas kernels  312 us (43%)
  waiting for transfers between devices  234 us (32%)
  other arithmetic  87.4 us (12%)
  starting transfers between devices  44 us (6%)
  local copies, waits for them, and re-layouts  21.8 us (3%)
  between operations  15.1 us (2%)
    pallas_call x18, Pallas kernels, run(): pl.pallas_call(kernel, grid_spec=pltpu.PrefetchScalarGridSpec(num_scalar_...  211 us
    ppermute x60, waiting for transfers between devices, permute(): return lax.ppermute(array, 'tp', [(idx, idx ^ bit) for idx in range(8)])  170 us
    pallas_call x9, Pallas kernels, weight_grads(): *stacks, token = call(*args)  82.7 us
    all_gather x8, waiting for transfers between devices, gather(): return lax.all_gather(shard, 'tp', axis=0, tiled=True)  63.6 us
    ppermute x60, starting transfers between devices, permute(): return lax.ppermute(array, 'tp', [(idx, idx ^ bit) for idx in range(8)])  43.2 us
    add x11, other arithmetic, sum_first(): pick(keep, 0) + pick(recv, 0)  25.3 us
    pallas_call x2, Pallas kernels, assemble(): pl.pallas_call(kernel, grid_spec=pltpu.PrefetchScalarGridSpec(num_scalar_...  18.4 us
    unnamed x101, local copies, waits for them, and re-layouts  16.9 us
  transfers between devices with their start and end apart: 68, of which 25 were waited for; matrix products, arithmetic and copies ran while one was open for 11% of the time, Pallas kernels for 40%

profile of v4, /device:TPU:0, one launch (start us, length us, event | category | flops | bytes accessed | tf_op | source)
XLA Modules:
  0.0 714.8 jit_solution(12350147723999484516)
XLA Ops:
  7.2 11.5 %shard_map.161 = (bf16[8,256,1280]{2,1,0:T(8,128)(2,1)}, bf16[8,256,640]{2,1,0:T(8,128)(2,1)}, bf16[8,256,640]{2,1,0:T(8,128)(2,1)}, bf16[8,256,1280]{2,1,0:T(8,...) custom-call(s32[1]{0:T(128)} %bitcast.rank_ref, f32[8,256,1280]{2,1,0:T(8,128)} %refs_0_.3, ...), custom_call_target="tpu_custom_call" | custom-call | flops 5033164800 | bytes 9177088 | tf_op jit(solution)/shard_map/pallas_call | solution.py:91
  19.5 11.5 %shard_map.162 = (bf16[8,256,1280]{2,1,0:T(8,128)(2,1)}, bf16[8,256,640]{2,1,0:T(8,128)(2,1)}, bf16[8,256,640]{2,1,0:T(8,128)(2,1)}, bf16[8,256,1280]{2,1,0:T(8,...) custom-call(s32[1]{0:T(128)} %bitcast.rank_ref, ...), custom_call_target="tpu_custom_call", output_to_operand_aliasing={{0}: (5, {}), {1}: (6, {}), {2}: (7, {}), {3}: (8, {})} | custom-call | flops 5033164800 | bytes 9177088 | tf_op jit(solution)/shard_map/pallas_call | solution.py:91
  31.0 2.4 slice_add_fusion.25
  34.4 6.0 shard_map.163
  40.9 2.9 collective-permute-start.2
  46.9 5.8 shard_map.164
  52.6 6.3 collective-permute-done.2
  64.5 4.0 bitcast_add_fusion.2
  68.4 3.1 slice_add_fusion.2
  71.6 8.9 %shard_map.165 = (f32[3,1280,640]{2,1,0:T(8,128)}, f32[8,128]{1,0:T(8,128)}) custom-call(bf16[2048,1280]{1,0:T(8,128)(2,1)} %bitcast.359, bf16[2048,640]{1,0:T(8,128)(2,1)} %bitcast.361, f32[8,128]{1,0:T(8,128)} %get-tuple-element.170.refs_2_, bf16[256,640]{1,0:T(8,128)(2,1)} %get-tuple-element.346.refs_3_, bf16[256,640]{1,0:T(8,128)(2,1)} %get-tuple-element.345.refs_4_, ...), custom_call_target="tpu_custom_call" | custom-call | flops 3355443200 | bytes 17367040 | tf_op jit(solution)/shard_map/pallas_call | solution.py:354
  83.7 3.4 fusion.68
  89.3 17.7 %shard_map.166 = (bf16[8,256,1280]{2,1,0:T(8,128)(2,1)}, f32[8,256,640]{2,1,0:T(8,128)}, bf16[8,256,640]{2,1,0:T(8,128)(2,1)}, f32[8,256,640]{2,1,0:T(8,128)}, b...) custom-call(s32[1]{0:T(128)} %bitcast.rank_ref, f32[8,256,1280]{2,1,0:T(8,128)} %bitcast.368, ...), custom_call_target="tpu_custom_call" | custom-call | flops 6710886400 | bytes 20975616 | tf_op jit(solution)/shard_map/pallas_call | solution.py:91
  106.9 28.0 %collective-permute-done.9 = f32[2,256,640]{2,1,0:T(8,128)} collective-permute-done((f32[2,256,640]{2,1,0:T(8,128)}, f32[2,256,640]{2,1,0:T(8,128)}, u32[]{:S(2)}, u32[]{:S(2)}) %collective-permute-start.9) | collective-permute-done | bytes 1310752 | tf_op jit(solution)/shard_map/ppermute | solution.py:359
  139.9 2.5 collective-permute-start.12
  142.4 5.7 shard_map.167
  148.1 5.8 shard_map.168
  160.4 4.6 collective-permute-done.10
  165.0 3.7 collective-permute-done.14
  168.7 3.3 slice_add_fusion.1
  175.0 15.1 %shard_map.169 = (bf16[8,256,1280]{2,1,0:T(8,128)(2,1)}, bf16[160,2048]{1,0:T(8,128)(2,1)}, bf16[480,2048]{1,0:T(8,128)(2,1)}, bf16[4,256,640]{2,1,0:T(8,128)(2,...) custom-call(s32[1]{0:T(128)} %bitcast.rank_ref, bf16[3,480,1280]{2,1,0:T(8,128)(2,1)} %bitcast.325, ...), custom_call_target="tpu_custom_call" | custom-call | flops 3523215360 | bytes 5244928 | tf_op jit(solution)/shard_map/pallas_call | solution.py:91
  190.6 15.0 %shard_map.170 = (bf16[8,256,1280]{2,1,0:T(8,128)(2,1)}, bf16[160,2048]{1,0:T(8,128)(2,1)}, bf16[480,2048]{1,0:T(8,128)(2,1)}, bf16[4,256,640]{2,1,0:T(8,128)(2,...) custom-call(s32[1]{0:T(128)} %bitcast.rank_ref, ...), custom_call_target="tpu_custom_call", output_to_operand_aliasing={{0}: (5, {}), {1}: (6, {}), {2}: (7, {})} | custom-call | flops 3523215360 | bytes 5244928 | tf_op jit(solution)/shard_map/pallas_call | solution.py:91
  205.6 11.4 %collective-permute-done.13 = f32[2,256,640]{2,1,0:T(8,128)} collective-permute-done((f32[2,256,640]{2,1,0:T(8,128)S(1)}, f32[2,256,640]{2,1,0:T(8,128)}, u32[]{:S(2)}, u32[]{:S(2)}) %collective-permute-start.13) | collective-permute-done | bytes 1310752 | tf_op jit(solution)/shard_map/ppermute | solution.py:359
  224.6 2.6 slice_add_fusion.14
  227.2 2.5 slice_add_fusion.13
  229.7 14.1 %shard_map.171 = (bf16[160,2048]{1,0:T(8,128)(2,1)}, bf16[480,2048]{1,0:T(8,128)(2,1)}, bf16[4,256,640]{2,1,0:T(8,128)(2,1)}, bf16[4,256,640]{2,1,0:T(8,128)(2,1)}, f32[8,128]{1,0:T(8,128)}) custom-call(s32[1]{0:T(128)} %bitcast.rank_ref, bf16[3,480,1280]{2,1,0:T(8,128)(2,1)} %bitcast.327, bf16[8,256,1280]{2,1,0:T(8,128)(2,1)} %all-gather.11.cloned.1.call-done.refs_1_, ...), custom_call_target="tpu_custom_call" | custom-call | flops 3523215360 | bytes 2623488 | tf_op jit(solution)/shard_map/pallas_call | solution.py:91
  245.7 14.2 %shard_map.172 = (bf16[160,2048]{1,0:T(8,128)(2,1)}, bf16[480,2048]{1,0:T(8,128)(2,1)}, bf16[4,256,640]{2,1,0:T(8,128)(2,1)}, bf16[4,256,640]{2,1,0:T(8,128)(2,1)}, f32[8,128]{1,0:T(8,128)}) custom-call(s32[1]{0:T(128)} %bitcast.rank_ref, bf16[3,480,1280]{2,1,0:T(8,128)(2,1)} %bitcast.328, ...), custom_call_target="tpu_custom_call", output_to_operand_aliasing={{0}: (5, {}), {1}: (6, {})} | custom-call | flops 3523215360 | bytes 2623488 | tf_op jit(solution)/shard_map/pallas_call | solution.py:91
  263.5 2.7 multiply_reduce_fusion.1
  266.2 2.4 slice_add_fusion.12
  269.3 2.4 fusion.7
  274.7 3.0 collective-permute-done.23
  279.4 9.5 %shard_map.173 = (f32[3,480,1280]{2,1,0:T(8,128)}, f32[3,160,1280]{2,1,0:T(8,128)}, f32[8,128]{1,0:T(8,128)}) custom-call(bf16[480,2048]{1,0:T(8,128)(2,1)} %get-tuple-element.216.refs_0_, bf16[2048,1280]{1,0:T(8,128)(2,1)} %bitcast.355, bf16[160,2048]{1,0:T(8,128)(2,1)} %get-tuple-element.218.refs_2_, bf16[2048,1280]{1,0:T(8,128)(2,1)} %bitcast.323, ...), custom_call_target="tpu_custom_call" | custom-call | flops 3355443200 | bytes 27852800 | tf_op jit(solution)/shard_map/pallas_call | solution.py:354
  295.4 9.7 %shard_map.174 = (f32[3,480,1280]{2,1,0:T(8,128)}, f32[3,160,1280]{2,1,0:T(8,128)}, f32[8,128]{1,0:T(8,128)}) custom-call(bf16[480,2048]{1,0:T(8,128)(2,1)} %get-tuple-element.228.refs_0_, bf16[2048,1280]{1,0:T(8,128)(2,1)} %bitcast.342, bf16[160,2048]{1,0:T(8,128)(2,1)} %get-tuple-element.229.refs_2_, ...), custom_call_target="tpu_custom_call", output_to_operand_aliasing={{0}: (4, {}), {1}: (5, {})} | custom-call | flops 3355443200 | bytes 27852800 | tf_op jit(solution)/shard_map/pallas_call | solution.py:354
  308.0 2.6 fusion.66
  313.6 6.0 collective-permute-done.30
  319.6 3.0 collective-permute-done.31
  326.4 3.1 fusion.65
  329.6 2.4 collective-permute-start.27
  332.0 8.8 %shard_map.175 = (f32[3,640,1280]{2,1,0:T(8,128)}, f32[8,128]{1,0:T(8,128)}) custom-call(bf16[2048,640]{1,0:T(8,128)(2,1)} %bitcast.349, bf16[2048,1280]{1,0:T(8,128)(2,1)} %bitcast.360, f32[8,128]{1,0:T(8,128)} %get-tuple-element.232.refs_2_, bf16[1,256,1280]{2,1,0:T(8,128)(2,1)} %get-tuple-element.238.refs_3_), custom_call_target="tpu_custom_call" | custom-call | flops 3355443200 | bytes 17367040 | tf_op jit(solution)/shard_map/pallas_call | solution.py:354
  340.8 30.0 %collective-permute-done.27.refs_4_.refs_2_ = f32[256,1280]{1,0:T(8,128)S(1)} collective-permute-done((f32[256,1280]{1,0:T(8,128)S(1)}, f32[256,1280]{1,0:T(8,128)S(1)}, u32[]{:S(2)}, u32[]{:S(2)}) %collective-permute-start.27) | collective-permute-done | bytes 1310752 | tf_op jit(solution)/shard_map/ppermute | solution.py:359
  376.3 10.7 %shard_map.176 = (bf16[8,256,640]{2,1,0:T(8,128)(2,1)}, f32[8,128]{1,0:T(8,128)}) custom-call(s32[1]{0:T(128)} %bitcast.rank_ref, bf16[8,256,1280]{2,1,0:T(8,128)(2,1)} %all-gather.13.cloned.1.call-done.refs_0_, bf16[3,640,1280]{2,1,0:T(8,128)(2,1)} %refs_1_.19, f32[8,256,640]{2,1,0:T(8,128)} %get-tuple-element.243.refs_2_, ...), custom_call_target="tpu_custom_call" | custom-call | flops 3355443200 | bytes 2625536 | tf_op jit(solution)/shard_map/pallas_call | solution.py:91
  387.0 5.4 collective-permute-done.36.refs_7_
  392.4 4.5 collective-permute-done.35.refs_6_
  399.4 9.2 %shard_map.177 = (f32[8,256,1280]{2,1,0:T(8,128)}, f32[8,128]{1,0:T(8,128)}) custom-call(s32[1]{0:T(128)} %bitcast.rank_ref, f32[256,1280]{1,0:T(8,128)} %bitcast.344, f32[256,1280]{1,0:T(8,128)} %collective-permute-done.26.refs_1_, f32[256,1280]{1,0:T(8,128)} %copy-done.2, f32[256,1280]{1,0:T(8,128)} %collective-permute-done.32.refs_3_, ...), custom_call_target="tpu_custom_call" | custom-call | flops 2000000000 | bytes 20971520 | tf_op jit(solution)/shard_map/pallas_call | solution.py:290
  408.6 15.0 %shard_map.178 = (bf16[8,256,1280]{2,1,0:T(8,128)(2,1)}, bf16[160,2048]{1,0:T(8,128)(2,1)}, bf16[480,2048]{1,0:T(8,128)(2,1)}, f32[8,128]{1,0:T(8,128)}) custom-call(s32[1]{0:T(128)} %bitcast.rank_ref, bf16[3,480,1280]{2,1,0:T(8,128)(2,1)} %bitcast.329, f32[8,256,1280]{2,1,0:T(8,128)} %get-tuple-element.356.refs_1_, f32[8,128]{1,0:T(8,128)} %get-tuple-element.248.refs_2_), custom_call_target="tpu_custom_call" | custom-call | flops 2852126720 | bytes 7868416 | tf_op jit(solution)/shard_map/pallas_call | solution.py:91
  423.6 12.2 %shard_map.179 = (bf16[8,256,640]{2,1,0:T(8,128)(2,1)}, bf16[4,256,640]{2,1,0:T(8,128)(2,1)}, bf16[4,256,640]{2,1,0:T(8,128)(2,1)}, f32[8,128]{1,0:T(8,128)}) custom-call(s32[1]{0:T(128)} %bitcast.rank_ref, bf16[8,256,1280]{2,1,0:T(8,128)(2,1)} %all-gather.17.cloned.1.call-done.refs_0_, bf16[3,640,1280]{2,1,0:T(8,128)(2,1)} %refs_1_.19, ...), custom_call_target="tpu_custom_call" | custom-call | flops 5033164800 | bytes 2623488 | tf_op jit(solution)/shard_map/pallas_call | solution.py:91
  436.3 12.1 %shard_map.180 = (bf16[8,256,640]{2,1,0:T(8,128)(2,1)}, bf16[4,256,640]{2,1,0:T(8,128)(2,1)}, bf16[4,256,640]{2,1,0:T(8,128)(2,1)}, f32[8,128]{1,0:T(8,128)}) custom-call(s32[1]{0:T(128)} %bitcast.rank_ref, bf16[8,256,1280]{2,1,0:T(8,128)(2,1)} %all-gather.17.cloned.1.call-done.refs_0_, ...), custom_call_target="tpu_custom_call", output_to_operand_aliasing={{0}: (7, {})} | custom-call | flops 5033164800 | bytes 2623488 | tf_op jit(solution)/shard_map/pallas_call | solution.py:91
  454.1 8.9 %shard_map.181 = (f32[3,1280,640]{2,1,0:T(8,128)}, f32[8,128]{1,0:T(8,128)}) custom-call(bf16[2048,1280]{1,0:T(8,128)(2,1)} %bitcast.352, bf16[2048,640]{1,0:T(8,128)(2,1)} %bitcast.356, f32[3,1280,640]{2,1,0:T(8,128)} %get-tuple-element.260.refs_2_, f32[8,128]{1,0:T(8,128)} %get-tuple-element.261.refs_3_, ...), custom_call_target="tpu_custom_call", output_to_operand_aliasing={{0}: (2, {})} | custom-call | flops 3355443200 | bytes 17367040 | tf_op jit(solution)/shard_map/pallas_call | solution.py:354
  463.1 5.2 collective-permute-done.40
  470.3 8.0 %collective-permute-done.42 = bf16[256,640]{1,0:T(8,128)(2,1)S(1)} collective-permute-done((bf16[256,640]{1,0:T(8,128)(2,1)S(1)}, bf16[256,640]{1,0:T(8,128)(2,1)S(1)}, u32[]{:S(2)}, u32[]{:S(2)}) %collective-permute-start.42) | collective-permute-done | bytes 327712 | tf_op jit(solution)/shard_map/ppermute | solution.py:359
  481.2 2.9 fusion.64
  488.0 49.2 %all-gather.19.cloned.1.call-done.refs_3_ = bf16[8,256,1280]{2,1,0:T(8,128)(2,1)} async-done(((bf16[1,256,1280]{2,1,0:T(8,128)(2,1)}), bf16[8,256,1280]{2,1,0:T(8,128)(2,1)}) %all-gather.19.cloned.1.call-update) | async-done | bytes 5242896 | tf_op jit(solution)/shard_map/all_gather | solution.py:401
  537.3 9.1 %shard_map.182 = (f32[3,640,1280]{2,1,0:T(8,128)}, f32[8,128]{1,0:T(8,128)}) custom-call(bf16[2048,640]{1,0:T(8,128)(2,1)} %bitcast.351, bf16[2048,1280]{1,0:T(8,128)(2,1)} %bitcast.341, f32[3,640,1280]{2,1,0:T(8,128)} %get-tuple-element.271.refs_2_, f32[8,128]{1,0:T(8,128)} %get-tuple-element.264.refs_3_, ...), custom_call_target="tpu_custom_call", output_to_operand_aliasing={{0}: (2, {})} | custom-call | flops 3355443200 | bytes 17367040 | tf_op jit(solution)/shard_map/pallas_call | solution.py:354
  546.4 8.9 %shard_map.183 = (f32[3,1280,640]{2,1,0:T(8,128)}, f32[8,128]{1,0:T(8,128)}) custom-call(bf16[2048,1280]{1,0:T(8,128)(2,1)} %bitcast.353, bf16[2048,640]{1,0:T(8,128)(2,1)} %bitcast.350, f32[3,1280,640]{2,1,0:T(8,128)} %get-tuple-element.273.refs_2_, f32[8,128]{1,0:T(8,128)} %get-tuple-element.274.refs_3_), custom_call_target="tpu_custom_call", output_to_operand_aliasing={{0}: (2, {})} | custom-call | flops 3355443200 | bytes 17367040 | tf_op jit(solution)/shard_map/pallas_call | solution.py:354
  555.3 8.8 %shard_map.184 = (f32[3,640,1280]{2,1,0:T(8,128)}, f32[8,128]{1,0:T(8,128)}) custom-call(bf16[2048,640]{1,0:T(8,128)(2,1)} %bitcast.362, bf16[2048,1280]{1,0:T(8,128)(2,1)} %bitcast.354, f32[3,640,1280]{2,1,0:T(8,128)} %get-tuple-element.272.refs_2_, f32[8,128]{1,0:T(8,128)} %get-tuple-element.275.refs_3_), custom_call_target="tpu_custom_call", output_to_operand_aliasing={{0}: (2, {})} | custom-call | flops 3355443200 | bytes 17367040 | tf_op jit(solution)/shard_map/pallas_call | solution.py:354
  565.6 11.1 %shard_map.185 = (bf16[480,2048]{1,0:T(8,128)(2,1)}, bf16[4,256,640]{2,1,0:T(8,128)(2,1)}, bf16[4,256,640]{2,1,0:T(8,128)(2,1)}, f32[8,128]{1,0:T(8,128)}) custom-call(s32[1]{0:T(128)} %bitcast.rank_ref, bf16[3,480,1280]{2,1,0:T(8,128)(2,1)} %bitcast.330, bf16[480,2048]{1,0:T(8,128)(2,1)} %get-tuple-element.269.refs_1_, bf16[3,160,1280]{2,1,0:T(8,128)(2,1)} %bitcast.338, ...), custom_call_target="tpu_custom_call" | custom-call | flops 2097152000 | bytes 2295808 | tf_op jit(solution)/shard_map/pallas_call | solution.py:91
  577.2 11.1 %shard_map.186 = (bf16[480,2048]{1,0:T(8,128)(2,1)}, bf16[4,256,640]{2,1,0:T(8,128)(2,1)}, bf16[4,256,640]{2,1,0:T(8,128)(2,1)}, f32[8,128]{1,0:T(8,128)}) custom-call(s32[1]{0:T(128)} %bitcast.rank_ref, bf16[3,480,1280]{2,1,0:T(8,128)(2,1)} %bitcast.331, bf16[480,2048]{1,0:T(8,128)(2,1)} %get-tuple-element.269.refs_1_, ...), custom_call_target="tpu_custom_call", output_to_operand_aliasing={{0}: (5, {})} | custom-call | flops 2097152000 | bytes 2295808 | tf_op jit(solution)/shard_map/pallas_call | solution.py:91
  593.9 10.0 %shard_map.187 = (f32[3,480,1280]{2,1,0:T(8,128)}, f32[3,160,1280]{2,1,0:T(8,128)}, f32[8,128]{1,0:T(8,128)}) custom-call(bf16[480,2048]{1,0:T(8,128)(2,1)} %get-tuple-element.280.refs_0_, bf16[2048,1280]{1,0:T(8,128)(2,1)} %bitcast.358, bf16[160,2048]{1,0:T(8,128)(2,1)} %get-tuple-element.249.refs_2_, ...), custom_call_target="tpu_custom_call", output_to_operand_aliasing={{0}: (4, {}), {1}: (5, {})} | custom-call | flops 3355443200 | bytes 27852800 | tf_op jit(solution)/shard_map/pallas_call | solution.py:354
  603.9 13.2 %collective-permute-done.49 = bf16[2,256,640]{2,1,0:T(8,128)(2,1)} collective-permute-done((bf16[2,256,640]{2,1,0:T(8,128)(2,1)S(1)}, bf16[2,256,640]{2,1,0:T(8,128)(2,1)}, u32[]{:S(2)}, u32[]{:S(2)}) %collective-permute-start.49) | collective-permute-done | bytes 655392 | tf_op jit(solution)/shard_map/ppermute | solution.py:359
  620.5 6.6 collective-permute-done.51
  635.3 21.4 %collective-permute-done.57.refs_7_ = f32[256,640]{1,0:T(8,128)S(1)} collective-permute-done((f32[256,640]{1,0:T(8,128)S(1)}, f32[256,640]{1,0:T(8,128)S(1)}, u32[]{:S(2)}, u32[]{:S(2)}) %collective-permute-start.57) | collective-permute-done | bytes 655392 | tf_op jit(solution)/shard_map/ppermute | solution.py:359
  658.9 16.4 %shard_map.188 = (f32[8,256,1280]{2,1,0:T(8,128)}, f32[8,128]{1,0:T(8,128)}) custom-call(s32[1]{0:T(128)} %bitcast.rank_ref, f32[8,256,1280]{2,1,0:T(8,128)} %bitcast.369, bf16[1280,2048]{1,0:T(8,128)(2,1)} %all-gather.15.cloned.1.call-done.refs_1_, bf16[1280,1280]{1,0:T(8,128)(2,1)} %all-gather.21.cloned.1.call-done.refs_2_, ...), custom_call_target="tpu_custom_call" | custom-call | flops 6710886400 | bytes 10489856 | tf_op jit(solution)/shard_map/pallas_call | solution.py:91
  675.3 9.3 %shard_map.189 = (f32[8,256,1280]{2,1,0:T(8,128)}, f32[8,128]{1,0:T(8,128)}) custom-call(s32[1]{0:T(128)} %bitcast.rank_ref, f32[256,1280]{1,0:T(8,128)} %bitcast.89.refs_0_, f32[256,1280]{1,0:T(8,128)} %collective-permute-done.53.refs_1_, f32[256,1280]{1,0:T(8,128)} %copy-done.3, f32[256,1280]{1,0:T(8,128)} %collective-permute-done.54.refs_3_, ...), custom_call_target="tpu_custom_call" | custom-call | flops 2000000000 | bytes 20971520 | tf_op jit(solution)/shard_map/pallas_call | solution.py:290
  684.6 14.3 %all-gather.23.cloned.1.call-done = f32[8,256,1280]{2,1,0:T(8,128)} async-done(((f32[1,256,1280]{2,1,0:T(8,128)}), f32[8,256,1280]{2,1,0:T(8,128)}) %all-gather.23.cloned.1.call-update) | async-done | bytes 10485776 | tf_op jit(solution)/shard_map/all_gather | solution.py:401
  698.9 8.8 %copy.57 = f32[8,256,1280]{2,1,0:T(8,128)} copy(f32[8,256,1280]{2,1,0:T(8,128)} %all-gather.23.cloned.1.call-done) | data formatting | bytes 20971520
  (281 shorter events, 109.7 us)
Async XLA Ops:
  7.2 167.8 %all-gather.9.cloned.1.call-start = ((), (), s32[]{:S(2)}) async-start(), calls=%async_computation | async-start | bytes 5898240 | tf_op jit(solution)/shard_map/all_gather | solution.py:401
  18.8 12.2 %collective-permute-start = (bf16[4,256,640]{2,1,0:T(8,128)(2,1)}, bf16[4,256,640]{2,1,0:T(8,128)(2,1)S(1)}, u32[]{:S(2)}, u32[]{:S(2)}) collective-permute-start(bf16[4,256,640]{2,1,0:T(8,128)(2,1)} %get-tuple-element.166), channel_id=1, source_target_pairs={{0,1},{1,0},{2,3},{3,2},{4,5},{5,4},{6,7},{7,6},{8,9},{9,8},{10,11... | collective-permute-start | bytes 3932168 | tf_op jit(solution)/shard_map/ppermute | solution.py:359
  19.5 13.9 %collective-permute-start.1 = (bf16[4,256,640]{2,1,0:T(8,128)(2,1)}, bf16[4,256,640]{2,1,0:T(8,128)(2,1)S(1)}, u32[]{:S(2)}, u32[]{:S(2)}) collective-permute-start(bf16[4,256,640]{2,1,0:T(8,128)(2,1)} %get-tuple-element.168), channel_id=1, source_target_pairs={{0,1},{1,0},{2,3},{3,2},{4,5},{5,4},{6,7},{7,6},{8,9},{9,8},{10,11... | collective-permute-start | bytes 3932168 | tf_op jit(solution)/shard_map/ppermute | solution.py:359
  40.4 24.0 %collective-permute-start.5 = (f32[4,256,640]{2,1,0:T(8,128)}, f32[4,256,640]{2,1,0:T(8,128)}, u32[]{:S(2)}, u32[]{:S(2)}) collective-permute-start(f32[4,256,640]{2,1,0:T(8,128)} %get-tuple-element.177), channel_id=1, source_target_pairs={{0,1},{1,0},{2,3},{3,2},{4,5},{5,4},{6,7},{7,6},{8,9},{9,8},{10,11... | collective-permute-start | bytes 7864328 | tf_op jit(solution)/shard_map/ppermute | solution.py:359
  40.9 23.6 %collective-permute-start.4 = (f32[4,256,640]{2,1,0:T(8,128)}, f32[4,256,640]{2,1,0:T(8,128)}, u32[]{:S(2)}, u32[]{:S(2)}) collective-permute-start(f32[4,256,640]{2,1,0:T(8,128)} %get-tuple-element.174), channel_id=1, source_target_pairs={{0,1},{1,0},{2,3},{3,2},{4,5},{5,4},{6,7},{7,6},{8,9},{9,8},{10,11... | collective-permute-start | bytes 7864328 | tf_op jit(solution)/shard_map/ppermute | solution.py:359
  40.9 18.0 %collective-permute-start.2 = (bf16[2,256,640]{2,1,0:T(8,128)(2,1)S(1)}, bf16[2,256,640]{2,1,0:T(8,128)(2,1)}, u32[]{:S(2)}, u32[]{:S(2)}) collective-permute-start(bf16[2,256,640]{2,1,0:T(8,128)(2,1)S(1)} %copy-done.15), channel_id=1, source_target_pairs={{0,2},{1,3},{2,0},{3,1},{4,6},{5,7},{6,4},{7,5},{8,10},{9,11},{10,... | collective-permute-start | bytes 1966088 | tf_op jit(solution)/shard_map/ppermute | solution.py:359
  43.9 16.4 %collective-permute-start.3 = (bf16[2,256,640]{2,1,0:T(8,128)(2,1)S(1)}, bf16[2,256,640]{2,1,0:T(8,128)(2,1)S(1)}, u32[]{:S(2)}, u32[]{:S(2)}) collective-permute-start(bf16[2,256,640]{2,1,0:T(8,128)(2,1)S(1)} %copy-done.16), channel_id=1, source_target_pairs={{0,4},{1,5},{2,6},{3,7},{4,0},{5,1},{6,2},{7,3},{8,12},{9,13},{10,... | collective-permute-start | bytes 1966088 | tf_op jit(solution)/shard_map/ppermute | solution.py:359
  62.4 18.1 %collective-permute-start.6 = (bf16[256,640]{1,0:T(8,128)(2,1)}, bf16[256,640]{1,0:T(8,128)(2,1)}, u32[]{:S(2)}, u32[]{:S(2)}) collective-permute-start(bf16[256,640]{1,0:T(8,128)(2,1)} %get-tuple-element.346.refs_3_), channel_id=1, source_target_pairs={{0,4},{1,5},{2,6},{3,7},{4,0},{5,1},{6,2},{7,3},{8,12},{9,13},{10,... | collective-permute-start | bytes 983048 | tf_op jit(solution)/shard_map/ppermute | solution.py:359
  63.9 17.9 %collective-permute-start.7 = (bf16[256,640]{1,0:T(8,128)(2,1)}, bf16[256,640]{1,0:T(8,128)(2,1)S(1)}, u32[]{:S(2)}, u32[]{:S(2)}) collective-permute-start(bf16[256,640]{1,0:T(8,128)(2,1)} %get-tuple-element.345.refs_4_), channel_id=1, source_target_pairs={{0,2},{1,3},{2,0},{3,1},{4,6},{5,7},{6,4},{7,5},{8,10},{9,11},{10,... | collective-permute-start | bytes 983048 | tf_op jit(solution)/shard_map/ppermute | solution.py:359
  87.2 142.5 %all-gather.11.cloned.1.call-start = ((), (), s32[]{:S(2)}) async-start(), calls=%async_computation.1 | async-start | bytes 5898240 | tf_op jit(solution)/shard_map/all_gather | solution.py:401
  87.2 47.7 %collective-permute-start.9 = (f32[2,256,640]{2,1,0:T(8,128)}, f32[2,256,640]{2,1,0:T(8,128)}, u32[]{:S(2)}, u32[]{:S(2)}) collective-permute-start(f32[2,256,640]{2,1,0:T(8,128)} %get-tuple-element.322.refs_6_), channel_id=1, source_target_pairs={{0,4},{1,5},{2,6},{3,7},{4,0},{5,1},{6,2},{7,3},{8,12},{9,13},{10,... | collective-permute-start | bytes 3932168 | tf_op jit(solution)/shard_map/ppermute | solution.py:359
  87.7 47.3 %collective-permute-start.8 = (f32[2,256,640]{2,1,0:T(8,128)}, f32[2,256,640]{2,1,0:T(8,128)}, u32[]{:S(2)}, u32[]{:S(2)}) collective-permute-start(f32[2,256,640]{2,1,0:T(8,128)} %get-tuple-element.324.refs_5_), channel_id=1, source_target_pairs={{0,2},{1,3},{2,0},{3,1},{4,6},{5,7},{6,4},{7,5},{8,10},{9,11},{10,... | collective-permute-start | bytes 3932168 | tf_op jit(solution)/shard_map/ppermute | solution.py:359
  136.2 17.8 %collective-permute-start.11 = (f32[256,640]{1,0:T(8,128)S(1)}, f32[256,640]{1,0:T(8,128)}, u32[]{:S(2)}, u32[]{:S(2)}) collective-permute-start(f32[256,640]{1,0:T(8,128)S(1)} %fusion.26.refs_3_), channel_id=1, source_target_pairs={{0,4},{1,5},{2,6},{3,7},{4,0},{5,1},{6,2},{7,3},{8,12},{9,13},{10,... | collective-permute-start | bytes 1966088 | tf_op jit(solution)/shard_map/ppermute | solution.py:359
  139.9 14.0 %collective-permute-start.12 = (f32[256,640]{1,0:T(8,128)}, f32[256,640]{1,0:T(8,128)}, u32[]{:S(2)}, u32[]{:S(2)}) collective-permute-start(f32[256,640]{1,0:T(8,128)} %fusion.24.refs_4_), channel_id=1, source_target_pairs={{0,2},{1,3},{2,0},{3,1},{4,6},{5,7},{6,4},{7,5},{8,10},{9,11},{10,... | collective-permute-start | bytes 1966088 | tf_op jit(solution)/shard_map/ppermute | solution.py:359
  159.3 216.9 %all-gather.13.cloned.1.call-start = ((), (), s32[]{:S(2)}) async-start(), calls=%async_computation.2 | async-start | bytes 5898240 | tf_op jit(solution)/shard_map/all_gather | solution.py:401
  172.1 45.0 %collective-permute-start.13 = (f32[2,256,640]{2,1,0:T(8,128)S(1)}, f32[2,256,640]{2,1,0:T(8,128)}, u32[]{:S(2)}, u32[]{:S(2)}) collective-permute-start(f32[2,256,640]{2,1,0:T(8,128)S(1)} %get-tuple-element.318.refs_5_), channel_id=1, source_target_pairs={{0,2},{1,3},{2,0},{3,1},{4,6},{5,7},{6,4},{7,5},{8,10},{9,11},{10,... | collective-permute-start | bytes 3932168 | tf_op jit(solution)/shard_map/ppermute | solution.py:359
  174.0 45.2 %collective-permute-start.18 = (f32[2,256,640]{2,1,0:T(8,128)}, f32[2,256,640]{2,1,0:T(8,128)}, u32[]{:S(2)}, u32[]{:S(2)}) collective-permute-start(f32[2,256,640]{2,1,0:T(8,128)} %get-tuple-element.319.refs_6_), channel_id=1, source_target_pairs={{0,4},{1,5},{2,6},{3,7},{4,0},{5,1},{6,2},{7,3},{8,12},{9,13},{10,... | collective-permute-start | bytes 3932168 | tf_op jit(solution)/shard_map/ppermute | solution.py:359
  190.1 34.5 %collective-permute-start.16 = (bf16[4,256,640]{2,1,0:T(8,128)(2,1)}, bf16[4,256,640]{2,1,0:T(8,128)(2,1)}, u32[]{:S(2)}, u32[]{:S(2)}) collective-permute-start(bf16[4,256,640]{2,1,0:T(8,128)(2,1)} %get-tuple-element.204), channel_id=1, source_target_pairs={{0,1},{1,0},{2,3},{3,2},{4,5},{5,4},{6,7},{7,6},{8,9},{9,8},{10,11... | collective-permute-start | bytes 3932168 | tf_op jit(solution)/shard_map/ppermute | solution.py:359
  190.1 37.1 %collective-permute-start.17 = (bf16[4,256,640]{2,1,0:T(8,128)(2,1)}, bf16[4,256,640]{2,1,0:T(8,128)(2,1)}, u32[]{:S(2)}, u32[]{:S(2)}) collective-permute-start(bf16[4,256,640]{2,1,0:T(8,128)(2,1)} %get-tuple-element.206), channel_id=1, source_target_pairs={{0,1},{1,0},{2,3},{3,2},{4,5},{5,4},{6,7},{7,6},{8,9},{9,8},{10,11... | collective-permute-start | bytes 3932168 | tf_op jit(solution)/shard_map/ppermute | solution.py:359
  221.4 38.5 %collective-permute-start.15 = (f32[256,640]{1,0:T(8,128)}, f32[256,640]{1,0:T(8,128)}, u32[]{:S(2)}, u32[]{:S(2)}) collective-permute-start(f32[256,640]{1,0:T(8,128)} %fusion.14.refs_7_), channel_id=1, source_target_pairs={{0,4},{1,5},{2,6},{3,7},{4,0},{5,1},{6,2},{7,3},{8,12},{9,13},{10,... | collective-permute-start | bytes 1966088 | tf_op jit(solution)/shard_map/ppermute | solution.py:359
  223.3 37.1 %collective-permute-start.19 = (f32[256,640]{1,0:T(8,128)S(1)}, f32[256,640]{1,0:T(8,128)}, u32[]{:S(2)}, u32[]{:S(2)}) collective-permute-start(f32[256,640]{1,0:T(8,128)S(1)} %fusion.11.refs_8_), channel_id=1, source_target_pairs={{0,2},{1,3},{2,0},{3,1},{4,6},{5,7},{6,4},{7,5},{8,10},{9,11},{10,... | collective-permute-start | bytes 1966088 | tf_op jit(solution)/shard_map/ppermute | solution.py:359
  243.8 22.3 %collective-permute-start.22 = (bf16[4,256,640]{2,1,0:T(8,128)(2,1)}, bf16[4,256,640]{2,1,0:T(8,128)(2,1)}, u32[]{:S(2)}, u32[]{:S(2)}) collective-permute-start(bf16[4,256,640]{2,1,0:T(8,128)(2,1)} %get-tuple-element.220), channel_id=1, source_target_pairs={{0,1},{1,0},{2,3},{3,2},{4,5},{5,4},{6,7},{7,6},{8,9},{9,8},{10,11... | collective-permute-start | bytes 3932168 | tf_op jit(solution)/shard_map/ppermute | solution.py:359
  243.8 29.2 %collective-permute-start.24 = (bf16[2,256,640]{2,1,0:T(8,128)(2,1)}, bf16[2,256,640]{2,1,0:T(8,128)(2,1)}, u32[]{:S(2)}, u32[]{:S(2)}) collective-permute-start(bf16[2,256,640]{2,1,0:T(8,128)(2,1)} %get-tuple-element.336.refs_6_), channel_id=1, source_target_pairs={{0,4},{1,5},{2,6},{3,7},{4,0},{5,1},{6,2},{7,3},{8,12},{9,13},{10,... | collective-permute-start | bytes 1966088 | tf_op jit(solution)/shard_map/ppermute | solution.py:359
  245.5 23.8 %collective-permute-start.20 = (bf16[4,256,640]{2,1,0:T(8,128)(2,1)}, bf16[4,256,640]{2,1,0:T(8,128)(2,1)}, u32[]{:S(2)}, u32[]{:S(2)}) collective-permute-start(bf16[4,256,640]{2,1,0:T(8,128)(2,1)} %get-tuple-element.215), channel_id=1, source_target_pairs={{0,1},{1,0},{2,3},{3,2},{4,5},{5,4},{6,7},{7,6},{8,9},{9,8},{10,11... | collective-permute-start | bytes 3932168 | tf_op jit(solution)/shard_map/ppermute | solution.py:359
  259.9 17.9 %collective-permute-start.23 = (bf16[2,256,640]{2,1,0:T(8,128)(2,1)}, bf16[2,256,640]{2,1,0:T(8,128)(2,1)S(1)}, u32[]{:S(2)}, u32[]{:S(2)}) collective-permute-start(bf16[2,256,640]{2,1,0:T(8,128)(2,1)} %get-tuple-element.338.refs_5_), channel_id=1, source_target_pairs={{0,2},{1,3},{2,0},{3,1},{4,6},{5,7},{6,4},{7,5},{8,10},{9,11},{10,... | collective-permute-start | bytes 1966088 | tf_op jit(solution)/shard_map/ppermute | solution.py:359
  268.6 20.3 %collective-permute-start.25 = (bf16[2,256,640]{2,1,0:T(8,128)(2,1)S(1)}, bf16[2,256,640]{2,1,0:T(8,128)(2,1)}, u32[]{:S(2)}, u32[]{:S(2)}) collective-permute-start(bf16[2,256,640]{2,1,0:T(8,128)(2,1)S(1)} %get-tuple-element.334.refs_6_), channel_id=1, source_target_pairs={{0,4},{1,5},{2,6},{3,7},{4,0},{5,1},{6,2},{7,3},{8,12},{9,13},{10,... | collective-permute-start | bytes 1966088 | tf_op jit(solution)/shard_map/ppermute | solution.py:359
  271.7 19.5 %collective-permute-start.21 = (bf16[2,256,640]{2,1,0:T(8,128)(2,1)S(1)}, bf16[2,256,640]{2,1,0:T(8,128)(2,1)}, u32[]{:S(2)}, u32[]{:S(2)}) collective-permute-start(bf16[2,256,640]{2,1,0:T(8,128)(2,1)S(1)} %get-tuple-element.339.refs_5_), channel_id=1, source_target_pairs={{0,2},{1,3},{2,0},{3,1},{4,6},{5,7},{6,4},{7,5},{8,10},{9,11},{10,... | collective-permute-start | bytes 1966088 | tf_op jit(solution)/shard_map/ppermute | solution.py:359
  293.1 12.1 %collective-permute-start.28 = (bf16[256,640]{1,0:T(8,128)(2,1)}, bf16[256,640]{1,0:T(8,128)(2,1)}, u32[]{:S(2)}, u32[]{:S(2)}) collective-permute-start(bf16[256,640]{1,0:T(8,128)(2,1)} %fusion.57.refs_7_), channel_id=1, source_target_pairs={{0,4},{1,5},{2,6},{3,7},{4,0},{5,1},{6,2},{7,3},{8,12},{9,13},{10,... | collective-permute-start | bytes 983048 | tf_op jit(solution)/shard_map/ppermute | solution.py:359
  294.6 11.8 %collective-permute-start.29 = (bf16[256,640]{1,0:T(8,128)(2,1)S(1)}, bf16[256,640]{1,0:T(8,128)(2,1)}, u32[]{:S(2)}, u32[]{:S(2)}) collective-permute-start(bf16[256,640]{1,0:T(8,128)(2,1)S(1)} %fusion.52.refs_8_), channel_id=1, source_target_pairs={{0,2},{1,3},{2,0},{3,1},{4,6},{5,7},{6,4},{7,5},{8,10},{9,11},{10,... | collective-permute-start | bytes 983048 | tf_op jit(solution)/shard_map/ppermute | solution.py:359
  310.6 113.0 %all-gather.17.cloned.1.call-start = ((), (), s32[]{:S(2)}) async-start(), calls=%async_computation.4 | async-start | bytes 5898240 | tf_op jit(solution)/shard_map/all_gather | solution.py:401
  310.6 8.9 %collective-permute-start.30 = (bf16[256,640]{1,0:T(8,128)(2,1)}, bf16[256,640]{1,0:T(8,128)(2,1)S(1)}, u32[]{:S(2)}, u32[]{:S(2)}) collective-permute-start(bf16[256,640]{1,0:T(8,128)(2,1)} %fusion.55.refs_7_), channel_id=1, source_target_pairs={{0,4},{1,5},{2,6},{3,7},{4,0},{5,1},{6,2},{7,3},{8,12},{9,13},{10,... | collective-permute-start | bytes 983048 | tf_op jit(solution)/shard_map/ppermute | solution.py:359
  312.2 10.4 %collective-permute-start.31 = (bf16[256,640]{1,0:T(8,128)(2,1)}, bf16[256,640]{1,0:T(8,128)(2,1)S(1)}, u32[]{:S(2)}, u32[]{:S(2)}) collective-permute-start(bf16[256,640]{1,0:T(8,128)(2,1)} %fusion.53.refs_8_), channel_id=1, source_target_pairs={{0,2},{1,3},{2,0},{3,1},{4,6},{5,7},{6,4},{7,5},{8,10},{9,11},{10,... | collective-permute-start | bytes 983048 | tf_op jit(solution)/shard_map/ppermute | solution.py:359
  329.5 207.7 %all-gather.19.cloned.1.call-start = ((), (), s32[]{:S(2)}) async-start(), calls=%async_computation.5 | async-start | bytes 5898240 | tf_op jit(solution)/shard_map/all_gather | solution.py:401
  329.6 41.2 %collective-permute-start.27 = (f32[256,1280]{1,0:T(8,128)S(1)}, f32[256,1280]{1,0:T(8,128)S(1)}, u32[]{:S(2)}, u32[]{:S(2)}) collective-permute-start(f32[256,1280]{1,0:T(8,128)S(1)} %bitcast.345), channel_id=1, source_target_pairs={{0,2},{1,3},{2,0},{3,1},{4,6},{5,7},{6,4},{7,5},{8,10},{9,11},{10,... | collective-permute-start | bytes 3932168 | tf_op jit(solution)/shard_map/ppermute | solution.py:359
  332.0 40.4 %collective-permute-start.33 = (f32[256,1280]{1,0:T(8,128)S(1)}, f32[256,1280]{1,0:T(8,128)}, u32[]{:S(2)}, u32[]{:S(2)}) collective-permute-start(f32[256,1280]{1,0:T(8,128)S(1)} %bitcast.346), channel_id=1, source_target_pairs={{0,4},{1,5},{2,6},{3,7},{4,0},{5,1},{6,2},{7,3},{8,12},{9,13},{10,... | collective-permute-start | bytes 3932168 | tf_op jit(solution)/shard_map/ppermute | solution.py:359
  332.0 64.8 %collective-permute-start.26 = (f32[256,1280]{1,0:T(8,128)S(1)}, f32[256,1280]{1,0:T(8,128)}, u32[]{:S(2)}, u32[]{:S(2)}) collective-permute-start(f32[256,1280]{1,0:T(8,128)S(1)} %bitcast.347), channel_id=1, source_target_pairs={{0,1},{1,0},{2,3},{3,2},{4,5},{5,4},{6,7},{7,6},{8,9},{9,8},{10,11... | collective-permute-start | bytes 3932168 | tf_op jit(solution)/shard_map/ppermute | solution.py:359
  371.7 20.6 %collective-permute-start.36 = (f32[256,640]{1,0:T(8,128)}, f32[256,640]{1,0:T(8,128)S(1)}, u32[]{:S(2)}, u32[]{:S(2)}) collective-permute-start(f32[256,640]{1,0:T(8,128)} %slice.509), channel_id=1, source_target_pairs={{0,4},{1,5},{2,6},{3,7},{4,0},{5,1},{6,2},{7,3},{8,12},{9,13},{10,... | collective-permute-start | bytes 1966088 | tf_op jit(solution)/shard_map/ppermute | solution.py:359
  374.4 22.4 %collective-permute-start.35 = (f32[256,640]{1,0:T(8,128)}, f32[256,640]{1,0:T(8,128)}, u32[]{:S(2)}, u32[]{:S(2)}) collective-permute-start(f32[256,640]{1,0:T(8,128)} %slice.508), channel_id=1, source_target_pairs={{0,2},{1,3},{2,0},{3,1},{4,6},{5,7},{6,4},{7,5},{8,10},{9,11},{10,... | collective-permute-start | bytes 1966088 | tf_op jit(solution)/shard_map/ppermute | solution.py:359
  375.8 21.1 %collective-permute-start.34 = (f32[256,1280]{1,0:T(8,128)}, f32[256,1280]{1,0:T(8,128)}, u32[]{:S(2)}, u32[]{:S(2)}) collective-permute-start(f32[256,1280]{1,0:T(8,128)} %collective-permute-done.33.refs_5_.refs_4_), channel_id=1, source_target_pairs={{0,1},{1,0},{2,3},{3,2},{4,5},{5,4},{6,7},{7,6},{8,9},{9,8},{10,11... | collective-permute-start | bytes 3932168 | tf_op jit(solution)/shard_map/ppermute | solution.py:359
  375.8 21.1 %collective-permute-start.32 = (f32[256,1280]{1,0:T(8,128)S(1)}, f32[256,1280]{1,0:T(8,128)}, u32[]{:S(2)}, u32[]{:S(2)}) collective-permute-start(f32[256,1280]{1,0:T(8,128)S(1)} %collective-permute-done.27.refs_4_.refs_2_), channel_id=1, source_target_pairs={{0,1},{1,0},{2,3},{3,2},{4,5},{5,4},{6,7},{7,6},{8,9},{9,8},{10,11... | collective-permute-start | bytes 3932168 | tf_op jit(solution)/shard_map/ppermute | solution.py:359
  435.7 12.7 %collective-permute-start.39 = (bf16[4,256,640]{2,1,0:T(8,128)(2,1)}, bf16[4,256,640]{2,1,0:T(8,128)(2,1)S(1)}, u32[]{:S(2)}, u32[]{:S(2)}) collective-permute-start(bf16[4,256,640]{2,1,0:T(8,128)(2,1)} %get-tuple-element.257), channel_id=1, source_target_pairs={{0,1},{1,0},{2,3},{3,2},{4,5},{5,4},{6,7},{7,6},{8,9},{9,8},{10,11... | collective-permute-start | bytes 3932168 | tf_op jit(solution)/shard_map/ppermute | solution.py:359
  435.9 16.3 %collective-permute-start.41 = (bf16[4,256,640]{2,1,0:T(8,128)(2,1)}, bf16[4,256,640]{2,1,0:T(8,128)(2,1)S(1)}, u32[]{:S(2)}, u32[]{:S(2)}) collective-permute-start(bf16[4,256,640]{2,1,0:T(8,128)(2,1)} %get-tuple-element.263), channel_id=1, source_target_pairs={{0,1},{1,0},{2,3},{3,2},{4,5},{5,4},{6,7},{7,6},{8,9},{9,8},{10,11... | collective-permute-start | bytes 3932168 | tf_op jit(solution)/shard_map/ppermute | solution.py:359
  451.4 16.9 %collective-permute-start.40 = (bf16[2,256,640]{2,1,0:T(8,128)(2,1)S(1)}, bf16[2,256,640]{2,1,0:T(8,128)(2,1)}, u32[]{:S(2)}, u32[]{:S(2)}) collective-permute-start(bf16[2,256,640]{2,1,0:T(8,128)(2,1)S(1)} %get-tuple-element.330.refs_4_), channel_id=1, source_target_pairs={{0,2},{1,3},{2,0},{3,1},{4,6},{5,7},{6,4},{7,5},{8,10},{9,11},{10,... | collective-permute-start | bytes 1966088 | tf_op jit(solution)/shard_map/ppermute | solution.py:359
  452.4 17.0 %collective-permute-start.43 = (bf16[2,256,640]{2,1,0:T(8,128)(2,1)S(1)}, bf16[2,256,640]{2,1,0:T(8,128)(2,1)S(1)}, u32[]{:S(2)}, u32[]{:S(2)}) collective-permute-start(bf16[2,256,640]{2,1,0:T(8,128)(2,1)S(1)} %get-tuple-element.331.refs_5_), channel_id=1, source_target_pairs={{0,4},{1,5},{2,6},{3,7},{4,0},{5,1},{6,2},{7,3},{8,12},{9,13},{10,... | collective-permute-start | bytes 1966088 | tf_op jit(solution)/shard_map/ppermute | solution.py:359
  469.3 8.9 %collective-permute-start.42 = (bf16[256,640]{1,0:T(8,128)(2,1)S(1)}, bf16[256,640]{1,0:T(8,128)(2,1)S(1)}, u32[]{:S(2)}, u32[]{:S(2)}) collective-permute-start(bf16[256,640]{1,0:T(8,128)(2,1)S(1)} %fusion.43), channel_id=1, source_target_pairs={{0,4},{1,5},{2,6},{3,7},{4,0},{5,1},{6,2},{7,3},{8,12},{9,13},{10,... | collective-permute-start | bytes 983048 | tf_op jit(solution)/shard_map/ppermute | solution.py:359
  469.4 9.9 %collective-permute-start.44 = (bf16[256,640]{1,0:T(8,128)(2,1)S(1)}, bf16[256,640]{1,0:T(8,128)(2,1)S(1)}, u32[]{:S(2)}, u32[]{:S(2)}) collective-permute-start(bf16[256,640]{1,0:T(8,128)(2,1)S(1)} %fusion.40), channel_id=1, source_target_pairs={{0,2},{1,3},{2,0},{3,1},{4,6},{5,7},{6,4},{7,5},{8,10},{9,11},{10,... | collective-permute-start | bytes 983048 | tf_op jit(solution)/shard_map/ppermute | solution.py:359
  484.2 174.7 %all-gather.15.cloned.1.call-start = ((), (), s32[]{:S(2)}) async-start(), calls=%async_computation.3 | async-start | bytes 5898240 | tf_op jit(solution)/shard_map/all_gather | solution.py:401
  484.8 174.1 %all-gather.21.cloned.1.call-start = ((), (), s32[]{:S(2)}) async-start(), calls=%async_computation.6 | async-start | bytes 3686400 | tf_op jit(solution)/shard_map/all_gather | solution.py:401
  484.8 79.3 %collective-permute-start.45 = (f32[256,1280]{1,0:T(8,128)}, f32[256,1280]{1,0:T(8,128)S(1)}, u32[]{:S(2)}, u32[]{:S(2)}) collective-permute-start(f32[256,1280]{1,0:T(8,128)} %bitcast.89.refs_0_), channel_id=1, source_target_pairs={{0,2},{1,3},{2,0},{3,1},{4,6},{5,7},{6,4},{7,5},{8,10},{9,11},{10,... | collective-permute-start | bytes 3932168 | tf_op jit(solution)/shard_map/ppermute | solution.py:359
  485.5 78.6 %collective-permute-start.46 = (f32[256,1280]{1,0:T(8,128)}, f32[256,1280]{1,0:T(8,128)S(1)}, u32[]{:S(2)}, u32[]{:S(2)}) collective-permute-start(f32[256,1280]{1,0:T(8,128)} %bitcast.89.refs_0_), channel_id=1, source_target_pairs={{0,4},{1,5},{2,6},{3,7},{4,0},{5,1},{6,2},{7,3},{8,12},{9,13},{10,... | collective-permute-start | bytes 3932168 | tf_op jit(solution)/shard_map/ppermute | solution.py:359
  537.3 161.6 %all-gather.23.cloned.1.call-start = ((), (), s32[]{:S(2)}) async-start(), calls=%async_computation.7 | async-start | bytes 11796480 | tf_op jit(solution)/shard_map/all_gather | solution.py:401
  576.7 11.6 %collective-permute-start.47 = (bf16[4,256,640]{2,1,0:T(8,128)(2,1)}, bf16[4,256,640]{2,1,0:T(8,128)(2,1)S(1)}, u32[]{:S(2)}, u32[]{:S(2)}) collective-permute-start(bf16[4,256,640]{2,1,0:T(8,128)(2,1)} %get-tuple-element.286), channel_id=1, source_target_pairs={{0,1},{1,0},{2,3},{3,2},{4,5},{5,4},{6,7},{7,6},{8,9},{9,8},{10,11... | collective-permute-start | bytes 3932168 | tf_op jit(solution)/shard_map/ppermute | solution.py:359
  576.9 15.9 %collective-permute-start.48 = (bf16[4,256,640]{2,1,0:T(8,128)(2,1)}, bf16[4,256,640]{2,1,0:T(8,128)(2,1)S(1)}, u32[]{:S(2)}, u32[]{:S(2)}) collective-permute-start(bf16[4,256,640]{2,1,0:T(8,128)(2,1)} %get-tuple-element.288), channel_id=1, source_target_pairs={{0,1},{1,0},{2,3},{3,2},{4,5},{5,4},{6,7},{7,6},{8,9},{9,8},{10,11... | collective-permute-start | bytes 3932168 | tf_op jit(solution)/shard_map/ppermute | solution.py:359
  591.3 25.8 %collective-permute-start.49 = (bf16[2,256,640]{2,1,0:T(8,128)(2,1)S(1)}, bf16[2,256,640]{2,1,0:T(8,128)(2,1)}, u32[]{:S(2)}, u32[]{:S(2)}) collective-permute-start(bf16[2,256,640]{2,1,0:T(8,128)(2,1)S(1)} %get-tuple-element.328.refs_7_), channel_id=1, source_target_pairs={{0,2},{1,3},{2,0},{3,1},{4,6},{5,7},{6,4},{7,5},{8,10},{9,11},{10,... | collective-permute-start | bytes 1966088 | tf_op jit(solution)/shard_map/ppermute | solution.py:359
  593.0 25.9 %collective-permute-start.50 = (bf16[2,256,640]{2,1,0:T(8,128)(2,1)S(1)}, bf16[2,256,640]{2,1,0:T(8,128)(2,1)S(1)}, u32[]{:S(2)}, u32[]{:S(2)}) collective-permute-start(bf16[2,256,640]{2,1,0:T(8,128)(2,1)S(1)} %get-tuple-element.326.refs_8_), channel_id=1, source_target_pairs={{0,4},{1,5},{2,6},{3,7},{4,0},{5,1},{6,2},{7,3},{8,12},{9,13},{10,... | collective-permute-start | bytes 1966088 | tf_op jit(solution)/shard_map/ppermute | solution.py:359
  618.1 9.0 %collective-permute-start.51 = (bf16[256,640]{1,0:T(8,128)(2,1)S(1)}, bf16[256,640]{1,0:T(8,128)(2,1)S(1)}, u32[]{:S(2)}, u32[]{:S(2)}) collective-permute-start(bf16[256,640]{1,0:T(8,128)(2,1)S(1)} %fusion.39.refs_4_), channel_id=1, source_target_pairs={{0,4},{1,5},{2,6},{3,7},{4,0},{5,1},{6,2},{7,3},{8,12},{9,13},{10,... | collective-permute-start | bytes 983048 | tf_op jit(solution)/shard_map/ppermute | solution.py:359
  619.0 9.2 %collective-permute-start.52 = (bf16[256,640]{1,0:T(8,128)(2,1)S(1)}, bf16[256,640]{1,0:T(8,128)(2,1)S(1)}, u32[]{:S(2)}, u32[]{:S(2)}) collective-permute-start(bf16[256,640]{1,0:T(8,128)(2,1)S(1)} %fusion.37.refs_5_), channel_id=1, source_target_pairs={{0,2},{1,3},{2,0},{3,1},{4,6},{5,7},{6,4},{7,5},{8,10},{9,11},{10,... | collective-permute-start | bytes 983048 | tf_op jit(solution)/shard_map/ppermute | solution.py:359
  632.4 24.3 %collective-permute-start.57 = (f32[256,640]{1,0:T(8,128)S(1)}, f32[256,640]{1,0:T(8,128)S(1)}, u32[]{:S(2)}, u32[]{:S(2)}) collective-permute-start(f32[256,640]{1,0:T(8,128)S(1)} %slice.548), channel_id=1, source_target_pairs={{0,4},{1,5},{2,6},{3,7},{4,0},{5,1},{6,2},{7,3},{8,12},{9,13},{10,... | collective-permute-start | bytes 1966088 | tf_op jit(solution)/shard_map/ppermute | solution.py:359
  633.3 25.6 %collective-permute-start.56 = (f32[256,640]{1,0:T(8,128)S(1)}, f32[256,640]{1,0:T(8,128)}, u32[]{:S(2)}, u32[]{:S(2)}) collective-permute-start(f32[256,640]{1,0:T(8,128)S(1)} %slice.547), channel_id=1, source_target_pairs={{0,2},{1,3},{2,0},{3,1},{4,6},{5,7},{6,4},{7,5},{8,10},{9,11},{10,... | collective-permute-start | bytes 1966088 | tf_op jit(solution)/shard_map/ppermute | solution.py:359
  634.8 40.5 %collective-permute-start.53 = (f32[256,1280]{1,0:T(8,128)}, f32[256,1280]{1,0:T(8,128)}, u32[]{:S(2)}, u32[]{:S(2)}) collective-permute-start(f32[256,1280]{1,0:T(8,128)} %bitcast.89.refs_0_), channel_id=1, source_target_pairs={{0,1},{1,0},{2,3},{3,2},{4,5},{5,4},{6,7},{7,6},{8,9},{9,8},{10,11... | collective-permute-start | bytes 3932168 | tf_op jit(solution)/shard_map/ppermute | solution.py:359
  634.8 40.5 %collective-permute-start.55 = (f32[256,1280]{1,0:T(8,128)S(1)}, f32[256,1280]{1,0:T(8,128)}, u32[]{:S(2)}, u32[]{:S(2)}) collective-permute-start(f32[256,1280]{1,0:T(8,128)S(1)} %copy-done.6), channel_id=1, source_target_pairs={{0,1},{1,0},{2,3},{3,2},{4,5},{5,4},{6,7},{7,6},{8,9},{9,8},{10,11... | collective-permute-start | bytes 3932168 | tf_op jit(solution)/shard_map/ppermute | solution.py:359
  635.3 40.0 %collective-permute-start.54 = (f32[256,1280]{1,0:T(8,128)S(1)}, f32[256,1280]{1,0:T(8,128)}, u32[]{:S(2)}, u32[]{:S(2)}) collective-permute-start(f32[256,1280]{1,0:T(8,128)S(1)} %copy-done.4), channel_id=1, source_target_pairs={{0,1},{1,0},{2,3},{3,2},{4,5},{5,4},{6,7},{7,6},{8,9},{9,8},{10,11... | collective-permute-start | bytes 3932168 | tf_op jit(solution)/shard_map/ppermute | solution.py:359
  656.7 18.5 %collective-permute-start.59 = (f32[256,640]{1,0:T(8,128)S(1)}, f32[256,640]{1,0:T(8,128)}, u32[]{:S(2)}, u32[]{:S(2)}) collective-permute-start(f32[256,640]{1,0:T(8,128)S(1)} %collective-permute-done.57.refs_7_), channel_id=1, source_target_pairs={{0,1},{1,0},{2,3},{3,2},{4,5},{5,4},{6,7},{7,6},{8,9},{9,8},{10,11... | collective-permute-start | bytes 1966088 | tf_op jit(solution)/shard_map/ppermute | solution.py:359
  658.8 16.4 %collective-permute-start.58 = (f32[256,640]{1,0:T(8,128)}, f32[256,640]{1,0:T(8,128)}, u32[]{:S(2)}, u32[]{:S(2)}) collective-permute-start(f32[256,640]{1,0:T(8,128)} %collective-permute-done.56.refs_6_), channel_id=1, source_target_pairs={{0,1},{1,0},{2,3},{3,2},{4,5},{5,4},{6,7},{7,6},{8,9},{9,8},{10,11... | collective-permute-start | bytes 1966088 | tf_op jit(solution)/shard_map/ppermute | solution.py:359
  (54 other events, 266.7 us)
Sparse Core Ops, SparseCore 0:
  87.3 55.5 all-gather.8
  159.4 50.6 all-gather.10
  310.7 52.5 all-gather.12
  365.0 45.2 all-gather.16
  484.3 52.8 all-gather.18
  538.9 37.2 all-gather.14
  578.1 37.8 all-gather.20
  631.2 67.6 all-gather.22

commit v5 on v4

--- a/solution.py
+++ b/solution.py
@@ -460,11 +460,10 @@
         sum_out = sum_cores(parts)
         value, sent, final = sum_second(sum_g, [tok])
         sum_out, sent_out = sum_first(sum_out, sent)
-        tok = mlp_grad("in", top, top_a, top_dh, [tok, *sent, *sent_out])
-        d_one = shard(dy_one) + rms_vjp(shard(y_one), sum_end(value, final, [tok]))
+        d_one = shard(dy_one) + rms_vjp(shard(y_one), sum_end(value, final, sent_out))
         rounded, d_one = lax.optimization_barrier((d_one.astype(BF), d_one))
         d_one_bf = gather(rounded)
-        s_a, sl_hi, act_hi, sl_lo, act_lo, tok = mlp_pair_fwd(rank, s_one, w_in, hi, lo, [tok, rounded])
+        s_a, sl_hi, act_hi, sl_lo, act_lo, tok = mlp_pair_fwd(rank, s_one, w_in, hi, lo, [tok, rounded, *sent_out])
         value, sent, final = sum_second(sum_out, [tok])
         *parts, tok = mlp_out(rank, act_lo, w_out, lo, [tok, *sent])
         x_two_top = shard(y_two) - sum_end(value, final, [tok])
@@ -474,7 +473,8 @@
             rank, head_dim, qkv_w, o_w, hi, x=s_two, norm=True, d=d_one_bf, after=[tok, *sent]
         )
         sum_hi, sent = sum_first(sum_cores(parts))
-        value_low, sent_low, final_low = sum_second(sum_out, [tok])
+        value_low, sent_low, final_low = sum_second(sum_out, [tok, *sent])
+        wo_all = gather(tie(o_w[lo], [f_top]))
         o_top, dqkv_top, *parts, tok = attn(rank, head_dim, qkv_w, o_w, top, x=f_top, d=d_one_bf, after=[tok, *sent, *sent_low])
         x_two = shard(s_two) - sum_end(value_low, final_low, [tok])
         sum_top, sent = sum_first(sum_cores(parts))
@@ -483,15 +483,16 @@
         value, sent, final = sum_second(sum_top, [tok])
         x_two_shard = tie(x_two, sent)[0]
         near = spread_first(x_two_shard)
-        tok = attn_grads(top, f_top, o_top, dqkv_top, d_one_bf, [tok, *sent, x_two_shard])
-        d_two = shard(dy_two) + rms_vjp(x_two_top, sum_end(value, final, [tok]))
+        d_two = shard(dy_two) + rms_vjp(x_two_top, sum_end(value, final, [x_two_shard]))
         rounded, d_two = lax.optimization_barrier((d_two.astype(BF), d_two))
         d_two_hi_bf = gather(rounded)
+        tok = attn_grads(top, f_top, o_top, dqkv_top, d_one_bf, [tok, rounded])
         d_two = d_two + rms_vjp(shard(s_two), sum_end(value_hi, final_hi, [tok]))
         rounded, d_two = lax.optimization_barrier((d_two.astype(BF), d_two))
         d_two_lo_bf = gather(rounded)
         tok = mlp_grad("out", top, top_act, d_two_bf, [tok, rounded])
         far, cross = spread_second(near, [tok])
+        tok = mlp_grad("in", top, top_a, top_dh, [tok, near[1], near[2]])
         dh_hi, tok = mlp_dhid(rank, d_two_hi_bf, w_out, hi, sl_hi, [tok, near[1], near[2]])
         pieces = spread_last(x_two_shard, near, far, cross, [tok])
         x_two_full, tok = assemble(rank, pieces, [tok])
@@ -504,19 +505,19 @@
         d_one = d_one + rms_vjp(shard(s_one), sum_end(value, final))
         rounded, d_one_shard = lax.optimization_barrier((d_one.astype(BF), d_one[0]))
         d_one_bf = gather(rounded)
-        near = spread_first(d_one_shard)
         tok = mlp_grad("out", lo, act_lo, d_two_lo_bf, [tok, rounded])
         tok = mlp_grad("in", hi, s_a, dh_hi, [tok])
         tok = mlp_grad("out", hi, act_hi, d_two_hi_bf, [tok])
-        far, cross = spread_second(near, [tok, d_one_bf])
-        wo_all = gather(tie(o_w[lo], [d_one_bf]))
-        dqkv_lo, *parts, tok = attn(rank, head_dim, qkv_w, o_w, lo, qkv=qkv_lo, d=d_one_bf, after=[tok, near[1], near[2]])
-        pieces = spread_last(d_one_shard, near, far, cross, [tok])
+        d_one_shard = tie(d_one_shard, [d_one_bf])
+        near = spread_first(d_one_shard)
+        dqkv_lo, *parts, tok = attn(rank, head_dim, qkv_w, o_w, lo, qkv=qkv_lo, d=d_one_bf, after=[tok])
         sum_lo, sent = sum_first(sum_cores(parts))
         tok = attn_grads(lo, f_lo, o_lo, dqkv_lo, d_one_bf, [tok, *sent])
         value, sent, final = sum_second(sum_lo, [tok])
         d_two = d_two + rms_vjp(x_two, sum_end(value, final))
+        far, cross = spread_second(near, [tok, *sent])
         x_one_full, tok = attn_value(rank, s_one, o_all, wo_all, [tok, *sent, d_two])
+        pieces = spread_last(d_one_shard, near, far, cross, [tok])
         d_one_full, _ = assemble(rank, pieces, [tok])
         grad_qkv = stacks["attn"][0].reshape(n_layers, 3, n_heads, head_dim, width).transpose(0, 4, 1, 2, 3)
         grad_o = stacks["attn"][1].reshape(w_o.shape)

time: 727 us -> 698 us (0.960)
  waiting for transfers between devices: 234 us -> 192 us
    all_gather x8, waiting for transfers between devices: 63.6 us -> 10.7 us  [gather(): return lax.all_gather(shard, 'tp', axis=0, tiled=True)]
    ppermute x60, waiting for transfers between devices: 170 us -> 181 us  [permute(): return lax.ppermute(array, 'tp', [(idx, idx ^ bit) for idx in range(8)])]
    unnamed x101 -> x111, local copies, waits for them, and re-layouts: 16.9 us -> 15.9 us
  transfers between devices with their start and end apart: 68 -> 68, of which waited for: 25 -> 28; matrix products, arithmetic and copies ran while one was open for 11% -> 12% of each run, Pallas kernels for 40% -> 39%
where the time goes in v5:
time: 698 us; the launch traced here: 687 us
  Pallas kernels  315 us (45%)
  waiting for transfers between devices  192 us (28%)
  other arithmetic  91.3 us (13%)
  starting transfers between devices  49.6 us (7%)
  local copies, waits for them, and re-layouts  23.8 us (3%)
  between operations  15 us (2%)
    pallas_call x18, Pallas kernels, run(): pl.pallas_call(kernel, grid_spec=pltpu.PrefetchScalarGridSpec(num_scalar_...  213 us
    ppermute x60, waiting for transfers between devices, permute(): return lax.ppermute(array, 'tp', [(idx, idx ^ bit) for idx in range(8)])  181 us
    pallas_call x9, Pallas kernels, weight_grads(): *stacks, token = call(*args)  83.5 us
    ppermute x60, starting transfers between devices, permute(): return lax.ppermute(array, 'tp', [(idx, idx ^ bit) for idx in range(8)])  49.3 us
    add x11, other arithmetic, sum_first(): pick(keep, 0) + pick(recv, 0)  28.5 us
    pallas_call x2, Pallas kernels, assemble(): pl.pallas_call(kernel, grid_spec=pltpu.PrefetchScalarGridSpec(num_scalar_...  18.3 us
    add x13, other arithmetic, sum_second(): sent.append(here[1] + recv[1])  16.5 us
    unnamed x111, local copies, waits for them, and re-layouts  15.9 us
  transfers between devices with their start and end apart: 68, of which 28 were waited for; matrix products, arithmetic and copies ran while one was open for 12% of the time, Pallas kernels for 39%

profile of v5, /device:TPU:0, one launch (start us, length us, event | category | flops | bytes accessed | tf_op | source)
XLA Modules:
  0.0 686.5 jit_solution(13345860226642080454)
XLA Ops:
  7.2 11.5 %shard_map.161 = (bf16[8,256,1280]{2,1,0:T(8,128)(2,1)}, bf16[8,256,640]{2,1,0:T(8,128)(2,1)}, bf16[8,256,640]{2,1,0:T(8,128)(2,1)}, bf16[8,256,1280]{2,1,0:T(8,...) custom-call(s32[1]{0:T(128)} %bitcast.rank_ref, f32[8,256,1280]{2,1,0:T(8,128)} %refs_0_.3, ...), custom_call_target="tpu_custom_call" | custom-call | flops 5033164800 | bytes 9177088 | tf_op jit(solution)/shard_map/pallas_call | solution.py:91
  19.5 11.5 %shard_map.162 = (bf16[8,256,1280]{2,1,0:T(8,128)(2,1)}, bf16[8,256,640]{2,1,0:T(8,128)(2,1)}, bf16[8,256,640]{2,1,0:T(8,128)(2,1)}, bf16[8,256,1280]{2,1,0:T(8,...) custom-call(s32[1]{0:T(128)} %bitcast.rank_ref, ...), custom_call_target="tpu_custom_call", output_to_operand_aliasing={{0}: (5, {}), {1}: (6, {}), {2}: (7, {}), {3}: (8, {})} | custom-call | flops 5033164800 | bytes 9177088 | tf_op jit(solution)/shard_map/pallas_call | solution.py:91
  31.0 2.4 slice_add_fusion.25
  34.4 6.0 shard_map.163
  40.9 2.9 collective-permute-start.2
  46.9 5.8 shard_map.164
  52.6 6.3 collective-permute-done.2
  63.6 4.0 bitcast_add_fusion.2
  67.6 3.1 slice_add_fusion.2
  73.9 3.4 fusion.68
  79.4 17.7 %shard_map.165 = (bf16[8,256,1280]{2,1,0:T(8,128)(2,1)}, f32[8,256,640]{2,1,0:T(8,128)}, bf16[8,256,640]{2,1,0:T(8,128)(2,1)}, f32[8,256,640]{2,1,0:T(8,128)}, b...) custom-call(s32[1]{0:T(128)} %bitcast.rank_ref, f32[8,256,1280]{2,1,0:T(8,128)} %bitcast.371, ...), custom_call_target="tpu_custom_call" | custom-call | flops 6710886400 | bytes 20975616 | tf_op jit(solution)/shard_map/pallas_call | solution.py:91
  97.1 28.1 %collective-permute-done.9 = f32[2,256,640]{2,1,0:T(8,128)} collective-permute-done((f32[2,256,640]{2,1,0:T(8,128)}, f32[2,256,640]{2,1,0:T(8,128)}, u32[]{:S(2)}, u32[]{:S(2)}) %collective-permute-start.9) | collective-permute-done | bytes 1310752 | tf_op jit(solution)/shard_map/ppermute | solution.py:359
  130.1 2.5 collective-permute-start.12
  132.6 5.7 shard_map.166
  138.3 5.8 shard_map.167
  150.0 4.6 collective-permute-done.10
  154.7 3.7 collective-permute-done.14
  158.4 3.7 slice_add_fusion.1
  163.9 15.5 %shard_map.168 = (bf16[8,256,1280]{2,1,0:T(8,128)(2,1)}, bf16[160,2048]{1,0:T(8,128)(2,1)}, bf16[480,2048]{1,0:T(8,128)(2,1)}, bf16[4,256,640]{2,1,0:T(8,128)(2,...) custom-call(s32[1]{0:T(128)} %bitcast.rank_ref, bf16[3,480,1280]{2,1,0:T(8,128)(2,1)} %bitcast.325, ...), custom_call_target="tpu_custom_call" | custom-call | flops 3523215360 | bytes 5244928 | tf_op jit(solution)/shard_map/pallas_call | solution.py:91
  181.1 15.1 %shard_map.169 = (bf16[8,256,1280]{2,1,0:T(8,128)(2,1)}, bf16[160,2048]{1,0:T(8,128)(2,1)}, bf16[480,2048]{1,0:T(8,128)(2,1)}, bf16[4,256,640]{2,1,0:T(8,128)(2,...) custom-call(s32[1]{0:T(128)} %bitcast.rank_ref, ...), custom_call_target="tpu_custom_call", output_to_operand_aliasing={{0}: (5, {}), {1}: (6, {}), {2}: (7, {})} | custom-call | flops 3523215360 | bytes 5244928 | tf_op jit(solution)/shard_map/pallas_call | solution.py:91
  196.2 3.0 slice_add_fusion.14
  199.2 2.6 slice_add_fusion.13
  201.9 10.8 %collective-permute-done.13 = f32[2,256,640]{2,1,0:T(8,128)} collective-permute-done((f32[2,256,640]{2,1,0:T(8,128)S(1)}, f32[2,256,640]{2,1,0:T(8,128)}, u32[]{:S(2)}, u32[]{:S(2)}) %collective-permute-start.13) | collective-permute-done | bytes 1310752 | tf_op jit(solution)/shard_map/ppermute | solution.py:359
  216.7 14.2 %shard_map.170 = (bf16[160,2048]{1,0:T(8,128)(2,1)}, bf16[480,2048]{1,0:T(8,128)(2,1)}, bf16[4,256,640]{2,1,0:T(8,128)(2,1)}, bf16[4,256,640]{2,1,0:T(8,128)(2,1)}, f32[8,128]{1,0:T(8,128)}) custom-call(s32[1]{0:T(128)} %bitcast.rank_ref, bf16[3,480,1280]{2,1,0:T(8,128)(2,1)} %bitcast.327, bf16[8,256,1280]{2,1,0:T(8,128)(2,1)} %all-gather.11.cloned.1.call-done.refs_1_, ...), custom_call_target="tpu_custom_call" | custom-call | flops 3523215360 | bytes 2623488 | tf_op jit(solution)/shard_map/pallas_call | solution.py:91
  234.4 14.2 %shard_map.171 = (bf16[160,2048]{1,0:T(8,128)(2,1)}, bf16[480,2048]{1,0:T(8,128)(2,1)}, bf16[4,256,640]{2,1,0:T(8,128)(2,1)}, bf16[4,256,640]{2,1,0:T(8,128)(2,1)}, f32[8,128]{1,0:T(8,128)}) custom-call(s32[1]{0:T(128)} %bitcast.rank_ref, bf16[3,480,1280]{2,1,0:T(8,128)(2,1)} %bitcast.328, ...), custom_call_target="tpu_custom_call", output_to_operand_aliasing={{0}: (5, {}), {1}: (6, {})} | custom-call | flops 3523215360 | bytes 2623488 | tf_op jit(solution)/shard_map/pallas_call | solution.py:91
  252.0 2.3 fusion.10
  254.3 2.4 slice_add_fusion.12
  257.4 2.4 fusion.7
  267.6 9.5 %shard_map.172 = (f32[3,480,1280]{2,1,0:T(8,128)}, f32[3,160,1280]{2,1,0:T(8,128)}, f32[8,128]{1,0:T(8,128)}) custom-call(bf16[480,2048]{1,0:T(8,128)(2,1)} %get-tuple-element.214.refs_0_, bf16[2048,1280]{1,0:T(8,128)(2,1)} %bitcast.350, bf16[160,2048]{1,0:T(8,128)(2,1)} %get-tuple-element.216.refs_2_, bf16[2048,1280]{1,0:T(8,128)(2,1)} %bitcast.323, ...), custom_call_target="tpu_custom_call" | custom-call | flops 3355443200 | bytes 27852800 | tf_op jit(solution)/shard_map/pallas_call | solution.py:354
  277.2 2.6 collective-permute-done.21
  285.9 3.9 collective-permute-done.28
  292.4 3.0 fusion.66
  297.6 10.1 %shard_map.173 = (f32[3,480,1280]{2,1,0:T(8,128)}, f32[3,160,1280]{2,1,0:T(8,128)}, f32[8,128]{1,0:T(8,128)}) custom-call(bf16[480,2048]{1,0:T(8,128)(2,1)} %get-tuple-element.226.refs_0_, bf16[2048,1280]{1,0:T(8,128)(2,1)} %bitcast.342, bf16[160,2048]{1,0:T(8,128)(2,1)} %get-tuple-element.227.refs_2_, ...), custom_call_target="tpu_custom_call", output_to_operand_aliasing={{0}: (4, {}), {1}: (5, {})} | custom-call | flops 3355443200 | bytes 27852800 | tf_op jit(solution)/shard_map/pallas_call | solution.py:354
  311.8 3.0 fusion.65
  317.0 8.8 %shard_map.174 = (f32[3,640,1280]{2,1,0:T(8,128)}, f32[8,128]{1,0:T(8,128)}) custom-call(bf16[2048,640]{1,0:T(8,128)(2,1)} %bitcast.344, bf16[2048,1280]{1,0:T(8,128)(2,1)} %bitcast.359, f32[8,128]{1,0:T(8,128)} %get-tuple-element.233.refs_2_, bf16[1,256,1280]{2,1,0:T(8,128)(2,1)} %get-tuple-element.237.refs_3_), custom_call_target="tpu_custom_call" | custom-call | flops 3355443200 | bytes 17367040 | tf_op jit(solution)/shard_map/pallas_call | solution.py:354
  325.8 32.5 %collective-permute-done.27.refs_3_.refs_4_.refs_2_ = f32[256,1280]{1,0:T(8,128)S(1)} collective-permute-done((f32[256,1280]{1,0:T(8,128)S(1)}, f32[256,1280]{1,0:T(8,128)S(1)}, u32[]{:S(2)}, u32[]{:S(2)}) %collective-permute-start.27) | collective-permute-done | bytes 1310752 | tf_op jit(solution)/shard_map/ppermute | solution.py:359
  364.1 8.9 %shard_map.175 = (f32[3,1280,640]{2,1,0:T(8,128)}, f32[8,128]{1,0:T(8,128)}) custom-call(bf16[2048,1280]{1,0:T(8,128)(2,1)} %bitcast.358, bf16[2048,640]{1,0:T(8,128)(2,1)} %bitcast.364, f32[8,128]{1,0:T(8,128)} %get-tuple-element.238.refs_2_, f32[256,1280]{1,0:T(8,128)} %copy-done.2, f32[256,1280]{1,0:T(8,128)} %collective-permute-done.33.refs_4_.refs_5_), custom_call_target="tpu_custom_call" | custom-call | flops 3355443200 | bytes 17367040 | tf_op jit(solution)/shard_map/pallas_call | solution.py:354
  373.1 11.4 %shard_map.176 = (bf16[8,256,640]{2,1,0:T(8,128)(2,1)}, f32[8,128]{1,0:T(8,128)}) custom-call(s32[1]{0:T(128)} %bitcast.rank_ref, bf16[8,256,1280]{2,1,0:T(8,128)(2,1)} %all-gather.13.cloned.1.call-done.refs_0_, bf16[3,640,1280]{2,1,0:T(8,128)(2,1)} %refs_1_.19, f32[8,256,640]{2,1,0:T(8,128)} %get-tuple-element.241.refs_2_, ...), custom_call_target="tpu_custom_call" | custom-call | flops 3355443200 | bytes 2625536 | tf_op jit(solution)/shard_map/pallas_call | solution.py:91
  388.0 9.2 %shard_map.177 = (f32[8,256,1280]{2,1,0:T(8,128)}, f32[8,128]{1,0:T(8,128)}) custom-call(s32[1]{0:T(128)} %bitcast.rank_ref, f32[256,1280]{1,0:T(8,128)} %bitcast.354, f32[256,1280]{1,0:T(8,128)} %collective-permute-done.26.refs_1_, f32[256,1280]{1,0:T(8,128)} %copy-done.2, f32[256,1280]{1,0:T(8,128)} %collective-permute-done.32.refs_3_, ...), custom_call_target="tpu_custom_call" | custom-call | flops 2000000000 | bytes 20971520 | tf_op jit(solution)/shard_map/pallas_call | solution.py:290
  397.2 14.9 %shard_map.178 = (bf16[8,256,1280]{2,1,0:T(8,128)(2,1)}, bf16[160,2048]{1,0:T(8,128)(2,1)}, bf16[480,2048]{1,0:T(8,128)(2,1)}, f32[8,128]{1,0:T(8,128)}) custom-call(s32[1]{0:T(128)} %bitcast.rank_ref, bf16[3,480,1280]{2,1,0:T(8,128)(2,1)} %bitcast.329, f32[8,256,1280]{2,1,0:T(8,128)} %get-tuple-element.358.refs_1_, f32[8,128]{1,0:T(8,128)} %get-tuple-element.249.refs_2_), custom_call_target="tpu_custom_call" | custom-call | flops 2852126720 | bytes 7868416 | tf_op jit(solution)/shard_map/pallas_call | solution.py:91
  412.1 12.2 %shard_map.179 = (bf16[8,256,640]{2,1,0:T(8,128)(2,1)}, bf16[4,256,640]{2,1,0:T(8,128)(2,1)}, bf16[4,256,640]{2,1,0:T(8,128)(2,1)}, f32[8,128]{1,0:T(8,128)}) custom-call(s32[1]{0:T(128)} %bitcast.rank_ref, bf16[8,256,1280]{2,1,0:T(8,128)(2,1)} %all-gather.19.cloned.1.call-done.refs_0_, bf16[3,640,1280]{2,1,0:T(8,128)(2,1)} %refs_1_.19, ...), custom_call_target="tpu_custom_call" | custom-call | flops 5033164800 | bytes 2623488 | tf_op jit(solution)/shard_map/pallas_call | solution.py:91
  424.8 12.2 %shard_map.180 = (bf16[8,256,640]{2,1,0:T(8,128)(2,1)}, bf16[4,256,640]{2,1,0:T(8,128)(2,1)}, bf16[4,256,640]{2,1,0:T(8,128)(2,1)}, f32[8,128]{1,0:T(8,128)}) custom-call(s32[1]{0:T(128)} %bitcast.rank_ref, bf16[8,256,1280]{2,1,0:T(8,128)(2,1)} %all-gather.19.cloned.1.call-done.refs_0_, ...), custom_call_target="tpu_custom_call", output_to_operand_aliasing={{0}: (7, {})} | custom-call | flops 5033164800 | bytes 2623488 | tf_op jit(solution)/shard_map/pallas_call | solution.py:91
  444.4 9.0 %shard_map.181 = (f32[3,1280,640]{2,1,0:T(8,128)}, f32[8,128]{1,0:T(8,128)}) custom-call(bf16[2048,1280]{1,0:T(8,128)(2,1)} %bitcast.347, bf16[2048,640]{1,0:T(8,128)(2,1)} %bitcast.355, f32[3,1280,640]{2,1,0:T(8,128)} %get-tuple-element.263.refs_2_, f32[8,128]{1,0:T(8,128)} %get-tuple-element.264.refs_3_, ...), custom_call_target="tpu_custom_call", output_to_operand_aliasing={{0}: (2, {})} | custom-call | flops 3355443200 | bytes 17367040 | tf_op jit(solution)/shard_map/pallas_call | solution.py:354
  453.4 3.5 collective-permute-done.40
  460.4 6.7 collective-permute-done.42
  470.6 2.5 fusion.64
  476.1 9.4 %shard_map.182 = (f32[3,640,1280]{2,1,0:T(8,128)}, f32[8,128]{1,0:T(8,128)}) custom-call(bf16[2048,640]{1,0:T(8,128)(2,1)} %bitcast.346, bf16[2048,1280]{1,0:T(8,128)(2,1)} %bitcast.341, f32[3,640,1280]{2,1,0:T(8,128)} %get-tuple-element.272.refs_2_, f32[8,128]{1,0:T(8,128)} %get-tuple-element.267.refs_3_, ...), custom_call_target="tpu_custom_call", output_to_operand_aliasing={{0}: (2, {})} | custom-call | flops 3355443200 | bytes 17367040 | tf_op jit(solution)/shard_map/pallas_call | solution.py:354
  485.5 9.2 %shard_map.183 = (f32[3,1280,640]{2,1,0:T(8,128)}, f32[8,128]{1,0:T(8,128)}) custom-call(bf16[2048,1280]{1,0:T(8,128)(2,1)} %bitcast.348, bf16[2048,640]{1,0:T(8,128)(2,1)} %bitcast.345, f32[3,1280,640]{2,1,0:T(8,128)} %get-tuple-element.274.refs_2_, f32[8,128]{1,0:T(8,128)} %get-tuple-element.275.refs_3_), custom_call_target="tpu_custom_call", output_to_operand_aliasing={{0}: (2, {})} | custom-call | flops 3355443200 | bytes 17367040 | tf_op jit(solution)/shard_map/pallas_call | solution.py:354
  494.7 8.8 %shard_map.184 = (f32[3,640,1280]{2,1,0:T(8,128)}, f32[8,128]{1,0:T(8,128)}) custom-call(bf16[2048,640]{1,0:T(8,128)(2,1)} %bitcast.365, bf16[2048,1280]{1,0:T(8,128)(2,1)} %bitcast.349, f32[3,640,1280]{2,1,0:T(8,128)} %get-tuple-element.273.refs_2_, f32[8,128]{1,0:T(8,128)} %get-tuple-element.276.refs_3_), custom_call_target="tpu_custom_call", output_to_operand_aliasing={{0}: (2, {})} | custom-call | flops 3355443200 | bytes 17367040 | tf_op jit(solution)/shard_map/pallas_call | solution.py:354
  503.5 5.9 all-gather.21.cloned.1.call-done.refs_3_
  509.4 11.1 %shard_map.185 = (bf16[480,2048]{1,0:T(8,128)(2,1)}, bf16[4,256,640]{2,1,0:T(8,128)(2,1)}, bf16[4,256,640]{2,1,0:T(8,128)(2,1)}, f32[8,128]{1,0:T(8,128)}) custom-call(s32[1]{0:T(128)} %bitcast.rank_ref, bf16[3,480,1280]{2,1,0:T(8,128)(2,1)} %bitcast.330, bf16[480,2048]{1,0:T(8,128)(2,1)} %get-tuple-element.252.refs_1_, bf16[3,160,1280]{2,1,0:T(8,128)(2,1)} %bitcast.338, ...), custom_call_target="tpu_custom_call" | custom-call | flops 2097152000 | bytes 2295808 | tf_op jit(solution)/shard_map/pallas_call | solution.py:91
  521.0 11.1 %shard_map.186 = (bf16[480,2048]{1,0:T(8,128)(2,1)}, bf16[4,256,640]{2,1,0:T(8,128)(2,1)}, bf16[4,256,640]{2,1,0:T(8,128)(2,1)}, f32[8,128]{1,0:T(8,128)}) custom-call(s32[1]{0:T(128)} %bitcast.rank_ref, bf16[3,480,1280]{2,1,0:T(8,128)(2,1)} %bitcast.331, bf16[480,2048]{1,0:T(8,128)(2,1)} %get-tuple-element.252.refs_1_, ...), custom_call_target="tpu_custom_call", output_to_operand_aliasing={{0}: (5, {})} | custom-call | flops 2097152000 | bytes 2295808 | tf_op jit(solution)/shard_map/pallas_call | solution.py:91
  539.6 9.7 %shard_map.187 = (f32[3,480,1280]{2,1,0:T(8,128)}, f32[3,160,1280]{2,1,0:T(8,128)}, f32[8,128]{1,0:T(8,128)}) custom-call(bf16[480,2048]{1,0:T(8,128)(2,1)} %get-tuple-element.280.refs_0_, bf16[2048,1280]{1,0:T(8,128)(2,1)} %bitcast.357, bf16[160,2048]{1,0:T(8,128)(2,1)} %get-tuple-element.250.refs_2_, ...), custom_call_target="tpu_custom_call", output_to_operand_aliasing={{0}: (4, {}), {1}: (5, {})} | custom-call | flops 3355443200 | bytes 27852800 | tf_op jit(solution)/shard_map/pallas_call | solution.py:354
  549.4 4.9 collective-permute-done.48
  554.3 6.7 collective-permute-done.47
  565.6 5.2 collective-permute-done.49
  571.9 6.5 collective-permute-done.50
  582.2 2.5 collective-permute-start.52
  584.7 41.3 %collective-permute-done.52.refs_2_ = f32[256,1280]{1,0:T(8,128)S(1)} collective-permute-done((f32[256,1280]{1,0:T(8,128)S(1)}, f32[256,1280]{1,0:T(8,128)S(1)}, u32[]{:S(2)}, u32[]{:S(2)}) %collective-permute-start.52) | collective-permute-done | bytes 1310752 | tf_op jit(solution)/shard_map/ppermute | solution.py:359
  632.4 17.2 %shard_map.188 = (f32[8,256,1280]{2,1,0:T(8,128)}, f32[8,128]{1,0:T(8,128)}) custom-call(s32[1]{0:T(128)} %bitcast.rank_ref, f32[8,256,1280]{2,1,0:T(8,128)} %bitcast.372, bf16[1280,2048]{1,0:T(8,128)(2,1)} %all-gather.15.cloned.1.call-done.refs_1_, bf16[1280,1280]{1,0:T(8,128)(2,1)} %all-gather.17.cloned.1.call-done.refs_2_, ...), custom_call_target="tpu_custom_call" | custom-call | flops 6710886400 | bytes 10489856 | tf_op jit(solution)/shard_map/pallas_call | solution.py:91
  650.4 3.1 collective-permute-done.56.refs_6_
  656.7 9.1 %shard_map.189 = (f32[8,256,1280]{2,1,0:T(8,128)}, f32[8,128]{1,0:T(8,128)}) custom-call(s32[1]{0:T(128)} %bitcast.rank_ref, f32[256,1280]{1,0:T(8,128)} %bitcast.363, f32[256,1280]{1,0:T(8,128)} %collective-permute-done.51.refs_1_, f32[256,1280]{1,0:T(8,128)} %copy-done.12, f32[256,1280]{1,0:T(8,128)} %collective-permute-done.53.refs_3_, ...), custom_call_target="tpu_custom_call" | custom-call | flops 2000000000 | bytes 20971520 | tf_op jit(solution)/shard_map/pallas_call | solution.py:290
  665.8 4.8 all-gather.23.cloned.1.call-done
  670.6 8.8 %copy.57 = f32[8,256,1280]{2,1,0:T(8,128)} copy(f32[8,256,1280]{2,1,0:T(8,128)} %all-gather.23.cloned.1.call-done) | data formatting | bytes 20971520
  (291 shorter events, 121.2 us)
Async XLA Ops:
  7.2 156.7 %all-gather.9.cloned.1.call-start = ((), (), s32[]{:S(2)}) async-start(), calls=%async_computation | async-start | bytes 5898240 | tf_op jit(solution)/shard_map/all_gather | solution.py:401
  18.8 12.2 %collective-permute-start = (bf16[4,256,640]{2,1,0:T(8,128)(2,1)}, bf16[4,256,640]{2,1,0:T(8,128)(2,1)S(1)}, u32[]{:S(2)}, u32[]{:S(2)}) collective-permute-start(bf16[4,256,640]{2,1,0:T(8,128)(2,1)} %get-tuple-element.165), channel_id=1, source_target_pairs={{0,1},{1,0},{2,3},{3,2},{4,5},{5,4},{6,7},{7,6},{8,9},{9,8},{10,11... | collective-permute-start | bytes 3932168 | tf_op jit(solution)/shard_map/ppermute | solution.py:359
  19.5 13.9 %collective-permute-start.1 = (bf16[4,256,640]{2,1,0:T(8,128)(2,1)}, bf16[4,256,640]{2,1,0:T(8,128)(2,1)S(1)}, u32[]{:S(2)}, u32[]{:S(2)}) collective-permute-start(bf16[4,256,640]{2,1,0:T(8,128)(2,1)} %get-tuple-element.167), channel_id=1, source_target_pairs={{0,1},{1,0},{2,3},{3,2},{4,5},{5,4},{6,7},{7,6},{8,9},{9,8},{10,11... | collective-permute-start | bytes 3932168 | tf_op jit(solution)/shard_map/ppermute | solution.py:359
  40.4 23.2 %collective-permute-start.6 = (f32[4,256,640]{2,1,0:T(8,128)}, f32[4,256,640]{2,1,0:T(8,128)}, u32[]{:S(2)}, u32[]{:S(2)}) collective-permute-start(f32[4,256,640]{2,1,0:T(8,128)} %get-tuple-element.176), channel_id=1, source_target_pairs={{0,1},{1,0},{2,3},{3,2},{4,5},{5,4},{6,7},{7,6},{8,9},{9,8},{10,11... | collective-permute-start | bytes 7864328 | tf_op jit(solution)/shard_map/ppermute | solution.py:359
  40.9 26.7 %collective-permute-start.4 = (f32[4,256,640]{2,1,0:T(8,128)}, f32[4,256,640]{2,1,0:T(8,128)}, u32[]{:S(2)}, u32[]{:S(2)}) collective-permute-start(f32[4,256,640]{2,1,0:T(8,128)} %get-tuple-element.172), channel_id=1, source_target_pairs={{0,1},{1,0},{2,3},{3,2},{4,5},{5,4},{6,7},{7,6},{8,9},{9,8},{10,11... | collective-permute-start | bytes 7864328 | tf_op jit(solution)/shard_map/ppermute | solution.py:359
  40.9 18.0 %collective-permute-start.2 = (bf16[2,256,640]{2,1,0:T(8,128)(2,1)S(1)}, bf16[2,256,640]{2,1,0:T(8,128)(2,1)}, u32[]{:S(2)}, u32[]{:S(2)}) collective-permute-start(bf16[2,256,640]{2,1,0:T(8,128)(2,1)S(1)} %copy-done.15), channel_id=1, source_target_pairs={{0,2},{1,3},{2,0},{3,1},{4,6},{5,7},{6,4},{7,5},{8,10},{9,11},{10,... | collective-permute-start | bytes 1966088 | tf_op jit(solution)/shard_map/ppermute | solution.py:359
  43.9 16.4 %collective-permute-start.5 = (bf16[2,256,640]{2,1,0:T(8,128)(2,1)S(1)}, bf16[2,256,640]{2,1,0:T(8,128)(2,1)S(1)}, u32[]{:S(2)}, u32[]{:S(2)}) collective-permute-start(bf16[2,256,640]{2,1,0:T(8,128)(2,1)S(1)} %copy-done.16), channel_id=1, source_target_pairs={{0,4},{1,5},{2,6},{3,7},{4,0},{5,1},{6,2},{7,3},{8,12},{9,13},{10,... | collective-permute-start | bytes 1966088 | tf_op jit(solution)/shard_map/ppermute | solution.py:359
  61.5 9.2 %collective-permute-start.3 = (bf16[256,640]{1,0:T(8,128)(2,1)S(1)}, bf16[256,640]{1,0:T(8,128)(2,1)S(1)}, u32[]{:S(2)}, u32[]{:S(2)}) collective-permute-start(bf16[256,640]{1,0:T(8,128)(2,1)S(1)} %get-tuple-element.348), channel_id=1, source_target_pairs={{0,4},{1,5},{2,6},{3,7},{4,0},{5,1},{6,2},{7,3},{8,12},{9,13},{10,... | collective-permute-start | bytes 983048 | tf_op jit(solution)/shard_map/ppermute | solution.py:359
  63.1 8.9 %collective-permute-start.7 = (bf16[256,640]{1,0:T(8,128)(2,1)S(1)}, bf16[256,640]{1,0:T(8,128)(2,1)S(1)}, u32[]{:S(2)}, u32[]{:S(2)}) collective-permute-start(bf16[256,640]{1,0:T(8,128)(2,1)S(1)} %get-tuple-element.347), channel_id=1, source_target_pairs={{0,2},{1,3},{2,0},{3,1},{4,6},{5,7},{6,4},{7,5},{8,10},{9,11},{10,... | collective-permute-start | bytes 983048 | tf_op jit(solution)/shard_map/ppermute | solution.py:359
  77.3 139.3 %all-gather.11.cloned.1.call-start = ((), (), s32[]{:S(2)}) async-start(), calls=%async_computation.1 | async-start | bytes 5898240 | tf_op jit(solution)/shard_map/all_gather | solution.py:401
  77.4 47.8 %collective-permute-start.9 = (f32[2,256,640]{2,1,0:T(8,128)}, f32[2,256,640]{2,1,0:T(8,128)}, u32[]{:S(2)}, u32[]{:S(2)}) collective-permute-start(f32[2,256,640]{2,1,0:T(8,128)} %get-tuple-element.324.refs_6_), channel_id=1, source_target_pairs={{0,4},{1,5},{2,6},{3,7},{4,0},{5,1},{6,2},{7,3},{8,12},{9,13},{10,... | collective-permute-start | bytes 3932168 | tf_op jit(solution)/shard_map/ppermute | solution.py:359
  78.2 47.0 %collective-permute-start.8 = (f32[2,256,640]{2,1,0:T(8,128)}, f32[2,256,640]{2,1,0:T(8,128)}, u32[]{:S(2)}, u32[]{:S(2)}) collective-permute-start(f32[2,256,640]{2,1,0:T(8,128)} %get-tuple-element.326.refs_5_), channel_id=1, source_target_pairs={{0,2},{1,3},{2,0},{3,1},{4,6},{5,7},{6,4},{7,5},{8,10},{9,11},{10,... | collective-permute-start | bytes 3932168 | tf_op jit(solution)/shard_map/ppermute | solution.py:359
  126.4 17.7 %collective-permute-start.11 = (f32[256,640]{1,0:T(8,128)S(1)}, f32[256,640]{1,0:T(8,128)}, u32[]{:S(2)}, u32[]{:S(2)}) collective-permute-start(f32[256,640]{1,0:T(8,128)S(1)} %fusion.26.refs_3_), channel_id=1, source_target_pairs={{0,4},{1,5},{2,6},{3,7},{4,0},{5,1},{6,2},{7,3},{8,12},{9,13},{10,... | collective-permute-start | bytes 1966088 | tf_op jit(solution)/shard_map/ppermute | solution.py:359
  130.1 14.0 %collective-permute-start.12 = (f32[256,640]{1,0:T(8,128)}, f32[256,640]{1,0:T(8,128)}, u32[]{:S(2)}, u32[]{:S(2)}) collective-permute-start(f32[256,640]{1,0:T(8,128)} %fusion.24.refs_4_), channel_id=1, source_target_pairs={{0,2},{1,3},{2,0},{3,1},{4,6},{5,7},{6,4},{7,5},{8,10},{9,11},{10,... | collective-permute-start | bytes 1966088 | tf_op jit(solution)/shard_map/ppermute | solution.py:359
  149.5 223.6 %all-gather.13.cloned.1.call-start = ((), (), s32[]{:S(2)}) async-start(), calls=%async_computation.2 | async-start | bytes 5898240 | tf_op jit(solution)/shard_map/all_gather | solution.py:401
  149.5 5.2 collective-permute-start.10
  149.6 8.9 %collective-permute-start.14 = (f32[4,256,640]{2,1,0:T(8,128)}, f32[4,256,640]{2,1,0:T(8,128)S(1)}, u32[]{:S(2)}, u32[]{:S(2)}) collective-permute-start(f32[4,256,640]{2,1,0:T(8,128)} %get-tuple-element.193), channel_id=1, source_target_pairs={{0,1},{1,0},{2,3},{3,2},{4,5},{5,4},{6,7},{7,6},{8,9},{9,8},{10,11... | collective-permute-start | bytes 7864328 | tf_op jit(solution)/shard_map/ppermute | solution.py:359
  179.4 16.8 %collective-permute-start.15 = (bf16[4,256,640]{2,1,0:T(8,128)(2,1)}, bf16[4,256,640]{2,1,0:T(8,128)(2,1)}, u32[]{:S(2)}, u32[]{:S(2)}) collective-permute-start(bf16[4,256,640]{2,1,0:T(8,128)(2,1)} %get-tuple-element.201), channel_id=1, source_target_pairs={{0,1},{1,0},{2,3},{3,2},{4,5},{5,4},{6,7},{7,6},{8,9},{9,8},{10,11... | collective-permute-start | bytes 3932168 | tf_op jit(solution)/shard_map/ppermute | solution.py:359
  179.6 19.7 %collective-permute-start.16 = (bf16[4,256,640]{2,1,0:T(8,128)(2,1)}, bf16[4,256,640]{2,1,0:T(8,128)(2,1)}, u32[]{:S(2)}, u32[]{:S(2)}) collective-permute-start(bf16[4,256,640]{2,1,0:T(8,128)(2,1)} %get-tuple-element.203), channel_id=1, source_target_pairs={{0,1},{1,0},{2,3},{3,2},{4,5},{5,4},{6,7},{7,6},{8,9},{9,8},{10,11... | collective-permute-start | bytes 3932168 | tf_op jit(solution)/shard_map/ppermute | solution.py:359
  179.9 32.7 %collective-permute-start.13 = (f32[2,256,640]{2,1,0:T(8,128)S(1)}, f32[2,256,640]{2,1,0:T(8,128)}, u32[]{:S(2)}, u32[]{:S(2)}) collective-permute-start(f32[2,256,640]{2,1,0:T(8,128)S(1)} %copy-done.3), channel_id=1, source_target_pairs={{0,2},{1,3},{2,0},{3,1},{4,6},{5,7},{6,4},{7,5},{8,10},{9,11},{10,... | collective-permute-start | bytes 3932168 | tf_op jit(solution)/shard_map/ppermute | solution.py:359
  180.0 32.6 %collective-permute-start.18 = (f32[2,256,640]{2,1,0:T(8,128)}, f32[2,256,640]{2,1,0:T(8,128)}, u32[]{:S(2)}, u32[]{:S(2)}) collective-permute-start(f32[2,256,640]{2,1,0:T(8,128)} %get-tuple-element.321.refs_6_), channel_id=1, source_target_pairs={{0,4},{1,5},{2,6},{3,7},{4,0},{5,1},{6,2},{7,3},{8,12},{9,13},{10,... | collective-permute-start | bytes 3932168 | tf_op jit(solution)/shard_map/ppermute | solution.py:359
  230.9 23.5 %collective-permute-start.22 = (bf16[4,256,640]{2,1,0:T(8,128)(2,1)}, bf16[4,256,640]{2,1,0:T(8,128)(2,1)}, u32[]{:S(2)}, u32[]{:S(2)}) collective-permute-start(bf16[4,256,640]{2,1,0:T(8,128)(2,1)} %get-tuple-element.218), channel_id=1, source_target_pairs={{0,1},{1,0},{2,3},{3,2},{4,5},{5,4},{6,7},{7,6},{8,9},{9,8},{10,11... | collective-permute-start | bytes 3932168 | tf_op jit(solution)/shard_map/ppermute | solution.py:359
  230.9 18.0 %collective-permute-start.17 = (f32[256,640]{1,0:T(8,128)}, f32[256,640]{1,0:T(8,128)}, u32[]{:S(2)}, u32[]{:S(2)}) collective-permute-start(f32[256,640]{1,0:T(8,128)} %fusion.13.refs_7_), channel_id=1, source_target_pairs={{0,4},{1,5},{2,6},{3,7},{4,0},{5,1},{6,2},{7,3},{8,12},{9,13},{10,... | collective-permute-start | bytes 1966088 | tf_op jit(solution)/shard_map/ppermute | solution.py:359
  232.4 17.9 %collective-permute-start.19 = (f32[256,640]{1,0:T(8,128)S(1)}, f32[256,640]{1,0:T(8,128)}, u32[]{:S(2)}, u32[]{:S(2)}) collective-permute-start(f32[256,640]{1,0:T(8,128)S(1)} %copy-done.13), channel_id=1, source_target_pairs={{0,2},{1,3},{2,0},{3,1},{4,6},{5,7},{6,4},{7,5},{8,10},{9,11},{10,... | collective-permute-start | bytes 1966088 | tf_op jit(solution)/shard_map/ppermute | solution.py:359
  232.9 24.4 %collective-permute-start.20 = (bf16[4,256,640]{2,1,0:T(8,128)(2,1)}, bf16[4,256,640]{2,1,0:T(8,128)(2,1)}, u32[]{:S(2)}, u32[]{:S(2)}) collective-permute-start(bf16[4,256,640]{2,1,0:T(8,128)(2,1)} %get-tuple-element.213), channel_id=1, source_target_pairs={{0,1},{1,0},{2,3},{3,2},{4,5},{5,4},{6,7},{7,6},{8,9},{9,8},{10,11... | collective-permute-start | bytes 3932168 | tf_op jit(solution)/shard_map/ppermute | solution.py:359
  232.9 29.9 %collective-permute-start.24 = (bf16[2,256,640]{2,1,0:T(8,128)(2,1)}, bf16[2,256,640]{2,1,0:T(8,128)(2,1)}, u32[]{:S(2)}, u32[]{:S(2)}) collective-permute-start(bf16[2,256,640]{2,1,0:T(8,128)(2,1)} %get-tuple-element.338.refs_6_), channel_id=1, source_target_pairs={{0,4},{1,5},{2,6},{3,7},{4,0},{5,1},{6,2},{7,3},{8,12},{9,13},{10,... | collective-permute-start | bytes 1966088 | tf_op jit(solution)/shard_map/ppermute | solution.py:359
  248.8 17.8 %collective-permute-start.23 = (bf16[2,256,640]{2,1,0:T(8,128)(2,1)}, bf16[2,256,640]{2,1,0:T(8,128)(2,1)S(1)}, u32[]{:S(2)}, u32[]{:S(2)}) collective-permute-start(bf16[2,256,640]{2,1,0:T(8,128)(2,1)} %get-tuple-element.340.refs_5_), channel_id=1, source_target_pairs={{0,2},{1,3},{2,0},{3,1},{4,6},{5,7},{6,4},{7,5},{8,10},{9,11},{10,... | collective-permute-start | bytes 1966088 | tf_op jit(solution)/shard_map/ppermute | solution.py:359
  256.8 20.4 %collective-permute-start.25 = (bf16[2,256,640]{2,1,0:T(8,128)(2,1)S(1)}, bf16[2,256,640]{2,1,0:T(8,128)(2,1)}, u32[]{:S(2)}, u32[]{:S(2)}) collective-permute-start(bf16[2,256,640]{2,1,0:T(8,128)(2,1)S(1)} %get-tuple-element.336.refs_6_), channel_id=1, source_target_pairs={{0,4},{1,5},{2,6},{3,7},{4,0},{5,1},{6,2},{7,3},{8,12},{9,13},{10,... | collective-permute-start | bytes 1966088 | tf_op jit(solution)/shard_map/ppermute | solution.py:359
  259.8 20.1 %collective-permute-start.21 = (bf16[2,256,640]{2,1,0:T(8,128)(2,1)S(1)}, bf16[2,256,640]{2,1,0:T(8,128)(2,1)}, u32[]{:S(2)}, u32[]{:S(2)}) collective-permute-start(bf16[2,256,640]{2,1,0:T(8,128)(2,1)S(1)} %get-tuple-element.341.refs_5_), channel_id=1, source_target_pairs={{0,2},{1,3},{2,0},{3,1},{4,6},{5,7},{6,4},{7,5},{8,10},{9,11},{10,... | collective-permute-start | bytes 1966088 | tf_op jit(solution)/shard_map/ppermute | solution.py:359
  281.0 8.8 %collective-permute-start.28 = (bf16[256,640]{1,0:T(8,128)(2,1)S(1)}, bf16[256,640]{1,0:T(8,128)(2,1)S(1)}, u32[]{:S(2)}, u32[]{:S(2)}) collective-permute-start(bf16[256,640]{1,0:T(8,128)(2,1)S(1)} %fusion.57), channel_id=1, source_target_pairs={{0,4},{1,5},{2,6},{3,7},{4,0},{5,1},{6,2},{7,3},{8,12},{9,13},{10,... | collective-permute-start | bytes 983048 | tf_op jit(solution)/shard_map/ppermute | solution.py:359
  282.7 8.3 %collective-permute-start.29 = (bf16[256,640]{1,0:T(8,128)(2,1)S(1)}, bf16[256,640]{1,0:T(8,128)(2,1)S(1)}, u32[]{:S(2)}, u32[]{:S(2)}) collective-permute-start(bf16[256,640]{1,0:T(8,128)(2,1)S(1)} %fusion.52), channel_id=1, source_target_pairs={{0,2},{1,3},{2,0},{3,1},{4,6},{5,7},{6,4},{7,5},{8,10},{9,11},{10,... | collective-permute-start | bytes 983048 | tf_op jit(solution)/shard_map/ppermute | solution.py:359
  295.5 116.6 %all-gather.19.cloned.1.call-start = ((), (), s32[]{:S(2)}) async-start(), calls=%async_computation.5 | async-start | bytes 5898240 | tf_op jit(solution)/shard_map/all_gather | solution.py:401
  295.6 12.1 %collective-permute-start.30 = (bf16[256,640]{1,0:T(8,128)(2,1)S(1)}, bf16[256,640]{1,0:T(8,128)(2,1)S(1)}, u32[]{:S(2)}, u32[]{:S(2)}) collective-permute-start(bf16[256,640]{1,0:T(8,128)(2,1)S(1)} %copy-done.44), channel_id=1, source_target_pairs={{0,4},{1,5},{2,6},{3,7},{4,0},{5,1},{6,2},{7,3},{8,12},{9,13},{10,... | collective-permute-start | bytes 983048 | tf_op jit(solution)/shard_map/ppermute | solution.py:359
  297.3 10.4 %collective-permute-start.31 = (bf16[256,640]{1,0:T(8,128)(2,1)S(1)}, bf16[256,640]{1,0:T(8,128)(2,1)}, u32[]{:S(2)}, u32[]{:S(2)}) collective-permute-start(bf16[256,640]{1,0:T(8,128)(2,1)S(1)} %copy-done.43), channel_id=1, source_target_pairs={{0,2},{1,3},{2,0},{3,1},{4,6},{5,7},{6,4},{7,5},{8,10},{9,11},{10,... | collective-permute-start | bytes 983048 | tf_op jit(solution)/shard_map/ppermute | solution.py:359
  314.8 194.6 %all-gather.21.cloned.1.call-start = ((), (), s32[]{:S(2)}) async-start(), calls=%async_computation.6 | async-start | bytes 5898240 | tf_op jit(solution)/shard_map/all_gather | solution.py:401
  314.9 43.4 %collective-permute-start.27 = (f32[256,1280]{1,0:T(8,128)S(1)}, f32[256,1280]{1,0:T(8,128)S(1)}, u32[]{:S(2)}, u32[]{:S(2)}) collective-permute-start(f32[256,1280]{1,0:T(8,128)S(1)} %bitcast.351), channel_id=1, source_target_pairs={{0,2},{1,3},{2,0},{3,1},{4,6},{5,7},{6,4},{7,5},{8,10},{9,11},{10,... | collective-permute-start | bytes 3932168 | tf_op jit(solution)/shard_map/ppermute | solution.py:359
  316.6 43.8 %collective-permute-start.33 = (f32[256,1280]{1,0:T(8,128)S(1)}, f32[256,1280]{1,0:T(8,128)}, u32[]{:S(2)}, u32[]{:S(2)}) collective-permute-start(f32[256,1280]{1,0:T(8,128)S(1)} %bitcast.352), channel_id=1, source_target_pairs={{0,4},{1,5},{2,6},{3,7},{4,0},{5,1},{6,2},{7,3},{8,12},{9,13},{10,... | collective-permute-start | bytes 3932168 | tf_op jit(solution)/shard_map/ppermute | solution.py:359
  317.0 68.0 %collective-permute-start.26 = (f32[256,1280]{1,0:T(8,128)S(1)}, f32[256,1280]{1,0:T(8,128)}, u32[]{:S(2)}, u32[]{:S(2)}) collective-permute-start(f32[256,1280]{1,0:T(8,128)S(1)} %bitcast.353), channel_id=1, source_target_pairs={{0,1},{1,0},{2,3},{3,2},{4,5},{5,4},{6,7},{7,6},{8,9},{9,8},{10,11... | collective-permute-start | bytes 3932168 | tf_op jit(solution)/shard_map/ppermute | solution.py:359
  359.2 25.3 %collective-permute-start.36 = (f32[256,640]{1,0:T(8,128)}, f32[256,640]{1,0:T(8,128)S(1)}, u32[]{:S(2)}, u32[]{:S(2)}) collective-permute-start(f32[256,640]{1,0:T(8,128)} %slice.509), channel_id=1, source_target_pairs={{0,4},{1,5},{2,6},{3,7},{4,0},{5,1},{6,2},{7,3},{8,12},{9,13},{10,... | collective-permute-start | bytes 1966088 | tf_op jit(solution)/shard_map/ppermute | solution.py:359
  362.4 22.1 %collective-permute-start.35 = (f32[256,640]{1,0:T(8,128)}, f32[256,640]{1,0:T(8,128)}, u32[]{:S(2)}, u32[]{:S(2)}) collective-permute-start(f32[256,640]{1,0:T(8,128)} %slice.508), channel_id=1, source_target_pairs={{0,2},{1,3},{2,0},{3,1},{4,6},{5,7},{6,4},{7,5},{8,10},{9,11},{10,... | collective-permute-start | bytes 1966088 | tf_op jit(solution)/shard_map/ppermute | solution.py:359
  363.6 21.4 %collective-permute-start.34 = (f32[256,1280]{1,0:T(8,128)}, f32[256,1280]{1,0:T(8,128)}, u32[]{:S(2)}, u32[]{:S(2)}) collective-permute-start(f32[256,1280]{1,0:T(8,128)} %collective-permute-done.33.refs_4_.refs_5_), channel_id=1, source_target_pairs={{0,1},{1,0},{2,3},{3,2},{4,5},{5,4},{6,7},{7,6},{8,9},{9,8},{10,11... | collective-permute-start | bytes 3932168 | tf_op jit(solution)/shard_map/ppermute | solution.py:359
  363.6 21.4 %collective-permute-start.32 = (f32[256,1280]{1,0:T(8,128)S(1)}, f32[256,1280]{1,0:T(8,128)}, u32[]{:S(2)}, u32[]{:S(2)}) collective-permute-start(f32[256,1280]{1,0:T(8,128)S(1)} %collective-permute-done.27.refs_3_.refs_4_.refs_2_), channel_id=1, source_target_pairs={{0,1},{1,0},{2,3},{3,2},{4,5},{5,4},{6,7},{7,6},{8,9},{9,8},{10,11... | collective-permute-start | bytes 3932168 | tf_op jit(solution)/shard_map/ppermute | solution.py:359
  424.3 12.7 %collective-permute-start.39 = (bf16[4,256,640]{2,1,0:T(8,128)(2,1)}, bf16[4,256,640]{2,1,0:T(8,128)(2,1)S(1)}, u32[]{:S(2)}, u32[]{:S(2)}) collective-permute-start(bf16[4,256,640]{2,1,0:T(8,128)(2,1)} %get-tuple-element.260), channel_id=1, source_target_pairs={{0,1},{1,0},{2,3},{3,2},{4,5},{5,4},{6,7},{7,6},{8,9},{9,8},{10,11... | collective-permute-start | bytes 3932168 | tf_op jit(solution)/shard_map/ppermute | solution.py:359
  424.4 15.6 %collective-permute-start.41 = (bf16[4,256,640]{2,1,0:T(8,128)(2,1)}, bf16[4,256,640]{2,1,0:T(8,128)(2,1)S(1)}, u32[]{:S(2)}, u32[]{:S(2)}) collective-permute-start(bf16[4,256,640]{2,1,0:T(8,128)(2,1)} %get-tuple-element.266), channel_id=1, source_target_pairs={{0,1},{1,0},{2,3},{3,2},{4,5},{5,4},{6,7},{7,6},{8,9},{9,8},{10,11... | collective-permute-start | bytes 3932168 | tf_op jit(solution)/shard_map/ppermute | solution.py:359
  440.0 16.9 %collective-permute-start.40 = (bf16[2,256,640]{2,1,0:T(8,128)(2,1)S(1)}, bf16[2,256,640]{2,1,0:T(8,128)(2,1)}, u32[]{:S(2)}, u32[]{:S(2)}) collective-permute-start(bf16[2,256,640]{2,1,0:T(8,128)(2,1)S(1)} %get-tuple-element.332.refs_4_), channel_id=1, source_target_pairs={{0,2},{1,3},{2,0},{3,1},{4,6},{5,7},{6,4},{7,5},{8,10},{9,11},{10,... | collective-permute-start | bytes 1966088 | tf_op jit(solution)/shard_map/ppermute | solution.py:359
  440.8 19.2 %collective-permute-start.43 = (bf16[2,256,640]{2,1,0:T(8,128)(2,1)S(1)}, bf16[2,256,640]{2,1,0:T(8,128)(2,1)S(1)}, u32[]{:S(2)}, u32[]{:S(2)}) collective-permute-start(bf16[2,256,640]{2,1,0:T(8,128)(2,1)S(1)} %get-tuple-element.333.refs_5_), channel_id=1, source_target_pairs={{0,4},{1,5},{2,6},{3,7},{4,0},{5,1},{6,2},{7,3},{8,12},{9,13},{10,... | collective-permute-start | bytes 1966088 | tf_op jit(solution)/shard_map/ppermute | solution.py:359
  457.9 9.3 %collective-permute-start.42 = (bf16[256,640]{1,0:T(8,128)(2,1)S(1)}, bf16[256,640]{1,0:T(8,128)(2,1)S(1)}, u32[]{:S(2)}, u32[]{:S(2)}) collective-permute-start(bf16[256,640]{1,0:T(8,128)(2,1)S(1)} %fusion.43), channel_id=1, source_target_pairs={{0,4},{1,5},{2,6},{3,7},{4,0},{5,1},{6,2},{7,3},{8,12},{9,13},{10,... | collective-permute-start | bytes 983048 | tf_op jit(solution)/shard_map/ppermute | solution.py:359
  460.1 8.6 %collective-permute-start.44 = (bf16[256,640]{1,0:T(8,128)(2,1)S(1)}, bf16[256,640]{1,0:T(8,128)(2,1)S(1)}, u32[]{:S(2)}, u32[]{:S(2)}) collective-permute-start(bf16[256,640]{1,0:T(8,128)(2,1)S(1)} %fusion.40), channel_id=1, source_target_pairs={{0,2},{1,3},{2,0},{3,1},{4,6},{5,7},{6,4},{7,5},{8,10},{9,11},{10,... | collective-permute-start | bytes 983048 | tf_op jit(solution)/shard_map/ppermute | solution.py:359
  473.1 159.3 %all-gather.17.cloned.1.call-start = ((), (), s32[]{:S(2)}) async-start(), calls=%async_computation.4 | async-start | bytes 3686400 | tf_op jit(solution)/shard_map/all_gather | solution.py:401
  475.3 157.1 %all-gather.15.cloned.1.call-start = ((), (), s32[]{:S(2)}) async-start(), calls=%async_computation.3 | async-start | bytes 5898240 | tf_op jit(solution)/shard_map/all_gather | solution.py:401
  476.0 194.6 %all-gather.23.cloned.1.call-start = ((), (), s32[]{:S(2)}) async-start(), calls=%async_computation.7 | async-start | bytes 11796480 | tf_op jit(solution)/shard_map/all_gather | solution.py:401
  520.5 11.6 %collective-permute-start.46 = (bf16[4,256,640]{2,1,0:T(8,128)(2,1)}, bf16[4,256,640]{2,1,0:T(8,128)(2,1)S(1)}, u32[]{:S(2)}, u32[]{:S(2)}) collective-permute-start(bf16[4,256,640]{2,1,0:T(8,128)(2,1)} %get-tuple-element.288), channel_id=1, source_target_pairs={{0,1},{1,0},{2,3},{3,2},{4,5},{5,4},{6,7},{7,6},{8,9},{9,8},{10,11... | collective-permute-start | bytes 3932168 | tf_op jit(solution)/shard_map/ppermute | solution.py:359
  520.8 15.7 %collective-permute-start.45 = (bf16[4,256,640]{2,1,0:T(8,128)(2,1)}, bf16[4,256,640]{2,1,0:T(8,128)(2,1)}, u32[]{:S(2)}, u32[]{:S(2)}) collective-permute-start(bf16[4,256,640]{2,1,0:T(8,128)(2,1)} %get-tuple-element.286), channel_id=1, source_target_pairs={{0,1},{1,0},{2,3},{3,2},{4,5},{5,4},{6,7},{7,6},{8,9},{9,8},{10,11... | collective-permute-start | bytes 3932168 | tf_op jit(solution)/shard_map/ppermute | solution.py:359
  535.2 19.2 %collective-permute-start.48 = (bf16[2,256,640]{2,1,0:T(8,128)(2,1)S(1)}, bf16[2,256,640]{2,1,0:T(8,128)(2,1)}, u32[]{:S(2)}, u32[]{:S(2)}) collective-permute-start(bf16[2,256,640]{2,1,0:T(8,128)(2,1)S(1)} %get-tuple-element.328.refs_8_), channel_id=1, source_target_pairs={{0,4},{1,5},{2,6},{3,7},{4,0},{5,1},{6,2},{7,3},{8,12},{9,13},{10,... | collective-permute-start | bytes 1966088 | tf_op jit(solution)/shard_map/ppermute | solution.py:359
  538.8 22.2 %collective-permute-start.47 = (bf16[2,256,640]{2,1,0:T(8,128)(2,1)S(1)}, bf16[2,256,640]{2,1,0:T(8,128)(2,1)}, u32[]{:S(2)}, u32[]{:S(2)}) collective-permute-start(bf16[2,256,640]{2,1,0:T(8,128)(2,1)S(1)} %get-tuple-element.330.refs_7_), channel_id=1, source_target_pairs={{0,2},{1,3},{2,0},{3,1},{4,6},{5,7},{6,4},{7,5},{8,10},{9,11},{10,... | collective-permute-start | bytes 1966088 | tf_op jit(solution)/shard_map/ppermute | solution.py:359
  562.1 8.7 %collective-permute-start.49 = (bf16[256,640]{1,0:T(8,128)(2,1)S(1)}, bf16[256,640]{1,0:T(8,128)(2,1)S(1)}, u32[]{:S(2)}, u32[]{:S(2)}) collective-permute-start(bf16[256,640]{1,0:T(8,128)(2,1)S(1)} %fusion.39.refs_4_), channel_id=1, source_target_pairs={{0,4},{1,5},{2,6},{3,7},{4,0},{5,1},{6,2},{7,3},{8,12},{9,13},{10,... | collective-permute-start | bytes 983048 | tf_op jit(solution)/shard_map/ppermute | solution.py:359
  563.3 15.1 %collective-permute-start.50 = (bf16[256,640]{1,0:T(8,128)(2,1)S(1)}, bf16[256,640]{1,0:T(8,128)(2,1)S(1)}, u32[]{:S(2)}, u32[]{:S(2)}) collective-permute-start(bf16[256,640]{1,0:T(8,128)(2,1)S(1)} %fusion.37.refs_5_), channel_id=1, source_target_pairs={{0,2},{1,3},{2,0},{3,1},{4,6},{5,7},{6,4},{7,5},{8,10},{9,11},{10,... | collective-permute-start | bytes 983048 | tf_op jit(solution)/shard_map/ppermute | solution.py:359
  582.2 43.8 %collective-permute-start.52 = (f32[256,1280]{1,0:T(8,128)S(1)}, f32[256,1280]{1,0:T(8,128)S(1)}, u32[]{:S(2)}, u32[]{:S(2)}) collective-permute-start(f32[256,1280]{1,0:T(8,128)S(1)} %bitcast.360), channel_id=1, source_target_pairs={{0,2},{1,3},{2,0},{3,1},{4,6},{5,7},{6,4},{7,5},{8,10},{9,11},{10,... | collective-permute-start | bytes 3932168 | tf_op jit(solution)/shard_map/ppermute | solution.py:359
  584.7 43.2 %collective-permute-start.54 = (f32[256,1280]{1,0:T(8,128)S(1)}, f32[256,1280]{1,0:T(8,128)}, u32[]{:S(2)}, u32[]{:S(2)}) collective-permute-start(f32[256,1280]{1,0:T(8,128)S(1)} %bitcast.361), channel_id=1, source_target_pairs={{0,4},{1,5},{2,6},{3,7},{4,0},{5,1},{6,2},{7,3},{8,12},{9,13},{10,... | collective-permute-start | bytes 3932168 | tf_op jit(solution)/shard_map/ppermute | solution.py:359
  626.9 22.7 %collective-permute-start.57 = (f32[256,640]{1,0:T(8,128)}, f32[256,640]{1,0:T(8,128)S(1)}, u32[]{:S(2)}, u32[]{:S(2)}) collective-permute-start(f32[256,640]{1,0:T(8,128)} %slice.548), channel_id=1, source_target_pairs={{0,4},{1,5},{2,6},{3,7},{4,0},{5,1},{6,2},{7,3},{8,12},{9,13},{10,... | collective-permute-start | bytes 1966088 | tf_op jit(solution)/shard_map/ppermute | solution.py:359
  629.9 23.6 %collective-permute-start.56 = (f32[256,640]{1,0:T(8,128)}, f32[256,640]{1,0:T(8,128)}, u32[]{:S(2)}, u32[]{:S(2)}) collective-permute-start(f32[256,640]{1,0:T(8,128)} %slice.547), channel_id=1, source_target_pairs={{0,2},{1,3},{2,0},{3,1},{4,6},{5,7},{6,4},{7,5},{8,10},{9,11},{10,... | collective-permute-start | bytes 1966088 | tf_op jit(solution)/shard_map/ppermute | solution.py:359
  631.9 21.6 %collective-permute-start.51 = (f32[256,1280]{1,0:T(8,128)S(1)}, f32[256,1280]{1,0:T(8,128)}, u32[]{:S(2)}, u32[]{:S(2)}) collective-permute-start(f32[256,1280]{1,0:T(8,128)S(1)} %bitcast.362), channel_id=1, source_target_pairs={{0,1},{1,0},{2,3},{3,2},{4,5},{5,4},{6,7},{7,6},{8,9},{9,8},{10,11... | collective-permute-start | bytes 3932168 | tf_op jit(solution)/shard_map/ppermute | solution.py:359
  631.9 24.8 %collective-permute-start.55 = (f32[256,1280]{1,0:T(8,128)}, f32[256,1280]{1,0:T(8,128)}, u32[]{:S(2)}, u32[]{:S(2)}) collective-permute-start(f32[256,1280]{1,0:T(8,128)} %collective-permute-done.54.refs_4_), channel_id=1, source_target_pairs={{0,1},{1,0},{2,3},{3,2},{4,5},{5,4},{6,7},{7,6},{8,9},{9,8},{10,11... | collective-permute-start | bytes 3932168 | tf_op jit(solution)/shard_map/ppermute | solution.py:359
  632.4 24.3 %collective-permute-start.53 = (f32[256,1280]{1,0:T(8,128)S(1)}, f32[256,1280]{1,0:T(8,128)}, u32[]{:S(2)}, u32[]{:S(2)}) collective-permute-start(f32[256,1280]{1,0:T(8,128)S(1)} %collective-permute-done.52.refs_2_), channel_id=1, source_target_pairs={{0,1},{1,0},{2,3},{3,2},{4,5},{5,4},{6,7},{7,6},{8,9},{9,8},{10,11... | collective-permute-start | bytes 3932168 | tf_op jit(solution)/shard_map/ppermute | solution.py:359
  (59 other events, 544.0 us)
Sparse Core Ops, SparseCore 0:
  77.5 55.6 all-gather.8
  149.6 38.1 all-gather.10
  295.6 51.3 all-gather.12
  348.7 46.3 all-gather.18
  473.2 36.1 all-gather.20
  511.1 29.5 all-gather.16
  542.5 50.4 all-gather.14
  595.4 75.1 all-gather.22

commit v6 on v5

--- a/solution.py
+++ b/solution.py
@@ -61,7 +61,9 @@
                 return pl.BlockSpec((shape[0], shape[1] // seqs), lambda g, rk: (0, seq(g, rk)))
             if kind == "layer":
                 return pl.BlockSpec((None,) + tuple(shape[1:]), lambda g, rk: (layer, 0, 0))
-            return pl.BlockSpec(tuple(shape), lambda g, rk: (0,) * len(shape))
+            if kind == "tail":
+                return pl.BlockSpec((shape[0], layer), lambda g, rk: (0, shape[1] // layer - seqs + seq(g, rk)))
+            return pl.BlockSpec((shape[0], layer), lambda g, rk: (0, 0))
 
         hidden = list(previous) + list(after)
         in_specs = [spec(kind, arr.shape, *layer) for kind, arr, *layer in ins] + [pl.BlockSpec(memory_space=pl.ANY)] * len(hidden)
@@ -256,14 +258,16 @@
     return seq_call(body, rank, ins, outs, [(rows, width, BF)] if backward else [], flops, after)
 
 
-def attn_value(rank, base, o_all, wo_all, after=()):
-    def body(in_refs, out_refs):
-        base_ref, o_ref, w_ref = in_refs
+def attn_value(rank, base, both, after=()):
+    _, rows, width = base.shape
+
+    def body(in_refs, out_refs):
+        base_ref, w_ref, o_ref = in_refs
         out_refs[0][...] = base_ref[...] - dot_tn(o_ref[...], w_ref[...])
         return ()
 
-    ins = [("row", base), ("col", o_all), ("all", wo_all)]
-    return seq_call(body, rank, ins, [("row", base.shape, F32)], [], 2 * base.size * wo_all.shape[0], after)
+    ins = [("row", base), ("head", both, width), ("tail", both, rows)]
+    return seq_call(body, rank, ins, [("row", base.shape, F32)], [], 2 * base.size * both.shape[0], after)
 
 
 def assemble(rank, pieces, after=()):
@@ -474,7 +478,6 @@
         )
         sum_hi, sent = sum_first(sum_cores(parts))
         value_low, sent_low, final_low = sum_second(sum_out, [tok, *sent])
-        wo_all = gather(tie(o_w[lo], [f_top]))
         o_top, dqkv_top, *parts, tok = attn(rank, head_dim, qkv_w, o_w, top, x=f_top, d=d_one_bf, after=[tok, *sent, *sent_low])
         x_two = shard(s_two) - sum_end(value_low, final_low, [tok])
         sum_top, sent = sum_first(sum_cores(parts))
@@ -497,7 +500,7 @@
         pieces = spread_last(x_two_shard, near, far, cross, [tok])
         x_two_full, tok = assemble(rank, pieces, [tok])
         f_lo, o_lo, qkv_lo, tok = attn(rank, head_dim, qkv_w, o_w, lo, x=x_two_full, norm=True, after=[tok])
-        o_all = gather(o_lo)
+        both = gather(jnp.concatenate([o_w[lo], o_lo], axis=1))
         dh_lo, *parts, tok = mlp_pair_back(rank, d_two_lo_bf, w_out, sl_lo, dh_hi, w_in, hi, lo, [tok])
         sum_g, sent = sum_first(sum_cores(parts))
         tok = mlp_grad("in", lo, s_a, dh_lo, [tok, *sent])
@@ -516,7 +519,7 @@
         value, sent, final = sum_second(sum_lo, [tok])
         d_two = d_two + rms_vjp(x_two, sum_end(value, final))
         far, cross = spread_second(near, [tok, *sent])
-        x_one_full, tok = attn_value(rank, s_one, o_all, wo_all, [tok, *sent, d_two])
+        x_one_full, tok = attn_value(rank, s_one, both, [tok, *sent, d_two])
         pieces = spread_last(d_one_shard, near, far, cross, [tok])
         d_one_full, _ = assemble(rank, pieces, [tok])
         grad_qkv = stacks["attn"][0].reshape(n_layers, 3, n_heads, head_dim, width).transpose(0, 4, 1, 2, 3)

time: 698 us -> 708 us (1.014)
  waiting for transfers between devices: 192 us -> 207 us
    ppermute x60, waiting for transfers between devices: 181 us -> 201 us  [permute(): return lax.ppermute(array, 'tp', [(idx, idx ^ bit) for idx in range(8)])]
  transfers between devices with their start and end apart: 68 -> 67, of which waited for: 28 -> 28; matrix products, arithmetic and copies ran while one was open for 12% -> 12% of each run, Pallas kernels for 39% -> 39%
where the time goes in v6:
time: 708 us; the launch traced here: 696 us
  Pallas kernels  313 us (44%)
  waiting for transfers between devices  207 us (29%)
  other arithmetic  92.4 us (13%)
  starting transfers between devices  46.4 us (7%)
  local copies, waits for them, and re-layouts  22.4 us (3%)
  between operations  15 us (2%)
    pallas_call x18, Pallas kernels, run(): pl.pallas_call(kernel, grid_spec=pltpu.PrefetchScalarGridSpec(num_scalar_...  211 us
    ppermute x60, waiting for transfers between devices, permute(): return lax.ppermute(array, 'tp', [(idx, idx ^ bit) for idx in range(8)])  201 us
    pallas_call x9, Pallas kernels, weight_grads(): *stacks, token = call(*args)  83.4 us
    ppermute x60, starting transfers between devices, permute(): return lax.ppermute(array, 'tp', [(idx, idx ^ bit) for idx in range(8)])  46.1 us
    add x11, other arithmetic, sum_first(): pick(keep, 0) + pick(recv, 0)  28.5 us
    pallas_call x2, Pallas kernels, assemble(): pl.pallas_call(kernel, grid_spec=pltpu.PrefetchScalarGridSpec(num_scalar_...  18.3 us
    add x13, other arithmetic, sum_second(): sent.append(here[1] + recv[1])  16.5 us
    unnamed x111, local copies, waits for them, and re-layouts  15 us
  transfers between devices with their start and end apart: 67, of which 28 were waited for; matrix products, arithmetic and copies ran while one was open for 12% of the time, Pallas kernels for 39%

profile of v6, /device:TPU:0, one launch (start us, length us, event | category | flops | bytes accessed | tf_op | source)
XLA Modules:
  0.0 695.7 jit_solution(14611427245375301792)
XLA Ops:
  7.2 11.5 %shard_map.161 = (bf16[8,256,1280]{2,1,0:T(8,128)(2,1)}, bf16[8,256,640]{2,1,0:T(8,128)(2,1)}, bf16[8,256,640]{2,1,0:T(8,128)(2,1)}, bf16[8,256,1280]{2,1,0:T(8,...) custom-call(s32[1]{0:T(128)} %bitcast.rank_ref, f32[8,256,1280]{2,1,0:T(8,128)} %refs_0_.3, ...), custom_call_target="tpu_custom_call" | custom-call | flops 5033164800 | bytes 9177088 | tf_op jit(solution)/shard_map/pallas_call | solution.py:93
  19.5 11.5 %shard_map.162 = (bf16[8,256,1280]{2,1,0:T(8,128)(2,1)}, bf16[8,256,640]{2,1,0:T(8,128)(2,1)}, bf16[8,256,640]{2,1,0:T(8,128)(2,1)}, bf16[8,256,1280]{2,1,0:T(8,...) custom-call(s32[1]{0:T(128)} %bitcast.rank_ref, ...), custom_call_target="tpu_custom_call", output_to_operand_aliasing={{0}: (5, {}), {1}: (6, {}), {2}: (7, {}), {3}: (8, {})} | custom-call | flops 5033164800 | bytes 9177088 | tf_op jit(solution)/shard_map/pallas_call | solution.py:93
  31.0 2.4 slice_add_fusion.25
  34.4 6.0 shard_map.163
  40.9 2.9 collective-permute-start.2
  46.9 5.8 shard_map.164
  52.6 6.3 collective-permute-done.2
  63.6 4.0 bitcast_add_fusion.2
  67.6 3.1 slice_add_fusion.2
  73.9 3.4 fusion.68
  79.5 17.7 %shard_map.165 = (bf16[8,256,1280]{2,1,0:T(8,128)(2,1)}, f32[8,256,640]{2,1,0:T(8,128)}, bf16[8,256,640]{2,1,0:T(8,128)(2,1)}, f32[8,256,640]{2,1,0:T(8,128)}, b...) custom-call(s32[1]{0:T(128)} %bitcast.rank_ref, f32[8,256,1280]{2,1,0:T(8,128)} %bitcast.355, ...), custom_call_target="tpu_custom_call" | custom-call | flops 6710886400 | bytes 20975616 | tf_op jit(solution)/shard_map/pallas_call | solution.py:93
  97.1 28.1 %collective-permute-done.9 = f32[2,256,640]{2,1,0:T(8,128)} collective-permute-done((f32[2,256,640]{2,1,0:T(8,128)}, f32[2,256,640]{2,1,0:T(8,128)}, u32[]{:S(2)}, u32[]{:S(2)}) %collective-permute-start.9) | collective-permute-done | bytes 1310752 | tf_op jit(solution)/shard_map/ppermute | solution.py:363
  130.2 2.5 collective-permute-start.12
  132.6 5.7 shard_map.166
  138.4 5.8 shard_map.167
  150.1 4.6 collective-permute-done.10
  154.8 3.7 collective-permute-done.14
  158.5 3.8 slice_add_fusion.1
  164.1 15.5 %shard_map.168 = (bf16[8,256,1280]{2,1,0:T(8,128)(2,1)}, bf16[160,2048]{1,0:T(8,128)(2,1)}, bf16[480,2048]{1,0:T(8,128)(2,1)}, bf16[4,256,640]{2,1,0:T(8,128)(2,...) custom-call(s32[1]{0:T(128)} %bitcast.rank_ref, bf16[3,480,1280]{2,1,0:T(8,128)(2,1)} %bitcast.325, ...), custom_call_target="tpu_custom_call" | custom-call | flops 3523215360 | bytes 5244928 | tf_op jit(solution)/shard_map/pallas_call | solution.py:93
  181.2 15.1 %shard_map.169 = (bf16[8,256,1280]{2,1,0:T(8,128)(2,1)}, bf16[160,2048]{1,0:T(8,128)(2,1)}, bf16[480,2048]{1,0:T(8,128)(2,1)}, bf16[4,256,640]{2,1,0:T(8,128)(2,...) custom-call(s32[1]{0:T(128)} %bitcast.rank_ref, ...), custom_call_target="tpu_custom_call", output_to_operand_aliasing={{0}: (5, {}), {1}: (6, {}), {2}: (7, {})} | custom-call | flops 3523215360 | bytes 5244928 | tf_op jit(solution)/shard_map/pallas_call | solution.py:93
  196.4 3.0 slice_add_fusion.14
  199.4 2.6 slice_add_fusion.13
  202.0 10.7 %collective-permute-done.13 = f32[2,256,640]{2,1,0:T(8,128)} collective-permute-done((f32[2,256,640]{2,1,0:T(8,128)S(1)}, f32[2,256,640]{2,1,0:T(8,128)}, u32[]{:S(2)}, u32[]{:S(2)}) %collective-permute-start.13) | collective-permute-done | bytes 1310752 | tf_op jit(solution)/shard_map/ppermute | solution.py:363
  216.7 14.2 %shard_map.170 = (bf16[160,2048]{1,0:T(8,128)(2,1)}, bf16[480,2048]{1,0:T(8,128)(2,1)}, bf16[4,256,640]{2,1,0:T(8,128)(2,1)}, bf16[4,256,640]{2,1,0:T(8,128)(2,1)}, f32[8,128]{1,0:T(8,128)}) custom-call(s32[1]{0:T(128)} %bitcast.rank_ref, bf16[3,480,1280]{2,1,0:T(8,128)(2,1)} %bitcast.327, bf16[8,256,1280]{2,1,0:T(8,128)(2,1)} %all-gather.10.cloned.1.call-done.refs_1_, ...), custom_call_target="tpu_custom_call" | custom-call | flops 3523215360 | bytes 2623488 | tf_op jit(solution)/shard_map/pallas_call | solution.py:93
  234.4 14.2 %shard_map.171 = (bf16[160,2048]{1,0:T(8,128)(2,1)}, bf16[480,2048]{1,0:T(8,128)(2,1)}, bf16[4,256,640]{2,1,0:T(8,128)(2,1)}, bf16[4,256,640]{2,1,0:T(8,128)(2,1)}, f32[8,128]{1,0:T(8,128)}) custom-call(s32[1]{0:T(128)} %bitcast.rank_ref, bf16[3,480,1280]{2,1,0:T(8,128)(2,1)} %bitcast.328, ...), custom_call_target="tpu_custom_call", output_to_operand_aliasing={{0}: (5, {}), {1}: (6, {})} | custom-call | flops 3523215360 | bytes 2623488 | tf_op jit(solution)/shard_map/pallas_call | solution.py:93
  252.0 2.3 fusion.10
  254.4 2.4 slice_add_fusion.12
  257.4 2.4 fusion.7
  267.7 9.5 %shard_map.172 = (f32[3,480,1280]{2,1,0:T(8,128)}, f32[3,160,1280]{2,1,0:T(8,128)}, f32[8,128]{1,0:T(8,128)}) custom-call(bf16[480,2048]{1,0:T(8,128)(2,1)} %get-tuple-element.213.refs_0_, bf16[2048,1280]{1,0:T(8,128)(2,1)} %bitcast.350, bf16[160,2048]{1,0:T(8,128)(2,1)} %get-tuple-element.215.refs_2_, bf16[2048,1280]{1,0:T(8,128)(2,1)} %bitcast.323, ...), custom_call_target="tpu_custom_call" | custom-call | flops 3355443200 | bytes 27852800 | tf_op jit(solution)/shard_map/pallas_call | solution.py:358
  277.2 2.7 collective-permute-done.21
  286.0 3.9 collective-permute-done.28
  292.5 3.0 fusion.66
  297.7 10.0 %shard_map.173 = (f32[3,480,1280]{2,1,0:T(8,128)}, f32[3,160,1280]{2,1,0:T(8,128)}, f32[8,128]{1,0:T(8,128)}) custom-call(bf16[480,2048]{1,0:T(8,128)(2,1)} %get-tuple-element.225.refs_0_, bf16[2048,1280]{1,0:T(8,128)(2,1)} %bitcast.342, bf16[160,2048]{1,0:T(8,128)(2,1)} %get-tuple-element.226.refs_2_, ...), custom_call_target="tpu_custom_call", output_to_operand_aliasing={{0}: (4, {}), {1}: (5, {})} | custom-call | flops 3355443200 | bytes 27852800 | tf_op jit(solution)/shard_map/pallas_call | solution.py:358
  311.9 2.9 fusion.65
  317.1 8.8 %shard_map.174 = (f32[3,640,1280]{2,1,0:T(8,128)}, f32[8,128]{1,0:T(8,128)}) custom-call(bf16[2048,640]{1,0:T(8,128)(2,1)} %bitcast.344, bf16[2048,1280]{1,0:T(8,128)(2,1)} %bitcast.361, f32[8,128]{1,0:T(8,128)} %get-tuple-element.232.refs_2_, bf16[1,256,1280]{2,1,0:T(8,128)(2,1)} %get-tuple-element.236.refs_3_), custom_call_target="tpu_custom_call" | custom-call | flops 3355443200 | bytes 17367040 | tf_op jit(solution)/shard_map/pallas_call | solution.py:358
  325.9 32.5 %collective-permute-done.27.refs_3_.refs_4_.refs_2_ = f32[256,1280]{1,0:T(8,128)S(1)} collective-permute-done((f32[256,1280]{1,0:T(8,128)S(1)}, f32[256,1280]{1,0:T(8,128)S(1)}, u32[]{:S(2)}, u32[]{:S(2)}) %collective-permute-start.27) | collective-permute-done | bytes 1310752 | tf_op jit(solution)/shard_map/ppermute | solution.py:363
  364.2 8.9 %shard_map.175 = (f32[3,1280,640]{2,1,0:T(8,128)}, f32[8,128]{1,0:T(8,128)}) custom-call(bf16[2048,1280]{1,0:T(8,128)(2,1)} %bitcast.360, bf16[2048,640]{1,0:T(8,128)(2,1)} %bitcast.366, f32[8,128]{1,0:T(8,128)} %get-tuple-element.237.refs_2_, f32[256,1280]{1,0:T(8,128)} %copy-done.2, f32[256,1280]{1,0:T(8,128)} %collective-permute-done.33.refs_4_.refs_5_), custom_call_target="tpu_custom_call" | custom-call | flops 3355443200 | bytes 17367040 | tf_op jit(solution)/shard_map/pallas_call | solution.py:358
  373.2 11.2 %shard_map.176 = (bf16[8,256,640]{2,1,0:T(8,128)(2,1)}, f32[8,128]{1,0:T(8,128)}) custom-call(s32[1]{0:T(128)} %bitcast.rank_ref, bf16[8,256,1280]{2,1,0:T(8,128)(2,1)} %all-gather.12.cloned.1.call-done.refs_0_, bf16[3,640,1280]{2,1,0:T(8,128)(2,1)} %refs_1_.19, f32[8,256,640]{2,1,0:T(8,128)} %get-tuple-element.240.refs_2_, ...), custom_call_target="tpu_custom_call" | custom-call | flops 3355443200 | bytes 2625536 | tf_op jit(solution)/shard_map/pallas_call | solution.py:93
  387.8 9.2 %shard_map.177 = (f32[8,256,1280]{2,1,0:T(8,128)}, f32[8,128]{1,0:T(8,128)}) custom-call(s32[1]{0:T(128)} %bitcast.rank_ref, f32[256,1280]{1,0:T(8,128)} %bitcast.354, f32[256,1280]{1,0:T(8,128)} %collective-permute-done.26.refs_1_, f32[256,1280]{1,0:T(8,128)} %copy-done.2, f32[256,1280]{1,0:T(8,128)} %collective-permute-done.32.refs_3_, ...), custom_call_target="tpu_custom_call" | custom-call | flops 2000000000 | bytes 20971520 | tf_op jit(solution)/shard_map/pallas_call | solution.py:294
  397.0 14.9 %shard_map.178 = (bf16[8,256,1280]{2,1,0:T(8,128)(2,1)}, bf16[160,2048]{1,0:T(8,128)(2,1)}, bf16[480,2048]{1,0:T(8,128)(2,1)}, f32[8,128]{1,0:T(8,128)}) custom-call(s32[1]{0:T(128)} %bitcast.rank_ref, bf16[3,480,1280]{2,1,0:T(8,128)(2,1)} %bitcast.329, f32[8,256,1280]{2,1,0:T(8,128)} %get-tuple-element.356.refs_1_, f32[8,128]{1,0:T(8,128)} %get-tuple-element.248.refs_2_), custom_call_target="tpu_custom_call" | custom-call | flops 2852126720 | bytes 7868416 | tf_op jit(solution)/shard_map/pallas_call | solution.py:93
  412.0 12.2 %shard_map.179 = (bf16[8,256,640]{2,1,0:T(8,128)(2,1)}, bf16[4,256,640]{2,1,0:T(8,128)(2,1)}, bf16[4,256,640]{2,1,0:T(8,128)(2,1)}, f32[8,128]{1,0:T(8,128)}) custom-call(s32[1]{0:T(128)} %bitcast.rank_ref, bf16[8,256,1280]{2,1,0:T(8,128)(2,1)} %all-gather.16.cloned.1.call-done.refs_0_, bf16[3,640,1280]{2,1,0:T(8,128)(2,1)} %refs_1_.19, ...), custom_call_target="tpu_custom_call" | custom-call | flops 5033164800 | bytes 2623488 | tf_op jit(solution)/shard_map/pallas_call | solution.py:93
  424.7 12.2 %shard_map.180 = (bf16[8,256,640]{2,1,0:T(8,128)(2,1)}, bf16[4,256,640]{2,1,0:T(8,128)(2,1)}, bf16[4,256,640]{2,1,0:T(8,128)(2,1)}, f32[8,128]{1,0:T(8,128)}) custom-call(s32[1]{0:T(128)} %bitcast.rank_ref, bf16[8,256,1280]{2,1,0:T(8,128)(2,1)} %all-gather.16.cloned.1.call-done.refs_0_, ...), custom_call_target="tpu_custom_call", output_to_operand_aliasing={{0}: (7, {})} | custom-call | flops 5033164800 | bytes 2623488 | tf_op jit(solution)/shard_map/pallas_call | solution.py:93
  444.5 9.0 %shard_map.181 = (f32[3,1280,640]{2,1,0:T(8,128)}, f32[8,128]{1,0:T(8,128)}) custom-call(bf16[2048,1280]{1,0:T(8,128)(2,1)} %bitcast.347, bf16[2048,640]{1,0:T(8,128)(2,1)} %bitcast.357, f32[3,1280,640]{2,1,0:T(8,128)} %get-tuple-element.261.refs_2_, f32[8,128]{1,0:T(8,128)} %get-tuple-element.262.refs_3_, ...), custom_call_target="tpu_custom_call", output_to_operand_aliasing={{0}: (2, {})} | custom-call | flops 3355443200 | bytes 17367040 | tf_op jit(solution)/shard_map/pallas_call | solution.py:358
  453.4 3.3 collective-permute-done.40
  457.7 2.3 collective-permute-start.42
  460.4 6.7 collective-permute-done.42
  470.6 2.5 fusion.64
  475.9 9.4 %shard_map.182 = (f32[3,640,1280]{2,1,0:T(8,128)}, f32[8,128]{1,0:T(8,128)}) custom-call(bf16[2048,640]{1,0:T(8,128)(2,1)} %bitcast.346, bf16[2048,1280]{1,0:T(8,128)(2,1)} %bitcast.341, f32[3,640,1280]{2,1,0:T(8,128)} %get-tuple-element.270.refs_2_, f32[8,128]{1,0:T(8,128)} %get-tuple-element.265.refs_3_, ...), custom_call_target="tpu_custom_call", output_to_operand_aliasing={{0}: (2, {})} | custom-call | flops 3355443200 | bytes 17367040 | tf_op jit(solution)/shard_map/pallas_call | solution.py:358
  485.3 9.2 %shard_map.183 = (f32[3,1280,640]{2,1,0:T(8,128)}, f32[8,128]{1,0:T(8,128)}) custom-call(bf16[2048,1280]{1,0:T(8,128)(2,1)} %bitcast.348, bf16[2048,640]{1,0:T(8,128)(2,1)} %bitcast.345, f32[3,1280,640]{2,1,0:T(8,128)} %get-tuple-element.272.refs_2_, f32[8,128]{1,0:T(8,128)} %get-tuple-element.273.refs_3_), custom_call_target="tpu_custom_call", output_to_operand_aliasing={{0}: (2, {})} | custom-call | flops 3355443200 | bytes 17367040 | tf_op jit(solution)/shard_map/pallas_call | solution.py:358
  494.5 8.8 %shard_map.184 = (f32[3,640,1280]{2,1,0:T(8,128)}, f32[8,128]{1,0:T(8,128)}) custom-call(bf16[2048,640]{1,0:T(8,128)(2,1)} %bitcast.367, bf16[2048,1280]{1,0:T(8,128)(2,1)} %bitcast.349, f32[3,640,1280]{2,1,0:T(8,128)} %get-tuple-element.271.refs_2_, f32[8,128]{1,0:T(8,128)} %get-tuple-element.274.refs_3_), custom_call_target="tpu_custom_call", output_to_operand_aliasing={{0}: (2, {})} | custom-call | flops 3355443200 | bytes 17367040 | tf_op jit(solution)/shard_map/pallas_call | solution.py:358
  503.3 6.1 all-gather.18.cloned.1.call-done.refs_3_
  509.5 11.1 %shard_map.185 = (bf16[480,2048]{1,0:T(8,128)(2,1)}, bf16[4,256,640]{2,1,0:T(8,128)(2,1)}, bf16[4,256,640]{2,1,0:T(8,128)(2,1)}, f32[8,128]{1,0:T(8,128)}) custom-call(s32[1]{0:T(128)} %bitcast.rank_ref, bf16[3,480,1280]{2,1,0:T(8,128)(2,1)} %bitcast.330, bf16[480,2048]{1,0:T(8,128)(2,1)} %get-tuple-element.250.refs_1_, bf16[3,160,1280]{2,1,0:T(8,128)(2,1)} %bitcast.338, ...), custom_call_target="tpu_custom_call" | custom-call | flops 2097152000 | bytes 2295808 | tf_op jit(solution)/shard_map/pallas_call | solution.py:93
  521.1 11.1 %shard_map.186 = (bf16[480,2048]{1,0:T(8,128)(2,1)}, bf16[4,256,640]{2,1,0:T(8,128)(2,1)}, bf16[4,256,640]{2,1,0:T(8,128)(2,1)}, f32[8,128]{1,0:T(8,128)}) custom-call(s32[1]{0:T(128)} %bitcast.rank_ref, bf16[3,480,1280]{2,1,0:T(8,128)(2,1)} %bitcast.331, bf16[480,2048]{1,0:T(8,128)(2,1)} %get-tuple-element.250.refs_1_, ...), custom_call_target="tpu_custom_call", output_to_operand_aliasing={{0}: (5, {})} | custom-call | flops 2097152000 | bytes 2295808 | tf_op jit(solution)/shard_map/pallas_call | solution.py:93
  539.9 9.7 %shard_map.187 = (f32[3,480,1280]{2,1,0:T(8,128)}, f32[3,160,1280]{2,1,0:T(8,128)}, f32[8,128]{1,0:T(8,128)}) custom-call(bf16[480,2048]{1,0:T(8,128)(2,1)} %get-tuple-element.278.refs_0_, bf16[2048,1280]{1,0:T(8,128)(2,1)} %bitcast.359, bf16[160,2048]{1,0:T(8,128)(2,1)} %get-tuple-element.249.refs_2_, ...), custom_call_target="tpu_custom_call", output_to_operand_aliasing={{0}: (4, {}), {1}: (5, {})} | custom-call | flops 3355443200 | bytes 27852800 | tf_op jit(solution)/shard_map/pallas_call | solution.py:358
  549.7 16.9 %collective-permute-done.48 = bf16[2,256,640]{2,1,0:T(8,128)(2,1)} collective-permute-done((bf16[2,256,640]{2,1,0:T(8,128)(2,1)S(1)}, bf16[2,256,640]{2,1,0:T(8,128)(2,1)}, u32[]{:S(2)}, u32[]{:S(2)}) %collective-permute-start.48) | collective-permute-done | bytes 655392 | tf_op jit(solution)/shard_map/ppermute | solution.py:363
  566.6 3.7 collective-permute-done.47
  575.1 6.3 collective-permute-done.49
  588.4 44.6 %collective-permute-done.52.refs_2_ = f32[256,1280]{1,0:T(8,128)S(1)} collective-permute-done((f32[256,1280]{1,0:T(8,128)S(1)}, f32[256,1280]{1,0:T(8,128)S(1)}, u32[]{:S(2)}, u32[]{:S(2)}) %collective-permute-start.52) | collective-permute-done | bytes 1310752 | tf_op jit(solution)/shard_map/ppermute | solution.py:363
  634.0 2.4 collective-permute-done.54.refs_4_
  639.0 15.3 %shard_map.188 = (f32[8,256,1280]{2,1,0:T(8,128)}, f32[8,128]{1,0:T(8,128)}) custom-call(s32[1]{0:T(128)} %bitcast.rank_ref, f32[8,256,1280]{2,1,0:T(8,128)} %bitcast.356, bf16[1280,3328]{1,0:T(8,128)(2,1)} %all-gather.14.cloned.1.call-done.refs_1_.refs_2_, bf16[1280,3328]{1,0:T(8,128)(2,1)} %all-gather.14.cloned.1.call-done.refs_1_.refs_2_, ...), custom_call_target="tpu_custom_call" | custom-call | flops 6710886400 | bytes 10489856 | tf_op jit(solution)/shard_map/pallas_call | solution.py:93
  654.3 10.3 %collective-permute-done.57.refs_7_ = f32[256,640]{1,0:T(8,128)S(1)} collective-permute-done((f32[256,640]{1,0:T(8,128)}, f32[256,640]{1,0:T(8,128)S(1)}, u32[]{:S(2)}, u32[]{:S(2)}) %collective-permute-start.57) | collective-permute-done | bytes 655392 | tf_op jit(solution)/shard_map/ppermute | solution.py:363
  664.6 3.6 collective-permute-done.56.refs_6_
  670.7 9.1 %shard_map.189 = (f32[8,256,1280]{2,1,0:T(8,128)}, f32[8,128]{1,0:T(8,128)}) custom-call(s32[1]{0:T(128)} %bitcast.rank_ref, f32[256,1280]{1,0:T(8,128)} %bitcast.365, f32[256,1280]{1,0:T(8,128)} %collective-permute-done.51.refs_1_, f32[256,1280]{1,0:T(8,128)} %copy-done.12, f32[256,1280]{1,0:T(8,128)} %collective-permute-done.53.refs_3_, ...), custom_call_target="tpu_custom_call" | custom-call | flops 2000000000 | bytes 20971520 | tf_op jit(solution)/shard_map/pallas_call | solution.py:294
  679.8 8.8 %copy.57 = f32[8,256,1280]{2,1,0:T(8,128)} copy(f32[8,256,1280]{2,1,0:T(8,128)} %all-gather.20.cloned.1.call-done) | data formatting | bytes 20971520
  (289 shorter events, 117.0 us)
Async XLA Ops:
  7.2 156.9 %all-gather.8.cloned.1.call-start = ((), (), s32[]{:S(2)}) async-start(), calls=%async_computation | async-start | bytes 5898240 | tf_op jit(solution)/shard_map/all_gather | solution.py:405
  18.8 12.2 %collective-permute-start = (bf16[4,256,640]{2,1,0:T(8,128)(2,1)}, bf16[4,256,640]{2,1,0:T(8,128)(2,1)S(1)}, u32[]{:S(2)}, u32[]{:S(2)}) collective-permute-start(bf16[4,256,640]{2,1,0:T(8,128)(2,1)} %get-tuple-element.164), channel_id=1, source_target_pairs={{0,1},{1,0},{2,3},{3,2},{4,5},{5,4},{6,7},{7,6},{8,9},{9,8},{10,11... | collective-permute-start | bytes 3932168 | tf_op jit(solution)/shard_map/ppermute | solution.py:363
  19.5 13.9 %collective-permute-start.1 = (bf16[4,256,640]{2,1,0:T(8,128)(2,1)}, bf16[4,256,640]{2,1,0:T(8,128)(2,1)S(1)}, u32[]{:S(2)}, u32[]{:S(2)}) collective-permute-start(bf16[4,256,640]{2,1,0:T(8,128)(2,1)} %get-tuple-element.166), channel_id=1, source_target_pairs={{0,1},{1,0},{2,3},{3,2},{4,5},{5,4},{6,7},{7,6},{8,9},{9,8},{10,11... | collective-permute-start | bytes 3932168 | tf_op jit(solution)/shard_map/ppermute | solution.py:363
  40.4 23.2 %collective-permute-start.6 = (f32[4,256,640]{2,1,0:T(8,128)}, f32[4,256,640]{2,1,0:T(8,128)}, u32[]{:S(2)}, u32[]{:S(2)}) collective-permute-start(f32[4,256,640]{2,1,0:T(8,128)} %get-tuple-element.175), channel_id=1, source_target_pairs={{0,1},{1,0},{2,3},{3,2},{4,5},{5,4},{6,7},{7,6},{8,9},{9,8},{10,11... | collective-permute-start | bytes 7864328 | tf_op jit(solution)/shard_map/ppermute | solution.py:363
  40.9 26.7 %collective-permute-start.4 = (f32[4,256,640]{2,1,0:T(8,128)}, f32[4,256,640]{2,1,0:T(8,128)}, u32[]{:S(2)}, u32[]{:S(2)}) collective-permute-start(f32[4,256,640]{2,1,0:T(8,128)} %get-tuple-element.171), channel_id=1, source_target_pairs={{0,1},{1,0},{2,3},{3,2},{4,5},{5,4},{6,7},{7,6},{8,9},{9,8},{10,11... | collective-permute-start | bytes 7864328 | tf_op jit(solution)/shard_map/ppermute | solution.py:363
  40.9 18.0 %collective-permute-start.2 = (bf16[2,256,640]{2,1,0:T(8,128)(2,1)S(1)}, bf16[2,256,640]{2,1,0:T(8,128)(2,1)}, u32[]{:S(2)}, u32[]{:S(2)}) collective-permute-start(bf16[2,256,640]{2,1,0:T(8,128)(2,1)S(1)} %copy-done.16), channel_id=1, source_target_pairs={{0,2},{1,3},{2,0},{3,1},{4,6},{5,7},{6,4},{7,5},{8,10},{9,11},{10,... | collective-permute-start | bytes 1966088 | tf_op jit(solution)/shard_map/ppermute | solution.py:363
  43.9 16.4 %collective-permute-start.5 = (bf16[2,256,640]{2,1,0:T(8,128)(2,1)S(1)}, bf16[2,256,640]{2,1,0:T(8,128)(2,1)S(1)}, u32[]{:S(2)}, u32[]{:S(2)}) collective-permute-start(bf16[2,256,640]{2,1,0:T(8,128)(2,1)S(1)} %copy-done.17), channel_id=1, source_target_pairs={{0,4},{1,5},{2,6},{3,7},{4,0},{5,1},{6,2},{7,3},{8,12},{9,13},{10,... | collective-permute-start | bytes 1966088 | tf_op jit(solution)/shard_map/ppermute | solution.py:363
  61.5 9.2 %collective-permute-start.3 = (bf16[256,640]{1,0:T(8,128)(2,1)S(1)}, bf16[256,640]{1,0:T(8,128)(2,1)S(1)}, u32[]{:S(2)}, u32[]{:S(2)}) collective-permute-start(bf16[256,640]{1,0:T(8,128)(2,1)S(1)} %get-tuple-element.346), channel_id=1, source_target_pairs={{0,4},{1,5},{2,6},{3,7},{4,0},{5,1},{6,2},{7,3},{8,12},{9,13},{10,... | collective-permute-start | bytes 983048 | tf_op jit(solution)/shard_map/ppermute | solution.py:363
  63.1 8.9 %collective-permute-start.7 = (bf16[256,640]{1,0:T(8,128)(2,1)S(1)}, bf16[256,640]{1,0:T(8,128)(2,1)S(1)}, u32[]{:S(2)}, u32[]{:S(2)}) collective-permute-start(bf16[256,640]{1,0:T(8,128)(2,1)S(1)} %get-tuple-element.345), channel_id=1, source_target_pairs={{0,2},{1,3},{2,0},{3,1},{4,6},{5,7},{6,4},{7,5},{8,10},{9,11},{10,... | collective-permute-start | bytes 983048 | tf_op jit(solution)/shard_map/ppermute | solution.py:363
  77.4 139.3 %all-gather.10.cloned.1.call-start = ((), (), s32[]{:S(2)}) async-start(), calls=%async_computation.1 | async-start | bytes 5898240 | tf_op jit(solution)/shard_map/all_gather | solution.py:405
  77.5 47.8 %collective-permute-start.9 = (f32[2,256,640]{2,1,0:T(8,128)}, f32[2,256,640]{2,1,0:T(8,128)}, u32[]{:S(2)}, u32[]{:S(2)}) collective-permute-start(f32[2,256,640]{2,1,0:T(8,128)} %get-tuple-element.322.refs_6_), channel_id=1, source_target_pairs={{0,4},{1,5},{2,6},{3,7},{4,0},{5,1},{6,2},{7,3},{8,12},{9,13},{10,... | collective-permute-start | bytes 3932168 | tf_op jit(solution)/shard_map/ppermute | solution.py:363
  78.2 47.0 %collective-permute-start.8 = (f32[2,256,640]{2,1,0:T(8,128)}, f32[2,256,640]{2,1,0:T(8,128)}, u32[]{:S(2)}, u32[]{:S(2)}) collective-permute-start(f32[2,256,640]{2,1,0:T(8,128)} %get-tuple-element.324.refs_5_), channel_id=1, source_target_pairs={{0,2},{1,3},{2,0},{3,1},{4,6},{5,7},{6,4},{7,5},{8,10},{9,11},{10,... | collective-permute-start | bytes 3932168 | tf_op jit(solution)/shard_map/ppermute | solution.py:363
  126.4 17.7 %collective-permute-start.11 = (f32[256,640]{1,0:T(8,128)S(1)}, f32[256,640]{1,0:T(8,128)}, u32[]{:S(2)}, u32[]{:S(2)}) collective-permute-start(f32[256,640]{1,0:T(8,128)S(1)} %fusion.26.refs_3_), channel_id=1, source_target_pairs={{0,4},{1,5},{2,6},{3,7},{4,0},{5,1},{6,2},{7,3},{8,12},{9,13},{10,... | collective-permute-start | bytes 1966088 | tf_op jit(solution)/shard_map/ppermute | solution.py:363
  130.2 14.0 %collective-permute-start.12 = (f32[256,640]{1,0:T(8,128)}, f32[256,640]{1,0:T(8,128)}, u32[]{:S(2)}, u32[]{:S(2)}) collective-permute-start(f32[256,640]{1,0:T(8,128)} %fusion.24.refs_4_), channel_id=1, source_target_pairs={{0,2},{1,3},{2,0},{3,1},{4,6},{5,7},{6,4},{7,5},{8,10},{9,11},{10,... | collective-permute-start | bytes 1966088 | tf_op jit(solution)/shard_map/ppermute | solution.py:363
  149.5 223.6 %all-gather.12.cloned.1.call-start = ((), (), s32[]{:S(2)}) async-start(), calls=%async_computation.2 | async-start | bytes 5898240 | tf_op jit(solution)/shard_map/all_gather | solution.py:405
  149.6 5.2 collective-permute-start.10
  149.6 8.9 %collective-permute-start.14 = (f32[4,256,640]{2,1,0:T(8,128)}, f32[4,256,640]{2,1,0:T(8,128)S(1)}, u32[]{:S(2)}, u32[]{:S(2)}) collective-permute-start(f32[4,256,640]{2,1,0:T(8,128)} %get-tuple-element.192), channel_id=1, source_target_pairs={{0,1},{1,0},{2,3},{3,2},{4,5},{5,4},{6,7},{7,6},{8,9},{9,8},{10,11... | collective-permute-start | bytes 7864328 | tf_op jit(solution)/shard_map/ppermute | solution.py:363
  179.6 16.7 %collective-permute-start.15 = (bf16[4,256,640]{2,1,0:T(8,128)(2,1)}, bf16[4,256,640]{2,1,0:T(8,128)(2,1)}, u32[]{:S(2)}, u32[]{:S(2)}) collective-permute-start(bf16[4,256,640]{2,1,0:T(8,128)(2,1)} %get-tuple-element.200), channel_id=1, source_target_pairs={{0,1},{1,0},{2,3},{3,2},{4,5},{5,4},{6,7},{7,6},{8,9},{9,8},{10,11... | collective-permute-start | bytes 3932168 | tf_op jit(solution)/shard_map/ppermute | solution.py:363
  179.7 19.6 %collective-permute-start.16 = (bf16[4,256,640]{2,1,0:T(8,128)(2,1)}, bf16[4,256,640]{2,1,0:T(8,128)(2,1)}, u32[]{:S(2)}, u32[]{:S(2)}) collective-permute-start(bf16[4,256,640]{2,1,0:T(8,128)(2,1)} %get-tuple-element.202), channel_id=1, source_target_pairs={{0,1},{1,0},{2,3},{3,2},{4,5},{5,4},{6,7},{7,6},{8,9},{9,8},{10,11... | collective-permute-start | bytes 3932168 | tf_op jit(solution)/shard_map/ppermute | solution.py:363
  180.1 32.6 %collective-permute-start.13 = (f32[2,256,640]{2,1,0:T(8,128)S(1)}, f32[2,256,640]{2,1,0:T(8,128)}, u32[]{:S(2)}, u32[]{:S(2)}) collective-permute-start(f32[2,256,640]{2,1,0:T(8,128)S(1)} %copy-done.3), channel_id=1, source_target_pairs={{0,2},{1,3},{2,0},{3,1},{4,6},{5,7},{6,4},{7,5},{8,10},{9,11},{10,... | collective-permute-start | bytes 3932168 | tf_op jit(solution)/shard_map/ppermute | solution.py:363
  180.2 32.5 %collective-permute-start.18 = (f32[2,256,640]{2,1,0:T(8,128)}, f32[2,256,640]{2,1,0:T(8,128)}, u32[]{:S(2)}, u32[]{:S(2)}) collective-permute-start(f32[2,256,640]{2,1,0:T(8,128)} %get-tuple-element.319.refs_6_), channel_id=1, source_target_pairs={{0,4},{1,5},{2,6},{3,7},{4,0},{5,1},{6,2},{7,3},{8,12},{9,13},{10,... | collective-permute-start | bytes 3932168 | tf_op jit(solution)/shard_map/ppermute | solution.py:363
  230.9 23.5 %collective-permute-start.22 = (bf16[4,256,640]{2,1,0:T(8,128)(2,1)}, bf16[4,256,640]{2,1,0:T(8,128)(2,1)}, u32[]{:S(2)}, u32[]{:S(2)}) collective-permute-start(bf16[4,256,640]{2,1,0:T(8,128)(2,1)} %get-tuple-element.217), channel_id=1, source_target_pairs={{0,1},{1,0},{2,3},{3,2},{4,5},{5,4},{6,7},{7,6},{8,9},{9,8},{10,11... | collective-permute-start | bytes 3932168 | tf_op jit(solution)/shard_map/ppermute | solution.py:363
  230.9 18.0 %collective-permute-start.17 = (f32[256,640]{1,0:T(8,128)}, f32[256,640]{1,0:T(8,128)}, u32[]{:S(2)}, u32[]{:S(2)}) collective-permute-start(f32[256,640]{1,0:T(8,128)} %fusion.13.refs_7_), channel_id=1, source_target_pairs={{0,4},{1,5},{2,6},{3,7},{4,0},{5,1},{6,2},{7,3},{8,12},{9,13},{10,... | collective-permute-start | bytes 1966088 | tf_op jit(solution)/shard_map/ppermute | solution.py:363
  232.4 17.9 %collective-permute-start.19 = (f32[256,640]{1,0:T(8,128)S(1)}, f32[256,640]{1,0:T(8,128)}, u32[]{:S(2)}, u32[]{:S(2)}) collective-permute-start(f32[256,640]{1,0:T(8,128)S(1)} %copy-done.14), channel_id=1, source_target_pairs={{0,2},{1,3},{2,0},{3,1},{4,6},{5,7},{6,4},{7,5},{8,10},{9,11},{10,... | collective-permute-start | bytes 1966088 | tf_op jit(solution)/shard_map/ppermute | solution.py:363
  233.0 24.4 %collective-permute-start.20 = (bf16[4,256,640]{2,1,0:T(8,128)(2,1)}, bf16[4,256,640]{2,1,0:T(8,128)(2,1)}, u32[]{:S(2)}, u32[]{:S(2)}) collective-permute-start(bf16[4,256,640]{2,1,0:T(8,128)(2,1)} %get-tuple-element.212), channel_id=1, source_target_pairs={{0,1},{1,0},{2,3},{3,2},{4,5},{5,4},{6,7},{7,6},{8,9},{9,8},{10,11... | collective-permute-start | bytes 3932168 | tf_op jit(solution)/shard_map/ppermute | solution.py:363
  233.0 29.9 %collective-permute-start.24 = (bf16[2,256,640]{2,1,0:T(8,128)(2,1)}, bf16[2,256,640]{2,1,0:T(8,128)(2,1)}, u32[]{:S(2)}, u32[]{:S(2)}) collective-permute-start(bf16[2,256,640]{2,1,0:T(8,128)(2,1)} %get-tuple-element.336.refs_6_), channel_id=1, source_target_pairs={{0,4},{1,5},{2,6},{3,7},{4,0},{5,1},{6,2},{7,3},{8,12},{9,13},{10,... | collective-permute-start | bytes 1966088 | tf_op jit(solution)/shard_map/ppermute | solution.py:363
  248.9 17.8 %collective-permute-start.23 = (bf16[2,256,640]{2,1,0:T(8,128)(2,1)}, bf16[2,256,640]{2,1,0:T(8,128)(2,1)S(1)}, u32[]{:S(2)}, u32[]{:S(2)}) collective-permute-start(bf16[2,256,640]{2,1,0:T(8,128)(2,1)} %get-tuple-element.338.refs_5_), channel_id=1, source_target_pairs={{0,2},{1,3},{2,0},{3,1},{4,6},{5,7},{6,4},{7,5},{8,10},{9,11},{10,... | collective-permute-start | bytes 1966088 | tf_op jit(solution)/shard_map/ppermute | solution.py:363
  256.8 20.4 %collective-permute-start.25 = (bf16[2,256,640]{2,1,0:T(8,128)(2,1)S(1)}, bf16[2,256,640]{2,1,0:T(8,128)(2,1)}, u32[]{:S(2)}, u32[]{:S(2)}) collective-permute-start(bf16[2,256,640]{2,1,0:T(8,128)(2,1)S(1)} %get-tuple-element.334.refs_6_), channel_id=1, source_target_pairs={{0,4},{1,5},{2,6},{3,7},{4,0},{5,1},{6,2},{7,3},{8,12},{9,13},{10,... | collective-permute-start | bytes 1966088 | tf_op jit(solution)/shard_map/ppermute | solution.py:363
  259.8 20.1 %collective-permute-start.21 = (bf16[2,256,640]{2,1,0:T(8,128)(2,1)S(1)}, bf16[2,256,640]{2,1,0:T(8,128)(2,1)}, u32[]{:S(2)}, u32[]{:S(2)}) collective-permute-start(bf16[2,256,640]{2,1,0:T(8,128)(2,1)S(1)} %get-tuple-element.339.refs_5_), channel_id=1, source_target_pairs={{0,2},{1,3},{2,0},{3,1},{4,6},{5,7},{6,4},{7,5},{8,10},{9,11},{10,... | collective-permute-start | bytes 1966088 | tf_op jit(solution)/shard_map/ppermute | solution.py:363
  281.0 8.8 %collective-permute-start.28 = (bf16[256,640]{1,0:T(8,128)(2,1)S(1)}, bf16[256,640]{1,0:T(8,128)(2,1)S(1)}, u32[]{:S(2)}, u32[]{:S(2)}) collective-permute-start(bf16[256,640]{1,0:T(8,128)(2,1)S(1)} %fusion.57), channel_id=1, source_target_pairs={{0,4},{1,5},{2,6},{3,7},{4,0},{5,1},{6,2},{7,3},{8,12},{9,13},{10,... | collective-permute-start | bytes 983048 | tf_op jit(solution)/shard_map/ppermute | solution.py:363
  282.8 8.3 %collective-permute-start.29 = (bf16[256,640]{1,0:T(8,128)(2,1)S(1)}, bf16[256,640]{1,0:T(8,128)(2,1)S(1)}, u32[]{:S(2)}, u32[]{:S(2)}) collective-permute-start(bf16[256,640]{1,0:T(8,128)(2,1)S(1)} %fusion.52), channel_id=1, source_target_pairs={{0,2},{1,3},{2,0},{3,1},{4,6},{5,7},{6,4},{7,5},{8,10},{9,11},{10,... | collective-permute-start | bytes 983048 | tf_op jit(solution)/shard_map/ppermute | solution.py:363
  295.6 116.4 %all-gather.16.cloned.1.call-start = ((), (), s32[]{:S(2)}) async-start(), calls=%async_computation.4 | async-start | bytes 5898240 | tf_op jit(solution)/shard_map/all_gather | solution.py:405
  295.6 12.1 %collective-permute-start.30 = (bf16[256,640]{1,0:T(8,128)(2,1)S(1)}, bf16[256,640]{1,0:T(8,128)(2,1)S(1)}, u32[]{:S(2)}, u32[]{:S(2)}) collective-permute-start(bf16[256,640]{1,0:T(8,128)(2,1)S(1)} %copy-done.47), channel_id=1, source_target_pairs={{0,4},{1,5},{2,6},{3,7},{4,0},{5,1},{6,2},{7,3},{8,12},{9,13},{10,... | collective-permute-start | bytes 983048 | tf_op jit(solution)/shard_map/ppermute | solution.py:363
  297.4 10.4 %collective-permute-start.31 = (bf16[256,640]{1,0:T(8,128)(2,1)S(1)}, bf16[256,640]{1,0:T(8,128)(2,1)}, u32[]{:S(2)}, u32[]{:S(2)}) collective-permute-start(bf16[256,640]{1,0:T(8,128)(2,1)S(1)} %copy-done.46), channel_id=1, source_target_pairs={{0,2},{1,3},{2,0},{3,1},{4,6},{5,7},{6,4},{7,5},{8,10},{9,11},{10,... | collective-permute-start | bytes 983048 | tf_op jit(solution)/shard_map/ppermute | solution.py:363
  314.9 194.6 %all-gather.18.cloned.1.call-start = ((), (), s32[]{:S(2)}) async-start(), calls=%async_computation.5 | async-start | bytes 5898240 | tf_op jit(solution)/shard_map/all_gather | solution.py:405
  314.9 43.4 %collective-permute-start.27 = (f32[256,1280]{1,0:T(8,128)S(1)}, f32[256,1280]{1,0:T(8,128)S(1)}, u32[]{:S(2)}, u32[]{:S(2)}) collective-permute-start(f32[256,1280]{1,0:T(8,128)S(1)} %bitcast.351), channel_id=1, source_target_pairs={{0,2},{1,3},{2,0},{3,1},{4,6},{5,7},{6,4},{7,5},{8,10},{9,11},{10,... | collective-permute-start | bytes 3932168 | tf_op jit(solution)/shard_map/ppermute | solution.py:363
  316.7 43.8 %collective-permute-start.33 = (f32[256,1280]{1,0:T(8,128)S(1)}, f32[256,1280]{1,0:T(8,128)}, u32[]{:S(2)}, u32[]{:S(2)}) collective-permute-start(f32[256,1280]{1,0:T(8,128)S(1)} %bitcast.352), channel_id=1, source_target_pairs={{0,4},{1,5},{2,6},{3,7},{4,0},{5,1},{6,2},{7,3},{8,12},{9,13},{10,... | collective-permute-start | bytes 3932168 | tf_op jit(solution)/shard_map/ppermute | solution.py:363
  317.1 67.9 %collective-permute-start.26 = (f32[256,1280]{1,0:T(8,128)S(1)}, f32[256,1280]{1,0:T(8,128)}, u32[]{:S(2)}, u32[]{:S(2)}) collective-permute-start(f32[256,1280]{1,0:T(8,128)S(1)} %bitcast.353), channel_id=1, source_target_pairs={{0,1},{1,0},{2,3},{3,2},{4,5},{5,4},{6,7},{7,6},{8,9},{9,8},{10,11... | collective-permute-start | bytes 3932168 | tf_op jit(solution)/shard_map/ppermute | solution.py:363
  359.2 25.1 %collective-permute-start.36 = (f32[256,640]{1,0:T(8,128)}, f32[256,640]{1,0:T(8,128)S(1)}, u32[]{:S(2)}, u32[]{:S(2)}) collective-permute-start(f32[256,640]{1,0:T(8,128)} %slice.510), channel_id=1, source_target_pairs={{0,4},{1,5},{2,6},{3,7},{4,0},{5,1},{6,2},{7,3},{8,12},{9,13},{10,... | collective-permute-start | bytes 1966088 | tf_op jit(solution)/shard_map/ppermute | solution.py:363
  362.4 22.0 %collective-permute-start.35 = (f32[256,640]{1,0:T(8,128)}, f32[256,640]{1,0:T(8,128)}, u32[]{:S(2)}, u32[]{:S(2)}) collective-permute-start(f32[256,640]{1,0:T(8,128)} %slice.509), channel_id=1, source_target_pairs={{0,2},{1,3},{2,0},{3,1},{4,6},{5,7},{6,4},{7,5},{8,10},{9,11},{10,... | collective-permute-start | bytes 1966088 | tf_op jit(solution)/shard_map/ppermute | solution.py:363
  363.7 21.3 %collective-permute-start.34 = (f32[256,1280]{1,0:T(8,128)}, f32[256,1280]{1,0:T(8,128)}, u32[]{:S(2)}, u32[]{:S(2)}) collective-permute-start(f32[256,1280]{1,0:T(8,128)} %collective-permute-done.33.refs_4_.refs_5_), channel_id=1, source_target_pairs={{0,1},{1,0},{2,3},{3,2},{4,5},{5,4},{6,7},{7,6},{8,9},{9,8},{10,11... | collective-permute-start | bytes 3932168 | tf_op jit(solution)/shard_map/ppermute | solution.py:363
  363.7 21.2 %collective-permute-start.32 = (f32[256,1280]{1,0:T(8,128)S(1)}, f32[256,1280]{1,0:T(8,128)}, u32[]{:S(2)}, u32[]{:S(2)}) collective-permute-start(f32[256,1280]{1,0:T(8,128)S(1)} %collective-permute-done.27.refs_3_.refs_4_.refs_2_), channel_id=1, source_target_pairs={{0,1},{1,0},{2,3},{3,2},{4,5},{5,4},{6,7},{7,6},{8,9},{9,8},{10,11... | collective-permute-start | bytes 3932168 | tf_op jit(solution)/shard_map/ppermute | solution.py:363
  424.1 12.7 %collective-permute-start.39 = (bf16[4,256,640]{2,1,0:T(8,128)(2,1)}, bf16[4,256,640]{2,1,0:T(8,128)(2,1)S(1)}, u32[]{:S(2)}, u32[]{:S(2)}) collective-permute-start(bf16[4,256,640]{2,1,0:T(8,128)(2,1)} %get-tuple-element.258), channel_id=1, source_target_pairs={{0,1},{1,0},{2,3},{3,2},{4,5},{5,4},{6,7},{7,6},{8,9},{9,8},{10,11... | collective-permute-start | bytes 3932168 | tf_op jit(solution)/shard_map/ppermute | solution.py:363
  424.2 15.6 %collective-permute-start.41 = (bf16[4,256,640]{2,1,0:T(8,128)(2,1)}, bf16[4,256,640]{2,1,0:T(8,128)(2,1)S(1)}, u32[]{:S(2)}, u32[]{:S(2)}) collective-permute-start(bf16[4,256,640]{2,1,0:T(8,128)(2,1)} %get-tuple-element.264), channel_id=1, source_target_pairs={{0,1},{1,0},{2,3},{3,2},{4,5},{5,4},{6,7},{7,6},{8,9},{9,8},{10,11... | collective-permute-start | bytes 3932168 | tf_op jit(solution)/shard_map/ppermute | solution.py:363
  439.8 16.9 %collective-permute-start.40 = (bf16[2,256,640]{2,1,0:T(8,128)(2,1)S(1)}, bf16[2,256,640]{2,1,0:T(8,128)(2,1)}, u32[]{:S(2)}, u32[]{:S(2)}) collective-permute-start(bf16[2,256,640]{2,1,0:T(8,128)(2,1)S(1)} %get-tuple-element.330.refs_4_), channel_id=1, source_target_pairs={{0,2},{1,3},{2,0},{3,1},{4,6},{5,7},{6,4},{7,5},{8,10},{9,11},{10,... | collective-permute-start | bytes 1966088 | tf_op jit(solution)/shard_map/ppermute | solution.py:363
  440.7 19.4 %collective-permute-start.43 = (bf16[2,256,640]{2,1,0:T(8,128)(2,1)S(1)}, bf16[2,256,640]{2,1,0:T(8,128)(2,1)S(1)}, u32[]{:S(2)}, u32[]{:S(2)}) collective-permute-start(bf16[2,256,640]{2,1,0:T(8,128)(2,1)S(1)} %get-tuple-element.331.refs_5_), channel_id=1, source_target_pairs={{0,4},{1,5},{2,6},{3,7},{4,0},{5,1},{6,2},{7,3},{8,12},{9,13},{10,... | collective-permute-start | bytes 1966088 | tf_op jit(solution)/shard_map/ppermute | solution.py:363
  457.7 9.5 %collective-permute-start.42 = (bf16[256,640]{1,0:T(8,128)(2,1)S(1)}, bf16[256,640]{1,0:T(8,128)(2,1)S(1)}, u32[]{:S(2)}, u32[]{:S(2)}) collective-permute-start(bf16[256,640]{1,0:T(8,128)(2,1)S(1)} %fusion.43), channel_id=1, source_target_pairs={{0,4},{1,5},{2,6},{3,7},{4,0},{5,1},{6,2},{7,3},{8,12},{9,13},{10,... | collective-permute-start | bytes 983048 | tf_op jit(solution)/shard_map/ppermute | solution.py:363
  460.1 8.6 %collective-permute-start.44 = (bf16[256,640]{1,0:T(8,128)(2,1)S(1)}, bf16[256,640]{1,0:T(8,128)(2,1)S(1)}, u32[]{:S(2)}, u32[]{:S(2)}) collective-permute-start(bf16[256,640]{1,0:T(8,128)(2,1)S(1)} %fusion.40), channel_id=1, source_target_pairs={{0,2},{1,3},{2,0},{3,1},{4,6},{5,7},{6,4},{7,5},{8,10},{9,11},{10,... | collective-permute-start | bytes 983048 | tf_op jit(solution)/shard_map/ppermute | solution.py:363
  473.1 165.9 %all-gather.14.cloned.1.call-start = ((), (), s32[]{:S(2)}) async-start(), calls=%async_computation.3 | async-start | bytes 9584640 | tf_op jit(solution)/shard_map/all_gather | solution.py:405
  475.9 203.9 %all-gather.20.cloned.1.call-start = ((), (), s32[]{:S(2)}) async-start(), calls=%async_computation.6 | async-start | bytes 11796480 | tf_op jit(solution)/shard_map/all_gather | solution.py:405
  520.6 11.6 %collective-permute-start.46 = (bf16[4,256,640]{2,1,0:T(8,128)(2,1)}, bf16[4,256,640]{2,1,0:T(8,128)(2,1)S(1)}, u32[]{:S(2)}, u32[]{:S(2)}) collective-permute-start(bf16[4,256,640]{2,1,0:T(8,128)(2,1)} %get-tuple-element.286), channel_id=1, source_target_pairs={{0,1},{1,0},{2,3},{3,2},{4,5},{5,4},{6,7},{7,6},{8,9},{9,8},{10,11... | collective-permute-start | bytes 3932168 | tf_op jit(solution)/shard_map/ppermute | solution.py:363
  520.8 15.7 %collective-permute-start.45 = (bf16[4,256,640]{2,1,0:T(8,128)(2,1)}, bf16[4,256,640]{2,1,0:T(8,128)(2,1)}, u32[]{:S(2)}, u32[]{:S(2)}) collective-permute-start(bf16[4,256,640]{2,1,0:T(8,128)(2,1)} %get-tuple-element.284), channel_id=1, source_target_pairs={{0,1},{1,0},{2,3},{3,2},{4,5},{5,4},{6,7},{7,6},{8,9},{9,8},{10,11... | collective-permute-start | bytes 3932168 | tf_op jit(solution)/shard_map/ppermute | solution.py:363
  535.2 31.4 %collective-permute-start.48 = (bf16[2,256,640]{2,1,0:T(8,128)(2,1)S(1)}, bf16[2,256,640]{2,1,0:T(8,128)(2,1)}, u32[]{:S(2)}, u32[]{:S(2)}) collective-permute-start(bf16[2,256,640]{2,1,0:T(8,128)(2,1)S(1)} %get-tuple-element.326.refs_8_), channel_id=1, source_target_pairs={{0,4},{1,5},{2,6},{3,7},{4,0},{5,1},{6,2},{7,3},{8,12},{9,13},{10,... | collective-permute-start | bytes 1966088 | tf_op jit(solution)/shard_map/ppermute | solution.py:363
  538.8 31.5 %collective-permute-start.47 = (bf16[2,256,640]{2,1,0:T(8,128)(2,1)S(1)}, bf16[2,256,640]{2,1,0:T(8,128)(2,1)}, u32[]{:S(2)}, u32[]{:S(2)}) collective-permute-start(bf16[2,256,640]{2,1,0:T(8,128)(2,1)S(1)} %get-tuple-element.328.refs_7_), channel_id=1, source_target_pairs={{0,2},{1,3},{2,0},{3,1},{4,6},{5,7},{6,4},{7,5},{8,10},{9,11},{10,... | collective-permute-start | bytes 1966088 | tf_op jit(solution)/shard_map/ppermute | solution.py:363
  571.4 10.0 %collective-permute-start.49 = (bf16[256,640]{1,0:T(8,128)(2,1)S(1)}, bf16[256,640]{1,0:T(8,128)(2,1)S(1)}, u32[]{:S(2)}, u32[]{:S(2)}) collective-permute-start(bf16[256,640]{1,0:T(8,128)(2,1)S(1)} %fusion.39.refs_4_), channel_id=1, source_target_pairs={{0,4},{1,5},{2,6},{3,7},{4,0},{5,1},{6,2},{7,3},{8,12},{9,13},{10,... | collective-permute-start | bytes 983048 | tf_op jit(solution)/shard_map/ppermute | solution.py:363
  573.6 8.9 %collective-permute-start.50 = (bf16[256,640]{1,0:T(8,128)(2,1)S(1)}, bf16[256,640]{1,0:T(8,128)(2,1)S(1)}, u32[]{:S(2)}, u32[]{:S(2)}) collective-permute-start(bf16[256,640]{1,0:T(8,128)(2,1)S(1)} %fusion.37.refs_5_), channel_id=1, source_target_pairs={{0,2},{1,3},{2,0},{3,1},{4,6},{5,7},{6,4},{7,5},{8,10},{9,11},{10,... | collective-permute-start | bytes 983048 | tf_op jit(solution)/shard_map/ppermute | solution.py:363
  586.3 46.7 %collective-permute-start.52 = (f32[256,1280]{1,0:T(8,128)S(1)}, f32[256,1280]{1,0:T(8,128)S(1)}, u32[]{:S(2)}, u32[]{:S(2)}) collective-permute-start(f32[256,1280]{1,0:T(8,128)S(1)} %bitcast.362), channel_id=1, source_target_pairs={{0,2},{1,3},{2,0},{3,1},{4,6},{5,7},{6,4},{7,5},{8,10},{9,11},{10,... | collective-permute-start | bytes 3932168 | tf_op jit(solution)/shard_map/ppermute | solution.py:363
  587.8 48.6 %collective-permute-start.54 = (f32[256,1280]{1,0:T(8,128)S(1)}, f32[256,1280]{1,0:T(8,128)}, u32[]{:S(2)}, u32[]{:S(2)}) collective-permute-start(f32[256,1280]{1,0:T(8,128)S(1)} %bitcast.363), channel_id=1, source_target_pairs={{0,4},{1,5},{2,6},{3,7},{4,0},{5,1},{6,2},{7,3},{8,12},{9,13},{10,... | collective-permute-start | bytes 3932168 | tf_op jit(solution)/shard_map/ppermute | solution.py:363
  588.4 79.8 %collective-permute-start.51 = (f32[256,1280]{1,0:T(8,128)S(1)}, f32[256,1280]{1,0:T(8,128)}, u32[]{:S(2)}, u32[]{:S(2)}) collective-permute-start(f32[256,1280]{1,0:T(8,128)S(1)} %bitcast.364), channel_id=1, source_target_pairs={{0,1},{1,0},{2,3},{3,2},{4,5},{5,4},{6,7},{7,6},{8,9},{9,8},{10,11... | collective-permute-start | bytes 3932168 | tf_op jit(solution)/shard_map/ppermute | solution.py:363
  634.0 30.6 %collective-permute-start.57 = (f32[256,640]{1,0:T(8,128)}, f32[256,640]{1,0:T(8,128)S(1)}, u32[]{:S(2)}, u32[]{:S(2)}) collective-permute-start(f32[256,640]{1,0:T(8,128)} %slice.548), channel_id=1, source_target_pairs={{0,4},{1,5},{2,6},{3,7},{4,0},{5,1},{6,2},{7,3},{8,12},{9,13},{10,... | collective-permute-start | bytes 1966088 | tf_op jit(solution)/shard_map/ppermute | solution.py:363
  638.5 29.8 %collective-permute-start.56 = (f32[256,640]{1,0:T(8,128)}, f32[256,640]{1,0:T(8,128)}, u32[]{:S(2)}, u32[]{:S(2)}) collective-permute-start(f32[256,640]{1,0:T(8,128)} %slice.547), channel_id=1, source_target_pairs={{0,2},{1,3},{2,0},{3,1},{4,6},{5,7},{6,4},{7,5},{8,10},{9,11},{10,... | collective-permute-start | bytes 1966088 | tf_op jit(solution)/shard_map/ppermute | solution.py:363
  638.5 29.8 %collective-permute-start.55 = (f32[256,1280]{1,0:T(8,128)}, f32[256,1280]{1,0:T(8,128)}, u32[]{:S(2)}, u32[]{:S(2)}) collective-permute-start(f32[256,1280]{1,0:T(8,128)} %collective-permute-done.54.refs_4_), channel_id=1, source_target_pairs={{0,1},{1,0},{2,3},{3,2},{4,5},{5,4},{6,7},{7,6},{8,9},{9,8},{10,11... | collective-permute-start | bytes 3932168 | tf_op jit(solution)/shard_map/ppermute | solution.py:363
  638.5 29.8 %collective-permute-start.53 = (f32[256,1280]{1,0:T(8,128)S(1)}, f32[256,1280]{1,0:T(8,128)}, u32[]{:S(2)}, u32[]{:S(2)}) collective-permute-start(f32[256,1280]{1,0:T(8,128)S(1)} %collective-permute-done.52.refs_2_), channel_id=1, source_target_pairs={{0,1},{1,0},{2,3},{3,2},{4,5},{5,4},{6,7},{7,6},{8,9},{9,8},{10,11... | collective-permute-start | bytes 3932168 | tf_op jit(solution)/shard_map/ppermute | solution.py:363
  664.6 3.7 collective-permute-start.59
  (58 other events, 494.7 us)
Sparse Core Ops, SparseCore 0:
  77.5 55.6 all-gather.7
  149.7 38.0 all-gather.9
  295.7 51.4 all-gather.11
  348.9 46.3 all-gather.15
  473.3 36.1 all-gather.17
  511.2 65.7 all-gather.13
  586.5 89.6 all-gather.19
